TPU v7x, 128 devices: a whole 4x4x4 slice. The times are simulated.
128 devices in a mesh: band: 32 (over z, y, x_hi), grid: 4 (over x_lo, core).
Axes of the slice: x: 4 (x_hi: 2, x_lo: 2; x = x_hi * 2 + x_lo), y: 4, z: 4, core: 2. Of those that a mesh axis runs over, the one named last changes fastest.
Arguments:
- orbitals: float32 [128, 110592], P('band', 'grid'), may hold values from -6 to 6
Outputs:
- exchange_vectors: float32 [128, 110592], P('band', 'grid')
- margin: float32 [128, 128], P('grid', 'band')
All inputs are finite; a program needn't handle non-finite values.
Results may differ from a plain program's by a relative error of at most 0.00012.
Values sent between devices are 32-bit elements; how exact they have to be, the bound alone decides.
No kernel may reach another device: no remote copies, remote signals or barrier semaphores. Data moves between devices by JAX's collectives and lax.ppermute only.
A program may use at most 128 MiB of HBM per device.

v0:
```python
import math

import jax
import jax.numpy as jnp
import numpy as np
from jax import lax
from jax.experimental import pallas as pl
from jax.experimental.pallas import tpu as pltpu
from jax.sharding import PartitionSpec as P

NG = 48
NCELL = 110592
PLANE = NG * NG
SLAB = 768
QX = 12
QCELL = QX * PLANE
F32 = jnp.float32
BF16 = jnp.bfloat16
R2 = math.sqrt(0.5)
C1 = math.cos(math.pi / 8)
C3 = math.cos(3 * math.pi / 8)
S3 = math.sqrt(3.0) / 2

ORDER = [("C", b) for b in range(9)] + [("S", b) for b in range(1, 8)]
SWAPPED = [("C", 0)] + [("S", b) for b in range(1, 8)] + [("C", 8)] + [("C", b) for b in range(1, 8)]


def sixteen(order):
    u = np.arange(16)
    cols = []
    for kind, b in order:
        col = np.cos(2 * np.pi * b * u / 16) if kind == "C" else np.sin(2 * np.pi * b * u / 16)
        cols.append(col / np.linalg.norm(col))
    return np.stack(cols, 1)


def forty_eight():
    z = np.arange(NG)
    cols, freqs = [], []
    for g in range(25):
        for kind in ("C", "S") if 0 < g < 24 else ("C",):
            col = np.cos(2 * np.pi * g * z / NG) if kind == "C" else np.sin(2 * np.pi * g * z / NG)
            cols.append(col / np.linalg.norm(col))
            freqs.append(g)
    return np.stack(cols, 1), np.array(freqs)


def folded(g):
    return (g + 24) % 48 - 24


def x_basis():
    keys, freqs, norms = [], [], []
    for b in range(9):
        keys.append(("A", "C", b)); freqs.append(3 * b); norms.append(48 if b in (0, 8) else 24)
    for b in range(1, 8):
        keys.append(("A", "S", b)); freqs.append(3 * b); norms.append(24)
    for b in (0, 8):
        for t in "cs":
            keys.append((t, "C", b)); freqs.append(16 + 3 * b); norms.append(24)
    for b in range(1, 8):
        for sign in (1, -1):
            for kind in ("cos", "sin"):
                keys.append((kind, sign, b)); freqs.append(16 + 3 * sign * b); norms.append(24)
    return keys, np.array(freqs), np.array(norms)


def kernel_values():
    _, gx, nx = x_basis()
    _, gz = forty_eight()
    gy = []
    for slab in "Auv":
        for kind, b in ORDER:
            if slab == "A":
                gy.append(3 * b)
            elif b in (0, 8):
                gy.append(16 + 3 * b)
            else:
                plus = (slab == "u") == (kind == "C")
                gy.append(16 + 3 * b if plus else 16 - 3 * b)
    gy = np.array(gy)
    q = (folded(gx)[:, None, None] ** 2 + folded(gy)[None, :, None] ** 2 + folded(gz)[None, None, :] ** 2).astype(np.float64)
    kern = np.where(q > 0, 40.0 * (1.0 - np.exp(-q / 16.0)) / np.where(q > 0, q, 1.0), 0.0)
    return (kern / (3.0 * nx[:, None, None])).reshape(NG, PLANE).astype(np.float32)


def thirds():
    u = np.arange(SLAB) // NG
    rows = [np.cos(2 * np.pi * (m + u) / 3) for m in range(3)] + [np.sin(2 * np.pi * (m + u) / 3) for m in range(3)]
    return np.concatenate([np.stack(rows), np.zeros((2, SLAB))]).astype(np.float32)


def factor_tables():
    za, _ = forty_eight()
    ta, ts = sixteen(ORDER), sixteen(SWAPPED)
    tens = np.stack([np.repeat(t, NG, 0) for t in (ta, ts, ta.T, ts.T)])
    zs = np.stack([np.tile(z, (16, 1)) for z in (za, za.T)])
    hot16 = np.repeat(np.eye(16), NG, 1)
    hot48 = np.tile(np.eye(NG), (1, 16))
    return [a.astype(np.float32) for a in (tens, zs, hot16, hot48)]


def tables_kernel(tens, zs, hot16, hot48, hi, lo):
    for way in range(2):
        z = jnp.dot(zs[way], hot48[...], precision=lax.Precision.HIGHEST, preferred_element_type=F32)
        for which in range(2):
            k = way * 2 + which
            t = jnp.dot(tens[k], hot16[...], precision=lax.Precision.HIGHEST, preferred_element_type=F32)
            w = t * z
            top = w.astype(BF16)
            hi[k] = top
            lo[k] = (w - top.astype(F32)).astype(BF16)


def plane_tables():
    out = jax.ShapeDtypeStruct((4, SLAB, SLAB), BF16)
    return pl.pallas_call(
        tables_kernel, out_shape=(out, out), name="plane_tables",
        compiler_params=pltpu.CompilerParams(vmem_limit_bytes=40 << 20),
    )(*[jnp.asarray(a) for a in factor_tables()])


def t16(f):
    o = [f[u] - f[u + 8] for u in range(8)]
    e = [f[u] + f[u + 8] for u in range(8)]
    ee = [e[u] + e[u + 4] for u in range(4)]
    eo = [e[u] - e[u + 4] for u in range(4)]
    c, s = {}, {}
    p0, p1 = ee[0] + ee[2], ee[1] + ee[3]
    c[0], c[8], c[4], s[4] = p0 + p1, p0 - p1, ee[0] - ee[2], ee[1] - ee[3]
    d, a = R2 * (eo[1] - eo[3]), R2 * (eo[1] + eo[3])
    c[2], c[6], s[2], s[6] = eo[0] + d, eo[0] - d, a + eo[2], a - eo[2]
    d1, d2, d3 = (o[u] - o[8 - u] for u in (1, 2, 3))
    s1, s2, s3 = (o[u] + o[8 - u] for u in (1, 2, 3))
    d2, s2 = R2 * d2, R2 * s2
    e1, e3 = o[0] + d2, o[0] - d2
    o1, o3 = C1 * d1 + C3 * d3, C3 * d1 - C1 * d3
    c[1], c[7], c[3], c[5] = e1 + o1, e1 - o1, e3 + o3, e3 - o3
    x1, x3 = o[4] + s2, o[4] - s2
    y1, y3 = C3 * s1 + C1 * s3, C1 * s1 - C3 * s3
    s[1], s[7], s[3], s[5] = y1 + x1, y1 - x1, y3 - x3, y3 + x3
    return c, s


def t16_back(c, s):
    e1, o1, e3, o3 = c[1] + c[7], c[1] - c[7], c[3] + c[5], c[3] - c[5]
    o0, d2 = e1 + e3, R2 * (e1 - e3)
    d1, d3 = C1 * o1 + C3 * o3, C3 * o1 - C1 * o3
    y1, x1, y3, x3 = s[1] + s[7], s[1] - s[7], s[3] + s[5], s[5] - s[3]
    o4, s2 = x1 + x3, R2 * (x1 - x3)
    s1, s3 = C3 * y1 + C1 * y3, C1 * y1 - C3 * y3
    o = [o0, d1 + s1, d2 + s2, d3 + s3, o4, s3 - d3, s2 - d2, s1 - d1]
    d, a = R2 * (c[2] - c[6]), R2 * (s[2] + s[6])
    eo = [c[2] + c[6], d + a, s[2] - s[6], a - d]
    p0, p1 = c[0] + c[8], c[0] - c[8]
    ee = [p0 + c[4], p1 + s[4], p0 - c[4], p1 - s[4]]
    e = [ee[u] + eo[u] for u in range(4)] + [ee[u] - eo[u] for u in range(4)]
    return [e[u] + o[u] for u in range(8)] + [e[u] - o[u] for u in range(8)]


def convolve_x(f, table):
    keys, _, _ = x_basis()
    row = {key: k for k, key in enumerate(keys)}
    place = {(x % 3, x % 16): x for x in range(NG)}
    part = {"A": [], "c": [], "s": []}
    for u in range(16):
        f0, f1, f2 = (f[place[t, u]] for t in range(3))
        a = f1 + f2
        part["A"].append(f0 + a)
        part["c"].append(f0 - 0.5 * a)
        part["s"].append(S3 * (f1 - f2))
    c, s = t16(part["A"])
    c = {b: v * table(row["A", "C", b]) for b, v in c.items()}
    s = {b: v * table(row["A", "S", b]) for b, v in s.items()}
    back_a = t16_back(c, s)
    cc, cs = t16(part["c"])
    sc, ss = t16(part["s"])
    for b in (0, 8):
        cc[b] = cc[b] * table(row["c", "C", b])
        sc[b] = sc[b] * table(row["s", "C", b])
    for b in range(1, 8):
        p = (cc[b] - ss[b]) * table(row["cos", 1, b])
        m = (cc[b] + ss[b]) * table(row["cos", -1, b])
        cc[b], ss[b] = p + m, m - p
        p = (sc[b] + cs[b]) * table(row["sin", 1, b])
        m = (sc[b] - cs[b]) * table(row["sin", -1, b])
        sc[b], cs[b] = p + m, p - m
    back_c, back_s = t16_back(cc, cs), t16_back(sc, ss)
    out = [None] * NG
    for u in range(16):
        a, c_, s_ = back_a[u], back_c[u], S3 * back_s[u]
        h = a - 0.5 * c_
        out[place[0, u]] = a + c_
        out[place[1, u]] = h + s_
        out[place[2, u]] = h - s_
    return out


def solve_kernel(q_ref, o0, o1, o2, o3, l0, l1, l2, l3, kern, third, whi_hbm, wlo_hbm, own_out, low_out,
                 right, left, hi, lo, field, whi, wlo, sems):
    q = q_ref[0]
    copies = []
    for way in range(2):
        part = pl.ds(2 * way, 2)
        copies.append([pltpu.make_async_copy(whi_hbm.at[part], whi.at[part], sems.at[2 * way]),
                       pltpu.make_async_copy(wlo_hbm.at[part], wlo.at[part], sems.at[2 * way + 1])])
        for copy in copies[-1]:
            copy.start()
    for delta, (own, low) in enumerate(((o0, l0), (o1, l1), (o2, l2), (o3, l3))):
        base = (q ^ delta) * QX

        for x in range(QX):
            span = pl.ds(x * PLANE, PLANE)
            bands = own[:, span]
            right[base + x, 0:4, :] = bands
            right[base + x, 4:8, :] = bands
            left[base + x, 0:4, :] = jnp.broadcast_to(own[pl.ds(q, 1), span], (4, PLANE))
            left[base + x, 4:8, :] = jnp.broadcast_to(low[:, span], (4, PLANE))

    def split(rows, m, value):
        top = value.astype(BF16)
        span = slice(m * SLAB, (m + 1) * SLAB)
        hi[rows, span] = top
        lo[rows, span] = (value - top.astype(F32)).astype(BF16)

    def densities(i, carry):
        x = pl.ds(2 * i, 2)
        rows = pl.ds(pl.multiple_of(16 * i, 16), 16)
        f = []
        for m in range(3):
            span = slice(m * SLAB, (m + 1) * SLAB)
            f.append((right[x, :, span] * left[x, :, span]).reshape(16, SLAB))
        split(rows, 0, f[0] + f[1] + f[2])
        split(rows, 1, f[0] * third[0:1, :] + f[1] * third[1:2, :] + f[2] * third[2:3, :])
        split(rows, 2, f[0] * third[3:4, :] + f[1] * third[4:5, :] + f[2] * third[5:6, :])
        return carry

    lax.fori_loop(0, NG // 2, densities, 0)

    def product(m, k, cols):
        span = slice(m * SLAB, (m + 1) * SLAB)
        a, b = hi[:, span], lo[:, span]
        lhs = jnp.concatenate([a, b, a], axis=1)
        w = jnp.concatenate([whi[k, :, cols], whi[k, :, cols], wlo[k, :, cols]], axis=0)
        return jnp.dot(lhs, w, preferred_element_type=F32)

    for copy in copies[0]:
        copy.wait()
    for j in range(3):
        cols = slice(j * 256, (j + 1) * 256)
        field[:, cols] = product(0, 0, cols)
        c = product(1, 0, cols)
        s = product(2, 1, cols)
        field[:, SLAB + j * 256 : SLAB + (j + 1) * 256] = c - s
        field[:, 2 * SLAB + j * 256 : 2 * SLAB + (j + 1) * 256] = c + s

    def along_x(i, carry):
        span = pl.ds(pl.multiple_of(128 * i, 128), 128)
        f = [field[8 * x : 8 * x + 8, span] for x in range(NG)]
        out = convolve_x(f, lambda k: kern[k : k + 1, span])
        for x in range(NG):
            field[8 * x : 8 * x + 8, span] = out[x]
        return carry

    lax.fori_loop(0, PLANE // 128, along_x, 0)

    def unmix(i, carry):
        rows = pl.ds(pl.multiple_of(16 * i, 16), 16)
        u = field[rows, SLAB : 2 * SLAB]
        v = field[rows, 2 * SLAB : 3 * SLAB]
        split(rows, 0, field[rows, 0:SLAB])
        split(rows, 1, u + v)
        split(rows, 2, v - u)
        return carry

    lax.fori_loop(0, NG // 2, unmix, 0)
    for copy in copies[1]:
        copy.wait()
    for j in range(3):
        cols = slice(j * 256, (j + 1) * 256)
        for m, k in ((0, 2), (1, 2), (2, 3)):
            field[:, m * SLAB + j * 256 : m * SLAB + (j + 1) * 256] = product(m, k, cols)

    mine = (lax.broadcasted_iota(jnp.int32, (8, SLAB), 0) == q).astype(F32)

    for delta in range(4):
        base = (q ^ delta) * QX

        def finish(i, carry):
            x = base + i
            rows = pl.ds(pl.multiple_of(x * 8, 8), 8)
            a = field[rows, 0:SLAB]
            c = field[rows, SLAB : 2 * SLAB]
            s = field[rows, 2 * SLAB : 3 * SLAB]
            for m in range(3):
                span = slice(m * SLAB, (m + 1) * SLAB)
                v = a + c * third[m : m + 1, :] + s * third[3 + m : 4 + m, :]
                pr = v * right[x, :, span]
                pr = pr + pltpu.roll(pr, 6, 0)
                pr = pr + pltpu.roll(pr, 7, 0)
                po = pltpu.roll(v * left[x, :, span], 4, 0) + mine * pr[0:1, :]
                at = pl.ds(pl.multiple_of(i * PLANE + m * SLAB, SLAB), SLAB)
                own_out[delta, :, at] = -po[0:4, :]
                low_out[delta, :, at] = -pr[4:5, :]
            return carry

        lax.fori_loop(0, QX, finish, 0)


def solve_pairs(q, owns, lows, tables):
    vmem = pl.BlockSpec(memory_space=pltpu.VMEM)
    hbm = pl.BlockSpec(memory_space=pl.ANY)
    return pl.pallas_call(
        solve_kernel,
        out_shape=(jax.ShapeDtypeStruct((4, 4, QCELL), F32), jax.ShapeDtypeStruct((4, 1, QCELL), F32)),
        in_specs=[pl.BlockSpec(memory_space=pltpu.SMEM)] + [vmem] * 10 + [hbm] * 2,
        out_specs=(vmem, vmem),
        scratch_shapes=[
            pltpu.VMEM((NG, 8, PLANE), F32),
            pltpu.VMEM((NG, 8, PLANE), F32),
            pltpu.VMEM((NG * 8, PLANE), BF16),
            pltpu.VMEM((NG * 8, PLANE), BF16),
            pltpu.VMEM((NG * 8, PLANE), F32),
            pltpu.VMEM((4, SLAB, SLAB), BF16),
            pltpu.VMEM((4, SLAB, SLAB), BF16),
            pltpu.SemaphoreType.DMA((4,)),
        ],
        name="solve_pairs",
        compiler_params=pltpu.CompilerParams(vmem_limit_bytes=56 << 20),
    )(q.reshape(1), *owns, *lows, jnp.asarray(kernel_values()), jnp.asarray(thirds()), *tables)


BOTH = ("band", "grid")


def move(value, blocks, flip):
    nb, nq = lax.axis_size("band"), lax.axis_size("grid")
    pairs = [(b * nq + q, (b + blocks) % nb * nq + (q ^ flip)) for b in range(nb) for q in range(nq)]
    return lax.ppermute(value, BOTH, pairs)


def spread(fields):
    nb = lax.axis_size("band")
    pieces = fields.reshape(4, nb, QCELL // nb).transpose(1, 0, 2)
    every = lax.all_to_all(pieces, "band", 0, 0, tiled=True)
    return every.reshape(4 * nb, QCELL // nb)


def on_device(orbitals):
    q = lax.axis_index("grid").astype(jnp.int32)
    two = move(orbitals, 0, 2)
    one = move(orbitals, 0, 1)
    lows = [move(lax.dynamic_slice_in_dim(orbitals, q ^ d, 1, 0), 1, d) for d in range(4)]
    tables = plane_tables()
    three = move(two, 0, 1)
    every_orbital = spread(orbitals)
    own, low = solve_pairs(q, (orbitals, one, two, three), lows, tables)
    owed = [move(low[d], -1, d) for d in range(4)]
    across = move(jnp.stack([own[1], own[3]]), 0, 1)
    far = move(own[2] + across[1], 0, 2)
    owed_rows = jnp.concatenate(
        [sum(jnp.where(q == (g ^ d), owed[d], 0.0) for d in range(4)) for g in range(4)], axis=0
    )
    vectors = own[0] + across[0] + far + owed_rows
    every_vector = spread(vectors)
    partial = lax.dot_general(
        every_orbital, every_vector, (((1,), (1,)), ((), ())),
        precision=lax.Precision.HIGHEST, preferred_element_type=F32,
    ) / NCELL
    nb, nq = lax.axis_size("band"), lax.axis_size("grid")
    pieces = partial.reshape(nq, 32, nb, 4).transpose(2, 0, 1, 3).reshape(nb * nq, 128)
    margin = jnp.sum(lax.all_to_all(pieces, BOTH, 0, 0, tiled=True), axis=0).reshape(32, 4)
    return vectors, margin


def solution(mesh):
    return jax.shard_map(
        on_device,
        mesh=mesh,
        in_specs=(P("band", "grid"),),
        out_specs=(P("band", "grid"), P("grid", "band")),
        check_vma=False,
    )
```

profile of v0, /device:TPU:1, one launch (start us, length us, event | category | flops | bytes accessed | tf_op | source)
XLA Modules:
  0.0 141.3 jit_solution(12660089220520984132)
XLA Ops:
  0.6 2.1 %collective-permute-start.1 = (f32[4,27648]{1,0:T(4,128)}, f32[4,27648]{1,0:T(4,128)S(1)}, u32[]{:S(2)}, u32[]{:S(2)}) collective-permute-start(f32[4,27648]{1,0:T(4,128)} %o0.1), channel_id=1, source_target_pairs={{0,2},{1,3},{2,0},{3,1},{4,6},{5,7},{6,4},{7,5},{8,10},{9,11},{10,... | collective-permute-start | bytes 1327112 | tf_op jit(solution)/shard_map/ppermute | solution.py:339
  3.7 8.7 %collective-permute-done.1.o2 = f32[4,27648]{1,0:T(4,128)S(1)} collective-permute-done((f32[4,27648]{1,0:T(4,128)}, f32[4,27648]{1,0:T(4,128)S(1)}, u32[]{:S(2)}, u32[]{:S(2)}) %collective-permute-start.1) | collective-permute-done | bytes 442400 | tf_op jit(solution)/shard_map/ppermute | solution.py:339
  12.4 1.7 %collective-permute-start.2 = (f32[4,27648]{1,0:T(4,128)S(1)}, f32[4,27648]{1,0:T(4,128)}, u32[]{:S(2)}, u32[]{:S(2)}) collective-permute-start(f32[4,27648]{1,0:T(4,128)S(1)} %collective-permute-done.1.o2), channel_id=1, source_target_pairs={{0,1},{1,0},{2,3},{3,2},{4,5},{5,4},{6,7},{7,6},{8,9},{9,8},{10,11... | collective-permute-start | bytes 1327112 | tf_op jit(solution)/shard_map/ppermute | solution.py:339
  14.1 2.7 %constant_dynamic-slice_fusion = (f32[1,27648]{1,0:T(1,128)}, f32[1,27648]{1,0:T(1,128)}, f32[1,27648]{1,0:T(1,128)}, f32[1,27648]{1,0:T(1,128)S(1)}) fusion(f32[4,27648]{1,0:T(4,128)} %o0.1, s32[]{:T(128)S(6)} %select_n.89, s32[]{:T(128)S(6)} %select_n.88, s32[]{:T(128)S(6)} %select_n.87, s32[]{:T(128)S(6)} %select_n.86), kind=kLoop, calls=%fused_computation.43 | loop fusion | bytes 884752 | tf_op jit(solution)/shard_map/dynamic_slice | solution.py:353
  16.8 3.0 %collective-permute-start.3 = (f32[1,27648]{1,0:T(1,128)S(1)}, f32[1,27648]{1,0:T(1,128)S(1)}, u32[]{:S(2)}, u32[]{:S(2)}) collective-permute-start(f32[1,27648]{1,0:T(1,128)S(1)} %get-tuple-element.29), channel_id=1, source_target_pairs={{0,4},{1,5},{2,6},{3,7},{4,8},{5,9},{6,10},{7,11},{8,12},{9,13},{1... | collective-permute-start | bytes 331784 | tf_op jit(solution)/shard_map/ppermute | solution.py:339
  19.8 1.4 collective-permute-start.4
  21.2 2.5 %collective-permute-start.5 = (f32[1,27648]{1,0:T(1,128)}, f32[1,27648]{1,0:T(1,128)}, u32[]{:S(2)}, u32[]{:S(2)}) collective-permute-start(f32[1,27648]{1,0:T(1,128)} %get-tuple-element.27), channel_id=1, source_target_pairs={{0,6},{1,7},{2,4},{3,5},{4,10},{5,11},{6,8},{7,9},{8,14},{9,15},{1... | collective-permute-start | bytes 331784 | tf_op jit(solution)/shard_map/ppermute | solution.py:339
  23.7 5.5 %collective-permute-done.3.l0 = f32[1,27648]{1,0:T(1,128)S(1)} collective-permute-done((f32[1,27648]{1,0:T(1,128)S(1)}, f32[1,27648]{1,0:T(1,128)S(1)}, u32[]{:S(2)}, u32[]{:S(2)}) %collective-permute-start.3) | collective-permute-done | bytes 110624 | tf_op jit(solution)/shard_map/ppermute | solution.py:339
  29.8 1.4 reshape.34
  32.3 9.2 %all-to-all-start.1 = ((f32[32,4,864]{2,1,0:T(4,128)}), f32[32,4,864]{2,1,0:T(4,128)S(1)}, u32[]{:S(2)}, u32[]{:S(2)}) async-start(f32[32,4,864]{2,1,0:T(4,128)} %bitcast.31), calls=%async_computation.1 | async-start | bytes 917504 | tf_op jit(solution)/shard_map/all_to_all | solution.py:345
  41.6 11.4 %plane_tables.1 = (bf16[4,768,768]{2,1,0:T(8,128)(2,1)S(1)}, bf16[4,768,768]{2,1,0:T(8,128)(2,1)S(1)}) custom-call(f32[4,768,16]{2,1,0:T(8,128)S(1)} %copy-done.2, f32[2,768,48]{2,1,0:T(8,128)S(1)} %copy-done.3, f32[16,768]{1,0:T(8,128)S(1)} %copy-done.5, f32[48,768]{1,0:T(8,128)S(1)} %copy-done.4), custom_call_target="tpu_custom_call" | custom-call | tf_op jit(solution)/shard_map/plane_tables/pallas_call | solution.py:117
  53.0 2.1 %copy-done = bf16[4,768,768]{2,1,0:T(8,128)(2,1)} copy-done((bf16[4,768,768]{2,1,0:T(8,128)(2,1)}, bf16[4,768,768]{2,1,0:T(8,128)(2,1)S(1)}, u32[]{:S(2)}) %copy-start) | copy-done | bytes 4718616
  55.1 2.2 %copy-done.1 = bf16[4,768,768]{2,1,0:T(8,128)(2,1)} copy-done((bf16[4,768,768]{2,1,0:T(8,128)(2,1)}, bf16[4,768,768]{2,1,0:T(8,128)(2,1)S(1)}, u32[]{:S(2)}) %copy-start.1) | copy-done | bytes 4718616
  57.3 20.3 %solve_pairs.1 = (f32[4,4,27648]{2,1,0:T(4,128)}, f32[4,1,27648]{2,1,0:T(1,128)}) custom-call(s32[1]{0:T(128)} %bitcast.q_ref, f32[4,27648]{1,0:T(4,128)} %o0.1, f32[4,27648]{1,0:T(4,128)} %collective-permute-done.o1, f32[4,27648]{1,0:T(4,128)} %copy-done.9, f32[4,27648]{1,0:T(4,128)} %collective-permute-done.2.o3, f32[1,27648]{1,0:T(1,128)} %copy-done.10, ...), custom_call_target="tpu_custom_call" | custom-call | tf_op jit(solution)/shard_map/solve_pairs/pallas_call | solution.py:313
  79.3 7.3 %collective-permute-start.10 = (f32[1,27648]{1,0:T(1,128)S(1)}, f32[1,27648]{1,0:T(1,128)S(1)}, u32[]{:S(2)}, u32[]{:S(2)}) collective-permute-start(f32[1,27648]{1,0:T(1,128)S(1)} %get-tuple-element.25), channel_id=1, source_target_pairs={{0,125},{1,124},{2,127},{3,126},{4,1},{5,0},{6,3},{7,2},{8,5},{9,4... | collective-permute-start | bytes 331784 | tf_op jit(solution)/shard_map/ppermute | solution.py:339
  87.0 2.8 %collective-permute-start.12 = (f32[1,27648]{1,0:T(1,128)S(1)}, f32[1,27648]{1,0:T(1,128)S(1)}, u32[]{:S(2)}, u32[]{:S(2)}) collective-permute-start(f32[1,27648]{1,0:T(1,128)S(1)} %get-tuple-element.23), channel_id=1, source_target_pairs={{0,127},{1,126},{2,125},{3,124},{4,3},{5,2},{6,1},{7,0},{8,7},{9,6... | collective-permute-start | bytes 331784 | tf_op jit(solution)/shard_map/ppermute | solution.py:339
  89.9 1.3 collective-permute-start.8
  91.3 3.1 %collective-permute-done.11 = f32[1,27648]{1,0:T(1,128)S(1)} collective-permute-done((f32[1,27648]{1,0:T(1,128)S(1)}, f32[1,27648]{1,0:T(1,128)S(1)}, u32[]{:S(2)}, u32[]{:S(2)}) %collective-permute-start.11) | collective-permute-done | bytes 110624 | tf_op jit(solution)/shard_map/ppermute | solution.py:339
  94.4 3.0 %collective-permute-done.12 = f32[1,27648]{1,0:T(1,128)S(1)} collective-permute-done((f32[1,27648]{1,0:T(1,128)S(1)}, f32[1,27648]{1,0:T(1,128)S(1)}, u32[]{:S(2)}, u32[]{:S(2)}) %collective-permute-start.12) | collective-permute-done | bytes 110624 | tf_op jit(solution)/shard_map/ppermute | solution.py:339
  98.2 5.6 %collective-permute-done.8 = f32[4,27648]{1,0:T(4,128)S(1)} collective-permute-done((f32[4,27648]{1,0:T(4,128)S(1)}, f32[4,27648]{1,0:T(4,128)S(1)}, u32[]{:S(2)}, u32[]{:S(2)}) %collective-permute-start.8) | collective-permute-done | bytes 442400 | tf_op jit(solution)/shard_map/ppermute | solution.py:339
  105.9 4.9 %all-to-all-start = ((f32[32,4,864]{2,1,0:T(4,128)}), f32[32,4,864]{2,1,0:T(4,128)S(1)}, u32[]{:S(2)}, u32[]{:S(2)}) async-start(f32[32,4,864]{2,1,0:T(4,128)} %bitcast.32), calls=%async_computation | async-start | bytes 917504 | tf_op jit(solution)/shard_map/all_to_all | solution.py:345
  110.9 11.5 %all-to-all-done = f32[32,4,864]{2,1,0:T(4,128)S(1)} async-done(((f32[32,4,864]{2,1,0:T(4,128)}), f32[32,4,864]{2,1,0:T(4,128)S(1)}, u32[]{:S(2)}, u32[]{:S(2)}) %all-to-all-start) | async-done | bytes 442400 | tf_op jit(solution)/shard_map/all_to_all | solution.py:345
  124.2 1.6 %all_to_all.14 = f32[128,1,128]{2,0,1:T(8,128)S(1)} reshape(f32[32,4,32,4]{3,2,1,0:T(8,128)S(1)} %bitcast.33) | data formatting | bytes 131072 | tf_op jit(solution)/shard_map/all_to_all | solution.py:372
  125.9 14.5 %all_to_all.19 = f32[128,1,128]{2,1,0:T(1,128)S(1)} all-to-all(f32[128,1,128]{2,1,0:T(1,128)S(1)} %bitcast.34), channel_id=1, replica_groups=mesh['band'=32,'grid'=4] {'band','grid'}, dimensions={0} | all-to-all | bytes 131072 | tf_op jit(solution)/shard_map/all_to_all | solution.py:372
  (51 shorter events, 10.5 us)
Async XLA Ops:
  0.6 11.8 %collective-permute-start.1 = (f32[4,27648]{1,0:T(4,128)}, f32[4,27648]{1,0:T(4,128)S(1)}, u32[]{:S(2)}, u32[]{:S(2)}) collective-permute-start(f32[4,27648]{1,0:T(4,128)} %o0.1), channel_id=1, source_target_pairs={{0,2},{1,3},{2,0},{3,1},{4,6},{5,7},{6,4},{7,5},{8,10},{9,11},{10,... | collective-permute-start | bytes 1327112 | tf_op jit(solution)/shard_map/ppermute | solution.py:339
  2.7 54.6 %collective-permute-start = (f32[4,27648]{1,0:T(4,128)}, f32[4,27648]{1,0:T(4,128)}, u32[]{:S(2)}, u32[]{:S(2)}) collective-permute-start(f32[4,27648]{1,0:T(4,128)} %o0.1), channel_id=1, source_target_pairs={{0,1},{1,0},{2,3},{3,2},{4,5},{5,4},{6,7},{7,6},{8,9},{9,8},{10,11... | collective-permute-start | bytes 1327112 | tf_op jit(solution)/shard_map/ppermute | solution.py:339
  3.7 37.8 %copy-start.2 = (f32[4,768,16]{2,1,0:T(8,128)S(1)}, f32[4,768,16]{2,1,0:T(8,128)}, u32[]{:S(2)}) copy-start(f32[4,768,16]{2,1,0:T(8,128)} %constant.31.clone.tens) | copy-start | bytes 589828
  3.7 37.9 %copy-start.3 = (f32[2,768,48]{2,1,0:T(8,128)S(1)}, f32[2,768,48]{2,1,0:T(8,128)}, u32[]{:S(2)}) copy-start(f32[2,768,48]{2,1,0:T(8,128)} %constant.32.clone.zs) | copy-start | bytes 884740
  3.7 37.9 %copy-start.4 = (f32[48,768]{1,0:T(8,128)S(1)}, f32[48,768]{1,0:T(8,128)}, u32[]{:S(2)}) copy-start(f32[48,768]{1,0:T(8,128)} %constant.34.clone.hot48) | copy-start | bytes 442372
  3.7 37.9 %copy-start.5 = (f32[16,768]{1,0:T(8,128)S(1)}, f32[16,768]{1,0:T(8,128)}, u32[]{:S(2)}) copy-start(f32[16,768]{1,0:T(8,128)} %constant.33.clone.hot16) | copy-start | bytes 147460
  12.4 19.9 %copy-start.9 = (f32[4,27648]{1,0:T(4,128)}, f32[4,27648]{1,0:T(4,128)S(1)}, u32[]{:S(2)}) copy-start(f32[4,27648]{1,0:T(4,128)S(1)} %collective-permute-done.1.o2) | copy-start | bytes 1327108
  12.4 44.9 %collective-permute-start.2 = (f32[4,27648]{1,0:T(4,128)S(1)}, f32[4,27648]{1,0:T(4,128)}, u32[]{:S(2)}, u32[]{:S(2)}) collective-permute-start(f32[4,27648]{1,0:T(4,128)S(1)} %collective-permute-done.1.o2), channel_id=1, source_target_pairs={{0,1},{1,0},{2,3},{3,2},{4,5},{5,4},{6,7},{7,6},{8,9},{9,8},{10,11... | collective-permute-start | bytes 1327112 | tf_op jit(solution)/shard_map/ppermute | solution.py:339
  16.8 12.3 %collective-permute-start.3 = (f32[1,27648]{1,0:T(1,128)S(1)}, f32[1,27648]{1,0:T(1,128)S(1)}, u32[]{:S(2)}, u32[]{:S(2)}) collective-permute-start(f32[1,27648]{1,0:T(1,128)S(1)} %get-tuple-element.29), channel_id=1, source_target_pairs={{0,4},{1,5},{2,6},{3,7},{4,8},{5,9},{6,10},{7,11},{8,12},{9,13},{1... | collective-permute-start | bytes 331784 | tf_op jit(solution)/shard_map/ppermute | solution.py:339
  19.8 37.5 %collective-permute-start.4 = (f32[1,27648]{1,0:T(1,128)}, f32[1,27648]{1,0:T(1,128)}, u32[]{:S(2)}, u32[]{:S(2)}) collective-permute-start(f32[1,27648]{1,0:T(1,128)} %get-tuple-element.28), channel_id=1, source_target_pairs={{0,5},{1,4},{2,7},{3,6},{4,9},{5,8},{6,11},{7,10},{8,13},{9,12},{1... | collective-permute-start | bytes 331784 | tf_op jit(solution)/shard_map/ppermute | solution.py:339
  21.2 36.1 %collective-permute-start.5 = (f32[1,27648]{1,0:T(1,128)}, f32[1,27648]{1,0:T(1,128)}, u32[]{:S(2)}, u32[]{:S(2)}) collective-permute-start(f32[1,27648]{1,0:T(1,128)} %get-tuple-element.27), channel_id=1, source_target_pairs={{0,6},{1,7},{2,4},{3,5},{4,10},{5,11},{6,8},{7,9},{8,14},{9,15},{1... | collective-permute-start | bytes 331784 | tf_op jit(solution)/shard_map/ppermute | solution.py:339
  29.8 27.5 %collective-permute-start.6 = (f32[1,27648]{1,0:T(1,128)}, f32[1,27648]{1,0:T(1,128)}, u32[]{:S(2)}, u32[]{:S(2)}) collective-permute-start(f32[1,27648]{1,0:T(1,128)} %get-tuple-element.26), channel_id=1, source_target_pairs={{0,7},{1,6},{2,5},{3,4},{4,11},{5,10},{6,9},{7,8},{8,15},{9,14},{1... | collective-permute-start | bytes 331784 | tf_op jit(solution)/shard_map/ppermute | solution.py:339
  32.3 73.6 %all-to-all-start.1 = ((f32[32,4,864]{2,1,0:T(4,128)}), f32[32,4,864]{2,1,0:T(4,128)S(1)}, u32[]{:S(2)}, u32[]{:S(2)}) async-start(f32[32,4,864]{2,1,0:T(4,128)} %bitcast.31), calls=%async_computation.1 | async-start | bytes 917504 | tf_op jit(solution)/shard_map/all_to_all | solution.py:345
  53.0 2.2 %copy-start = (bf16[4,768,768]{2,1,0:T(8,128)(2,1)}, bf16[4,768,768]{2,1,0:T(8,128)(2,1)S(1)}, u32[]{:S(2)}) copy-start(bf16[4,768,768]{2,1,0:T(8,128)(2,1)S(1)} %get-tuple-element.6.whi_hbm) | copy-start | bytes 14155780
  55.1 2.2 %copy-start.1 = (bf16[4,768,768]{2,1,0:T(8,128)(2,1)}, bf16[4,768,768]{2,1,0:T(8,128)(2,1)S(1)}, u32[]{:S(2)}) copy-start(bf16[4,768,768]{2,1,0:T(8,128)(2,1)S(1)} %get-tuple-element.7.wlo_hbm) | copy-start | bytes 14155780
  79.0 10.9 %copy-start.6 = (f32[4,4,27648]{2,1,0:T(4,128)S(1)}, f32[4,4,27648]{2,1,0:T(4,128)}, u32[]{:S(2)}) copy-start(f32[4,4,27648]{2,1,0:T(4,128)} %get-tuple-element.8) | copy-start | bytes 5308420
  79.2 10.6 %collective-permute-start.7 = (f32[2,4,27648]{2,1,0:T(4,128)S(1)}, f32[2,4,27648]{2,1,0:T(4,128)S(1)}, u32[]{:S(2)}, u32[]{:S(2)}) collective-permute-start(f32[2,4,27648]{2,1,0:T(4,128)S(1)} %pad_maximum_fusion), channel_id=1, source_target_pairs={{0,1},{1,0},{2,3},{3,2},{4,5},{5,4},{6,7},{7,6},{8,9},{9,8},{10,11... | collective-permute-start | bytes 2654216 | tf_op jit(solution)/shard_map/ppermute | solution.py:339
  79.3 11.9 %collective-permute-start.10 = (f32[1,27648]{1,0:T(1,128)S(1)}, f32[1,27648]{1,0:T(1,128)S(1)}, u32[]{:S(2)}, u32[]{:S(2)}) collective-permute-start(f32[1,27648]{1,0:T(1,128)S(1)} %get-tuple-element.25), channel_id=1, source_target_pairs={{0,125},{1,124},{2,127},{3,126},{4,1},{5,0},{6,3},{7,2},{8,5},{9,4... | collective-permute-start | bytes 331784 | tf_op jit(solution)/shard_map/ppermute | solution.py:339
  86.6 7.8 %collective-permute-start.11 = (f32[1,27648]{1,0:T(1,128)S(1)}, f32[1,27648]{1,0:T(1,128)S(1)}, u32[]{:S(2)}, u32[]{:S(2)}) collective-permute-start(f32[1,27648]{1,0:T(1,128)S(1)} %get-tuple-element.24), channel_id=1, source_target_pairs={{0,126},{1,127},{2,124},{3,125},{4,2},{5,3},{6,0},{7,1},{8,6},{9,7... | collective-permute-start | bytes 331784 | tf_op jit(solution)/shard_map/ppermute | solution.py:339
  87.0 10.3 %collective-permute-start.12 = (f32[1,27648]{1,0:T(1,128)S(1)}, f32[1,27648]{1,0:T(1,128)S(1)}, u32[]{:S(2)}, u32[]{:S(2)}) collective-permute-start(f32[1,27648]{1,0:T(1,128)S(1)} %get-tuple-element.23), channel_id=1, source_target_pairs={{0,127},{1,126},{2,125},{3,124},{4,3},{5,2},{6,1},{7,0},{8,7},{9,6... | collective-permute-start | bytes 331784 | tf_op jit(solution)/shard_map/ppermute | solution.py:339
  89.8 7.6 %collective-permute-start.9 = (f32[1,27648]{1,0:T(1,128)S(1)}, f32[1,27648]{1,0:T(1,128)S(1)}, u32[]{:S(2)}, u32[]{:S(2)}) collective-permute-start(f32[1,27648]{1,0:T(1,128)S(1)} %get-tuple-element.22), channel_id=1, source_target_pairs={{0,124},{1,125},{2,126},{3,127},{4,0},{5,1},{6,2},{7,3},{8,4},{9,5... | collective-permute-start | bytes 331784 | tf_op jit(solution)/shard_map/ppermute | solution.py:339
  89.9 13.9 %collective-permute-start.8 = (f32[4,27648]{1,0:T(4,128)S(1)}, f32[4,27648]{1,0:T(4,128)S(1)}, u32[]{:S(2)}, u32[]{:S(2)}) collective-permute-start(f32[4,27648]{1,0:T(4,128)S(1)} %fusion.1), channel_id=1, source_target_pairs={{0,2},{1,3},{2,0},{3,1},{4,6},{5,7},{6,4},{7,5},{8,10},{9,11},{10,... | collective-permute-start | bytes 1327112 | tf_op jit(solution)/shard_map/ppermute | solution.py:339
  104.4 6.5 %copy-start.7 = (f32[4,27648]{1,0:T(4,128)}, f32[4,27648]{1,0:T(4,128)S(1)}, u32[]{:S(2)}) copy-start(f32[4,27648]{1,0:T(4,128)S(1)} %fusion.4) | copy-start | bytes 1327108
  105.9 16.6 %all-to-all-start = ((f32[32,4,864]{2,1,0:T(4,128)}), f32[32,4,864]{2,1,0:T(4,128)S(1)}, u32[]{:S(2)}, u32[]{:S(2)}) async-start(f32[32,4,864]{2,1,0:T(4,128)} %bitcast.32), calls=%async_computation | async-start | bytes 917504 | tf_op jit(solution)/shard_map/all_to_all | solution.py:345
  (2 other events, 2.2 us)
where the time goes:
time: 142 us; the launch traced here: 141 us
  starting transfers between devices  37.6 us (26%)
  waiting for transfers between devices  37.5 us (26%)
  Pallas kernels  31.7 us (22%)
  local copies, waits for them, and re-layouts  16.7 us (12%)
  blocking collectives  14.5 us (10%)
  other arithmetic  1.82 us (1%)
    ppermute x13, waiting for transfers between devices, move(): return lax.ppermute(value, BOTH, pairs)  25.9 us
    ppermute x13, starting transfers between devices, move(): return lax.ppermute(value, BOTH, pairs)  23.5 us
    pallas_call x1, Pallas kernels, solve_pairs(): pl.pallas_call(solve_kernel, out_shape=(jax.ShapeDtypeStruct((4, 4, QCELL...  20.3 us
    all_to_all x1, blocking collectives, on_device(): lax.all_to_all(pieces, BOTH, 0, 0, tiled=True)  14.5 us
    all_to_all x2, starting transfers between devices, spread(): every = lax.all_to_all(pieces, 'band', 0, 0, tiled=True)  14.1 us
    all_to_all x2, waiting for transfers between devices, spread(): every = lax.all_to_all(pieces, 'band', 0, 0, tiled=True)  11.5 us
    pallas_call x1, Pallas kernels, plane_tables(): pl.pallas_call(tables_kernel, out_shape=(out, out), name='plane_tables',...  11.4 us
    unnamed x23, local copies, waits for them, and re-layouts  5.67 us
  transfers between devices with their start and end apart: 15, of which 6 were waited for; matrix products, arithmetic and copies ran while one was open for 7% of the time, Pallas kernels for 22%

commit v1 on v0

--- a/solution.py
+++ b/solution.py
@@ -93,30 +93,32 @@
 def factor_tables():
     za, _ = forty_eight()
     ta, ts = sixteen(ORDER), sixteen(SWAPPED)
-    tens = np.stack([np.repeat(t, NG, 0) for t in (ta, ts, ta.T, ts.T)])
-    zs = np.stack([np.tile(z, (16, 1)) for z in (za, za.T)])
-    hot16 = np.repeat(np.eye(16), NG, 1)
-    hot48 = np.tile(np.eye(NG), (1, 16))
-    return [a.astype(np.float32) for a in (tens, zs, hot16, hot48)]
-
-
-def tables_kernel(tens, zs, hot16, hot48, hi, lo):
+    tens = np.stack([np.repeat(t, NG, 1) for t in (ta, ts, ta.T, ts.T)])
+    zs = np.stack([np.tile(z, (1, 16)) for z in (za, za.T)])
+    return [a.astype(np.float32) for a in (tens, zs)]
+
+
+def tables_kernel(tens, zs, hi, lo):
     for way in range(2):
-        z = jnp.dot(zs[way], hot48[...], precision=lax.Precision.HIGHEST, preferred_element_type=F32)
         for which in range(2):
             k = way * 2 + which
-            t = jnp.dot(tens[k], hot16[...], precision=lax.Precision.HIGHEST, preferred_element_type=F32)
-            w = t * z
-            top = w.astype(BF16)
-            hi[k] = top
-            lo[k] = (w - top.astype(F32)).astype(BF16)
+
+            def block(u, carry):
+                w = zs[way] * tens[k, pl.ds(u, 1), :]
+                top = w.astype(BF16)
+                rows = pl.ds(pl.multiple_of(u * NG, 16), NG)
+                hi[k, rows, :] = top
+                lo[k, rows, :] = (w - top.astype(F32)).astype(BF16)
+                return carry
+
+            lax.fori_loop(0, 16, block, 0)
 
 
 def plane_tables():
     out = jax.ShapeDtypeStruct((4, SLAB, SLAB), BF16)
     return pl.pallas_call(
         tables_kernel, out_shape=(out, out), name="plane_tables",
-        compiler_params=pltpu.CompilerParams(vmem_limit_bytes=40 << 20),
+        compiler_params=pltpu.CompilerParams(vmem_limit_bytes=16 << 20),
     )(*[jnp.asarray(a) for a in factor_tables()])
 
 
@@ -196,26 +198,22 @@
     return out
 
 
-def solve_kernel(q_ref, o0, o1, o2, o3, l0, l1, l2, l3, kern, third, whi_hbm, wlo_hbm, own_out, low_out,
-                 right, left, hi, lo, field, whi, wlo, sems):
+def solve_kernel(q_ref, o0, o1, o2, o3, l0, l1, l2, l3, kern, third, whi, wlo, near0, near2, cross, low0, low1, low2, low3,
+                 right, left, hi, lo, field):
     q = q_ref[0]
-    copies = []
-    for way in range(2):
-        part = pl.ds(2 * way, 2)
-        copies.append([pltpu.make_async_copy(whi_hbm.at[part], whi.at[part], sems.at[2 * way]),
-                       pltpu.make_async_copy(wlo_hbm.at[part], wlo.at[part], sems.at[2 * way + 1])])
-        for copy in copies[-1]:
-            copy.start()
     for delta, (own, low) in enumerate(((o0, l0), (o1, l1), (o2, l2), (o3, l3))):
         base = (q ^ delta) * QX
 
-        for x in range(QX):
-            span = pl.ds(x * PLANE, PLANE)
+        def place(x, carry):
+            span = pl.ds(pl.multiple_of(x * PLANE, 128), PLANE)
             bands = own[:, span]
             right[base + x, 0:4, :] = bands
             right[base + x, 4:8, :] = bands
             left[base + x, 0:4, :] = jnp.broadcast_to(own[pl.ds(q, 1), span], (4, PLANE))
             left[base + x, 4:8, :] = jnp.broadcast_to(low[:, span], (4, PLANE))
+            return carry
+
+        lax.fori_loop(0, QX, place, 0)
 
     def split(rows, m, value):
         top = value.astype(BF16)
@@ -244,8 +242,6 @@
         w = jnp.concatenate([whi[k, :, cols], whi[k, :, cols], wlo[k, :, cols]], axis=0)
         return jnp.dot(lhs, w, preferred_element_type=F32)
 
-    for copy in copies[0]:
-        copy.wait()
     for j in range(3):
         cols = slice(j * 256, (j + 1) * 256)
         field[:, cols] = product(0, 0, cols)
@@ -274,8 +270,6 @@
         return carry
 
     lax.fori_loop(0, NG // 2, unmix, 0)
-    for copy in copies[1]:
-        copy.wait()
     for j in range(3):
         cols = slice(j * 256, (j + 1) * 256)
         for m, k in ((0, 2), (1, 2), (2, 3)):
@@ -300,8 +294,12 @@
                 pr = pr + pltpu.roll(pr, 7, 0)
                 po = pltpu.roll(v * left[x, :, span], 4, 0) + mine * pr[0:1, :]
                 at = pl.ds(pl.multiple_of(i * PLANE + m * SLAB, SLAB), SLAB)
-                own_out[delta, :, at] = -po[0:4, :]
-                low_out[delta, :, at] = -pr[4:5, :]
+                bands = -po[0:4, :]
+                if delta % 2:
+                    cross[delta // 2, :, at] = bands
+                else:
+                    (near0, near2)[delta // 2][:, at] = bands
+                (low0, low1, low2, low3)[delta][:, at] = -pr[4:5, :]
             return carry
 
         lax.fori_loop(0, QX, finish, 0)
@@ -309,73 +307,171 @@
 
 def solve_pairs(q, owns, lows, tables):
     vmem = pl.BlockSpec(memory_space=pltpu.VMEM)
-    hbm = pl.BlockSpec(memory_space=pl.ANY)
     return pl.pallas_call(
         solve_kernel,
-        out_shape=(jax.ShapeDtypeStruct((4, 4, QCELL), F32), jax.ShapeDtypeStruct((4, 1, QCELL), F32)),
-        in_specs=[pl.BlockSpec(memory_space=pltpu.SMEM)] + [vmem] * 10 + [hbm] * 2,
-        out_specs=(vmem, vmem),
+        out_shape=[jax.ShapeDtypeStruct(shape, F32) for shape in [(4, QCELL)] * 2 + [(2, 4, QCELL)] + [(1, QCELL)] * 4],
+        in_specs=[pl.BlockSpec(memory_space=pltpu.SMEM)] + [vmem] * 12,
+        out_specs=[vmem] * 7,
         scratch_shapes=[
             pltpu.VMEM((NG, 8, PLANE), F32),
             pltpu.VMEM((NG, 8, PLANE), F32),
             pltpu.VMEM((NG * 8, PLANE), BF16),
             pltpu.VMEM((NG * 8, PLANE), BF16),
             pltpu.VMEM((NG * 8, PLANE), F32),
-            pltpu.VMEM((4, SLAB, SLAB), BF16),
-            pltpu.VMEM((4, SLAB, SLAB), BF16),
-            pltpu.SemaphoreType.DMA((4,)),
         ],
         name="solve_pairs",
-        compiler_params=pltpu.CompilerParams(vmem_limit_bytes=56 << 20),
+        compiler_params=pltpu.CompilerParams(vmem_limit_bytes=34 << 20),
     )(q.reshape(1), *owns, *lows, jnp.asarray(kernel_values()), jnp.asarray(thirds()), *tables)
 
 
 BOTH = ("band", "grid")
-
-
-def move(value, blocks, flip):
+CHUNK = QCELL // 4
+
+
+def small_call(body, outs, scratch=()):
+    vmem = pl.BlockSpec(memory_space=pltpu.VMEM)
+
+    def call(where, *arrays):
+        return pl.pallas_call(
+            body,
+            out_shape=[jax.ShapeDtypeStruct(shape, F32) for shape in outs],
+            in_specs=[pl.BlockSpec(memory_space=pltpu.SMEM)] + [vmem] * len(arrays),
+            out_specs=[vmem] * len(outs),
+            scratch_shapes=list(scratch),
+            compiler_params=pltpu.CompilerParams(vmem_limit_bytes=24 << 20),
+        )(where, *arrays)
+
+    return call
+
+
+def chunk_of(where, k):
+    return pl.ds(pl.multiple_of(((where[1] + k) % 4) * CHUNK, 128), CHUNK)
+
+
+def prepare_kernel(where, orbitals, *outs):
+    q = where[0]
+    for d in range(4):
+        outs[d][...] = orbitals[pl.ds(q ^ d, 1), :]
+        outs[4 + d][...] = orbitals[:, chunk_of(where, d)]
+
+
+def finalize_kernel(where, near, across, far, o0, o1, o2, o3, vectors, *chunks):
+    q = where[0]
+    row = lax.broadcasted_iota(jnp.int32, (4, CHUNK), 0)
+    for c in range(4):
+        span = pl.ds(c * CHUNK, CHUNK)
+        total = near[:, span] + across[0, :, span] + far[:, span]
+        for d, owed in enumerate((o0, o1, o2, o3)):
+            total = total + jnp.where(row == (q ^ d), jnp.broadcast_to(owed[:, span], (4, CHUNK)), 0.0)
+        vectors[:, span] = total
+    for k in range(4):
+        chunks[k][...] = vectors[:, chunk_of(where, k)]
+
+
+def add_kernel(where, near, across, out):
+    out[...] = near[...] + across[1]
+
+
+def pair_kernel(where, f0, f1, f2, f3, other, out):
+    mine_first = where[3] == 0
+    for k, f in enumerate((f0, f1, f2, f3)):
+        a, b = f[...], other[k]
+        out[k, 0:4, :] = jnp.where(mine_first, a, b)
+        out[k, 4:8, :] = jnp.where(mine_first, b, a)
+
+
+def margin_kernel(where, p0, p1, p2, p3, v0, v1, v2, v3, m0, m1, m2, m3, block):
+    z, y = where[1], where[2]
+
+    def halves(a):
+        top = a.astype(BF16)
+        return top, (a - top.astype(F32)).astype(BF16)
+
+    bands = jnp.concatenate([v0[...], v1[...], v2[...], v3[...]], axis=0)
+    vt, vl = halves(bands)
+    dims = (((1,), (1,)), ((), ()))
+    for dy, part in enumerate((p0, p1, p2, p3)):
+        ft, fl = halves(part[...].reshape(32, CHUNK))
+        got = (
+            lax.dot_general(ft, vt, dims, preferred_element_type=F32)
+            + lax.dot_general(fl, vt, dims, preferred_element_type=F32)
+            + lax.dot_general(ft, vl, dims, preferred_element_type=F32)
+        )
+        for dz in range(4):
+            at = ((z + 4 - dz) % 4) * 4 + (y + 4 - dy) % 4
+            block[at, :, :] = got[8 * dz : 8 * dz + 8, :]
+    out = block[...].reshape(128, 16).T * (1.0 / NCELL)
+    for k, m in enumerate((m0, m1, m2, m3)):
+        m[...] = out[4 * k : 4 * k + 4, :]
+
+
+def move(value, target):
     nb, nq = lax.axis_size("band"), lax.axis_size("grid")
-    pairs = [(b * nq + q, (b + blocks) % nb * nq + (q ^ flip)) for b in range(nb) for q in range(nq)]
+    pairs = []
+    for b in range(nb):
+        for q in range(nq):
+            z, y, h, q_to = target(b // 8, b // 2 % 4, b % 2, q)
+            pairs.append((b * nq + q, ((z % 4) * 8 + (y % 4) * 2 + h) * nq + q_to))
     return lax.ppermute(value, BOTH, pairs)
 
 
-def spread(fields):
-    nb = lax.axis_size("band")
-    pieces = fields.reshape(4, nb, QCELL // nb).transpose(1, 0, 2)
-    every = lax.all_to_all(pieces, "band", 0, 0, tiled=True)
-    return every.reshape(4 * nb, QCELL // nb)
-
-
-def on_device(orbitals):
+def along_z(value, k):
+    return move(value, lambda z, y, h, q: (z + k, y, h, q))
+
+
+def along_y(value, k):
+    return move(value, lambda z, y, h, q: (z, y + k, h, q))
+
+
+def within(value, flip):
+    return move(value, lambda z, y, h, q: (z, y, h, q ^ flip))
+
+
+def around(value, blocks, flip):
+    def target(z, y, h, q):
+        b = (z * 8 + y * 2 + h + blocks) % 32
+        return b // 8, b // 2 % 4, b % 2, q ^ flip
+
+    return move(value, target)
+
+
+def step(orbitals):
+    b = lax.axis_index("band").astype(jnp.int32)
     q = lax.axis_index("grid").astype(jnp.int32)
-    two = move(orbitals, 0, 2)
-    one = move(orbitals, 0, 1)
-    lows = [move(lax.dynamic_slice_in_dim(orbitals, q ^ d, 1, 0), 1, d) for d in range(4)]
+    where = jnp.stack([q, b // 8, b // 2 % 4, b % 2])
+    two = within(orbitals, 2)
+    one = within(orbitals, 1)
+    prepare = small_call(prepare_kernel, [(1, QCELL)] * 4 + [(4, CHUNK)] * 4)
+    ready = prepare(where, orbitals)
+    lows = [around(ready[d], 1, d) for d in range(4)]
+    pieces = [ready[4]] + [along_z(ready[4 + k], k) for k in (1, 2, 3)]
     tables = plane_tables()
-    three = move(two, 0, 1)
-    every_orbital = spread(orbitals)
-    own, low = solve_pairs(q, (orbitals, one, two, three), lows, tables)
-    owed = [move(low[d], -1, d) for d in range(4)]
-    across = move(jnp.stack([own[1], own[3]]), 0, 1)
-    far = move(own[2] + across[1], 0, 2)
-    owed_rows = jnp.concatenate(
-        [sum(jnp.where(q == (g ^ d), owed[d], 0.0) for d in range(4)) for g in range(4)], axis=0
-    )
-    vectors = own[0] + across[0] + far + owed_rows
-    every_vector = spread(vectors)
-    partial = lax.dot_general(
-        every_orbital, every_vector, (((1,), (1,)), ((), ())),
-        precision=lax.Precision.HIGHEST, preferred_element_type=F32,
-    ) / NCELL
-    nb, nq = lax.axis_size("band"), lax.axis_size("grid")
-    pieces = partial.reshape(nq, 32, nb, 4).transpose(2, 0, 1, 3).reshape(nb * nq, 128)
-    margin = jnp.sum(lax.all_to_all(pieces, BOTH, 0, 0, tiled=True), axis=0).reshape(32, 4)
+    stacked = jnp.stack(pieces)
+    two, tables, stacked = lax.optimization_barrier((two, tables, stacked))
+    three = within(two, 1)
+    other = move(stacked, lambda z, y, h, q: (z, y, 1 - h, q))
+    near0, near2, cross, *low = solve_pairs(q, (orbitals, one, two, three), lows, tables)
+    across = within(cross, 1)
+    owed = [around(low[d], -1, d) for d in range(4)]
+    both = small_call(add_kernel, [(4, QCELL)])(where, near2, across)[0]
+    far = within(both, 2)
+    other, _ = lax.optimization_barrier((other, near0))
+    (paired,) = small_call(pair_kernel, [(4, 8, CHUNK)])(where, *pieces, other)
+    parts = [paired] + [along_y(paired, k) for k in (1, 2, 3)]
+    finalize = small_call(finalize_kernel, [(4, QCELL)] + [(4, CHUNK)] * 4)
+    vectors, *chunks = finalize(where, near0, across, far, *owed)
+    given = [chunks[0]] + [along_z(chunks[k], k) for k in (1, 2, 3)]
+    margin_part = small_call(margin_kernel, [(4, 128)] * 4, [pltpu.VMEM((16, 8, 16), F32)])
+    sums = margin_part(where, *parts, *given)
+    mine = sums[0] + sum(along_z(sums[k], -k) for k in (1, 2, 3))
+    total = mine + sum(within(mine, d) for d in (1, 2, 3))
+    margin = lax.dynamic_slice_in_dim(total, q * 32, 32, 1).T
     return vectors, margin
 
 
 def solution(mesh):
     return jax.shard_map(
-        on_device,
+        step,
         mesh=mesh,
         in_specs=(P("band", "grid"),),
         out_specs=(P("band", "grid"), P("grid", "band")),

time: 142 us -> 142 us (level)
  starting transfers between devices: 37.6 us -> 55 us
  waiting for transfers between devices: 37.5 us -> 54.3 us
  blocking collectives: 14.5 us -> 0 us
  local copies, waits for them, and re-layouts: 16.7 us -> 6.32 us
  Pallas kernels: 31.7 us -> 25.1 us
  other arithmetic: 1.82 us -> 0.19 us
    ppermute x13 -> x29, starting transfers between devices: 23.5 us -> 55 us  [move(): return lax.ppermute(value, BOTH, pairs)]
    ppermute x13 -> x29, waiting for transfers between devices: 25.9 us -> 54.3 us  [move(): return lax.ppermute(value, BOTH, pairs)]
    all_to_all x1 -> x0, blocking collectives: 14.5 us -> none  [on_device(): lax.all_to_all(pieces, BOTH, 0, 0, tiled=True)]
    all_to_all x2 -> x0, starting transfers between devices: 14.1 us -> none  [spread(): every = lax.all_to_all(pieces, 'band', 0, 0, tiled=True)]
    all_to_all x2 -> x0, waiting for transfers between devices: 11.5 us -> none  [spread(): every = lax.all_to_all(pieces, 'band', 0, 0, tiled=True)]
    pallas_call x1, Pallas kernels: 11.4 us -> 1.95 us  [plane_tables(): pl.pallas_call(tables_kernel, out_shape=(out, out), name='plane_tables',...]
    reshape x9 -> x0, local copies, waits for them, and re-layouts: 5.34 us -> none  [the longest x4 3.94 us: spread(): pieces = fields.reshape(4, nb, QCELL // nb).transpose(1, 0, 2)]
    pallas_call x1 -> x6, Pallas kernels: 20.3 us -> 23.2 us  [the longest x1 17.4 us: solve_pairs(): pl.pallas_call(solve_kernel, out_shape=[jax.ShapeDtypeStruct(shape, F32)...]
  transfers between devices with their start and end apart: 15 -> 29, of which waited for: 6 -> 17; matrix products, arithmetic and copies ran while one was open for 7% -> 0% of each run, Pallas kernels for 22% -> 4%
where the time goes in v1:
time: 142 us
  starting transfers between devices  55 us (39%)
  waiting for transfers between devices  54.3 us (38%)
  Pallas kernels  25.1 us (18%)
  local copies, waits for them, and re-layouts  6.32 us (4%)
    ppermute x29, starting transfers between devices, move(): return lax.ppermute(value, BOTH, pairs)  55 us
    ppermute x29, waiting for transfers between devices, move(): return lax.ppermute(value, BOTH, pairs)  54.3 us
    pallas_call x1, Pallas kernels, solve_pairs(): pl.pallas_call(solve_kernel, out_shape=[jax.ShapeDtypeStruct(shape, F32)...  17.4 us
    pallas_call x5, Pallas kernels, call(): pl.pallas_call(body, out_shape=[jax.ShapeDtypeStruct(shape, F32) for shap...  5.78 us
    unnamed x12, local copies, waits for them, and re-layouts  5.66 us
  transfers between devices with their start and end apart: 29, of which 17 were waited for; matrix products, arithmetic and copies ran while one was open for 0% of the time, Pallas kernels for 4%

profile of v1, /device:TPU:1, one launch (start us, length us, event | category | flops | bytes accessed | tf_op | source)
XLA Modules:
  0.0 141.7 jit_solution(17638586804574094459)
XLA Ops:
  2.4 2.5 %collective-permute-start.2 = (f32[4,6912]{1,0:T(4,128)S(1)}, f32[4,6912]{1,0:T(4,128)S(1)}, u32[]{:S(2)}, u32[]{:S(2)}) collective-permute-start(f32[4,6912]{1,0:T(4,128)S(1)} %get-tuple-element.36), channel_id=1, source_target_pairs={{0,32},{1,33},{2,34},{3,35},{4,36},{5,37},{6,38},{7,39},{8,40},{9,... | collective-permute-start | bytes 331784 | tf_op jit(solution)/shard_map/ppermute | solution.py:415
  4.9 3.3 %collective-permute-start.3 = (f32[4,6912]{1,0:T(4,128)S(1)}, f32[4,6912]{1,0:T(4,128)S(1)}, u32[]{:S(2)}, u32[]{:S(2)}) collective-permute-start(f32[4,6912]{1,0:T(4,128)S(1)} %get-tuple-element.37), channel_id=1, source_target_pairs={{0,64},{1,65},{2,66},{3,67},{4,68},{5,69},{6,70},{7,71},{8,72},{9,... | collective-permute-start | bytes 331784 | tf_op jit(solution)/shard_map/ppermute | solution.py:415
  16.0 3.2 %collective-permute-done.1.o2 = f32[4,27648]{1,0:T(4,128)S(1)} collective-permute-done((f32[4,27648]{1,0:T(4,128)S(1)}, f32[4,27648]{1,0:T(4,128)S(1)}, u32[]{:S(2)}, u32[]{:S(2)}) %collective-permute-start.1) | collective-permute-done | bytes 442400 | tf_op jit(solution)/shard_map/ppermute | solution.py:415
  19.2 2.4 %collective-permute-start.5 = (f32[4,27648]{1,0:T(4,128)S(1)}, f32[4,27648]{1,0:T(4,128)S(1)}, u32[]{:S(2)}, u32[]{:S(2)}) collective-permute-start(f32[4,27648]{1,0:T(4,128)S(1)} %collective-permute-done.1.o2), channel_id=1, source_target_pairs={{0,1},{1,0},{2,3},{3,2},{4,5},{5,4},{6,7},{7,6},{8,9},{9,8},{10,11... | collective-permute-start | bytes 1327112 | tf_op jit(solution)/shard_map/ppermute | solution.py:415
  21.5 2.7 %collective-permute-start.6 = (f32[1,27648]{1,0:T(1,128)S(1)}, f32[1,27648]{1,0:T(1,128)S(1)}, u32[]{:S(2)}, u32[]{:S(2)}) collective-permute-start(f32[1,27648]{1,0:T(1,128)S(1)} %get-tuple-element.40), channel_id=1, source_target_pairs={{0,4},{1,5},{2,6},{3,7},{4,8},{5,9},{6,10},{7,11},{8,12},{9,13},{1... | collective-permute-start | bytes 331784 | tf_op jit(solution)/shard_map/ppermute | solution.py:415
  25.7 2.5 %collective-permute-start.8 = (f32[1,27648]{1,0:T(1,128)S(1)}, f32[1,27648]{1,0:T(1,128)S(1)}, u32[]{:S(2)}, u32[]{:S(2)}) collective-permute-start(f32[1,27648]{1,0:T(1,128)S(1)} %get-tuple-element.42), channel_id=1, source_target_pairs={{0,6},{1,7},{2,4},{3,5},{4,10},{5,11},{6,8},{7,9},{8,14},{9,15},{1... | collective-permute-start | bytes 331784 | tf_op jit(solution)/shard_map/ppermute | solution.py:415
  28.2 3.7 %collective-permute-done.6.l0 = f32[1,27648]{1,0:T(1,128)S(1)} collective-permute-done((f32[1,27648]{1,0:T(1,128)S(1)}, f32[1,27648]{1,0:T(1,128)S(1)}, u32[]{:S(2)}, u32[]{:S(2)}) %collective-permute-start.6) | collective-permute-done | bytes 110624 | tf_op jit(solution)/shard_map/ppermute | solution.py:415
  31.9 3.2 %collective-permute-done.7.l1 = f32[1,27648]{1,0:T(1,128)S(1)} collective-permute-done((f32[1,27648]{1,0:T(1,128)S(1)}, f32[1,27648]{1,0:T(1,128)S(1)}, u32[]{:S(2)}, u32[]{:S(2)}) %collective-permute-start.7) | collective-permute-done | bytes 110624 | tf_op jit(solution)/shard_map/ppermute | solution.py:415
  35.1 2.5 %collective-permute-done.8.l2 = f32[1,27648]{1,0:T(1,128)S(1)} collective-permute-done((f32[1,27648]{1,0:T(1,128)S(1)}, f32[1,27648]{1,0:T(1,128)S(1)}, u32[]{:S(2)}, u32[]{:S(2)}) %collective-permute-start.8) | collective-permute-done | bytes 110624 | tf_op jit(solution)/shard_map/ppermute | solution.py:415
  37.6 5.2 %collective-permute-done.9.l3 = f32[1,27648]{1,0:T(1,128)S(1)} collective-permute-done((f32[1,27648]{1,0:T(1,128)S(1)}, f32[1,27648]{1,0:T(1,128)S(1)}, u32[]{:S(2)}, u32[]{:S(2)}) %collective-permute-start.9) | collective-permute-done | bytes 110624 | tf_op jit(solution)/shard_map/ppermute | solution.py:415
  45.6 17.4 %solve_pairs.1 = (f32[4,27648]{1,0:T(4,128)S(1)}, f32[4,27648]{1,0:T(4,128)S(1)}, f32[2,4,27648]{2,1,0:T(4,128)S(1)}, f32[1,27648]{1,0:T(1,128)S(1)}, f32[1,2764...) custom-call(s32[1]{0:T(128)} %bitcast.q_ref, f32[4,27648]{1,0:T(4,128)S(1)} %copy-done.1, ...), custom_call_target="tpu_custom_call" | custom-call | tf_op jit(solution)/shard_map/solve_pairs/pallas_call | solution.py:310
  63.6 13.1 %collective-permute-done.16.other = f32[4,4,6912]{2,1,0:T(4,128)S(1)} collective-permute-done((f32[4,4,6912]{2,1,0:T(4,128)S(1)}, f32[4,4,6912]{2,1,0:T(4,128)S(1)}, u32[]{:S(2)}, u32[]{:S(2)}) %collective-permute-start.16) | collective-permute-done | bytes 442400 | tf_op jit(solution)/shard_map/ppermute | solution.py:415
  77.6 2.6 %collective-permute-start.19 = (f32[4,8,6912]{2,1,0:T(8,128)S(1)}, f32[4,8,6912]{2,1,0:T(8,128)S(1)}, u32[]{:S(2)}, u32[]{:S(2)}) collective-permute-start(f32[4,8,6912]{2,1,0:T(8,128)S(1)} %shard_map.71.p0), channel_id=1, source_target_pairs={{0,24},{1,25},{2,26},{3,27},{4,28},{5,29},{6,30},{7,31},{8,0},{9,1... | collective-permute-start | bytes 2654216 | tf_op jit(solution)/shard_map/ppermute | solution.py:415
  80.9 4.4 %collective-permute-done.12.o0 = f32[1,27648]{1,0:T(1,128)S(1)} collective-permute-done((f32[1,27648]{1,0:T(1,128)S(1)}, f32[1,27648]{1,0:T(1,128)S(1)}, u32[]{:S(2)}, u32[]{:S(2)}) %collective-permute-start.12) | collective-permute-done | bytes 110624 | tf_op jit(solution)/shard_map/ppermute | solution.py:415
  85.3 8.2 %collective-permute-start.13 = (f32[1,27648]{1,0:T(1,128)S(1)}, f32[1,27648]{1,0:T(1,128)S(1)}, u32[]{:S(2)}, u32[]{:S(2)}) collective-permute-start(f32[1,27648]{1,0:T(1,128)S(1)} %get-tuple-element.50), channel_id=1, source_target_pairs={{0,125},{1,124},{2,127},{3,126},{4,1},{5,0},{6,3},{7,2},{8,5},{9,4... | collective-permute-start | bytes 331784 | tf_op jit(solution)/shard_map/ppermute | solution.py:415
  93.5 5.2 %collective-permute-done.13.o1 = f32[1,27648]{1,0:T(1,128)S(1)} collective-permute-done((f32[1,27648]{1,0:T(1,128)S(1)}, f32[1,27648]{1,0:T(1,128)S(1)}, u32[]{:S(2)}, u32[]{:S(2)}) %collective-permute-start.13) | collective-permute-done | bytes 110624 | tf_op jit(solution)/shard_map/ppermute | solution.py:415
  98.7 4.2 %collective-permute-start.14 = (f32[1,27648]{1,0:T(1,128)S(1)}, f32[1,27648]{1,0:T(1,128)S(1)}, u32[]{:S(2)}, u32[]{:S(2)}) collective-permute-start(f32[1,27648]{1,0:T(1,128)S(1)} %get-tuple-element.51), channel_id=1, source_target_pairs={{0,126},{1,127},{2,124},{3,125},{4,2},{5,3},{6,0},{7,1},{8,6},{9,7... | collective-permute-start | bytes 331784 | tf_op jit(solution)/shard_map/ppermute | solution.py:415
  104.6 10.4 %collective-permute-start.15 = (f32[1,27648]{1,0:T(1,128)S(1)}, f32[1,27648]{1,0:T(1,128)S(1)}, u32[]{:S(2)}, u32[]{:S(2)}) collective-permute-start(f32[1,27648]{1,0:T(1,128)S(1)} %get-tuple-element.52), channel_id=1, source_target_pairs={{0,127},{1,126},{2,125},{3,124},{4,3},{5,2},{6,1},{7,0},{8,7},{9,6... | collective-permute-start | bytes 331784 | tf_op jit(solution)/shard_map/ppermute | solution.py:415
  119.1 2.4 %collective-permute-start.22 = (f32[4,6912]{1,0:T(4,128)S(1)}, f32[4,6912]{1,0:T(4,128)S(1)}, u32[]{:S(2)}, u32[]{:S(2)}) collective-permute-start(f32[4,6912]{1,0:T(4,128)S(1)} %get-tuple-element.59), channel_id=1, source_target_pairs={{0,96},{1,97},{2,98},{3,99},{4,100},{5,101},{6,102},{7,103},{8,104... | collective-permute-start | bytes 331784 | tf_op jit(solution)/shard_map/ppermute | solution.py:415
  121.5 4.4 %collective-permute-done.20.v1 = f32[4,6912]{1,0:T(4,128)S(1)} collective-permute-done((f32[4,6912]{1,0:T(4,128)S(1)}, f32[4,6912]{1,0:T(4,128)S(1)}, u32[]{:S(2)}, u32[]{:S(2)}) %collective-permute-start.20) | collective-permute-done | bytes 110624 | tf_op jit(solution)/shard_map/ppermute | solution.py:415
  126.8 2.1 %shard_map.72 = (f32[4,128]{1,0:T(4,128)S(1)}, f32[4,128]{1,0:T(4,128)S(1)}, f32[4,128]{1,0:T(4,128)S(1)}, f32[4,128]{1,0:T(4,128)S(1)}) custom-call(s32[4]{0:T(128)S(1)} %pad_add_fusion.where, f32[4,8,6912]{2,1,0:T(8,128)S(1)} %shard_map.71.p0, f32[4,8,6912]{2,1,0:T(8,128)S(1)} %collective-permute-done.17.p1, f32[4,8,6912]{2,1,0:T(8,128)S(1)} %collective-permute-done.18.p2, ...), custom_call_target="tpu_custom_call" | custom-call | tf_op jit(solution)/shard_map/pallas_call | solution.py:335
  128.9 2.7 %collective-permute-start.23 = (f32[4,128]{1,0:T(4,128)S(1)}, f32[4,128]{1,0:T(4,128)S(1)}, u32[]{:S(2)}, u32[]{:S(2)}) collective-permute-start(f32[4,128]{1,0:T(4,128)S(1)} %get-tuple-element.61), channel_id=1, source_target_pairs={{0,96},{1,97},{2,98},{3,99},{4,100},{5,101},{6,102},{7,103},{8,104... | collective-permute-start | bytes 6152 | tf_op jit(solution)/shard_map/ppermute | solution.py:415
  132.3 3.2 %collective-permute-done.24 = f32[4,128]{1,0:T(4,128)S(1)} collective-permute-done((f32[4,128]{1,0:T(4,128)S(1)}, f32[4,128]{1,0:T(4,128)S(1)}, u32[]{:S(2)}, u32[]{:S(2)}) %collective-permute-start.24) | collective-permute-done | bytes 2080 | tf_op jit(solution)/shard_map/ppermute | solution.py:415
  135.6 2.1 %collective-permute-start.26 = (f32[4,128]{1,0:T(4,128)S(1)}, f32[4,128]{1,0:T(4,128)S(1)}, u32[]{:S(2)}, u32[]{:S(2)}) collective-permute-start(f32[4,128]{1,0:T(4,128)S(1)} %add_add_fusion.1), channel_id=1, source_target_pairs={{0,1},{1,0},{2,3},{3,2},{4,5},{5,4},{6,7},{7,6},{8,9},{9,8},{10,11... | collective-permute-start | bytes 6152 | tf_op jit(solution)/shard_map/ppermute | solution.py:415
  (58 shorter events, 27.2 us)
Async XLA Ops:
  2.4 13.4 %collective-permute-start.2 = (f32[4,6912]{1,0:T(4,128)S(1)}, f32[4,6912]{1,0:T(4,128)S(1)}, u32[]{:S(2)}, u32[]{:S(2)}) collective-permute-start(f32[4,6912]{1,0:T(4,128)S(1)} %get-tuple-element.36), channel_id=1, source_target_pairs={{0,32},{1,33},{2,34},{3,35},{4,36},{5,37},{6,38},{7,39},{8,40},{9,... | collective-permute-start | bytes 331784 | tf_op jit(solution)/shard_map/ppermute | solution.py:415
  4.9 10.9 %collective-permute-start.3 = (f32[4,6912]{1,0:T(4,128)S(1)}, f32[4,6912]{1,0:T(4,128)S(1)}, u32[]{:S(2)}, u32[]{:S(2)}) collective-permute-start(f32[4,6912]{1,0:T(4,128)S(1)} %get-tuple-element.37), channel_id=1, source_target_pairs={{0,64},{1,65},{2,66},{3,67},{4,68},{5,69},{6,70},{7,71},{8,72},{9,... | collective-permute-start | bytes 331784 | tf_op jit(solution)/shard_map/ppermute | solution.py:415
  8.2 7.6 %collective-permute-start.4 = (f32[4,6912]{1,0:T(4,128)S(1)}, f32[4,6912]{1,0:T(4,128)S(1)}, u32[]{:S(2)}, u32[]{:S(2)}) collective-permute-start(f32[4,6912]{1,0:T(4,128)S(1)} %get-tuple-element.38), channel_id=1, source_target_pairs={{0,96},{1,97},{2,98},{3,99},{4,100},{5,101},{6,102},{7,103},{8,104... | collective-permute-start | bytes 331784 | tf_op jit(solution)/shard_map/ppermute | solution.py:415
  9.0 10.2 %collective-permute-start.1 = (f32[4,27648]{1,0:T(4,128)S(1)}, f32[4,27648]{1,0:T(4,128)S(1)}, u32[]{:S(2)}, u32[]{:S(2)}) collective-permute-start(f32[4,27648]{1,0:T(4,128)S(1)} %copy-done), channel_id=1, source_target_pairs={{0,2},{1,3},{2,0},{3,1},{4,6},{5,7},{6,4},{7,5},{8,10},{9,11},{10,... | collective-permute-start | bytes 1327112 | tf_op jit(solution)/shard_map/ppermute | solution.py:415
  10.2 32.6 %collective-permute-start = (f32[4,27648]{1,0:T(4,128)S(1)}, f32[4,27648]{1,0:T(4,128)S(1)}, u32[]{:S(2)}, u32[]{:S(2)}) collective-permute-start(f32[4,27648]{1,0:T(4,128)S(1)} %copy-done), channel_id=1, source_target_pairs={{0,1},{1,0},{2,3},{3,2},{4,5},{5,4},{6,7},{7,6},{8,9},{9,8},{10,11... | collective-permute-start | bytes 1327112 | tf_op jit(solution)/shard_map/ppermute | solution.py:415
  19.2 23.6 %collective-permute-start.5 = (f32[4,27648]{1,0:T(4,128)S(1)}, f32[4,27648]{1,0:T(4,128)S(1)}, u32[]{:S(2)}, u32[]{:S(2)}) collective-permute-start(f32[4,27648]{1,0:T(4,128)S(1)} %collective-permute-done.1.o2), channel_id=1, source_target_pairs={{0,1},{1,0},{2,3},{3,2},{4,5},{5,4},{6,7},{7,6},{8,9},{9,8},{10,11... | collective-permute-start | bytes 1327112 | tf_op jit(solution)/shard_map/ppermute | solution.py:415
  21.5 10.3 %collective-permute-start.6 = (f32[1,27648]{1,0:T(1,128)S(1)}, f32[1,27648]{1,0:T(1,128)S(1)}, u32[]{:S(2)}, u32[]{:S(2)}) collective-permute-start(f32[1,27648]{1,0:T(1,128)S(1)} %get-tuple-element.40), channel_id=1, source_target_pairs={{0,4},{1,5},{2,6},{3,7},{4,8},{5,9},{6,10},{7,11},{8,12},{9,13},{1... | collective-permute-start | bytes 331784 | tf_op jit(solution)/shard_map/ppermute | solution.py:415
  24.3 10.8 %collective-permute-start.7 = (f32[1,27648]{1,0:T(1,128)S(1)}, f32[1,27648]{1,0:T(1,128)S(1)}, u32[]{:S(2)}, u32[]{:S(2)}) collective-permute-start(f32[1,27648]{1,0:T(1,128)S(1)} %get-tuple-element.41), channel_id=1, source_target_pairs={{0,5},{1,4},{2,7},{3,6},{4,9},{5,8},{6,11},{7,10},{8,13},{9,12},{1... | collective-permute-start | bytes 331784 | tf_op jit(solution)/shard_map/ppermute | solution.py:415
  25.7 11.9 %collective-permute-start.8 = (f32[1,27648]{1,0:T(1,128)S(1)}, f32[1,27648]{1,0:T(1,128)S(1)}, u32[]{:S(2)}, u32[]{:S(2)}) collective-permute-start(f32[1,27648]{1,0:T(1,128)S(1)} %get-tuple-element.42), channel_id=1, source_target_pairs={{0,6},{1,7},{2,4},{3,5},{4,10},{5,11},{6,8},{7,9},{8,14},{9,15},{1... | collective-permute-start | bytes 331784 | tf_op jit(solution)/shard_map/ppermute | solution.py:415
  31.9 10.9 %collective-permute-start.9 = (f32[1,27648]{1,0:T(1,128)S(1)}, f32[1,27648]{1,0:T(1,128)S(1)}, u32[]{:S(2)}, u32[]{:S(2)}) collective-permute-start(f32[1,27648]{1,0:T(1,128)S(1)} %get-tuple-element.43), channel_id=1, source_target_pairs={{0,7},{1,6},{2,5},{3,4},{4,11},{5,10},{6,9},{7,8},{8,15},{9,14},{1... | collective-permute-start | bytes 331784 | tf_op jit(solution)/shard_map/ppermute | solution.py:415
  63.0 17.2 %collective-permute-start.10 = (f32[2,4,27648]{2,1,0:T(4,128)S(1)}, f32[2,4,27648]{2,1,0:T(4,128)S(1)}, u32[]{:S(2)}, u32[]{:S(2)}) collective-permute-start(f32[2,4,27648]{2,1,0:T(4,128)S(1)} %get-tuple-element.47), channel_id=1, source_target_pairs={{0,1},{1,0},{2,3},{3,2},{4,5},{5,4},{6,7},{7,6},{8,9},{9,8},{10,11... | collective-permute-start | bytes 2654216 | tf_op jit(solution)/shard_map/ppermute | solution.py:415
  63.6 13.1 %collective-permute-start.16 = (f32[4,4,6912]{2,1,0:T(4,128)S(1)}, f32[4,4,6912]{2,1,0:T(4,128)S(1)}, u32[]{:S(2)}, u32[]{:S(2)}) collective-permute-start(f32[4,4,6912]{2,1,0:T(4,128)S(1)} %pad_maximum_fusion), channel_id=1, source_target_pairs={{0,4},{1,5},{2,6},{3,7},{4,0},{5,1},{6,2},{7,3},{8,12},{9,13},{10,... | collective-permute-start | bytes 1327112 | tf_op jit(solution)/shard_map/ppermute | solution.py:415
  77.4 41.7 %collective-permute-start.17 = (f32[4,8,6912]{2,1,0:T(8,128)S(1)}, f32[4,8,6912]{2,1,0:T(8,128)S(1)}, u32[]{:S(2)}, u32[]{:S(2)}) collective-permute-start(f32[4,8,6912]{2,1,0:T(8,128)S(1)} %shard_map.71.p0), channel_id=1, source_target_pairs={{0,8},{1,9},{2,10},{3,11},{4,12},{5,13},{6,14},{7,15},{8,16},{9,17... | collective-permute-start | bytes 2654216 | tf_op jit(solution)/shard_map/ppermute | solution.py:415
  77.5 44.0 %collective-permute-start.18 = (f32[4,8,6912]{2,1,0:T(8,128)S(1)}, f32[4,8,6912]{2,1,0:T(8,128)S(1)}, u32[]{:S(2)}, u32[]{:S(2)}) collective-permute-start(f32[4,8,6912]{2,1,0:T(8,128)S(1)} %shard_map.71.p0), channel_id=1, source_target_pairs={{0,16},{1,17},{2,18},{3,19},{4,20},{5,21},{6,22},{7,23},{8,24},{9,... | collective-permute-start | bytes 2654216 | tf_op jit(solution)/shard_map/ppermute | solution.py:415
  77.6 43.9 %collective-permute-start.19 = (f32[4,8,6912]{2,1,0:T(8,128)S(1)}, f32[4,8,6912]{2,1,0:T(8,128)S(1)}, u32[]{:S(2)}, u32[]{:S(2)}) collective-permute-start(f32[4,8,6912]{2,1,0:T(8,128)S(1)} %shard_map.71.p0), channel_id=1, source_target_pairs={{0,24},{1,25},{2,26},{3,27},{4,28},{5,29},{6,30},{7,31},{8,0},{9,1... | collective-permute-start | bytes 2654216 | tf_op jit(solution)/shard_map/ppermute | solution.py:415
  80.2 5.1 %collective-permute-start.12 = (f32[1,27648]{1,0:T(1,128)S(1)}, f32[1,27648]{1,0:T(1,128)S(1)}, u32[]{:S(2)}, u32[]{:S(2)}) collective-permute-start(f32[1,27648]{1,0:T(1,128)S(1)} %get-tuple-element.49), channel_id=1, source_target_pairs={{0,124},{1,125},{2,126},{3,127},{4,0},{5,1},{6,2},{7,3},{8,4},{9,5... | collective-permute-start | bytes 331784 | tf_op jit(solution)/shard_map/ppermute | solution.py:415
  80.8 36.0 %collective-permute-start.11 = (f32[4,27648]{1,0:T(4,128)S(1)}, f32[4,27648]{1,0:T(4,128)S(1)}, u32[]{:S(2)}, u32[]{:S(2)}) collective-permute-start(f32[4,27648]{1,0:T(4,128)S(1)} %shard_map.69), channel_id=1, source_target_pairs={{0,2},{1,3},{2,0},{3,1},{4,6},{5,7},{6,4},{7,5},{8,10},{9,11},{10,... | collective-permute-start | bytes 1327112 | tf_op jit(solution)/shard_map/ppermute | solution.py:415
  85.3 13.4 %collective-permute-start.13 = (f32[1,27648]{1,0:T(1,128)S(1)}, f32[1,27648]{1,0:T(1,128)S(1)}, u32[]{:S(2)}, u32[]{:S(2)}) collective-permute-start(f32[1,27648]{1,0:T(1,128)S(1)} %get-tuple-element.50), channel_id=1, source_target_pairs={{0,125},{1,124},{2,127},{3,126},{4,1},{5,0},{6,3},{7,2},{8,5},{9,4... | collective-permute-start | bytes 331784 | tf_op jit(solution)/shard_map/ppermute | solution.py:415
  98.7 5.9 %collective-permute-start.14 = (f32[1,27648]{1,0:T(1,128)S(1)}, f32[1,27648]{1,0:T(1,128)S(1)}, u32[]{:S(2)}, u32[]{:S(2)}) collective-permute-start(f32[1,27648]{1,0:T(1,128)S(1)} %get-tuple-element.51), channel_id=1, source_target_pairs={{0,126},{1,127},{2,124},{3,125},{4,2},{5,3},{6,0},{7,1},{8,6},{9,7... | collective-permute-start | bytes 331784 | tf_op jit(solution)/shard_map/ppermute | solution.py:415
  104.6 12.1 %collective-permute-start.15 = (f32[1,27648]{1,0:T(1,128)S(1)}, f32[1,27648]{1,0:T(1,128)S(1)}, u32[]{:S(2)}, u32[]{:S(2)}) collective-permute-start(f32[1,27648]{1,0:T(1,128)S(1)} %get-tuple-element.52), channel_id=1, source_target_pairs={{0,127},{1,126},{2,125},{3,124},{4,3},{5,2},{6,1},{7,0},{8,7},{9,6... | collective-permute-start | bytes 331784 | tf_op jit(solution)/shard_map/ppermute | solution.py:415
  118.5 7.4 %collective-permute-start.20 = (f32[4,6912]{1,0:T(4,128)S(1)}, f32[4,6912]{1,0:T(4,128)S(1)}, u32[]{:S(2)}, u32[]{:S(2)}) collective-permute-start(f32[4,6912]{1,0:T(4,128)S(1)} %get-tuple-element.57), channel_id=1, source_target_pairs={{0,32},{1,33},{2,34},{3,35},{4,36},{5,37},{6,38},{7,39},{8,40},{9,... | collective-permute-start | bytes 331784 | tf_op jit(solution)/shard_map/ppermute | solution.py:415
  119.1 6.8 %collective-permute-start.21 = (f32[4,6912]{1,0:T(4,128)S(1)}, f32[4,6912]{1,0:T(4,128)S(1)}, u32[]{:S(2)}, u32[]{:S(2)}) collective-permute-start(f32[4,6912]{1,0:T(4,128)S(1)} %get-tuple-element.58), channel_id=1, source_target_pairs={{0,64},{1,65},{2,66},{3,67},{4,68},{5,69},{6,70},{7,71},{8,72},{9,... | collective-permute-start | bytes 331784 | tf_op jit(solution)/shard_map/ppermute | solution.py:415
  119.1 7.7 %collective-permute-start.22 = (f32[4,6912]{1,0:T(4,128)S(1)}, f32[4,6912]{1,0:T(4,128)S(1)}, u32[]{:S(2)}, u32[]{:S(2)}) collective-permute-start(f32[4,6912]{1,0:T(4,128)S(1)} %get-tuple-element.59), channel_id=1, source_target_pairs={{0,96},{1,97},{2,98},{3,99},{4,100},{5,101},{6,102},{7,103},{8,104... | collective-permute-start | bytes 331784 | tf_op jit(solution)/shard_map/ppermute | solution.py:415
  131.6 3.9 %collective-permute-start.24 = (f32[4,128]{1,0:T(4,128)S(1)}, f32[4,128]{1,0:T(4,128)S(1)}, u32[]{:S(2)}, u32[]{:S(2)}) collective-permute-start(f32[4,128]{1,0:T(4,128)S(1)} %get-tuple-element.62), channel_id=1, source_target_pairs={{0,64},{1,65},{2,66},{3,67},{4,68},{5,69},{6,70},{7,71},{8,72},{9,... | collective-permute-start | bytes 6152 | tf_op jit(solution)/shard_map/ppermute | solution.py:415
  (11 other events, 22.3 us)

commit v2 on v1

--- a/solution.py
+++ b/solution.py
@@ -198,19 +198,32 @@
     return out
 
 
-def solve_kernel(q_ref, o0, o1, o2, o3, l0, l1, l2, l3, kern, third, whi, wlo, near0, near2, cross, low0, low1, low2, low3,
-                 right, left, hi, lo, field):
+def solve_kernel(q_ref, own, two, one, low_a, low_b, core, kern, third, whi_hbm, wlo_hbm, near0, near2, cross, low0, low2,
+                 right, left, hi, lo, field, whi, wlo, sems):
     q = q_ref[0]
-    for delta, (own, low) in enumerate(((o0, l0), (o1, l1), (o2, l2), (o3, l3))):
+    copies = []
+    for way in range(2):
+        part = pl.ds(2 * way, 2)
+        copies.append([pltpu.make_async_copy(whi_hbm.at[part], whi.at[part], sems.at[2 * way]),
+                       pltpu.make_async_copy(wlo_hbm.at[part], wlo.at[part], sems.at[2 * way + 1])])
+        for copy in copies[-1]:
+            copy.start()
+    sources = (
+        (own, 0, low_a, 0),
+        (one, 0, core, 4),
+        (two, 0, low_b, 0),
+        (core, 0, core, 6),
+    )
+    for delta, (bands_ref, first, low_ref, low_first) in enumerate(sources):
         base = (q ^ delta) * QX
 
         def place(x, carry):
             span = pl.ds(pl.multiple_of(x * PLANE, 128), PLANE)
-            bands = own[:, span]
+            bands = bands_ref[first : first + 4, span]
             right[base + x, 0:4, :] = bands
             right[base + x, 4:8, :] = bands
-            left[base + x, 0:4, :] = jnp.broadcast_to(own[pl.ds(q, 1), span], (4, PLANE))
-            left[base + x, 4:8, :] = jnp.broadcast_to(low[:, span], (4, PLANE))
+            left[base + x, 0:4, :] = jnp.broadcast_to(bands_ref[pl.ds(first + q, 1), span], (4, PLANE))
+            left[base + x, 4:8, :] = jnp.broadcast_to(low_ref[pl.ds(low_first + q % 2, 1), span], (4, PLANE))
             return carry
 
         lax.fori_loop(0, QX, place, 0)
@@ -242,6 +255,8 @@
         w = jnp.concatenate([whi[k, :, cols], whi[k, :, cols], wlo[k, :, cols]], axis=0)
         return jnp.dot(lhs, w, preferred_element_type=F32)
 
+    for copy in copies[0]:
+        copy.wait()
     for j in range(3):
         cols = slice(j * 256, (j + 1) * 256)
         field[:, cols] = product(0, 0, cols)
@@ -270,6 +285,8 @@
         return carry
 
     lax.fori_loop(0, NG // 2, unmix, 0)
+    for copy in copies[1]:
+        copy.wait()
     for j in range(3):
         cols = slice(j * 256, (j + 1) * 256)
         for m, k in ((0, 2), (1, 2), (2, 3)):
@@ -294,41 +311,45 @@
                 pr = pr + pltpu.roll(pr, 7, 0)
                 po = pltpu.roll(v * left[x, :, span], 4, 0) + mine * pr[0:1, :]
                 at = pl.ds(pl.multiple_of(i * PLANE + m * SLAB, SLAB), SLAB)
-                bands = -po[0:4, :]
+                bands, low = -po[0:4, :], -pr[4:5, :]
                 if delta % 2:
-                    cross[delta // 2, :, at] = bands
+                    cross[delta // 2 * 4 : delta // 2 * 4 + 4, at] = bands
+                    cross[8 + delta // 2 : 9 + delta // 2, at] = low
                 else:
                     (near0, near2)[delta // 2][:, at] = bands
-                (low0, low1, low2, low3)[delta][:, at] = -pr[4:5, :]
+                    (low0, low2)[delta // 2][:, at] = low
             return carry
 
         lax.fori_loop(0, QX, finish, 0)
 
 
-def solve_pairs(q, owns, lows, tables):
+def solve_pairs(q, bands, tables):
     vmem = pl.BlockSpec(memory_space=pltpu.VMEM)
     return pl.pallas_call(
         solve_kernel,
-        out_shape=[jax.ShapeDtypeStruct(shape, F32) for shape in [(4, QCELL)] * 2 + [(2, 4, QCELL)] + [(1, QCELL)] * 4],
-        in_specs=[pl.BlockSpec(memory_space=pltpu.SMEM)] + [vmem] * 12,
-        out_specs=[vmem] * 7,
+        out_shape=[jax.ShapeDtypeStruct(shape, F32) for shape in [(4, QCELL)] * 2 + [(10, QCELL)] + [(1, QCELL)] * 2],
+        in_specs=[pl.BlockSpec(memory_space=pltpu.SMEM)] + [vmem] * 8 + [pl.BlockSpec(memory_space=pltpu.HBM)] * 2,
+        out_specs=[vmem] * 5,
         scratch_shapes=[
             pltpu.VMEM((NG, 8, PLANE), F32),
             pltpu.VMEM((NG, 8, PLANE), F32),
             pltpu.VMEM((NG * 8, PLANE), BF16),
             pltpu.VMEM((NG * 8, PLANE), BF16),
             pltpu.VMEM((NG * 8, PLANE), F32),
+            pltpu.VMEM((4, SLAB, SLAB), BF16),
+            pltpu.VMEM((4, SLAB, SLAB), BF16),
+            pltpu.SemaphoreType.DMA((4,)),
         ],
         name="solve_pairs",
-        compiler_params=pltpu.CompilerParams(vmem_limit_bytes=34 << 20),
-    )(q.reshape(1), *owns, *lows, jnp.asarray(kernel_values()), jnp.asarray(thirds()), *tables)
+        compiler_params=pltpu.CompilerParams(vmem_limit_bytes=40 << 20),
+    )(q.reshape(1), *bands, jnp.asarray(kernel_values()), jnp.asarray(thirds()), *tables)
 
 
 BOTH = ("band", "grid")
 CHUNK = QCELL // 4
 
 
-def small_call(body, outs, scratch=()):
+def small_call(body, outs, scratch=(), limit=8):
     vmem = pl.BlockSpec(memory_space=pltpu.VMEM)
 
     def call(where, *arrays):
@@ -338,71 +359,73 @@
             in_specs=[pl.BlockSpec(memory_space=pltpu.SMEM)] + [vmem] * len(arrays),
             out_specs=[vmem] * len(outs),
             scratch_shapes=list(scratch),
-            compiler_params=pltpu.CompilerParams(vmem_limit_bytes=24 << 20),
+            compiler_params=pltpu.CompilerParams(vmem_limit_bytes=limit << 20),
         )(where, *arrays)
 
     return call
 
 
 def chunk_of(where, k):
-    return pl.ds(pl.multiple_of(((where[1] + k) % 4) * CHUNK, 128), CHUNK)
-
-
-def prepare_kernel(where, orbitals, *outs):
-    q = where[0]
-    for d in range(4):
-        outs[d][...] = orbitals[pl.ds(q ^ d, 1), :]
-        outs[4 + d][...] = orbitals[:, chunk_of(where, d)]
-
-
-def finalize_kernel(where, near, across, far, o0, o1, o2, o3, vectors, *chunks):
-    q = where[0]
-    row = lax.broadcasted_iota(jnp.int32, (4, CHUNK), 0)
-    for c in range(4):
-        span = pl.ds(c * CHUNK, CHUNK)
-        total = near[:, span] + across[0, :, span] + far[:, span]
-        for d, owed in enumerate((o0, o1, o2, o3)):
-            total = total + jnp.where(row == (q ^ d), jnp.broadcast_to(owed[:, span], (4, CHUNK)), 0.0)
-        vectors[:, span] = total
+    return pl.ds(pl.multiple_of((where[1] ^ k) * CHUNK, 128), CHUNK)
+
+
+def prepare_kernel(where, orbitals, sel_a, sel_b, *chunks):
+    lower = where[0] < 2
+    a, b = orbitals[0:2, :], orbitals[2:4, :]
+    sel_a[...] = jnp.where(lower, a, b)
+    sel_b[...] = jnp.where(lower, b, a)
+    for k in range(4):
+        chunks[k][...] = orbitals[:, chunk_of(where, k)]
+
+
+def stack_kernel(where, two, low_a, low_b, out):
+    out[0:4, :] = two[...]
+    out[4:6, :] = low_a[...]
+    out[6:8, :] = low_b[...]
+
+
+def merge_kernel(where, near0, near2, low0, low2, across, near, far, owed_a, owed_b):
+    first = where[0] % 2 == 0
+    near[...] = near0[...] + across[0:4, :]
+    far[...] = near2[...] + across[4:8, :]
+    for out, low, row in ((owed_a, low0, 8), (owed_b, low2, 9)):
+        a, b = low[...], across[row : row + 1, :]
+        out[0:1, :] = jnp.where(first, a, b)
+        out[1:2, :] = jnp.where(first, b, a)
+
+
+def finalize_kernel(where, near, far, owed_a, owed_b, vectors, *chunks):
+    lower = where[0] < 2
+    a, b = owed_a[...], owed_b[...]
+    total = near[...] + far[...]
+    vectors[0:2, :] = total[0:2, :] + jnp.where(lower, a, b)
+    vectors[2:4, :] = total[2:4, :] + jnp.where(lower, b, a)
     for k in range(4):
         chunks[k][...] = vectors[:, chunk_of(where, k)]
 
 
-def add_kernel(where, near, across, out):
-    out[...] = near[...] + across[1]
-
-
-def pair_kernel(where, f0, f1, f2, f3, other, out):
-    mine_first = where[3] == 0
-    for k, f in enumerate((f0, f1, f2, f3)):
-        a, b = f[...], other[k]
-        out[k, 0:4, :] = jnp.where(mine_first, a, b)
-        out[k, 4:8, :] = jnp.where(mine_first, b, a)
-
-
-def margin_kernel(where, p0, p1, p2, p3, v0, v1, v2, v3, m0, m1, m2, m3, block):
-    z, y = where[1], where[2]
+def margin_kernel(where, gathered, v0, v1, v2, v3, m01, m23, block):
+    z = where[1]
 
     def halves(a):
         top = a.astype(BF16)
         return top, (a - top.astype(F32)).astype(BF16)
 
-    bands = jnp.concatenate([v0[...], v1[...], v2[...], v3[...]], axis=0)
-    vt, vl = halves(bands)
+    vt, vl = halves(jnp.concatenate([v0[...], v1[...], v2[...], v3[...]], axis=0))
+    ft, fl = halves(gathered[...])
     dims = (((1,), (1,)), ((), ()))
-    for dy, part in enumerate((p0, p1, p2, p3)):
-        ft, fl = halves(part[...].reshape(32, CHUNK))
-        got = (
-            lax.dot_general(ft, vt, dims, preferred_element_type=F32)
-            + lax.dot_general(fl, vt, dims, preferred_element_type=F32)
-            + lax.dot_general(ft, vl, dims, preferred_element_type=F32)
-        )
+    got = (
+        lax.dot_general(ft, vt, dims, preferred_element_type=F32)
+        + lax.dot_general(fl, vt, dims, preferred_element_type=F32)
+        + lax.dot_general(ft, vl, dims, preferred_element_type=F32)
+    )
+    for m in range(8):
         for dz in range(4):
-            at = ((z + 4 - dz) % 4) * 4 + (y + 4 - dy) % 4
-            block[at, :, :] = got[8 * dz : 8 * dz + 8, :]
-    out = block[...].reshape(128, 16).T * (1.0 / NCELL)
-    for k, m in enumerate((m0, m1, m2, m3)):
-        m[...] = out[4 * k : 4 * k + 4, :]
+            row = 16 * m + 4 * dz
+            block[(z ^ dz) * 8 + m, :, :] = got[row : row + 4, :]
+    out = jnp.concatenate([block[i] for i in range(32)], axis=0).T * (1.0 / NCELL)
+    m01[...] = out[0:8, :]
+    m23[...] = out[8:16, :]
 
 
 def move(value, target):
@@ -415,12 +438,8 @@
     return lax.ppermute(value, BOTH, pairs)
 
 
-def along_z(value, k):
-    return move(value, lambda z, y, h, q: (z + k, y, h, q))
-
-
-def along_y(value, k):
-    return move(value, lambda z, y, h, q: (z, y + k, h, q))
+def along_z(value, flip):
+    return move(value, lambda z, y, h, q: (z ^ flip, y, h, q))
 
 
 def within(value, flip):
@@ -438,34 +457,39 @@
 def step(orbitals):
     b = lax.axis_index("band").astype(jnp.int32)
     q = lax.axis_index("grid").astype(jnp.int32)
-    where = jnp.stack([q, b // 8, b // 2 % 4, b % 2])
+    where = jnp.stack([q, b // 8])
     two = within(orbitals, 2)
+    prepare = small_call(prepare_kernel, [(2, QCELL)] * 2 + [(4, CHUNK)] * 4)
+    sel_a, sel_b, *zc = prepare(where, orbitals)
+    low_a = around(sel_a, 1, 0)
+    low_b = around(sel_b, 1, 2)
     one = within(orbitals, 1)
-    prepare = small_call(prepare_kernel, [(1, QCELL)] * 4 + [(4, CHUNK)] * 4)
-    ready = prepare(where, orbitals)
-    lows = [around(ready[d], 1, d) for d in range(4)]
-    pieces = [ready[4]] + [along_z(ready[4 + k], k) for k in (1, 2, 3)]
+    pieces = [zc[0]] + [along_z(zc[k], k) for k in (1, 2, 3)]
     tables = plane_tables()
-    stacked = jnp.stack(pieces)
-    two, tables, stacked = lax.optimization_barrier((two, tables, stacked))
-    three = within(two, 1)
-    other = move(stacked, lambda z, y, h, q: (z, y, 1 - h, q))
-    near0, near2, cross, *low = solve_pairs(q, (orbitals, one, two, three), lows, tables)
+    together = jnp.concatenate(pieces, axis=0)
+    groups = [[z * 8 + i for i in range(8)] for z in range(4)]
+    gathered = lax.all_gather(together, "band", axis_index_groups=groups, axis=0, tiled=True)
+    two, together = lax.optimization_barrier((two, together))
+    (stacked,) = small_call(stack_kernel, [(8, QCELL)])(where, two, low_a, low_b)
+    core = within(stacked, 1)
+    near0, near2, cross, low0, low2 = solve_pairs(q, (orbitals, two, one, low_a, low_b, core), tables)
     across = within(cross, 1)
-    owed = [around(low[d], -1, d) for d in range(4)]
-    both = small_call(add_kernel, [(4, QCELL)])(where, near2, across)[0]
+    merge = small_call(merge_kernel, [(4, QCELL)] * 2 + [(2, QCELL)] * 2)
+    near, both, owe_a, owe_b = merge(where, near0, near2, low0, low2, across)
     far = within(both, 2)
-    other, _ = lax.optimization_barrier((other, near0))
-    (paired,) = small_call(pair_kernel, [(4, 8, CHUNK)])(where, *pieces, other)
-    parts = [paired] + [along_y(paired, k) for k in (1, 2, 3)]
+    owed_a = around(owe_a, -1, 0)
+    owed_b = around(owe_b, -1, 2)
     finalize = small_call(finalize_kernel, [(4, QCELL)] + [(4, CHUNK)] * 4)
-    vectors, *chunks = finalize(where, near0, across, far, *owed)
-    given = [chunks[0]] + [along_z(chunks[k], k) for k in (1, 2, 3)]
-    margin_part = small_call(margin_kernel, [(4, 128)] * 4, [pltpu.VMEM((16, 8, 16), F32)])
-    sums = margin_part(where, *parts, *given)
-    mine = sums[0] + sum(along_z(sums[k], -k) for k in (1, 2, 3))
-    total = mine + sum(within(mine, d) for d in (1, 2, 3))
-    margin = lax.dynamic_slice_in_dim(total, q * 32, 32, 1).T
+    vectors, *vc = finalize(where, near, far, owed_a, owed_b)
+    given = [vc[0]] + [along_z(vc[k], k) for k in (1, 2, 3)]
+    gathered, _ = lax.optimization_barrier((gathered, vc[0]))
+    margin_part = small_call(margin_kernel, [(8, 128)] * 2, [pltpu.VMEM((32, 4, 16), F32)], 20)
+    m01, m23 = margin_part(where, gathered, *given)
+    m01 = m01 + along_z(m23, 2)
+    mine = m01[0:4] + along_z(m01[4:8], 1)
+    mine = mine + within(mine, 1)
+    mine = mine + within(mine, 2)
+    margin = lax.dynamic_slice_in_dim(mine, q * 32, 32, 1).T
     return vectors, margin
 
 

time: 142 us -> 134 us (0.944)
  starting transfers between devices: 55 us -> 26.7 us
  between operations: 0.79 us -> 14.2 us
  waiting for transfers between devices: 54.3 us -> 60.5 us
    ppermute x29 -> x19, starting transfers between devices: 55 us -> 26.6 us  [move(): return lax.ppermute(value, BOTH, pairs)]
    ppermute x29 -> x19, waiting for transfers between devices: 54.3 us -> 60.5 us  [move(): return lax.ppermute(value, BOTH, pairs)]
    unnamed x12 -> x16, local copies, waits for them, and re-layouts: 5.66 us -> 5.16 us
  transfers between devices with their start and end apart: 29 -> 20, of which waited for: 17 -> 13; matrix products, arithmetic and copies ran while one was open for 0% -> 0% of each run, Pallas kernels for 4% -> 17%
where the time goes in v2:
time: 134 us
  waiting for transfers between devices  60.5 us (45%)
  starting transfers between devices  26.7 us (20%)
  Pallas kernels  25.5 us (19%)
  between operations  14.2 us (11%)
  local copies, waits for them, and re-layouts  5.82 us (4%)
    ppermute x19, waiting for transfers between devices, move(): return lax.ppermute(value, BOTH, pairs)  60.5 us
    ppermute x19, starting transfers between devices, move(): return lax.ppermute(value, BOTH, pairs)  26.6 us
    pallas_call x1, Pallas kernels, solve_pairs(): pl.pallas_call(solve_kernel, out_shape=[jax.ShapeDtypeStruct(shape, F32)...  17.9 us
    pallas_call x5, Pallas kernels, call(): pl.pallas_call(body, out_shape=[jax.ShapeDtypeStruct(shape, F32) for shap...  5.72 us
    unnamed x16, local copies, waits for them, and re-layouts  5.16 us
  transfers between devices with their start and end apart: 20, of which 13 were waited for; matrix products, arithmetic and copies ran while one was open for 0% of the time, Pallas kernels for 17%

profile of v2, /device:TPU:1, one launch (start us, length us, event | category | flops | bytes accessed | tf_op | source)
XLA Modules:
  0.0 133.7 jit_solution(4873520129600871796)
XLA Ops:
  9.0 2.5 %collective-permute-start.1 = (f32[4,6912]{1,0:T(4,128)S(1)}, f32[4,6912]{1,0:T(4,128)S(1)}, u32[]{:S(2)}, u32[]{:S(2)}) collective-permute-start(f32[4,6912]{1,0:T(4,128)S(1)} %get-tuple-element.29), channel_id=1, source_target_pairs={{0,32},{1,33},{2,34},{3,35},{4,36},{5,37},{6,38},{7,39},{8,40},{9,... | collective-permute-start | bytes 331784 | tf_op jit(solution)/shard_map/ppermute | solution.py:438
  11.6 3.3 %collective-permute-start.2 = (f32[4,6912]{1,0:T(4,128)S(1)}, f32[4,6912]{1,0:T(4,128)S(1)}, u32[]{:S(2)}, u32[]{:S(2)}) collective-permute-start(f32[4,6912]{1,0:T(4,128)S(1)} %get-tuple-element.30), channel_id=1, source_target_pairs={{0,64},{1,65},{2,66},{3,67},{4,68},{5,69},{6,70},{7,71},{8,72},{9,... | collective-permute-start | bytes 331784 | tf_op jit(solution)/shard_map/ppermute | solution.py:438
  14.9 4.8 %collective-permute-done.2 = f32[4,6912]{1,0:T(4,128)S(1)} collective-permute-done((f32[4,6912]{1,0:T(4,128)S(1)}, f32[4,6912]{1,0:T(4,128)S(1)}, u32[]{:S(2)}, u32[]{:S(2)}) %collective-permute-start.2) | collective-permute-done | bytes 110624 | tf_op jit(solution)/shard_map/ppermute | solution.py:438
  19.7 2.6 %collective-permute-done.3 = f32[4,6912]{1,0:T(4,128)S(1)} collective-permute-done((f32[4,6912]{1,0:T(4,128)S(1)}, f32[4,6912]{1,0:T(4,128)S(1)}, u32[]{:S(2)}, u32[]{:S(2)}) %collective-permute-start.3) | collective-permute-done | bytes 110624 | tf_op jit(solution)/shard_map/ppermute | solution.py:438
  24.5 2.5 %collective-permute-start.5 = (f32[2,27648]{1,0:T(2,128)S(1)}, f32[2,27648]{1,0:T(2,128)S(1)}, u32[]{:S(2)}, u32[]{:S(2)}) collective-permute-start(f32[2,27648]{1,0:T(2,128)S(1)} %get-tuple-element.33), channel_id=1, source_target_pairs={{0,4},{1,5},{2,6},{3,7},{4,8},{5,9},{6,10},{7,11},{8,12},{9,13},{1... | collective-permute-start | bytes 663560 | tf_op jit(solution)/shard_map/ppermute | solution.py:438
  28.2 6.2 %collective-permute-done.two = f32[4,27648]{1,0:T(4,128)S(1)} collective-permute-done((f32[4,27648]{1,0:T(4,128)}, f32[4,27648]{1,0:T(4,128)S(1)}, u32[]{:S(2)}, u32[]{:S(2)}) %collective-permute-start) | collective-permute-done | bytes 442400 | tf_op jit(solution)/shard_map/ppermute | solution.py:438
  34.4 12.0 %collective-permute-done.5.low_a = f32[2,27648]{1,0:T(2,128)S(1)} collective-permute-done((f32[2,27648]{1,0:T(2,128)S(1)}, f32[2,27648]{1,0:T(2,128)S(1)}, u32[]{:S(2)}, u32[]{:S(2)}) %collective-permute-start.5) | collective-permute-done | bytes 221216 | tf_op jit(solution)/shard_map/ppermute | solution.py:438
  47.1 3.7 %collective-permute-start.7 = (f32[8,27648]{1,0:T(8,128)S(1)}, f32[8,27648]{1,0:T(8,128)S(1)}, u32[]{:S(2)}, u32[]{:S(2)}) collective-permute-start(f32[8,27648]{1,0:T(8,128)S(1)} %shard_map.69), channel_id=1, source_target_pairs={{0,1},{1,0},{2,3},{3,2},{4,5},{5,4},{6,7},{7,6},{8,9},{9,8},{10,11... | collective-permute-start | bytes 2654216 | tf_op jit(solution)/shard_map/ppermute | solution.py:438
  50.9 1.9 %plane_tables.1 = (bf16[4,768,768]{2,1,0:T(8,128)(2,1)S(1)}, bf16[4,768,768]{2,1,0:T(8,128)(2,1)S(1)}) custom-call(f32[4,16,768]{2,1,0:T(8,128)S(1)} %copy-done.6, f32[2,48,768]{2,1,0:T(8,128)S(1)} %copy-done.5), custom_call_target="tpu_custom_call" | custom-call | tf_op jit(solution)/shard_map/plane_tables/pallas_call | solution.py:119
  52.9 2.1 %copy-done = bf16[4,768,768]{2,1,0:T(8,128)(2,1)} copy-done((bf16[4,768,768]{2,1,0:T(8,128)(2,1)}, bf16[4,768,768]{2,1,0:T(8,128)(2,1)S(1)}, u32[]{:S(2)}) %copy-start) | copy-done | bytes 4718616
  55.0 17.9 %solve_pairs.1 = (f32[4,27648]{1,0:T(4,128)S(1)}, f32[4,27648]{1,0:T(4,128)S(1)}, f32[10,27648]{1,0:T(8,128)S(1)}, f32[1,27648]{1,0:T(1,128)S(1)}, f32[1,27648]{1,0:T(1,128)S(1)}) custom-call(s32[1]{0:T(128)} %bitcast.q_ref, f32[4,27648]{1,0:T(4,128)S(1)} %copy-done.3, f32[4,27648]{1,0:T(4,128)S(1)} %collective-permute-done.two, ...), custom_call_target="tpu_custom_call" | custom-call | tf_op jit(solution)/shard_map/solve_pairs/pallas_call | solution.py:328
  73.4 3.3 %collective-permute-done.8.across = f32[10,27648]{1,0:T(8,128)S(1)} collective-permute-done((f32[10,27648]{1,0:T(8,128)S(1)}, f32[10,27648]{1,0:T(8,128)S(1)}, u32[]{:S(2)}, u32[]{:S(2)}) %collective-permute-start.8) | collective-permute-done | bytes 1105952 | tf_op jit(solution)/shard_map/ppermute | solution.py:438
  78.3 3.2 %collective-permute-start.11 = (f32[2,27648]{1,0:T(2,128)S(1)}, f32[2,27648]{1,0:T(2,128)S(1)}, u32[]{:S(2)}, u32[]{:S(2)}) collective-permute-start(f32[2,27648]{1,0:T(2,128)S(1)} %get-tuple-element.45), channel_id=1, source_target_pairs={{0,126},{1,127},{2,124},{3,125},{4,2},{5,3},{6,0},{7,1},{8,6},{9,7... | collective-permute-start | bytes 663560 | tf_op jit(solution)/shard_map/ppermute | solution.py:438
  81.5 14.9 %collective-permute-done.10.owed_a = f32[2,27648]{1,0:T(2,128)S(1)} collective-permute-done((f32[2,27648]{1,0:T(2,128)S(1)}, f32[2,27648]{1,0:T(2,128)S(1)}, u32[]{:S(2)}, u32[]{:S(2)}) %collective-permute-start.10) | collective-permute-done | bytes 221216 | tf_op jit(solution)/shard_map/ppermute | solution.py:438
  96.3 1.5 %shard_map.71 = (f32[4,27648]{1,0:T(4,128)}, f32[4,6912]{1,0:T(4,128)S(1)}, f32[4,6912]{1,0:T(4,128)S(1)}, f32[4,6912]{1,0:T(4,128)S(1)}, f32[4,6912]{1,0:T(4,128)S(1)}) custom-call(s32[2]{0:T(128)S(1)} %pad_add_fusion.where, f32[4,27648]{1,0:T(4,128)S(1)} %get-tuple-element.42.near, f32[4,27648]{1,0:T(4,128)S(1)} %collective-permute-done.9.far, ...), custom_call_target="tpu_custom_call" | custom-call | tf_op jit(solution)/shard_map/pallas_call | solution.py:356
  99.1 2.6 %collective-permute-start.13 = (f32[4,6912]{1,0:T(4,128)S(1)}, f32[4,6912]{1,0:T(4,128)S(1)}, u32[]{:S(2)}, u32[]{:S(2)}) collective-permute-start(f32[4,6912]{1,0:T(4,128)S(1)} %get-tuple-element.50), channel_id=1, source_target_pairs={{0,64},{1,65},{2,66},{3,67},{4,68},{5,69},{6,70},{7,71},{8,72},{9,... | collective-permute-start | bytes 331784 | tf_op jit(solution)/shard_map/ppermute | solution.py:438
  101.8 4.8 %collective-permute-done.13.v2 = f32[4,6912]{1,0:T(4,128)S(1)} collective-permute-done((f32[4,6912]{1,0:T(4,128)S(1)}, f32[4,6912]{1,0:T(4,128)S(1)}, u32[]{:S(2)}, u32[]{:S(2)}) %collective-permute-start.13) | collective-permute-done | bytes 110624 | tf_op jit(solution)/shard_map/ppermute | solution.py:438
  106.6 2.6 %collective-permute-done.14.v3 = f32[4,6912]{1,0:T(4,128)S(1)} collective-permute-done((f32[4,6912]{1,0:T(4,128)S(1)}, f32[4,6912]{1,0:T(4,128)S(1)}, u32[]{:S(2)}, u32[]{:S(2)}) %collective-permute-start.14) | collective-permute-done | bytes 110624 | tf_op jit(solution)/shard_map/ppermute | solution.py:438
  109.2 2.0 %copy-done.1 = f32[128,6912]{1,0:T(8,128)S(1)} copy-done((f32[128,6912]{1,0:T(8,128)S(1)}, f32[128,6912]{1,0:T(8,128)}, u32[]{:S(2)}) %copy-start.1) | copy-done | bytes 3538968
  111.2 2.1 %shard_map.72 = (f32[8,128]{1,0:T(8,128)S(1)}, f32[8,128]{1,0:T(8,128)S(1)}) custom-call(s32[2]{0:T(128)S(1)} %pad_add_fusion.where, f32[128,6912]{1,0:T(8,128)S(1)} %copy-done.1, f32[4,6912]{1,0:T(4,128)S(1)} %get-tuple-element.47.v0, f32[4,6912]{1,0:T(4,128)S(1)} %collective-permute-done.12.v1, f32[4,6912]{1,0:T(4,128)S(1)} %collective-permute-done.13.v2, ...), custom_call_target="tpu_custom_call" | custom-call | tf_op jit(solution)/shard_map/pallas_call | solution.py:356
  113.4 3.9 %collective-permute-done.15 = f32[8,128]{1,0:T(8,128)S(1)} collective-permute-done((f32[8,128]{1,0:T(8,128)S(1)}, f32[8,128]{1,0:T(8,128)S(1)}, u32[]{:S(2)}, u32[]{:S(2)}) %collective-permute-start.15) | collective-permute-done | bytes 4128 | tf_op jit(solution)/shard_map/ppermute | solution.py:438
  117.4 2.4 %collective-permute-done.16 = f32[4,128]{1,0:T(4,128)S(1)} collective-permute-done((f32[4,128]{1,0:T(4,128)S(1)}, f32[4,128]{1,0:T(4,128)S(1)}, u32[]{:S(2)}, u32[]{:S(2)}) %collective-permute-start.16) | collective-permute-done | bytes 2080 | tf_op jit(solution)/shard_map/ppermute | solution.py:438
  119.8 3.2 %collective-permute-start.17 = (f32[4,128]{1,0:T(4,128)S(1)}, f32[4,128]{1,0:T(4,128)S(1)}, u32[]{:S(2)}, u32[]{:S(2)}) collective-permute-start(f32[4,128]{1,0:T(4,128)S(1)} %slice_add_fusion), channel_id=1, source_target_pairs={{0,1},{1,0},{2,3},{3,2},{4,5},{5,4},{6,7},{7,6},{8,9},{9,8},{10,11... | collective-permute-start | bytes 6152 | tf_op jit(solution)/shard_map/ppermute | solution.py:438
  124.2 2.0 %collective-permute-done.18 = f32[4,128]{1,0:T(4,128)S(1)} collective-permute-done((f32[4,128]{1,0:T(4,128)S(1)}, f32[4,128]{1,0:T(4,128)S(1)}, u32[]{:S(2)}, u32[]{:S(2)}) %collective-permute-start.18) | collective-permute-done | bytes 2080 | tf_op jit(solution)/shard_map/ppermute | solution.py:438
  (48 shorter events, 11.5 us)
Async XLA Ops:
  7.2 47.9 %copy-start.7 = (f32[8,768]{1,0:T(8,128)S(1)}, f32[8,768]{1,0:T(8,128)}, u32[]{:S(2)}) copy-start(f32[8,768]{1,0:T(8,128)} %constant.41.clone.third) | copy-start | bytes 73732
  7.2 94.5 %all-gather.2.cloned.1.call-start = ((), (), s32[]{:S(2)}) async-start(), calls=%async_computation | async-start | bytes 3981312 | tf_op jit(solution)/shard_map/all_gather | solution.py:471
  8.3 42.6 %copy-start.5 = (f32[2,48,768]{2,1,0:T(8,128)S(1)}, f32[2,48,768]{2,1,0:T(8,128)}, u32[]{:S(2)}) copy-start(f32[2,48,768]{2,1,0:T(8,128)} %constant.39.clone.zs) | copy-start | bytes 884740
  8.3 42.6 %copy-start.6 = (f32[4,16,768]{2,1,0:T(8,128)S(1)}, f32[4,16,768]{2,1,0:T(8,128)}, u32[]{:S(2)}) copy-start(f32[4,16,768]{2,1,0:T(8,128)} %constant.38.clone.tens) | copy-start | bytes 589828
  8.3 46.7 %copy-start.4 = (f32[48,2304]{1,0:T(8,128)S(1)}, f32[48,2304]{1,0:T(8,128)}, u32[]{:S(2)}) copy-start(f32[48,2304]{1,0:T(8,128)} %constant.40.clone.kern) | copy-start | bytes 1327108
  9.0 5.8 %collective-permute-start.1 = (f32[4,6912]{1,0:T(4,128)S(1)}, f32[4,6912]{1,0:T(4,128)S(1)}, u32[]{:S(2)}, u32[]{:S(2)}) collective-permute-start(f32[4,6912]{1,0:T(4,128)S(1)} %get-tuple-element.29), channel_id=1, source_target_pairs={{0,32},{1,33},{2,34},{3,35},{4,36},{5,37},{6,38},{7,39},{8,40},{9,... | collective-permute-start | bytes 331784 | tf_op jit(solution)/shard_map/ppermute | solution.py:438
  11.6 8.2 %collective-permute-start.2 = (f32[4,6912]{1,0:T(4,128)S(1)}, f32[4,6912]{1,0:T(4,128)S(1)}, u32[]{:S(2)}, u32[]{:S(2)}) collective-permute-start(f32[4,6912]{1,0:T(4,128)S(1)} %get-tuple-element.30), channel_id=1, source_target_pairs={{0,64},{1,65},{2,66},{3,67},{4,68},{5,69},{6,70},{7,71},{8,72},{9,... | collective-permute-start | bytes 331784 | tf_op jit(solution)/shard_map/ppermute | solution.py:438
  14.9 7.4 %collective-permute-start.3 = (f32[4,6912]{1,0:T(4,128)S(1)}, f32[4,6912]{1,0:T(4,128)S(1)}, u32[]{:S(2)}, u32[]{:S(2)}) collective-permute-start(f32[4,6912]{1,0:T(4,128)S(1)} %get-tuple-element.31), channel_id=1, source_target_pairs={{0,96},{1,97},{2,98},{3,99},{4,100},{5,101},{6,102},{7,103},{8,104... | collective-permute-start | bytes 331784 | tf_op jit(solution)/shard_map/ppermute | solution.py:438
  23.2 11.1 %collective-permute-start = (f32[4,27648]{1,0:T(4,128)}, f32[4,27648]{1,0:T(4,128)S(1)}, u32[]{:S(2)}, u32[]{:S(2)}) collective-permute-start(f32[4,27648]{1,0:T(4,128)} %own.1), channel_id=1, source_target_pairs={{0,2},{1,3},{2,0},{3,1},{4,6},{5,7},{6,4},{7,5},{8,10},{9,11},{10,... | collective-permute-start | bytes 1327112 | tf_op jit(solution)/shard_map/ppermute | solution.py:438
  24.5 21.8 %collective-permute-start.5 = (f32[2,27648]{1,0:T(2,128)S(1)}, f32[2,27648]{1,0:T(2,128)S(1)}, u32[]{:S(2)}, u32[]{:S(2)}) collective-permute-start(f32[2,27648]{1,0:T(2,128)S(1)} %get-tuple-element.33), channel_id=1, source_target_pairs={{0,4},{1,5},{2,6},{3,7},{4,8},{5,9},{6,10},{7,11},{8,12},{9,13},{1... | collective-permute-start | bytes 663560 | tf_op jit(solution)/shard_map/ppermute | solution.py:438
  27.0 19.4 %collective-permute-start.6 = (f32[2,27648]{1,0:T(2,128)S(1)}, f32[2,27648]{1,0:T(2,128)S(1)}, u32[]{:S(2)}, u32[]{:S(2)}) collective-permute-start(f32[2,27648]{1,0:T(2,128)S(1)} %get-tuple-element.34), channel_id=1, source_target_pairs={{0,6},{1,7},{2,4},{3,5},{4,10},{5,11},{6,8},{7,9},{8,14},{9,15},{1... | collective-permute-start | bytes 663560 | tf_op jit(solution)/shard_map/ppermute | solution.py:438
  47.1 7.9 %collective-permute-start.7 = (f32[8,27648]{1,0:T(8,128)S(1)}, f32[8,27648]{1,0:T(8,128)S(1)}, u32[]{:S(2)}, u32[]{:S(2)}) collective-permute-start(f32[8,27648]{1,0:T(8,128)S(1)} %shard_map.69), channel_id=1, source_target_pairs={{0,1},{1,0},{2,3},{3,2},{4,5},{5,4},{6,7},{7,6},{8,9},{9,8},{10,11... | collective-permute-start | bytes 2654216 | tf_op jit(solution)/shard_map/ppermute | solution.py:438
  50.8 4.2 %collective-permute-start.4 = (f32[4,27648]{1,0:T(4,128)S(1)}, f32[4,27648]{1,0:T(4,128)S(1)}, u32[]{:S(2)}, u32[]{:S(2)}) collective-permute-start(f32[4,27648]{1,0:T(4,128)S(1)} %copy-done.3), channel_id=1, source_target_pairs={{0,1},{1,0},{2,3},{3,2},{4,5},{5,4},{6,7},{7,6},{8,9},{9,8},{10,11... | collective-permute-start | bytes 1327112 | tf_op jit(solution)/shard_map/ppermute | solution.py:438
  72.9 3.8 %collective-permute-start.8 = (f32[10,27648]{1,0:T(8,128)S(1)}, f32[10,27648]{1,0:T(8,128)S(1)}, u32[]{:S(2)}, u32[]{:S(2)}) collective-permute-start(f32[10,27648]{1,0:T(8,128)S(1)} %get-tuple-element.41), channel_id=1, source_target_pairs={{0,1},{1,0},{2,3},{3,2},{4,5},{5,4},{6,7},{7,6},{8,9},{9,8},{10,11... | collective-permute-start | bytes 3317768 | tf_op jit(solution)/shard_map/ppermute | solution.py:438
  77.4 18.9 %collective-permute-start.9 = (f32[4,27648]{1,0:T(4,128)S(1)}, f32[4,27648]{1,0:T(4,128)S(1)}, u32[]{:S(2)}, u32[]{:S(2)}) collective-permute-start(f32[4,27648]{1,0:T(4,128)S(1)} %get-tuple-element.43), channel_id=1, source_target_pairs={{0,2},{1,3},{2,0},{3,1},{4,6},{5,7},{6,4},{7,5},{8,10},{9,11},{10,... | collective-permute-start | bytes 1327112 | tf_op jit(solution)/shard_map/ppermute | solution.py:438
  77.5 18.8 %collective-permute-start.10 = (f32[2,27648]{1,0:T(2,128)S(1)}, f32[2,27648]{1,0:T(2,128)S(1)}, u32[]{:S(2)}, u32[]{:S(2)}) collective-permute-start(f32[2,27648]{1,0:T(2,128)S(1)} %get-tuple-element.44), channel_id=1, source_target_pairs={{0,124},{1,125},{2,126},{3,127},{4,0},{5,1},{6,2},{7,3},{8,4},{9,5... | collective-permute-start | bytes 663560 | tf_op jit(solution)/shard_map/ppermute | solution.py:438
  78.3 18.0 %collective-permute-start.11 = (f32[2,27648]{1,0:T(2,128)S(1)}, f32[2,27648]{1,0:T(2,128)S(1)}, u32[]{:S(2)}, u32[]{:S(2)}) collective-permute-start(f32[2,27648]{1,0:T(2,128)S(1)} %get-tuple-element.45), channel_id=1, source_target_pairs={{0,126},{1,127},{2,124},{3,125},{4,2},{5,3},{6,0},{7,1},{8,6},{9,7... | collective-permute-start | bytes 663560 | tf_op jit(solution)/shard_map/ppermute | solution.py:438
  97.8 4.0 %collective-permute-start.12 = (f32[4,6912]{1,0:T(4,128)S(1)}, f32[4,6912]{1,0:T(4,128)S(1)}, u32[]{:S(2)}, u32[]{:S(2)}) collective-permute-start(f32[4,6912]{1,0:T(4,128)S(1)} %get-tuple-element.49), channel_id=1, source_target_pairs={{0,32},{1,33},{2,34},{3,35},{4,36},{5,37},{6,38},{7,39},{8,40},{9,... | collective-permute-start | bytes 331784 | tf_op jit(solution)/shard_map/ppermute | solution.py:438
  99.1 7.5 %collective-permute-start.13 = (f32[4,6912]{1,0:T(4,128)S(1)}, f32[4,6912]{1,0:T(4,128)S(1)}, u32[]{:S(2)}, u32[]{:S(2)}) collective-permute-start(f32[4,6912]{1,0:T(4,128)S(1)} %get-tuple-element.50), channel_id=1, source_target_pairs={{0,64},{1,65},{2,66},{3,67},{4,68},{5,69},{6,70},{7,71},{8,72},{9,... | collective-permute-start | bytes 331784 | tf_op jit(solution)/shard_map/ppermute | solution.py:438
  101.7 7.5 %collective-permute-start.14 = (f32[4,6912]{1,0:T(4,128)S(1)}, f32[4,6912]{1,0:T(4,128)S(1)}, u32[]{:S(2)}, u32[]{:S(2)}) collective-permute-start(f32[4,6912]{1,0:T(4,128)S(1)} %get-tuple-element.51), channel_id=1, source_target_pairs={{0,96},{1,97},{2,98},{3,99},{4,100},{5,101},{6,102},{7,103},{8,104... | collective-permute-start | bytes 331784 | tf_op jit(solution)/shard_map/ppermute | solution.py:438
  113.3 4.0 %collective-permute-start.15 = (f32[8,128]{1,0:T(8,128)S(1)}, f32[8,128]{1,0:T(8,128)S(1)}, u32[]{:S(2)}, u32[]{:S(2)}) collective-permute-start(f32[8,128]{1,0:T(8,128)S(1)} %get-tuple-element.53), channel_id=1, source_target_pairs={{0,64},{1,65},{2,66},{3,67},{4,68},{5,69},{6,70},{7,71},{8,72},{9,... | collective-permute-start | bytes 12296 | tf_op jit(solution)/shard_map/ppermute | solution.py:438
  117.4 2.4 %collective-permute-start.16 = (f32[4,128]{1,0:T(4,128)S(1)}, f32[4,128]{1,0:T(4,128)S(1)}, u32[]{:S(2)}, u32[]{:S(2)}) collective-permute-start(f32[4,128]{1,0:T(4,128)S(1)} %slice.7), channel_id=1, source_target_pairs={{0,32},{1,33},{2,34},{3,35},{4,36},{5,37},{6,38},{7,39},{8,40},{9,... | collective-permute-start | bytes 6152 | tf_op jit(solution)/shard_map/ppermute | solution.py:438
  119.8 4.0 %collective-permute-start.17 = (f32[4,128]{1,0:T(4,128)S(1)}, f32[4,128]{1,0:T(4,128)S(1)}, u32[]{:S(2)}, u32[]{:S(2)}) collective-permute-start(f32[4,128]{1,0:T(4,128)S(1)} %slice_add_fusion), channel_id=1, source_target_pairs={{0,1},{1,0},{2,3},{3,2},{4,5},{5,4},{6,7},{7,6},{8,9},{9,8},{10,11... | collective-permute-start | bytes 6152 | tf_op jit(solution)/shard_map/ppermute | solution.py:438
  123.8 2.4 %collective-permute-start.18 = (f32[4,128]{1,0:T(4,128)S(1)}, f32[4,128]{1,0:T(4,128)S(1)}, u32[]{:S(2)}, u32[]{:S(2)}) collective-permute-start(f32[4,128]{1,0:T(4,128)S(1)} %add.18), channel_id=1, source_target_pairs={{0,2},{1,3},{2,0},{3,1},{4,6},{5,7},{6,4},{7,5},{8,10},{9,11},{10,... | collective-permute-start | bytes 6152 | tf_op jit(solution)/shard_map/ppermute | solution.py:438
  (4 other events, 47.7 us)
Sparse Core Ops, SparseCore 0:
  23.4 69.5 all-gather.1

commit v3 on v2

--- a/solution.py
+++ b/solution.py
@@ -98,26 +98,25 @@
     return [a.astype(np.float32) for a in (tens, zs)]
 
 
-def tables_kernel(tens, zs, hi, lo):
-    for way in range(2):
+def tables_kernel(tens, zs, hi_there, lo_there, hi_back, lo_back):
+    for way, (hi, lo) in enumerate(((hi_there, lo_there), (hi_back, lo_back))):
         for which in range(2):
-            k = way * 2 + which
 
             def block(u, carry):
-                w = zs[way] * tens[k, pl.ds(u, 1), :]
+                w = zs[way] * tens[2 * way + which, pl.ds(u, 1), :]
                 top = w.astype(BF16)
                 rows = pl.ds(pl.multiple_of(u * NG, 16), NG)
-                hi[k, rows, :] = top
-                lo[k, rows, :] = (w - top.astype(F32)).astype(BF16)
+                hi[which, rows, :] = top
+                lo[which, rows, :] = (w - top.astype(F32)).astype(BF16)
                 return carry
 
             lax.fori_loop(0, 16, block, 0)
 
 
 def plane_tables():
-    out = jax.ShapeDtypeStruct((4, SLAB, SLAB), BF16)
+    out = [jax.ShapeDtypeStruct((2, SLAB, SLAB), BF16)] * 4
     return pl.pallas_call(
-        tables_kernel, out_shape=(out, out), name="plane_tables",
+        tables_kernel, out_shape=out, name="plane_tables",
         compiler_params=pltpu.CompilerParams(vmem_limit_bytes=16 << 20),
     )(*[jnp.asarray(a) for a in factor_tables()])
 
@@ -198,16 +197,23 @@
     return out
 
 
-def solve_kernel(q_ref, own, two, one, low_a, low_b, core, kern, third, whi_hbm, wlo_hbm, near0, near2, cross, low0, low2,
-                 right, left, hi, lo, field, whi, wlo, sems):
+def split(hi, lo, rows, m, value):
+    top = value.astype(BF16)
+    span = slice(m * SLAB, (m + 1) * SLAB)
+    hi[rows, span] = top
+    lo[rows, span] = (value - top.astype(F32)).astype(BF16)
+
+
+def product(hi, lo, whi, wlo, m, k, cols):
+    span = slice(m * SLAB, (m + 1) * SLAB)
+    a, b = hi[:, span], lo[:, span]
+    lhs = jnp.concatenate([a, b, a], axis=1)
+    w = jnp.concatenate([whi[k, :, cols], whi[k, :, cols], wlo[k, :, cols]], axis=0)
+    return jnp.dot(lhs, w, preferred_element_type=F32)
+
+
+def spectrum_kernel(q_ref, own, two, one, low_a, low_b, core, kern, third, whi, wlo, right, left, field, hi, lo):
     q = q_ref[0]
-    copies = []
-    for way in range(2):
-        part = pl.ds(2 * way, 2)
-        copies.append([pltpu.make_async_copy(whi_hbm.at[part], whi.at[part], sems.at[2 * way]),
-                       pltpu.make_async_copy(wlo_hbm.at[part], wlo.at[part], sems.at[2 * way + 1])])
-        for copy in copies[-1]:
-            copy.start()
     sources = (
         (own, 0, low_a, 0),
         (one, 0, core, 4),
@@ -228,12 +234,6 @@
 
         lax.fori_loop(0, QX, place, 0)
 
-    def split(rows, m, value):
-        top = value.astype(BF16)
-        span = slice(m * SLAB, (m + 1) * SLAB)
-        hi[rows, span] = top
-        lo[rows, span] = (value - top.astype(F32)).astype(BF16)
-
     def densities(i, carry):
         x = pl.ds(2 * i, 2)
         rows = pl.ds(pl.multiple_of(16 * i, 16), 16)
@@ -241,27 +241,18 @@
         for m in range(3):
             span = slice(m * SLAB, (m + 1) * SLAB)
             f.append((right[x, :, span] * left[x, :, span]).reshape(16, SLAB))
-        split(rows, 0, f[0] + f[1] + f[2])
-        split(rows, 1, f[0] * third[0:1, :] + f[1] * third[1:2, :] + f[2] * third[2:3, :])
-        split(rows, 2, f[0] * third[3:4, :] + f[1] * third[4:5, :] + f[2] * third[5:6, :])
+        split(hi, lo, rows, 0, f[0] + f[1] + f[2])
+        split(hi, lo, rows, 1, f[0] * third[0:1, :] + f[1] * third[1:2, :] + f[2] * third[2:3, :])
+        split(hi, lo, rows, 2, f[0] * third[3:4, :] + f[1] * third[4:5, :] + f[2] * third[5:6, :])
         return carry
 
     lax.fori_loop(0, NG // 2, densities, 0)
 
-    def product(m, k, cols):
-        span = slice(m * SLAB, (m + 1) * SLAB)
-        a, b = hi[:, span], lo[:, span]
-        lhs = jnp.concatenate([a, b, a], axis=1)
-        w = jnp.concatenate([whi[k, :, cols], whi[k, :, cols], wlo[k, :, cols]], axis=0)
-        return jnp.dot(lhs, w, preferred_element_type=F32)
-
-    for copy in copies[0]:
-        copy.wait()
     for j in range(3):
         cols = slice(j * 256, (j + 1) * 256)
-        field[:, cols] = product(0, 0, cols)
-        c = product(1, 0, cols)
-        s = product(2, 1, cols)
+        field[:, cols] = product(hi, lo, whi, wlo, 0, 0, cols)
+        c = product(hi, lo, whi, wlo, 1, 0, cols)
+        s = product(hi, lo, whi, wlo, 2, 1, cols)
         field[:, SLAB + j * 256 : SLAB + (j + 1) * 256] = c - s
         field[:, 2 * SLAB + j * 256 : 2 * SLAB + (j + 1) * 256] = c + s
 
@@ -275,22 +266,24 @@
 
     lax.fori_loop(0, PLANE // 128, along_x, 0)
 
+
+def terms_kernel(q_ref, right, left, field, third, whi, wlo, near0, near2, cross, low0, low2, hi, lo, back):
+    q = q_ref[0]
+
     def unmix(i, carry):
         rows = pl.ds(pl.multiple_of(16 * i, 16), 16)
         u = field[rows, SLAB : 2 * SLAB]
         v = field[rows, 2 * SLAB : 3 * SLAB]
-        split(rows, 0, field[rows, 0:SLAB])
-        split(rows, 1, u + v)
-        split(rows, 2, v - u)
+        split(hi, lo, rows, 0, field[rows, 0:SLAB])
+        split(hi, lo, rows, 1, u + v)
+        split(hi, lo, rows, 2, v - u)
         return carry
 
     lax.fori_loop(0, NG // 2, unmix, 0)
-    for copy in copies[1]:
-        copy.wait()
     for j in range(3):
         cols = slice(j * 256, (j + 1) * 256)
-        for m, k in ((0, 2), (1, 2), (2, 3)):
-            field[:, m * SLAB + j * 256 : m * SLAB + (j + 1) * 256] = product(m, k, cols)
+        for m, k in ((0, 0), (1, 0), (2, 1)):
+            back[:, m * SLAB + j * 256 : m * SLAB + (j + 1) * 256] = product(hi, lo, whi, wlo, m, k, cols)
 
     mine = (lax.broadcasted_iota(jnp.int32, (8, SLAB), 0) == q).astype(F32)
 
@@ -300,9 +293,9 @@
         def finish(i, carry):
             x = base + i
             rows = pl.ds(pl.multiple_of(x * 8, 8), 8)
-            a = field[rows, 0:SLAB]
-            c = field[rows, SLAB : 2 * SLAB]
-            s = field[rows, 2 * SLAB : 3 * SLAB]
+            a = back[rows, 0:SLAB]
+            c = back[rows, SLAB : 2 * SLAB]
+            s = back[rows, 2 * SLAB : 3 * SLAB]
             for m in range(3):
                 span = slice(m * SLAB, (m + 1) * SLAB)
                 v = a + c * third[m : m + 1, :] + s * third[3 + m : 4 + m, :]
@@ -323,26 +316,33 @@
         lax.fori_loop(0, QX, finish, 0)
 
 
-def solve_pairs(q, bands, tables):
-    vmem = pl.BlockSpec(memory_space=pltpu.VMEM)
+VMEM_SPEC = pl.BlockSpec(memory_space=pltpu.VMEM)
+SMEM_SPEC = pl.BlockSpec(memory_space=pltpu.SMEM)
+SPLIT = [pltpu.VMEM((NG * 8, PLANE), BF16)] * 2
+
+
+def spectrum(q, bands, tables):
     return pl.pallas_call(
-        solve_kernel,
+        spectrum_kernel,
+        out_shape=[jax.ShapeDtypeStruct((NG, 8, PLANE), F32)] * 2 + [jax.ShapeDtypeStruct((NG * 8, PLANE), F32)],
+        in_specs=[SMEM_SPEC] + [VMEM_SPEC] * 10,
+        out_specs=[VMEM_SPEC] * 3,
+        scratch_shapes=SPLIT,
+        name="spectrum",
+        compiler_params=pltpu.CompilerParams(vmem_limit_bytes=24 << 20),
+    )(q.reshape(1), *bands, jnp.asarray(kernel_values()), jnp.asarray(thirds()), *tables)
+
+
+def terms(q, right, left, field, tables):
+    return pl.pallas_call(
+        terms_kernel,
         out_shape=[jax.ShapeDtypeStruct(shape, F32) for shape in [(4, QCELL)] * 2 + [(10, QCELL)] + [(1, QCELL)] * 2],
-        in_specs=[pl.BlockSpec(memory_space=pltpu.SMEM)] + [vmem] * 8 + [pl.BlockSpec(memory_space=pltpu.HBM)] * 2,
-        out_specs=[vmem] * 5,
-        scratch_shapes=[
-            pltpu.VMEM((NG, 8, PLANE), F32),
-            pltpu.VMEM((NG, 8, PLANE), F32),
-            pltpu.VMEM((NG * 8, PLANE), BF16),
-            pltpu.VMEM((NG * 8, PLANE), BF16),
-            pltpu.VMEM((NG * 8, PLANE), F32),
-            pltpu.VMEM((4, SLAB, SLAB), BF16),
-            pltpu.VMEM((4, SLAB, SLAB), BF16),
-            pltpu.SemaphoreType.DMA((4,)),
-        ],
-        name="solve_pairs",
-        compiler_params=pltpu.CompilerParams(vmem_limit_bytes=40 << 20),
-    )(q.reshape(1), *bands, jnp.asarray(kernel_values()), jnp.asarray(thirds()), *tables)
+        in_specs=[SMEM_SPEC] + [VMEM_SPEC] * 6,
+        out_specs=[VMEM_SPEC] * 5,
+        scratch_shapes=SPLIT + [pltpu.VMEM((NG * 8, PLANE), F32)],
+        name="terms",
+        compiler_params=pltpu.CompilerParams(vmem_limit_bytes=28 << 20),
+    )(q.reshape(1), right, left, field, jnp.asarray(thirds()), *tables)
 
 
 BOTH = ("band", "grid")
@@ -404,26 +404,35 @@
         chunks[k][...] = vectors[:, chunk_of(where, k)]
 
 
-def margin_kernel(where, gathered, v0, v1, v2, v3, m01, m23, block):
-    z = where[1]
+def pair_kernel(where, f0, f1, f2, f3, other, out):
+    first = where[3] == 0
+    for k, f in enumerate((f0, f1, f2, f3)):
+        a, b = f[...], other[4 * k : 4 * k + 4, :]
+        out[8 * k : 8 * k + 4, :] = jnp.where(first, a, b)
+        out[8 * k + 4 : 8 * k + 8, :] = jnp.where(first, b, a)
+
+
+def margin_kernel(where, p0, p1, p3, p2a, p2b, v0, v1, v2, v3, m01, m23, block):
+    z, y = where[1], where[2]
 
     def halves(a):
         top = a.astype(BF16)
         return top, (a - top.astype(F32)).astype(BF16)
 
     vt, vl = halves(jnp.concatenate([v0[...], v1[...], v2[...], v3[...]], axis=0))
-    ft, fl = halves(gathered[...])
     dims = (((1,), (1,)), ((), ()))
+    parts = jnp.concatenate([p0[...], p1[...], p2a[...], p2b[...], p3[...]], axis=0)
+    ft, fl = halves(parts)
     got = (
         lax.dot_general(ft, vt, dims, preferred_element_type=F32)
         + lax.dot_general(fl, vt, dims, preferred_element_type=F32)
         + lax.dot_general(ft, vl, dims, preferred_element_type=F32)
     )
-    for m in range(8):
+    for dy in range(4):
         for dz in range(4):
-            row = 16 * m + 4 * dz
-            block[(z ^ dz) * 8 + m, :, :] = got[row : row + 4, :]
-    out = jnp.concatenate([block[i] for i in range(32)], axis=0).T * (1.0 / NCELL)
+            row = 32 * dy + 8 * dz
+            block[(z ^ dz) * 4 + (y + 4 - dy) % 4, :, :] = got[row : row + 8, :]
+    out = block[...].reshape(128, 16).T * (1.0 / NCELL)
     m01[...] = out[0:8, :]
     m23[...] = out[8:16, :]
 
@@ -442,6 +451,10 @@
     return move(value, lambda z, y, h, q: (z ^ flip, y, h, q))
 
 
+def along_y(value, k):
+    return move(value, lambda z, y, h, q: (z, y + k, h, q))
+
+
 def within(value, flip):
     return move(value, lambda z, y, h, q: (z, y, h, q ^ flip))
 
@@ -457,7 +470,7 @@
 def step(orbitals):
     b = lax.axis_index("band").astype(jnp.int32)
     q = lax.axis_index("grid").astype(jnp.int32)
-    where = jnp.stack([q, b // 8])
+    where = jnp.stack([q, b // 8, b // 2 % 4, b % 2])
     two = within(orbitals, 2)
     prepare = small_call(prepare_kernel, [(2, QCELL)] * 2 + [(4, CHUNK)] * 4)
     sel_a, sel_b, *zc = prepare(where, orbitals)
@@ -467,24 +480,28 @@
     pieces = [zc[0]] + [along_z(zc[k], k) for k in (1, 2, 3)]
     tables = plane_tables()
     together = jnp.concatenate(pieces, axis=0)
-    groups = [[z * 8 + i for i in range(8)] for z in range(4)]
-    gathered = lax.all_gather(together, "band", axis_index_groups=groups, axis=0, tiled=True)
     two, together = lax.optimization_barrier((two, together))
     (stacked,) = small_call(stack_kernel, [(8, QCELL)])(where, two, low_a, low_b)
     core = within(stacked, 1)
-    near0, near2, cross, low0, low2 = solve_pairs(q, (orbitals, two, one, low_a, low_b, core), tables)
+    other = move(together, lambda z, y, h, q: (z, y, 1 - h, q))
+    right, left, field = spectrum(q, (orbitals, two, one, low_a, low_b, core), tables[:2])
+    (p0,) = small_call(pair_kernel, [(32, CHUNK)])(where, *pieces, other)
+    p1 = along_y(p0, 1)
+    p3 = along_y(p0, 3)
+    near0, near2, cross, low0, low2 = terms(q, right, left, field, tables[2:])
     across = within(cross, 1)
     merge = small_call(merge_kernel, [(4, QCELL)] * 2 + [(2, QCELL)] * 2)
     near, both, owe_a, owe_b = merge(where, near0, near2, low0, low2, across)
     far = within(both, 2)
     owed_a = around(owe_a, -1, 0)
     owed_b = around(owe_b, -1, 2)
+    p2a = along_y(p1[:16], 1)
+    p2b = along_y(p3[16:], 3)
     finalize = small_call(finalize_kernel, [(4, QCELL)] + [(4, CHUNK)] * 4)
     vectors, *vc = finalize(where, near, far, owed_a, owed_b)
     given = [vc[0]] + [along_z(vc[k], k) for k in (1, 2, 3)]
-    gathered, _ = lax.optimization_barrier((gathered, vc[0]))
-    margin_part = small_call(margin_kernel, [(8, 128)] * 2, [pltpu.VMEM((32, 4, 16), F32)], 20)
-    m01, m23 = margin_part(where, gathered, *given)
+    margin_part = small_call(margin_kernel, [(8, 128)] * 2, [pltpu.VMEM((16, 8, 16), F32)], 20)
+    m01, m23 = margin_part(where, p0, p1, p3, p2a, p2b, *given)
     m01 = m01 + along_z(m23, 2)
     mine = m01[0:4] + along_z(m01[4:8], 1)
     mine = mine + within(mine, 1)

time: 134 us -> 121 us (0.903)
  between operations: 14.2 us -> 0.82 us
  local copies, waits for them, and re-layouts: 5.82 us -> 0.75 us
  waiting for transfers between devices: 60.5 us -> 62.6 us
  starting transfers between devices: 26.7 us -> 28.5 us
  Pallas kernels: 25.5 us -> 27 us
    unnamed x16 -> x8, local copies, waits for them, and re-layouts: 5.16 us -> 0.03 us
    ppermute x19 -> x24, waiting for transfers between devices: 60.5 us -> 62.6 us  [move(): return lax.ppermute(value, BOTH, pairs)]
    ppermute x19 -> x24, starting transfers between devices: 26.6 us -> 28.5 us  [move(): return lax.ppermute(value, BOTH, pairs)]
    pallas_call x5 -> x6, Pallas kernels: 5.72 us -> 7.11 us  [call(): pl.pallas_call(body, out_shape=[jax.ShapeDtypeStruct(shape, F32) for shap...]
    pallas_call x2 -> x3, Pallas kernels: 19.8 us -> 19.9 us  [the longest x1 10.2 us: spectrum(): pl.pallas_call(spectrum_kernel, out_shape=[jax.ShapeDtypeStruct((NG, 8, P...]
  transfers between devices with their start and end apart: 20 -> 24, of which waited for: 13 -> 14; matrix products, arithmetic and copies ran while one was open for 0% -> 0% of each run, Pallas kernels for 17% -> 19%
where the time goes in v3:
time: 121 us; the launch traced here: 120 us
  waiting for transfers between devices  62.6 us (52%)
  starting transfers between devices  28.5 us (24%)
  Pallas kernels  27 us (22%)
    ppermute x24, waiting for transfers between devices, move(): return lax.ppermute(value, BOTH, pairs)  62.6 us
    ppermute x24, starting transfers between devices, move(): return lax.ppermute(value, BOTH, pairs)  28.5 us
    pallas_call x1, Pallas kernels, spectrum(): pl.pallas_call(spectrum_kernel, out_shape=[jax.ShapeDtypeStruct((NG, 8, P...  10.2 us
    pallas_call x1, Pallas kernels, terms(): pl.pallas_call(terms_kernel, out_shape=[jax.ShapeDtypeStruct(shape, F32)...  7.72 us
    pallas_call x6, Pallas kernels, call(): pl.pallas_call(body, out_shape=[jax.ShapeDtypeStruct(shape, F32) for shap...  7.11 us
  transfers between devices with their start and end apart: 24, of which 14 were waited for; matrix products, arithmetic and copies ran while one was open for 0% of the time, Pallas kernels for 19%

profile of v3, /device:TPU:1, one launch (start us, length us, event | category | flops | bytes accessed | tf_op | source)
XLA Modules:
  0.0 119.8 jit_solution(6862303900586564747)
XLA Ops:
  2.1 2.5 %collective-permute-start.1 = (f32[4,6912]{1,0:T(4,128)S(1)}, f32[4,6912]{1,0:T(4,128)S(1)}, u32[]{:S(2)}, u32[]{:S(2)}) collective-permute-start(f32[4,6912]{1,0:T(4,128)S(1)} %get-tuple-element.34), channel_id=1, source_target_pairs={{0,32},{1,33},{2,34},{3,35},{4,36},{5,37},{6,38},{7,39},{8,40},{9,... | collective-permute-start | bytes 331784 | tf_op jit(solution)/shard_map/ppermute | solution.py:447
  4.6 3.3 %collective-permute-start.2 = (f32[4,6912]{1,0:T(4,128)S(1)}, f32[4,6912]{1,0:T(4,128)S(1)}, u32[]{:S(2)}, u32[]{:S(2)}) collective-permute-start(f32[4,6912]{1,0:T(4,128)S(1)} %get-tuple-element.35), channel_id=1, source_target_pairs={{0,64},{1,65},{2,66},{3,67},{4,68},{5,69},{6,70},{7,71},{8,72},{9,... | collective-permute-start | bytes 331784 | tf_op jit(solution)/shard_map/ppermute | solution.py:447
  9.1 2.5 %collective-permute-start.5 = (f32[2,27648]{1,0:T(2,128)S(1)}, f32[2,27648]{1,0:T(2,128)S(1)}, u32[]{:S(2)}, u32[]{:S(2)}) collective-permute-start(f32[2,27648]{1,0:T(2,128)S(1)} %get-tuple-element.38), channel_id=1, source_target_pairs={{0,4},{1,5},{2,6},{3,7},{4,8},{5,9},{6,10},{7,11},{8,12},{9,13},{1... | collective-permute-start | bytes 663560 | tf_op jit(solution)/shard_map/ppermute | solution.py:447
  12.8 2.5 %collective-permute-done.3.f3 = f32[4,6912]{1,0:T(4,128)S(1)} collective-permute-done((f32[4,6912]{1,0:T(4,128)S(1)}, f32[4,6912]{1,0:T(4,128)S(1)}, u32[]{:S(2)}, u32[]{:S(2)}) %collective-permute-start.3) | collective-permute-done | bytes 110624 | tf_op jit(solution)/shard_map/ppermute | solution.py:447
  15.5 3.2 %collective-permute-done.two = f32[4,27648]{1,0:T(4,128)S(1)} collective-permute-done((f32[4,27648]{1,0:T(4,128)}, f32[4,27648]{1,0:T(4,128)S(1)}, u32[]{:S(2)}, u32[]{:S(2)}) %collective-permute-start) | collective-permute-done | bytes 442400 | tf_op jit(solution)/shard_map/ppermute | solution.py:447
  18.6 11.5 %collective-permute-done.5.low_a = f32[2,27648]{1,0:T(2,128)S(1)} collective-permute-done((f32[2,27648]{1,0:T(2,128)S(1)}, f32[2,27648]{1,0:T(2,128)S(1)}, u32[]{:S(2)}, u32[]{:S(2)}) %collective-permute-start.5) | collective-permute-done | bytes 221216 | tf_op jit(solution)/shard_map/ppermute | solution.py:447
  30.9 2.5 %collective-permute-start.7 = (f32[8,27648]{1,0:T(8,128)S(1)}, f32[8,27648]{1,0:T(8,128)S(1)}, u32[]{:S(2)}, u32[]{:S(2)}) collective-permute-start(f32[8,27648]{1,0:T(8,128)S(1)} %shard_map.78), channel_id=1, source_target_pairs={{0,1},{1,0},{2,3},{3,2},{4,5},{5,4},{6,7},{7,6},{8,9},{9,8},{10,11... | collective-permute-start | bytes 2654216 | tf_op jit(solution)/shard_map/ppermute | solution.py:447
  33.4 1.9 %plane_tables.1 = (bf16[2,768,768]{2,1,0:T(8,128)(2,1)S(1)}, bf16[2,768,768]{2,1,0:T(8,128)(2,1)S(1)}, bf16[2,768,768]{2,1,0:T(8,128)(2,1)S(1)}, bf16[2,768,768]{2,1,0:T(8,128)(2,1)S(1)}) custom-call(f32[4,16,768]{2,1,0:T(8,128)S(1)} %copy-done.2, f32[2,48,768]{2,1,0:T(8,128)S(1)} %copy-done.1), custom_call_target="tpu_custom_call" | custom-call | tf_op jit(solution)/shard_map/plane_tables/pallas_call | solution.py:118
  36.0 10.2 %spectrum.1 = (f32[48,8,2304]{2,1,0:T(8,128)S(1)}, f32[48,8,2304]{2,1,0:T(8,128)S(1)}, f32[384,2304]{1,0:T(8,128)S(1)}) custom-call(s32[1]{0:T(128)} %bitcast.q_ref, f32[4,27648]{1,0:T(4,128)} %own.1, f32[4,27648]{1,0:T(4,128)S(1)} %collective-permute-done.two, f32[4,27648]{1,0:T(4,128)S(1)} %collective-permute-done.4.one, ...), custom_call_target="tpu_custom_call" | custom-call | tf_op jit(solution)/shard_map/spectrum/pallas_call | solution.py:325
  46.2 7.7 %terms.1 = (f32[4,27648]{1,0:T(4,128)S(1)}, f32[4,27648]{1,0:T(4,128)S(1)}, f32[10,27648]{1,0:T(8,128)S(1)}, f32[1,27648]{1,0:T(1,128)S(1)}, f32[1,27648]{1,0:T(1,128)S(1)}) custom-call(s32[1]{0:T(128)} %bitcast.q_ref, f32[48,8,2304]{2,1,0:T(8,128)S(1)} %get-tuple-element.42.right, f32[48,8,2304]{2,1,0:T(8,128)S(1)} %get-tuple-element.43.left, ...), custom_call_target="tpu_custom_call" | custom-call | tf_op jit(solution)/shard_map/terms/pallas_call | solution.py:337
  55.2 2.7 %collective-permute-start.14 = (f32[32,6912]{1,0:T(8,128)S(1)}, f32[32,6912]{1,0:T(8,128)S(1)}, u32[]{:S(2)}, u32[]{:S(2)}) collective-permute-start(f32[32,6912]{1,0:T(8,128)S(1)} %shard_map.81.p0), channel_id=1, source_target_pairs={{0,24},{1,25},{2,26},{3,27},{4,28},{5,29},{6,30},{7,31},{8,0},{9,1... | collective-permute-start | bytes 2654216 | tf_op jit(solution)/shard_map/ppermute | solution.py:447
  58.7 18.8 %collective-permute-done.13.p1 = f32[32,6912]{1,0:T(8,128)S(1)} collective-permute-done((f32[32,6912]{1,0:T(8,128)S(1)}, f32[32,6912]{1,0:T(8,128)S(1)}, u32[]{:S(2)}, u32[]{:S(2)}) %collective-permute-start.13) | collective-permute-done | bytes 884768 | tf_op jit(solution)/shard_map/ppermute | solution.py:447
  77.8 2.7 %collective-permute-start.16 = (f32[16,6912]{1,0:T(8,128)S(1)}, f32[16,6912]{1,0:T(8,128)S(1)}, u32[]{:S(2)}, u32[]{:S(2)}) collective-permute-start(f32[16,6912]{1,0:T(8,128)S(1)} %slice.17), channel_id=1, source_target_pairs={{0,24},{1,25},{2,26},{3,27},{4,28},{5,29},{6,30},{7,31},{8,0},{9,1... | collective-permute-start | bytes 1327112 | tf_op jit(solution)/shard_map/ppermute | solution.py:447
  81.8 5.8 %collective-permute-done.10.owed_a = f32[2,27648]{1,0:T(2,128)S(1)} collective-permute-done((f32[2,27648]{1,0:T(2,128)S(1)}, f32[2,27648]{1,0:T(2,128)S(1)}, u32[]{:S(2)}, u32[]{:S(2)}) %collective-permute-start.10) | collective-permute-done | bytes 221216 | tf_op jit(solution)/shard_map/ppermute | solution.py:447
  87.6 6.6 %collective-permute-done.11.owed_b = f32[2,27648]{1,0:T(2,128)S(1)} collective-permute-done((f32[2,27648]{1,0:T(2,128)S(1)}, f32[2,27648]{1,0:T(2,128)S(1)}, u32[]{:S(2)}, u32[]{:S(2)}) %collective-permute-start.11) | collective-permute-done | bytes 221216 | tf_op jit(solution)/shard_map/ppermute | solution.py:447
  94.2 1.5 %shard_map.80 = (f32[4,27648]{1,0:T(4,128)}, f32[4,6912]{1,0:T(4,128)S(1)}, f32[4,6912]{1,0:T(4,128)S(1)}, f32[4,6912]{1,0:T(4,128)S(1)}, f32[4,6912]{1,0:T(4,128)S(1)}) custom-call(s32[4]{0:T(128)S(1)} %pad_add_fusion.where, f32[4,27648]{1,0:T(4,128)S(1)} %get-tuple-element.52.near, f32[4,27648]{1,0:T(4,128)S(1)} %collective-permute-done.9.far, ...), custom_call_target="tpu_custom_call" | custom-call | tf_op jit(solution)/shard_map/pallas_call | solution.py:356
  95.7 3.8 %collective-permute-start.19 = (f32[4,6912]{1,0:T(4,128)S(1)}, f32[4,6912]{1,0:T(4,128)S(1)}, u32[]{:S(2)}, u32[]{:S(2)}) collective-permute-start(f32[4,6912]{1,0:T(4,128)S(1)} %get-tuple-element.61), channel_id=1, source_target_pairs={{0,96},{1,97},{2,98},{3,99},{4,100},{5,101},{6,102},{7,103},{8,104... | collective-permute-start | bytes 331784 | tf_op jit(solution)/shard_map/ppermute | solution.py:447
  99.8 1.5 %collective-permute-done.18.v2 = f32[4,6912]{1,0:T(4,128)S(1)} collective-permute-done((f32[4,6912]{1,0:T(4,128)S(1)}, f32[4,6912]{1,0:T(4,128)S(1)}, u32[]{:S(2)}, u32[]{:S(2)}) %collective-permute-start.18) | collective-permute-done | bytes 110624 | tf_op jit(solution)/shard_map/ppermute | solution.py:447
  101.3 3.3 %collective-permute-done.19.v3 = f32[4,6912]{1,0:T(4,128)S(1)} collective-permute-done((f32[4,6912]{1,0:T(4,128)S(1)}, f32[4,6912]{1,0:T(4,128)S(1)}, u32[]{:S(2)}, u32[]{:S(2)}) %collective-permute-start.19) | collective-permute-done | bytes 110624 | tf_op jit(solution)/shard_map/ppermute | solution.py:447
  104.5 2.1 %shard_map.82 = (f32[8,128]{1,0:T(8,128)S(1)}, f32[8,128]{1,0:T(8,128)S(1)}) custom-call(s32[4]{0:T(128)S(1)} %pad_add_fusion.where, f32[32,6912]{1,0:T(8,128)S(1)} %shard_map.81.p0, f32[32,6912]{1,0:T(8,128)S(1)} %collective-permute-done.13.p1, f32[32,6912]{1,0:T(8,128)S(1)} %collective-permute-done.14.p3, f32[16,6912]{1,0:T(8,128)S(1)} %collective-permute-done.15.p2a, ...), custom_call_target="tpu_custom_call" | custom-call | tf_op jit(solution)/shard_map/pallas_call | solution.py:356
  107.5 3.1 %collective-permute-done.20 = f32[8,128]{1,0:T(8,128)S(1)} collective-permute-done((f32[8,128]{1,0:T(8,128)S(1)}, f32[8,128]{1,0:T(8,128)S(1)}, u32[]{:S(2)}, u32[]{:S(2)}) %collective-permute-start.20) | collective-permute-done | bytes 4128 | tf_op jit(solution)/shard_map/ppermute | solution.py:447
  110.9 2.2 %collective-permute-done.21 = f32[4,128]{1,0:T(4,128)S(1)} collective-permute-done((f32[4,128]{1,0:T(4,128)S(1)}, f32[4,128]{1,0:T(4,128)S(1)}, u32[]{:S(2)}, u32[]{:S(2)}) %collective-permute-start.21) | collective-permute-done | bytes 2080 | tf_op jit(solution)/shard_map/ppermute | solution.py:447
  113.1 2.8 %collective-permute-start.22 = (f32[4,128]{1,0:T(4,128)S(1)}, f32[4,128]{1,0:T(4,128)S(1)}, u32[]{:S(2)}, u32[]{:S(2)}) collective-permute-start(f32[4,128]{1,0:T(4,128)S(1)} %slice_add_fusion), channel_id=1, source_target_pairs={{0,1},{1,0},{2,3},{3,2},{4,5},{5,4},{6,7},{7,6},{8,9},{9,8},{10,11... | collective-permute-start | bytes 6152 | tf_op jit(solution)/shard_map/ppermute | solution.py:447
  116.7 2.4 %collective-permute-done.23 = f32[4,128]{1,0:T(4,128)S(1)} collective-permute-done((f32[4,128]{1,0:T(4,128)S(1)}, f32[4,128]{1,0:T(4,128)S(1)}, u32[]{:S(2)}, u32[]{:S(2)}) %collective-permute-start.23) | collective-permute-done | bytes 2080 | tf_op jit(solution)/shard_map/ppermute | solution.py:447
  (51 shorter events, 12.0 us)
Async XLA Ops:
  2.1 9.5 %collective-permute-start.1 = (f32[4,6912]{1,0:T(4,128)S(1)}, f32[4,6912]{1,0:T(4,128)S(1)}, u32[]{:S(2)}, u32[]{:S(2)}) collective-permute-start(f32[4,6912]{1,0:T(4,128)S(1)} %get-tuple-element.34), channel_id=1, source_target_pairs={{0,32},{1,33},{2,34},{3,35},{4,36},{5,37},{6,38},{7,39},{8,40},{9,... | collective-permute-start | bytes 331784 | tf_op jit(solution)/shard_map/ppermute | solution.py:447
  4.6 8.2 %collective-permute-start.2 = (f32[4,6912]{1,0:T(4,128)S(1)}, f32[4,6912]{1,0:T(4,128)S(1)}, u32[]{:S(2)}, u32[]{:S(2)}) collective-permute-start(f32[4,6912]{1,0:T(4,128)S(1)} %get-tuple-element.35), channel_id=1, source_target_pairs={{0,64},{1,65},{2,66},{3,67},{4,68},{5,69},{6,70},{7,71},{8,72},{9,... | collective-permute-start | bytes 331784 | tf_op jit(solution)/shard_map/ppermute | solution.py:447
  7.9 7.4 %collective-permute-start.3 = (f32[4,6912]{1,0:T(4,128)S(1)}, f32[4,6912]{1,0:T(4,128)S(1)}, u32[]{:S(2)}, u32[]{:S(2)}) collective-permute-start(f32[4,6912]{1,0:T(4,128)S(1)} %get-tuple-element.36), channel_id=1, source_target_pairs={{0,96},{1,97},{2,98},{3,99},{4,100},{5,101},{6,102},{7,103},{8,104... | collective-permute-start | bytes 331784 | tf_op jit(solution)/shard_map/ppermute | solution.py:447
  7.9 10.7 %collective-permute-start = (f32[4,27648]{1,0:T(4,128)}, f32[4,27648]{1,0:T(4,128)S(1)}, u32[]{:S(2)}, u32[]{:S(2)}) collective-permute-start(f32[4,27648]{1,0:T(4,128)} %own.1), channel_id=1, source_target_pairs={{0,2},{1,3},{2,0},{3,1},{4,6},{5,7},{6,4},{7,5},{8,10},{9,11},{10,... | collective-permute-start | bytes 1327112 | tf_op jit(solution)/shard_map/ppermute | solution.py:447
  9.1 21.0 %collective-permute-start.5 = (f32[2,27648]{1,0:T(2,128)S(1)}, f32[2,27648]{1,0:T(2,128)S(1)}, u32[]{:S(2)}, u32[]{:S(2)}) collective-permute-start(f32[2,27648]{1,0:T(2,128)S(1)} %get-tuple-element.38), channel_id=1, source_target_pairs={{0,4},{1,5},{2,6},{3,7},{4,8},{5,9},{6,10},{7,11},{8,12},{9,13},{1... | collective-permute-start | bytes 663560 | tf_op jit(solution)/shard_map/ppermute | solution.py:447
  11.6 18.5 %collective-permute-start.6 = (f32[2,27648]{1,0:T(2,128)S(1)}, f32[2,27648]{1,0:T(2,128)S(1)}, u32[]{:S(2)}, u32[]{:S(2)}) collective-permute-start(f32[2,27648]{1,0:T(2,128)S(1)} %get-tuple-element.39), channel_id=1, source_target_pairs={{0,6},{1,7},{2,4},{3,5},{4,10},{5,11},{6,8},{7,9},{8,14},{9,15},{1... | collective-permute-start | bytes 663560 | tf_op jit(solution)/shard_map/ppermute | solution.py:447
  30.9 5.1 %collective-permute-start.7 = (f32[8,27648]{1,0:T(8,128)S(1)}, f32[8,27648]{1,0:T(8,128)S(1)}, u32[]{:S(2)}, u32[]{:S(2)}) collective-permute-start(f32[8,27648]{1,0:T(8,128)S(1)} %shard_map.78), channel_id=1, source_target_pairs={{0,1},{1,0},{2,3},{3,2},{4,5},{5,4},{6,7},{7,6},{8,9},{9,8},{10,11... | collective-permute-start | bytes 2654216 | tf_op jit(solution)/shard_map/ppermute | solution.py:447
  33.3 2.7 %collective-permute-start.4 = (f32[4,27648]{1,0:T(4,128)}, f32[4,27648]{1,0:T(4,128)S(1)}, u32[]{:S(2)}, u32[]{:S(2)}) collective-permute-start(f32[4,27648]{1,0:T(4,128)} %own.1), channel_id=1, source_target_pairs={{0,1},{1,0},{2,3},{3,2},{4,5},{5,4},{6,7},{7,6},{8,9},{9,8},{10,11... | collective-permute-start | bytes 1327112 | tf_op jit(solution)/shard_map/ppermute | solution.py:447
  33.4 21.0 %collective-permute-start.12 = (f32[16,6912]{1,0:T(8,128)S(1)}, f32[16,6912]{1,0:T(8,128)S(1)}, u32[]{:S(2)}, u32[]{:S(2)}) collective-permute-start(f32[16,6912]{1,0:T(8,128)S(1)} %pad_maximum_fusion), channel_id=1, source_target_pairs={{0,4},{1,5},{2,6},{3,7},{4,0},{5,1},{6,2},{7,3},{8,12},{9,13},{10,... | collective-permute-start | bytes 1327112 | tf_op jit(solution)/shard_map/ppermute | solution.py:447
  53.9 3.9 %collective-permute-start.8 = (f32[10,27648]{1,0:T(8,128)S(1)}, f32[10,27648]{1,0:T(8,128)S(1)}, u32[]{:S(2)}, u32[]{:S(2)}) collective-permute-start(f32[10,27648]{1,0:T(8,128)S(1)} %get-tuple-element.51), channel_id=1, source_target_pairs={{0,1},{1,0},{2,3},{3,2},{4,5},{5,4},{6,7},{7,6},{8,9},{9,8},{10,11... | collective-permute-start | bytes 3317768 | tf_op jit(solution)/shard_map/ppermute | solution.py:447
  55.1 22.4 %collective-permute-start.13 = (f32[32,6912]{1,0:T(8,128)S(1)}, f32[32,6912]{1,0:T(8,128)S(1)}, u32[]{:S(2)}, u32[]{:S(2)}) collective-permute-start(f32[32,6912]{1,0:T(8,128)S(1)} %shard_map.81.p0), channel_id=1, source_target_pairs={{0,8},{1,9},{2,10},{3,11},{4,12},{5,13},{6,14},{7,15},{8,16},{9,17... | collective-permute-start | bytes 2654216 | tf_op jit(solution)/shard_map/ppermute | solution.py:447
  55.2 22.6 %collective-permute-start.14 = (f32[32,6912]{1,0:T(8,128)S(1)}, f32[32,6912]{1,0:T(8,128)S(1)}, u32[]{:S(2)}, u32[]{:S(2)}) collective-permute-start(f32[32,6912]{1,0:T(8,128)S(1)} %shard_map.81.p0), channel_id=1, source_target_pairs={{0,24},{1,25},{2,26},{3,27},{4,28},{5,29},{6,30},{7,31},{8,0},{9,1... | collective-permute-start | bytes 2654216 | tf_op jit(solution)/shard_map/ppermute | solution.py:447
  58.6 35.5 %collective-permute-start.9 = (f32[4,27648]{1,0:T(4,128)S(1)}, f32[4,27648]{1,0:T(4,128)S(1)}, u32[]{:S(2)}, u32[]{:S(2)}) collective-permute-start(f32[4,27648]{1,0:T(4,128)S(1)} %get-tuple-element.53), channel_id=1, source_target_pairs={{0,2},{1,3},{2,0},{3,1},{4,6},{5,7},{6,4},{7,5},{8,10},{9,11},{10,... | collective-permute-start | bytes 1327112 | tf_op jit(solution)/shard_map/ppermute | solution.py:447
  77.5 22.0 %collective-permute-start.15 = (f32[16,6912]{1,0:T(8,128)S(1)}, f32[16,6912]{1,0:T(8,128)S(1)}, u32[]{:S(2)}, u32[]{:S(2)}) collective-permute-start(f32[16,6912]{1,0:T(8,128)S(1)} %slice.16), channel_id=1, source_target_pairs={{0,8},{1,9},{2,10},{3,11},{4,12},{5,13},{6,14},{7,15},{8,16},{9,17... | collective-permute-start | bytes 1327112 | tf_op jit(solution)/shard_map/ppermute | solution.py:447
  77.8 21.7 %collective-permute-start.16 = (f32[16,6912]{1,0:T(8,128)S(1)}, f32[16,6912]{1,0:T(8,128)S(1)}, u32[]{:S(2)}, u32[]{:S(2)}) collective-permute-start(f32[16,6912]{1,0:T(8,128)S(1)} %slice.17), channel_id=1, source_target_pairs={{0,24},{1,25},{2,26},{3,27},{4,28},{5,29},{6,30},{7,31},{8,0},{9,1... | collective-permute-start | bytes 1327112 | tf_op jit(solution)/shard_map/ppermute | solution.py:447
  80.6 7.0 %collective-permute-start.10 = (f32[2,27648]{1,0:T(2,128)S(1)}, f32[2,27648]{1,0:T(2,128)S(1)}, u32[]{:S(2)}, u32[]{:S(2)}) collective-permute-start(f32[2,27648]{1,0:T(2,128)S(1)} %get-tuple-element.54), channel_id=1, source_target_pairs={{0,124},{1,125},{2,126},{3,127},{4,0},{5,1},{6,2},{7,3},{8,4},{9,5... | collective-permute-start | bytes 663560 | tf_op jit(solution)/shard_map/ppermute | solution.py:447
  81.8 12.4 %collective-permute-start.11 = (f32[2,27648]{1,0:T(2,128)S(1)}, f32[2,27648]{1,0:T(2,128)S(1)}, u32[]{:S(2)}, u32[]{:S(2)}) collective-permute-start(f32[2,27648]{1,0:T(2,128)S(1)} %get-tuple-element.55), channel_id=1, source_target_pairs={{0,126},{1,127},{2,124},{3,125},{4,2},{5,3},{6,0},{7,1},{8,6},{9,7... | collective-permute-start | bytes 663560 | tf_op jit(solution)/shard_map/ppermute | solution.py:447
  95.7 4.1 %collective-permute-start.17 = (f32[4,6912]{1,0:T(4,128)S(1)}, f32[4,6912]{1,0:T(4,128)S(1)}, u32[]{:S(2)}, u32[]{:S(2)}) collective-permute-start(f32[4,6912]{1,0:T(4,128)S(1)} %get-tuple-element.59), channel_id=1, source_target_pairs={{0,32},{1,33},{2,34},{3,35},{4,36},{5,37},{6,38},{7,39},{8,40},{9,... | collective-permute-start | bytes 331784 | tf_op jit(solution)/shard_map/ppermute | solution.py:447
  95.7 5.6 %collective-permute-start.18 = (f32[4,6912]{1,0:T(4,128)S(1)}, f32[4,6912]{1,0:T(4,128)S(1)}, u32[]{:S(2)}, u32[]{:S(2)}) collective-permute-start(f32[4,6912]{1,0:T(4,128)S(1)} %get-tuple-element.60), channel_id=1, source_target_pairs={{0,64},{1,65},{2,66},{3,67},{4,68},{5,69},{6,70},{7,71},{8,72},{9,... | collective-permute-start | bytes 331784 | tf_op jit(solution)/shard_map/ppermute | solution.py:447
  95.7 8.8 %collective-permute-start.19 = (f32[4,6912]{1,0:T(4,128)S(1)}, f32[4,6912]{1,0:T(4,128)S(1)}, u32[]{:S(2)}, u32[]{:S(2)}) collective-permute-start(f32[4,6912]{1,0:T(4,128)S(1)} %get-tuple-element.61), channel_id=1, source_target_pairs={{0,96},{1,97},{2,98},{3,99},{4,100},{5,101},{6,102},{7,103},{8,104... | collective-permute-start | bytes 331784 | tf_op jit(solution)/shard_map/ppermute | solution.py:447
  106.6 4.0 %collective-permute-start.20 = (f32[8,128]{1,0:T(8,128)S(1)}, f32[8,128]{1,0:T(8,128)S(1)}, u32[]{:S(2)}, u32[]{:S(2)}) collective-permute-start(f32[8,128]{1,0:T(8,128)S(1)} %get-tuple-element.63), channel_id=1, source_target_pairs={{0,64},{1,65},{2,66},{3,67},{4,68},{5,69},{6,70},{7,71},{8,72},{9,... | collective-permute-start | bytes 12296 | tf_op jit(solution)/shard_map/ppermute | solution.py:447
  110.7 2.4 %collective-permute-start.21 = (f32[4,128]{1,0:T(4,128)S(1)}, f32[4,128]{1,0:T(4,128)S(1)}, u32[]{:S(2)}, u32[]{:S(2)}) collective-permute-start(f32[4,128]{1,0:T(4,128)S(1)} %slice.15), channel_id=1, source_target_pairs={{0,32},{1,33},{2,34},{3,35},{4,36},{5,37},{6,38},{7,39},{8,40},{9,... | collective-permute-start | bytes 6152 | tf_op jit(solution)/shard_map/ppermute | solution.py:447
  113.1 3.6 %collective-permute-start.22 = (f32[4,128]{1,0:T(4,128)S(1)}, f32[4,128]{1,0:T(4,128)S(1)}, u32[]{:S(2)}, u32[]{:S(2)}) collective-permute-start(f32[4,128]{1,0:T(4,128)S(1)} %slice_add_fusion), channel_id=1, source_target_pairs={{0,1},{1,0},{2,3},{3,2},{4,5},{5,4},{6,7},{7,6},{8,9},{9,8},{10,11... | collective-permute-start | bytes 6152 | tf_op jit(solution)/shard_map/ppermute | solution.py:447
  116.7 2.4 %collective-permute-start.23 = (f32[4,128]{1,0:T(4,128)S(1)}, f32[4,128]{1,0:T(4,128)S(1)}, u32[]{:S(2)}, u32[]{:S(2)}) collective-permute-start(f32[4,128]{1,0:T(4,128)S(1)} %add.28), channel_id=1, source_target_pairs={{0,2},{1,3},{2,0},{3,1},{4,6},{5,7},{6,4},{7,5},{8,10},{9,11},{10,... | collective-permute-start | bytes 6152 | tf_op jit(solution)/shard_map/ppermute | solution.py:447
  (4 other events, 136.3 us)

commit v4 on v3

--- a/solution.py
+++ b/solution.py
@@ -412,7 +412,7 @@
         out[8 * k + 4 : 8 * k + 8, :] = jnp.where(first, b, a)
 
 
-def margin_kernel(where, p0, p1, p3, p2a, p2b, v0, v1, v2, v3, m01, m23, block):
+def margin_kernel(where, p0, p1, p3, p2a, p2b, v0, v1, v2, v3, pieces, block):
     z, y = where[1], where[2]
 
     def halves(a):
@@ -433,8 +433,17 @@
             row = 32 * dy + 8 * dz
             block[(z ^ dz) * 4 + (y + 4 - dy) % 4, :, :] = got[row : row + 8, :]
     out = block[...].reshape(128, 16).T * (1.0 / NCELL)
-    m01[...] = out[0:8, :]
-    m23[...] = out[8:16, :]
+    turned = [out] + [pltpu.roll(out, 32 * r, 1) for r in (1, 2, 3)]
+    third_of = lax.broadcasted_iota(jnp.int32, (16, 128), 1) // 32
+    keep = third_of == lax.broadcasted_iota(jnp.int32, (16, 128), 0) % 4
+    for q_to in range(4):
+        picked = turned[(3 - q_to) % 4]
+        for j in range(3):
+            picked = jnp.where(third_of == j, turned[(j - q_to) % 4], picked)
+        picked = jnp.where(keep, picked, 0.0)
+        for dz in range(4):
+            row = jnp.sum(picked[4 * dz : 4 * dz + 4, :], axis=0, keepdims=True)
+            pieces[pl.ds((z ^ dz) * 4 + q_to, 1), :] = row
 
 
 def move(value, target):
@@ -500,13 +509,11 @@
     finalize = small_call(finalize_kernel, [(4, QCELL)] + [(4, CHUNK)] * 4)
     vectors, *vc = finalize(where, near, far, owed_a, owed_b)
     given = [vc[0]] + [along_z(vc[k], k) for k in (1, 2, 3)]
-    margin_part = small_call(margin_kernel, [(8, 128)] * 2, [pltpu.VMEM((16, 8, 16), F32)], 20)
-    m01, m23 = margin_part(where, p0, p1, p3, p2a, p2b, *given)
-    m01 = m01 + along_z(m23, 2)
-    mine = m01[0:4] + along_z(m01[4:8], 1)
-    mine = mine + within(mine, 1)
-    mine = mine + within(mine, 2)
-    margin = lax.dynamic_slice_in_dim(mine, q * 32, 32, 1).T
+    margin_part = small_call(margin_kernel, [(16, 128)], [pltpu.VMEM((16, 8, 16), F32)], 20)
+    (sums,) = margin_part(where, p0, p1, p3, p2a, p2b, *given)
+    groups = [[(z * 8 + r) * 4 + p for z in range(4) for p in range(4)] for r in range(8)]
+    sums = lax.all_to_all(sums, BOTH, 0, 0, tiled=True, axis_index_groups=groups)
+    margin = jnp.sum(sums, axis=0).reshape(4, 32).T
     return vectors, margin
 
 

time: 121 us -> 118 us (0.975)
  blocking collectives: 0 us -> 10.3 us
  waiting for transfers between devices: 62.6 us -> 54 us
  starting transfers between devices: 28.5 us -> 24.6 us
    all_to_all x0 -> x1, blocking collectives: none -> 10.3 us  [step(): lax.all_to_all(sums, BOTH, 0, 0, tiled=True, axis_index_groups=groups)]
    ppermute x24 -> x20, waiting for transfers between devices: 62.6 us -> 54 us  [move(): return lax.ppermute(value, BOTH, pairs)]
    ppermute x24 -> x20, starting transfers between devices: 28.5 us -> 24.6 us  [move(): return lax.ppermute(value, BOTH, pairs)]
  transfers between devices with their start and end apart: 24 -> 20, of which waited for: 14 -> 10; matrix products, arithmetic and copies ran while one was open for 0% -> 0% of each run, Pallas kernels for 19% -> 19%
where the time goes in v4:
time: 118 us
  waiting for transfers between devices  54 us (46%)
  Pallas kernels  27.1 us (23%)
  starting transfers between devices  24.6 us (21%)
  blocking collectives  10.3 us (9%)
    ppermute x20, waiting for transfers between devices, move(): return lax.ppermute(value, BOTH, pairs)  54 us
    ppermute x20, starting transfers between devices, move(): return lax.ppermute(value, BOTH, pairs)  24.6 us
    all_to_all x1, blocking collectives, step(): lax.all_to_all(sums, BOTH, 0, 0, tiled=True, axis_index_groups=groups)  10.3 us
    pallas_call x1, Pallas kernels, spectrum(): pl.pallas_call(spectrum_kernel, out_shape=[jax.ShapeDtypeStruct((NG, 8, P...  10.2 us
    pallas_call x1, Pallas kernels, terms(): pl.pallas_call(terms_kernel, out_shape=[jax.ShapeDtypeStruct(shape, F32)...  7.72 us
    pallas_call x6, Pallas kernels, call(): pl.pallas_call(body, out_shape=[jax.ShapeDtypeStruct(shape, F32) for shap...  7.23 us
  transfers between devices with their start and end apart: 20, of which 10 were waited for; matrix products, arithmetic and copies ran while one was open for 0% of the time, Pallas kernels for 19%

profile of v4, /device:TPU:1, one launch (start us, length us, event | category | flops | bytes accessed | tf_op | source)
XLA Modules:
  0.0 117.8 jit_solution(7505802236629128213)
XLA Ops:
  0.8 1.3 %shard_map.77 = (f32[2,27648]{1,0:T(2,128)S(1)}, f32[2,27648]{1,0:T(2,128)S(1)}, f32[4,6912]{1,0:T(4,128)S(1)}, f32[4,6912]{1,0:T(4,128)S(1)}, f32[4,6912]{1,0:T(4,128)S(1)}, /*index=5*/f32[4,6912]{1,0:T(4,128)S(1)}) custom-call(s32[4]{0:T(128)S(1)} %pad_add_fusion.where, f32[4,27648]{1,0:T(4,128)} %own.1), custom_call_target="tpu_custom_call" | custom-call | tf_op jit(solution)/shard_map/pallas_call | solution.py:356
  2.1 2.5 %collective-permute-start.1 = (f32[4,6912]{1,0:T(4,128)S(1)}, f32[4,6912]{1,0:T(4,128)S(1)}, u32[]{:S(2)}, u32[]{:S(2)}) collective-permute-start(f32[4,6912]{1,0:T(4,128)S(1)} %get-tuple-element.32), channel_id=1, source_target_pairs={{0,32},{1,33},{2,34},{3,35},{4,36},{5,37},{6,38},{7,39},{8,40},{9,... | collective-permute-start | bytes 331784 | tf_op jit(solution)/shard_map/ppermute | solution.py:456
  4.6 3.3 %collective-permute-start.2 = (f32[4,6912]{1,0:T(4,128)S(1)}, f32[4,6912]{1,0:T(4,128)S(1)}, u32[]{:S(2)}, u32[]{:S(2)}) collective-permute-start(f32[4,6912]{1,0:T(4,128)S(1)} %get-tuple-element.33), channel_id=1, source_target_pairs={{0,64},{1,65},{2,66},{3,67},{4,68},{5,69},{6,70},{7,71},{8,72},{9,... | collective-permute-start | bytes 331784 | tf_op jit(solution)/shard_map/ppermute | solution.py:456
  7.9 1.2 %collective-permute-start = (f32[4,27648]{1,0:T(4,128)}, f32[4,27648]{1,0:T(4,128)S(1)}, u32[]{:S(2)}, u32[]{:S(2)}) collective-permute-start(f32[4,27648]{1,0:T(4,128)} %own.1), channel_id=1, source_target_pairs={{0,2},{1,3},{2,0},{3,1},{4,6},{5,7},{6,4},{7,5},{8,10},{9,11},{10,... | collective-permute-start | bytes 1327112 | tf_op jit(solution)/shard_map/ppermute | solution.py:456
  9.1 2.5 %collective-permute-start.5 = (f32[2,27648]{1,0:T(2,128)S(1)}, f32[2,27648]{1,0:T(2,128)S(1)}, u32[]{:S(2)}, u32[]{:S(2)}) collective-permute-start(f32[2,27648]{1,0:T(2,128)S(1)} %get-tuple-element.36), channel_id=1, source_target_pairs={{0,4},{1,5},{2,6},{3,7},{4,8},{5,9},{6,10},{7,11},{8,12},{9,13},{1... | collective-permute-start | bytes 663560 | tf_op jit(solution)/shard_map/ppermute | solution.py:456
  12.8 2.5 %collective-permute-done.3.f3 = f32[4,6912]{1,0:T(4,128)S(1)} collective-permute-done((f32[4,6912]{1,0:T(4,128)S(1)}, f32[4,6912]{1,0:T(4,128)S(1)}, u32[]{:S(2)}, u32[]{:S(2)}) %collective-permute-start.3) | collective-permute-done | bytes 110624 | tf_op jit(solution)/shard_map/ppermute | solution.py:456
  15.5 3.2 %collective-permute-done.two = f32[4,27648]{1,0:T(4,128)S(1)} collective-permute-done((f32[4,27648]{1,0:T(4,128)}, f32[4,27648]{1,0:T(4,128)S(1)}, u32[]{:S(2)}, u32[]{:S(2)}) %collective-permute-start) | collective-permute-done | bytes 442400 | tf_op jit(solution)/shard_map/ppermute | solution.py:456
  18.6 11.5 %collective-permute-done.5.low_a = f32[2,27648]{1,0:T(2,128)S(1)} collective-permute-done((f32[2,27648]{1,0:T(2,128)S(1)}, f32[2,27648]{1,0:T(2,128)S(1)}, u32[]{:S(2)}, u32[]{:S(2)}) %collective-permute-start.5) | collective-permute-done | bytes 221216 | tf_op jit(solution)/shard_map/ppermute | solution.py:456
  30.9 2.5 %collective-permute-start.7 = (f32[8,27648]{1,0:T(8,128)S(1)}, f32[8,27648]{1,0:T(8,128)S(1)}, u32[]{:S(2)}, u32[]{:S(2)}) collective-permute-start(f32[8,27648]{1,0:T(8,128)S(1)} %shard_map.78), channel_id=1, source_target_pairs={{0,1},{1,0},{2,3},{3,2},{4,5},{5,4},{6,7},{7,6},{8,9},{9,8},{10,11... | collective-permute-start | bytes 2654216 | tf_op jit(solution)/shard_map/ppermute | solution.py:456
  33.4 1.9 %plane_tables.1 = (bf16[2,768,768]{2,1,0:T(8,128)(2,1)S(1)}, bf16[2,768,768]{2,1,0:T(8,128)(2,1)S(1)}, bf16[2,768,768]{2,1,0:T(8,128)(2,1)S(1)}, bf16[2,768,768]{2,1,0:T(8,128)(2,1)S(1)}) custom-call(f32[4,16,768]{2,1,0:T(8,128)S(1)} %copy-done.2, f32[2,48,768]{2,1,0:T(8,128)S(1)} %copy-done.1), custom_call_target="tpu_custom_call" | custom-call | tf_op jit(solution)/shard_map/plane_tables/pallas_call | solution.py:118
  36.0 10.2 %spectrum.1 = (f32[48,8,2304]{2,1,0:T(8,128)S(1)}, f32[48,8,2304]{2,1,0:T(8,128)S(1)}, f32[384,2304]{1,0:T(8,128)S(1)}) custom-call(s32[1]{0:T(128)} %bitcast.q_ref, f32[4,27648]{1,0:T(4,128)} %own.1, f32[4,27648]{1,0:T(4,128)S(1)} %collective-permute-done.two, f32[4,27648]{1,0:T(4,128)S(1)} %collective-permute-done.4.one, ...), custom_call_target="tpu_custom_call" | custom-call | tf_op jit(solution)/shard_map/spectrum/pallas_call | solution.py:325
  46.2 7.7 %terms.1 = (f32[4,27648]{1,0:T(4,128)S(1)}, f32[4,27648]{1,0:T(4,128)S(1)}, f32[10,27648]{1,0:T(8,128)S(1)}, f32[1,27648]{1,0:T(1,128)S(1)}, f32[1,27648]{1,0:T(1,128)S(1)}) custom-call(s32[1]{0:T(128)} %bitcast.q_ref, f32[48,8,2304]{2,1,0:T(8,128)S(1)} %get-tuple-element.40.right, f32[48,8,2304]{2,1,0:T(8,128)S(1)} %get-tuple-element.41.left, ...), custom_call_target="tpu_custom_call" | custom-call | tf_op jit(solution)/shard_map/terms/pallas_call | solution.py:337
  55.2 2.7 %collective-permute-start.14 = (f32[32,6912]{1,0:T(8,128)S(1)}, f32[32,6912]{1,0:T(8,128)S(1)}, u32[]{:S(2)}, u32[]{:S(2)}) collective-permute-start(f32[32,6912]{1,0:T(8,128)S(1)} %shard_map.81.p0), channel_id=1, source_target_pairs={{0,24},{1,25},{2,26},{3,27},{4,28},{5,29},{6,30},{7,31},{8,0},{9,1... | collective-permute-start | bytes 2654216 | tf_op jit(solution)/shard_map/ppermute | solution.py:456
  58.7 18.8 %collective-permute-done.13.p1 = f32[32,6912]{1,0:T(8,128)S(1)} collective-permute-done((f32[32,6912]{1,0:T(8,128)S(1)}, f32[32,6912]{1,0:T(8,128)S(1)}, u32[]{:S(2)}, u32[]{:S(2)}) %collective-permute-start.13) | collective-permute-done | bytes 884768 | tf_op jit(solution)/shard_map/ppermute | solution.py:456
  77.8 2.7 %collective-permute-start.16 = (f32[16,6912]{1,0:T(8,128)S(1)}, f32[16,6912]{1,0:T(8,128)S(1)}, u32[]{:S(2)}, u32[]{:S(2)}) collective-permute-start(f32[16,6912]{1,0:T(8,128)S(1)} %slice.9), channel_id=1, source_target_pairs={{0,24},{1,25},{2,26},{3,27},{4,28},{5,29},{6,30},{7,31},{8,0},{9,1... | collective-permute-start | bytes 1327112 | tf_op jit(solution)/shard_map/ppermute | solution.py:456
  80.6 1.2 %collective-permute-start.10 = (f32[2,27648]{1,0:T(2,128)S(1)}, f32[2,27648]{1,0:T(2,128)S(1)}, u32[]{:S(2)}, u32[]{:S(2)}) collective-permute-start(f32[2,27648]{1,0:T(2,128)S(1)} %get-tuple-element.52), channel_id=1, source_target_pairs={{0,124},{1,125},{2,126},{3,127},{4,0},{5,1},{6,2},{7,3},{8,4},{9,5... | collective-permute-start | bytes 663560 | tf_op jit(solution)/shard_map/ppermute | solution.py:456
  81.8 5.8 %collective-permute-done.10.owed_a = f32[2,27648]{1,0:T(2,128)S(1)} collective-permute-done((f32[2,27648]{1,0:T(2,128)S(1)}, f32[2,27648]{1,0:T(2,128)S(1)}, u32[]{:S(2)}, u32[]{:S(2)}) %collective-permute-start.10) | collective-permute-done | bytes 221216 | tf_op jit(solution)/shard_map/ppermute | solution.py:456
  87.6 6.6 %collective-permute-done.11.owed_b = f32[2,27648]{1,0:T(2,128)S(1)} collective-permute-done((f32[2,27648]{1,0:T(2,128)S(1)}, f32[2,27648]{1,0:T(2,128)S(1)}, u32[]{:S(2)}, u32[]{:S(2)}) %collective-permute-start.11) | collective-permute-done | bytes 221216 | tf_op jit(solution)/shard_map/ppermute | solution.py:456
  94.2 1.5 %shard_map.80 = (f32[4,27648]{1,0:T(4,128)}, f32[4,6912]{1,0:T(4,128)S(1)}, f32[4,6912]{1,0:T(4,128)S(1)}, f32[4,6912]{1,0:T(4,128)S(1)}, f32[4,6912]{1,0:T(4,128)S(1)}) custom-call(s32[4]{0:T(128)S(1)} %pad_add_fusion.where, f32[4,27648]{1,0:T(4,128)S(1)} %get-tuple-element.50.near, f32[4,27648]{1,0:T(4,128)S(1)} %collective-permute-done.9.far, ...), custom_call_target="tpu_custom_call" | custom-call | tf_op jit(solution)/shard_map/pallas_call | solution.py:356
  95.7 3.8 %collective-permute-start.19 = (f32[4,6912]{1,0:T(4,128)S(1)}, f32[4,6912]{1,0:T(4,128)S(1)}, u32[]{:S(2)}, u32[]{:S(2)}) collective-permute-start(f32[4,6912]{1,0:T(4,128)S(1)} %get-tuple-element.59), channel_id=1, source_target_pairs={{0,96},{1,97},{2,98},{3,99},{4,100},{5,101},{6,102},{7,103},{8,104... | collective-permute-start | bytes 331784 | tf_op jit(solution)/shard_map/ppermute | solution.py:456
  99.8 1.5 %collective-permute-done.18.v2 = f32[4,6912]{1,0:T(4,128)S(1)} collective-permute-done((f32[4,6912]{1,0:T(4,128)S(1)}, f32[4,6912]{1,0:T(4,128)S(1)}, u32[]{:S(2)}, u32[]{:S(2)}) %collective-permute-start.18) | collective-permute-done | bytes 110624 | tf_op jit(solution)/shard_map/ppermute | solution.py:456
  101.3 3.3 %collective-permute-done.19.v3 = f32[4,6912]{1,0:T(4,128)S(1)} collective-permute-done((f32[4,6912]{1,0:T(4,128)S(1)}, f32[4,6912]{1,0:T(4,128)S(1)}, u32[]{:S(2)}, u32[]{:S(2)}) %collective-permute-start.19) | collective-permute-done | bytes 110624 | tf_op jit(solution)/shard_map/ppermute | solution.py:456
  104.5 2.2 %shard_map.82 = f32[16,128]{1,0:T(8,128)S(1)} custom-call(s32[4]{0:T(128)S(1)} %pad_add_fusion.where, f32[32,6912]{1,0:T(8,128)S(1)} %shard_map.81.p0, f32[32,6912]{1,0:T(8,128)S(1)} %collective-permute-done.13.p1, f32[32,6912]{1,0:T(8,128)S(1)} %collective-permute-done.14.p3, f32[16,6912]{1,0:T(8,128)S(1)} %collective-permute-done.15.p2a, ...), custom_call_target="tpu_custom_call" | custom-call | tf_op jit(solution)/shard_map/pallas_call | solution.py:356
  106.8 10.3 %all_to_all.9 = f32[16,1,128]{2,1,0:T(1,128)S(1)} all-to-all(f32[16,1,128]{2,1,0:T(1,128)S(1)} %bitcast.8), channel_id=1, replica_groups={{0,1,2,3,32,33,34,35,64,65,66,67,96,97,98,99},{4,5,6,7,36,37,38,39,68,6..., dimensions={0} | all-to-all | bytes 16384 | tf_op jit(solution)/shard_map/all_to_all | solution.py:515
  (40 shorter events, 6.4 us)
Async XLA Ops:
  0.6 32.8 %copy-start.2 = (f32[4,16,768]{2,1,0:T(8,128)S(1)}, f32[4,16,768]{2,1,0:T(8,128)}, u32[]{:S(2)}) copy-start(f32[4,16,768]{2,1,0:T(8,128)} %constant.63.clone.tens) | copy-start | bytes 589828
  0.6 32.8 %copy-start.1 = (f32[2,48,768]{2,1,0:T(8,128)S(1)}, f32[2,48,768]{2,1,0:T(8,128)}, u32[]{:S(2)}) copy-start(f32[2,48,768]{2,1,0:T(8,128)} %constant.64.clone.zs) | copy-start | bytes 884740
  0.7 35.4 %copy-start = (f32[48,2304]{1,0:T(8,128)S(1)}, f32[48,2304]{1,0:T(8,128)}, u32[]{:S(2)}) copy-start(f32[48,2304]{1,0:T(8,128)} %constant.65.clone.kern) | copy-start | bytes 1327108
  0.7 35.3 %copy-start.3 = (f32[8,768]{1,0:T(8,128)S(1)}, f32[8,768]{1,0:T(8,128)}, u32[]{:S(2)}) copy-start(f32[8,768]{1,0:T(8,128)} %constant.66.clone.third) | copy-start | bytes 73732
  2.1 9.5 %collective-permute-start.1 = (f32[4,6912]{1,0:T(4,128)S(1)}, f32[4,6912]{1,0:T(4,128)S(1)}, u32[]{:S(2)}, u32[]{:S(2)}) collective-permute-start(f32[4,6912]{1,0:T(4,128)S(1)} %get-tuple-element.32), channel_id=1, source_target_pairs={{0,32},{1,33},{2,34},{3,35},{4,36},{5,37},{6,38},{7,39},{8,40},{9,... | collective-permute-start | bytes 331784 | tf_op jit(solution)/shard_map/ppermute | solution.py:456
  4.6 8.2 %collective-permute-start.2 = (f32[4,6912]{1,0:T(4,128)S(1)}, f32[4,6912]{1,0:T(4,128)S(1)}, u32[]{:S(2)}, u32[]{:S(2)}) collective-permute-start(f32[4,6912]{1,0:T(4,128)S(1)} %get-tuple-element.33), channel_id=1, source_target_pairs={{0,64},{1,65},{2,66},{3,67},{4,68},{5,69},{6,70},{7,71},{8,72},{9,... | collective-permute-start | bytes 331784 | tf_op jit(solution)/shard_map/ppermute | solution.py:456
  7.9 7.4 %collective-permute-start.3 = (f32[4,6912]{1,0:T(4,128)S(1)}, f32[4,6912]{1,0:T(4,128)S(1)}, u32[]{:S(2)}, u32[]{:S(2)}) collective-permute-start(f32[4,6912]{1,0:T(4,128)S(1)} %get-tuple-element.34), channel_id=1, source_target_pairs={{0,96},{1,97},{2,98},{3,99},{4,100},{5,101},{6,102},{7,103},{8,104... | collective-permute-start | bytes 331784 | tf_op jit(solution)/shard_map/ppermute | solution.py:456
  7.9 10.7 %collective-permute-start = (f32[4,27648]{1,0:T(4,128)}, f32[4,27648]{1,0:T(4,128)S(1)}, u32[]{:S(2)}, u32[]{:S(2)}) collective-permute-start(f32[4,27648]{1,0:T(4,128)} %own.1), channel_id=1, source_target_pairs={{0,2},{1,3},{2,0},{3,1},{4,6},{5,7},{6,4},{7,5},{8,10},{9,11},{10,... | collective-permute-start | bytes 1327112 | tf_op jit(solution)/shard_map/ppermute | solution.py:456
  9.1 21.0 %collective-permute-start.5 = (f32[2,27648]{1,0:T(2,128)S(1)}, f32[2,27648]{1,0:T(2,128)S(1)}, u32[]{:S(2)}, u32[]{:S(2)}) collective-permute-start(f32[2,27648]{1,0:T(2,128)S(1)} %get-tuple-element.36), channel_id=1, source_target_pairs={{0,4},{1,5},{2,6},{3,7},{4,8},{5,9},{6,10},{7,11},{8,12},{9,13},{1... | collective-permute-start | bytes 663560 | tf_op jit(solution)/shard_map/ppermute | solution.py:456
  11.6 18.5 %collective-permute-start.6 = (f32[2,27648]{1,0:T(2,128)S(1)}, f32[2,27648]{1,0:T(2,128)S(1)}, u32[]{:S(2)}, u32[]{:S(2)}) collective-permute-start(f32[2,27648]{1,0:T(2,128)S(1)} %get-tuple-element.37), channel_id=1, source_target_pairs={{0,6},{1,7},{2,4},{3,5},{4,10},{5,11},{6,8},{7,9},{8,14},{9,15},{1... | collective-permute-start | bytes 663560 | tf_op jit(solution)/shard_map/ppermute | solution.py:456
  30.9 5.1 %collective-permute-start.7 = (f32[8,27648]{1,0:T(8,128)S(1)}, f32[8,27648]{1,0:T(8,128)S(1)}, u32[]{:S(2)}, u32[]{:S(2)}) collective-permute-start(f32[8,27648]{1,0:T(8,128)S(1)} %shard_map.78), channel_id=1, source_target_pairs={{0,1},{1,0},{2,3},{3,2},{4,5},{5,4},{6,7},{7,6},{8,9},{9,8},{10,11... | collective-permute-start | bytes 2654216 | tf_op jit(solution)/shard_map/ppermute | solution.py:456
  33.3 2.7 %collective-permute-start.4 = (f32[4,27648]{1,0:T(4,128)}, f32[4,27648]{1,0:T(4,128)S(1)}, u32[]{:S(2)}, u32[]{:S(2)}) collective-permute-start(f32[4,27648]{1,0:T(4,128)} %own.1), channel_id=1, source_target_pairs={{0,1},{1,0},{2,3},{3,2},{4,5},{5,4},{6,7},{7,6},{8,9},{9,8},{10,11... | collective-permute-start | bytes 1327112 | tf_op jit(solution)/shard_map/ppermute | solution.py:456
  33.4 21.0 %collective-permute-start.12 = (f32[16,6912]{1,0:T(8,128)S(1)}, f32[16,6912]{1,0:T(8,128)S(1)}, u32[]{:S(2)}, u32[]{:S(2)}) collective-permute-start(f32[16,6912]{1,0:T(8,128)S(1)} %pad_maximum_fusion), channel_id=1, source_target_pairs={{0,4},{1,5},{2,6},{3,7},{4,0},{5,1},{6,2},{7,3},{8,12},{9,13},{10,... | collective-permute-start | bytes 1327112 | tf_op jit(solution)/shard_map/ppermute | solution.py:456
  53.9 3.9 %collective-permute-start.8 = (f32[10,27648]{1,0:T(8,128)S(1)}, f32[10,27648]{1,0:T(8,128)S(1)}, u32[]{:S(2)}, u32[]{:S(2)}) collective-permute-start(f32[10,27648]{1,0:T(8,128)S(1)} %get-tuple-element.49), channel_id=1, source_target_pairs={{0,1},{1,0},{2,3},{3,2},{4,5},{5,4},{6,7},{7,6},{8,9},{9,8},{10,11... | collective-permute-start | bytes 3317768 | tf_op jit(solution)/shard_map/ppermute | solution.py:456
  55.1 22.4 %collective-permute-start.13 = (f32[32,6912]{1,0:T(8,128)S(1)}, f32[32,6912]{1,0:T(8,128)S(1)}, u32[]{:S(2)}, u32[]{:S(2)}) collective-permute-start(f32[32,6912]{1,0:T(8,128)S(1)} %shard_map.81.p0), channel_id=1, source_target_pairs={{0,8},{1,9},{2,10},{3,11},{4,12},{5,13},{6,14},{7,15},{8,16},{9,17... | collective-permute-start | bytes 2654216 | tf_op jit(solution)/shard_map/ppermute | solution.py:456
  55.2 22.6 %collective-permute-start.14 = (f32[32,6912]{1,0:T(8,128)S(1)}, f32[32,6912]{1,0:T(8,128)S(1)}, u32[]{:S(2)}, u32[]{:S(2)}) collective-permute-start(f32[32,6912]{1,0:T(8,128)S(1)} %shard_map.81.p0), channel_id=1, source_target_pairs={{0,24},{1,25},{2,26},{3,27},{4,28},{5,29},{6,30},{7,31},{8,0},{9,1... | collective-permute-start | bytes 2654216 | tf_op jit(solution)/shard_map/ppermute | solution.py:456
  58.6 35.5 %collective-permute-start.9 = (f32[4,27648]{1,0:T(4,128)S(1)}, f32[4,27648]{1,0:T(4,128)S(1)}, u32[]{:S(2)}, u32[]{:S(2)}) collective-permute-start(f32[4,27648]{1,0:T(4,128)S(1)} %get-tuple-element.51), channel_id=1, source_target_pairs={{0,2},{1,3},{2,0},{3,1},{4,6},{5,7},{6,4},{7,5},{8,10},{9,11},{10,... | collective-permute-start | bytes 1327112 | tf_op jit(solution)/shard_map/ppermute | solution.py:456
  77.5 22.0 %collective-permute-start.15 = (f32[16,6912]{1,0:T(8,128)S(1)}, f32[16,6912]{1,0:T(8,128)S(1)}, u32[]{:S(2)}, u32[]{:S(2)}) collective-permute-start(f32[16,6912]{1,0:T(8,128)S(1)} %slice.8), channel_id=1, source_target_pairs={{0,8},{1,9},{2,10},{3,11},{4,12},{5,13},{6,14},{7,15},{8,16},{9,17... | collective-permute-start | bytes 1327112 | tf_op jit(solution)/shard_map/ppermute | solution.py:456
  77.8 21.7 %collective-permute-start.16 = (f32[16,6912]{1,0:T(8,128)S(1)}, f32[16,6912]{1,0:T(8,128)S(1)}, u32[]{:S(2)}, u32[]{:S(2)}) collective-permute-start(f32[16,6912]{1,0:T(8,128)S(1)} %slice.9), channel_id=1, source_target_pairs={{0,24},{1,25},{2,26},{3,27},{4,28},{5,29},{6,30},{7,31},{8,0},{9,1... | collective-permute-start | bytes 1327112 | tf_op jit(solution)/shard_map/ppermute | solution.py:456
  80.6 7.0 %collective-permute-start.10 = (f32[2,27648]{1,0:T(2,128)S(1)}, f32[2,27648]{1,0:T(2,128)S(1)}, u32[]{:S(2)}, u32[]{:S(2)}) collective-permute-start(f32[2,27648]{1,0:T(2,128)S(1)} %get-tuple-element.52), channel_id=1, source_target_pairs={{0,124},{1,125},{2,126},{3,127},{4,0},{5,1},{6,2},{7,3},{8,4},{9,5... | collective-permute-start | bytes 663560 | tf_op jit(solution)/shard_map/ppermute | solution.py:456
  81.8 12.4 %collective-permute-start.11 = (f32[2,27648]{1,0:T(2,128)S(1)}, f32[2,27648]{1,0:T(2,128)S(1)}, u32[]{:S(2)}, u32[]{:S(2)}) collective-permute-start(f32[2,27648]{1,0:T(2,128)S(1)} %get-tuple-element.53), channel_id=1, source_target_pairs={{0,126},{1,127},{2,124},{3,125},{4,2},{5,3},{6,0},{7,1},{8,6},{9,7... | collective-permute-start | bytes 663560 | tf_op jit(solution)/shard_map/ppermute | solution.py:456
  95.7 4.1 %collective-permute-start.17 = (f32[4,6912]{1,0:T(4,128)S(1)}, f32[4,6912]{1,0:T(4,128)S(1)}, u32[]{:S(2)}, u32[]{:S(2)}) collective-permute-start(f32[4,6912]{1,0:T(4,128)S(1)} %get-tuple-element.57), channel_id=1, source_target_pairs={{0,32},{1,33},{2,34},{3,35},{4,36},{5,37},{6,38},{7,39},{8,40},{9,... | collective-permute-start | bytes 331784 | tf_op jit(solution)/shard_map/ppermute | solution.py:456
  95.7 5.6 %collective-permute-start.18 = (f32[4,6912]{1,0:T(4,128)S(1)}, f32[4,6912]{1,0:T(4,128)S(1)}, u32[]{:S(2)}, u32[]{:S(2)}) collective-permute-start(f32[4,6912]{1,0:T(4,128)S(1)} %get-tuple-element.58), channel_id=1, source_target_pairs={{0,64},{1,65},{2,66},{3,67},{4,68},{5,69},{6,70},{7,71},{8,72},{9,... | collective-permute-start | bytes 331784 | tf_op jit(solution)/shard_map/ppermute | solution.py:456
  95.7 8.8 %collective-permute-start.19 = (f32[4,6912]{1,0:T(4,128)S(1)}, f32[4,6912]{1,0:T(4,128)S(1)}, u32[]{:S(2)}, u32[]{:S(2)}) collective-permute-start(f32[4,6912]{1,0:T(4,128)S(1)} %get-tuple-element.59), channel_id=1, source_target_pairs={{0,96},{1,97},{2,98},{3,99},{4,100},{5,101},{6,102},{7,103},{8,104... | collective-permute-start | bytes 331784 | tf_op jit(solution)/shard_map/ppermute | solution.py:456

commit v5 on v4

--- a/solution.py
+++ b/solution.py
@@ -404,16 +404,8 @@
         chunks[k][...] = vectors[:, chunk_of(where, k)]
 
 
-def pair_kernel(where, f0, f1, f2, f3, other, out):
-    first = where[3] == 0
-    for k, f in enumerate((f0, f1, f2, f3)):
-        a, b = f[...], other[4 * k : 4 * k + 4, :]
-        out[8 * k : 8 * k + 4, :] = jnp.where(first, a, b)
-        out[8 * k + 4 : 8 * k + 8, :] = jnp.where(first, b, a)
-
-
-def margin_kernel(where, p0, p1, p3, p2a, p2b, v0, v1, v2, v3, pieces, block):
-    z, y = where[1], where[2]
+def margin_kernel(where, own0, oth0, own1, oth1, own2, oth2, own3, oth3, v0, v1, v2, v3, pieces, block):
+    z, y, h = where[1], where[2], where[3]
 
     def halves(a):
         top = a.astype(BF16)
@@ -421,7 +413,7 @@
 
     vt, vl = halves(jnp.concatenate([v0[...], v1[...], v2[...], v3[...]], axis=0))
     dims = (((1,), (1,)), ((), ()))
-    parts = jnp.concatenate([p0[...], p1[...], p2a[...], p2b[...], p3[...]], axis=0)
+    parts = jnp.concatenate([r[...] for r in (own0, oth0, own1, oth1, own2, oth2, own3, oth3)], axis=0)
     ft, fl = halves(parts)
     got = (
         lax.dot_general(ft, vt, dims, preferred_element_type=F32)
@@ -430,8 +422,11 @@
     )
     for dy in range(4):
         for dz in range(4):
-            row = 32 * dy + 8 * dz
-            block[(z ^ dz) * 4 + (y + 4 - dy) % 4, :, :] = got[row : row + 8, :]
+            row = 32 * dy + 4 * dz
+            pair = got[row : row + 4, :], got[row + 16 : row + 20, :]
+            at = (z ^ dz) * 4 + (y + 4 - dy) % 4
+            block[at, 0:4, :] = jnp.where(h == 0, pair[0], pair[1])
+            block[at, 4:8, :] = jnp.where(h == 0, pair[1], pair[0])
     out = block[...].reshape(128, 16).T * (1.0 / NCELL)
     turned = [out] + [pltpu.roll(out, 32 * r, 1) for r in (1, 2, 3)]
     third_of = lax.broadcasted_iota(jnp.int32, (16, 128), 1) // 32
@@ -493,10 +488,12 @@
     (stacked,) = small_call(stack_kernel, [(8, QCELL)])(where, two, low_a, low_b)
     core = within(stacked, 1)
     other = move(together, lambda z, y, h, q: (z, y, 1 - h, q))
+    own1 = along_y(together, 1)
+    own3 = along_y(together, 3)
     right, left, field = spectrum(q, (orbitals, two, one, low_a, low_b, core), tables[:2])
-    (p0,) = small_call(pair_kernel, [(32, CHUNK)])(where, *pieces, other)
-    p1 = along_y(p0, 1)
-    p3 = along_y(p0, 3)
+    oth1 = along_y(other, 1)
+    oth3 = along_y(other, 3)
+    own2 = along_y(own1, 1)
     near0, near2, cross, low0, low2 = terms(q, right, left, field, tables[2:])
     across = within(cross, 1)
     merge = small_call(merge_kernel, [(4, QCELL)] * 2 + [(2, QCELL)] * 2)
@@ -504,13 +501,12 @@
     far = within(both, 2)
     owed_a = around(owe_a, -1, 0)
     owed_b = around(owe_b, -1, 2)
-    p2a = along_y(p1[:16], 1)
-    p2b = along_y(p3[16:], 3)
+    oth2 = along_y(oth1, 1)
     finalize = small_call(finalize_kernel, [(4, QCELL)] + [(4, CHUNK)] * 4)
     vectors, *vc = finalize(where, near, far, owed_a, owed_b)
     given = [vc[0]] + [along_z(vc[k], k) for k in (1, 2, 3)]
     margin_part = small_call(margin_kernel, [(16, 128)], [pltpu.VMEM((16, 8, 16), F32)], 20)
-    (sums,) = margin_part(where, p0, p1, p3, p2a, p2b, *given)
+    (sums,) = margin_part(where, together, other, own1, oth1, own2, oth2, own3, oth3, *given)
     groups = [[(z * 8 + r) * 4 + p for z in range(4) for p in range(4)] for r in range(8)]
     sums = lax.all_to_all(sums, BOTH, 0, 0, tiled=True, axis_index_groups=groups)
     margin = jnp.sum(sums, axis=0).reshape(4, 32).T

time: 118 us -> 114 us (0.966)
  starting transfers between devices: 24.6 us -> 22.7 us
  waiting for transfers between devices: 54 us -> 52.3 us
    ppermute x20 -> x22, starting transfers between devices: 24.6 us -> 22.7 us  [move(): return lax.ppermute(value, BOTH, pairs)]
    ppermute x20 -> x22, waiting for transfers between devices: 54 us -> 52.3 us  [move(): return lax.ppermute(value, BOTH, pairs)]
    pallas_call x6 -> x5, Pallas kernels: 7.23 us -> 6.47 us  [call(): pl.pallas_call(body, out_shape=[jax.ShapeDtypeStruct(shape, F32) for shap...]
  transfers between devices with their start and end apart: 20 -> 22, of which waited for: 10 -> 10; matrix products, arithmetic and copies ran while one was open for 0% -> 0% of each run, Pallas kernels for 19% -> 4%
where the time goes in v5:
time: 114 us
  waiting for transfers between devices  52.3 us (46%)
  Pallas kernels  26.3 us (23%)
  starting transfers between devices  22.7 us (20%)
  blocking collectives  10.7 us (9%)
    ppermute x22, waiting for transfers between devices, move(): return lax.ppermute(value, BOTH, pairs)  52.3 us
    ppermute x22, starting transfers between devices, move(): return lax.ppermute(value, BOTH, pairs)  22.7 us
    all_to_all x1, blocking collectives, step(): lax.all_to_all(sums, BOTH, 0, 0, tiled=True, axis_index_groups=groups)  10.7 us
    pallas_call x1, Pallas kernels, spectrum(): pl.pallas_call(spectrum_kernel, out_shape=[jax.ShapeDtypeStruct((NG, 8, P...  10.2 us
    pallas_call x1, Pallas kernels, terms(): pl.pallas_call(terms_kernel, out_shape=[jax.ShapeDtypeStruct(shape, F32)...  7.72 us
    pallas_call x5, Pallas kernels, call(): pl.pallas_call(body, out_shape=[jax.ShapeDtypeStruct(shape, F32) for shap...  6.47 us
  transfers between devices with their start and end apart: 22, of which 10 were waited for; matrix products, arithmetic and copies ran while one was open for 0% of the time, Pallas kernels for 4%

profile of v5, /device:TPU:1, one launch (start us, length us, event | category | flops | bytes accessed | tf_op | source)
XLA Modules:
  0.0 113.7 jit_solution(10632048388351708703)
XLA Ops:
  0.8 1.3 %shard_map.77 = (f32[2,27648]{1,0:T(2,128)S(1)}, f32[2,27648]{1,0:T(2,128)S(1)}, f32[4,6912]{1,0:T(4,128)S(1)}, f32[4,6912]{1,0:T(4,128)S(1)}, f32[4,6912]{1,0:T(4,128)S(1)}, /*index=5*/f32[4,6912]{1,0:T(4,128)S(1)}) custom-call(s32[4]{0:T(128)S(1)} %pad_add_fusion.where, f32[4,27648]{1,0:T(4,128)} %own.1), custom_call_target="tpu_custom_call" | custom-call | tf_op jit(solution)/shard_map/pallas_call | solution.py:356
  2.1 2.5 %collective-permute-start.1 = (f32[4,6912]{1,0:T(4,128)S(1)}, f32[4,6912]{1,0:T(4,128)S(1)}, u32[]{:S(2)}, u32[]{:S(2)}) collective-permute-start(f32[4,6912]{1,0:T(4,128)S(1)} %get-tuple-element.32), channel_id=1, source_target_pairs={{0,32},{1,33},{2,34},{3,35},{4,36},{5,37},{6,38},{7,39},{8,40},{9,... | collective-permute-start | bytes 331784 | tf_op jit(solution)/shard_map/ppermute | solution.py:451
  4.6 3.3 %collective-permute-start.2 = (f32[4,6912]{1,0:T(4,128)S(1)}, f32[4,6912]{1,0:T(4,128)S(1)}, u32[]{:S(2)}, u32[]{:S(2)}) collective-permute-start(f32[4,6912]{1,0:T(4,128)S(1)} %get-tuple-element.33), channel_id=1, source_target_pairs={{0,64},{1,65},{2,66},{3,67},{4,68},{5,69},{6,70},{7,71},{8,72},{9,... | collective-permute-start | bytes 331784 | tf_op jit(solution)/shard_map/ppermute | solution.py:451
  7.9 1.2 %collective-permute-start = (f32[4,27648]{1,0:T(4,128)}, f32[4,27648]{1,0:T(4,128)S(1)}, u32[]{:S(2)}, u32[]{:S(2)}) collective-permute-start(f32[4,27648]{1,0:T(4,128)} %own.1), channel_id=1, source_target_pairs={{0,2},{1,3},{2,0},{3,1},{4,6},{5,7},{6,4},{7,5},{8,10},{9,11},{10,... | collective-permute-start | bytes 1327112 | tf_op jit(solution)/shard_map/ppermute | solution.py:451
  9.1 2.5 %collective-permute-start.5 = (f32[2,27648]{1,0:T(2,128)S(1)}, f32[2,27648]{1,0:T(2,128)S(1)}, u32[]{:S(2)}, u32[]{:S(2)}) collective-permute-start(f32[2,27648]{1,0:T(2,128)S(1)} %get-tuple-element.36), channel_id=1, source_target_pairs={{0,4},{1,5},{2,6},{3,7},{4,8},{5,9},{6,10},{7,11},{8,12},{9,13},{1... | collective-permute-start | bytes 663560 | tf_op jit(solution)/shard_map/ppermute | solution.py:451
  12.8 2.5 %collective-permute-done.3 = f32[4,6912]{1,0:T(4,128)S(1)} collective-permute-done((f32[4,6912]{1,0:T(4,128)S(1)}, f32[4,6912]{1,0:T(4,128)S(1)}, u32[]{:S(2)}, u32[]{:S(2)}) %collective-permute-start.3) | collective-permute-done | bytes 110624 | tf_op jit(solution)/shard_map/ppermute | solution.py:451
  15.5 3.2 %collective-permute-done.two = f32[4,27648]{1,0:T(4,128)S(1)} collective-permute-done((f32[4,27648]{1,0:T(4,128)}, f32[4,27648]{1,0:T(4,128)S(1)}, u32[]{:S(2)}, u32[]{:S(2)}) %collective-permute-start) | collective-permute-done | bytes 442400 | tf_op jit(solution)/shard_map/ppermute | solution.py:451
  18.6 11.5 %collective-permute-done.5.low_a = f32[2,27648]{1,0:T(2,128)S(1)} collective-permute-done((f32[2,27648]{1,0:T(2,128)S(1)}, f32[2,27648]{1,0:T(2,128)S(1)}, u32[]{:S(2)}, u32[]{:S(2)}) %collective-permute-start.5) | collective-permute-done | bytes 221216 | tf_op jit(solution)/shard_map/ppermute | solution.py:451
  30.9 2.5 %collective-permute-start.7 = (f32[8,27648]{1,0:T(8,128)S(1)}, f32[8,27648]{1,0:T(8,128)S(1)}, u32[]{:S(2)}, u32[]{:S(2)}) collective-permute-start(f32[8,27648]{1,0:T(8,128)S(1)} %shard_map.78), channel_id=1, source_target_pairs={{0,1},{1,0},{2,3},{3,2},{4,5},{5,4},{6,7},{7,6},{8,9},{9,8},{10,11... | collective-permute-start | bytes 2654216 | tf_op jit(solution)/shard_map/ppermute | solution.py:451
  33.4 1.9 %plane_tables.1 = (bf16[2,768,768]{2,1,0:T(8,128)(2,1)S(1)}, bf16[2,768,768]{2,1,0:T(8,128)(2,1)S(1)}, bf16[2,768,768]{2,1,0:T(8,128)(2,1)S(1)}, bf16[2,768,768]{2,1,0:T(8,128)(2,1)S(1)}) custom-call(f32[4,16,768]{2,1,0:T(8,128)S(1)} %copy-done.2, f32[2,48,768]{2,1,0:T(8,128)S(1)} %copy-done.1), custom_call_target="tpu_custom_call" | custom-call | tf_op jit(solution)/shard_map/plane_tables/pallas_call | solution.py:118
  36.0 10.2 %spectrum.1 = (f32[48,8,2304]{2,1,0:T(8,128)S(1)}, f32[48,8,2304]{2,1,0:T(8,128)S(1)}, f32[384,2304]{1,0:T(8,128)S(1)}) custom-call(s32[1]{0:T(128)} %bitcast.q_ref, f32[4,27648]{1,0:T(4,128)} %own.1, f32[4,27648]{1,0:T(4,128)S(1)} %collective-permute-done.two, f32[4,27648]{1,0:T(4,128)S(1)} %collective-permute-done.4.one, ...), custom_call_target="tpu_custom_call" | custom-call | tf_op jit(solution)/shard_map/spectrum/pallas_call | solution.py:325
  46.2 7.7 %terms.1 = (f32[4,27648]{1,0:T(4,128)S(1)}, f32[4,27648]{1,0:T(4,128)S(1)}, f32[10,27648]{1,0:T(8,128)S(1)}, f32[1,27648]{1,0:T(1,128)S(1)}, f32[1,27648]{1,0:T(1,128)S(1)}) custom-call(s32[1]{0:T(128)} %bitcast.q_ref, f32[48,8,2304]{2,1,0:T(8,128)S(1)} %get-tuple-element.40.right, f32[48,8,2304]{2,1,0:T(8,128)S(1)} %get-tuple-element.41.left, ...), custom_call_target="tpu_custom_call" | custom-call | tf_op jit(solution)/shard_map/terms/pallas_call | solution.py:337
  54.4 13.1 %collective-permute-done.12.oth0 = f32[16,6912]{1,0:T(8,128)S(1)} collective-permute-done((f32[16,6912]{1,0:T(8,128)S(1)}, f32[16,6912]{1,0:T(8,128)S(1)}, u32[]{:S(2)}, u32[]{:S(2)}) %collective-permute-start.12) | collective-permute-done | bytes 442400 | tf_op jit(solution)/shard_map/ppermute | solution.py:451
  68.2 1.3 %collective-permute-start.10 = (f32[2,27648]{1,0:T(2,128)S(1)}, f32[2,27648]{1,0:T(2,128)S(1)}, u32[]{:S(2)}, u32[]{:S(2)}) collective-permute-start(f32[2,27648]{1,0:T(2,128)S(1)} %get-tuple-element.52), channel_id=1, source_target_pairs={{0,124},{1,125},{2,126},{3,127},{4,0},{5,1},{6,2},{7,3},{8,4},{9,5... | collective-permute-start | bytes 663560 | tf_op jit(solution)/shard_map/ppermute | solution.py:451
  69.6 2.1 %collective-permute-start.11 = (f32[2,27648]{1,0:T(2,128)S(1)}, f32[2,27648]{1,0:T(2,128)S(1)}, u32[]{:S(2)}, u32[]{:S(2)}) collective-permute-start(f32[2,27648]{1,0:T(2,128)S(1)} %get-tuple-element.53), channel_id=1, source_target_pairs={{0,126},{1,127},{2,124},{3,125},{4,2},{5,3},{6,0},{7,1},{8,6},{9,7... | collective-permute-start | bytes 663560 | tf_op jit(solution)/shard_map/ppermute | solution.py:451
  71.9 7.5 %collective-permute-done.14.oth1 = f32[16,6912]{1,0:T(8,128)S(1)} collective-permute-done((f32[16,6912]{1,0:T(8,128)S(1)}, f32[16,6912]{1,0:T(8,128)S(1)}, u32[]{:S(2)}, u32[]{:S(2)}) %collective-permute-start.14) | collective-permute-done | bytes 442400 | tf_op jit(solution)/shard_map/ppermute | solution.py:451
  79.5 2.7 %collective-permute-start.18 = (f32[16,6912]{1,0:T(8,128)S(1)}, f32[16,6912]{1,0:T(8,128)S(1)}, u32[]{:S(2)}, u32[]{:S(2)}) collective-permute-start(f32[16,6912]{1,0:T(8,128)S(1)} %collective-permute-done.12.oth0), channel_id=1, source_target_pairs={{0,24},{1,25},{2,26},{3,27},{4,28},{5,29},{6,30},{7,31},{8,0},{9,1... | collective-permute-start | bytes 1327112 | tf_op jit(solution)/shard_map/ppermute | solution.py:451
  82.2 1.7 %collective-permute-done.9.far = f32[4,27648]{1,0:T(4,128)S(1)} collective-permute-done((f32[4,27648]{1,0:T(4,128)S(1)}, f32[4,27648]{1,0:T(4,128)S(1)}, u32[]{:S(2)}, u32[]{:S(2)}) %collective-permute-start.9) | collective-permute-done | bytes 442400 | tf_op jit(solution)/shard_map/ppermute | solution.py:451
  83.8 1.5 %shard_map.80 = (f32[4,27648]{1,0:T(4,128)}, f32[4,6912]{1,0:T(4,128)S(1)}, f32[4,6912]{1,0:T(4,128)S(1)}, f32[4,6912]{1,0:T(4,128)S(1)}, f32[4,6912]{1,0:T(4,128)S(1)}) custom-call(s32[4]{0:T(128)S(1)} %pad_add_fusion.where, f32[4,27648]{1,0:T(4,128)S(1)} %get-tuple-element.50.near, f32[4,27648]{1,0:T(4,128)S(1)} %collective-permute-done.9.far, ...), custom_call_target="tpu_custom_call" | custom-call | tf_op jit(solution)/shard_map/pallas_call | solution.py:356
  85.3 2.6 %collective-permute-start.19 = (f32[4,6912]{1,0:T(4,128)S(1)}, f32[4,6912]{1,0:T(4,128)S(1)}, u32[]{:S(2)}, u32[]{:S(2)}) collective-permute-start(f32[4,6912]{1,0:T(4,128)S(1)} %get-tuple-element.57), channel_id=1, source_target_pairs={{0,32},{1,33},{2,34},{3,35},{4,36},{5,37},{6,38},{7,39},{8,40},{9,... | collective-permute-start | bytes 331784 | tf_op jit(solution)/shard_map/ppermute | solution.py:451
  87.9 2.7 %collective-permute-done.15.own2 = f32[16,6912]{1,0:T(8,128)S(1)} collective-permute-done((f32[16,6912]{1,0:T(8,128)S(1)}, f32[16,6912]{1,0:T(8,128)S(1)}, u32[]{:S(2)}, u32[]{:S(2)}) %collective-permute-start.15) | collective-permute-done | bytes 442400 | tf_op jit(solution)/shard_map/ppermute | solution.py:451
  91.7 8.4 %collective-permute-done.16.oth2 = f32[16,6912]{1,0:T(8,128)S(1)} collective-permute-done((f32[16,6912]{1,0:T(8,128)S(1)}, f32[16,6912]{1,0:T(8,128)S(1)}, u32[]{:S(2)}, u32[]{:S(2)}) %collective-permute-start.16) | collective-permute-done | bytes 442400 | tf_op jit(solution)/shard_map/ppermute | solution.py:451
  100.1 2.2 %shard_map.81 = f32[16,128]{1,0:T(8,128)S(1)} custom-call(s32[4]{0:T(128)S(1)} %pad_add_fusion.where, f32[16,6912]{1,0:T(8,128)S(1)} %pad_maximum_fusion.own0, f32[16,6912]{1,0:T(8,128)S(1)} %collective-permute-done.12.oth0, f32[16,6912]{1,0:T(8,128)S(1)} %collective-permute-done.13.own1, f32[16,6912]{1,0:T(8,128)S(1)} %collective-permute-done.14.oth1, ...), custom_call_target="tpu_custom_call" | custom-call | tf_op jit(solution)/shard_map/pallas_call | solution.py:356
  102.3 10.7 %all_to_all.9 = f32[16,1,128]{2,1,0:T(1,128)S(1)} all-to-all(f32[16,1,128]{2,1,0:T(1,128)S(1)} %bitcast.8), channel_id=1, replica_groups={{0,1,2,3,32,33,34,35,64,65,66,67,96,97,98,99},{4,5,6,7,36,37,38,39,68,6..., dimensions={0} | all-to-all | bytes 16384 | tf_op jit(solution)/shard_map/all_to_all | solution.py:511
  (41 shorter events, 6.2 us)
Async XLA Ops:
  0.7 35.4 %copy-start = (f32[48,2304]{1,0:T(8,128)S(1)}, f32[48,2304]{1,0:T(8,128)}, u32[]{:S(2)}) copy-start(f32[48,2304]{1,0:T(8,128)} %constant.65.clone.kern) | copy-start | bytes 1327108
  0.7 35.3 %copy-start.3 = (f32[8,768]{1,0:T(8,128)S(1)}, f32[8,768]{1,0:T(8,128)}, u32[]{:S(2)}) copy-start(f32[8,768]{1,0:T(8,128)} %constant.66.clone.third) | copy-start | bytes 73732
  2.1 9.5 %collective-permute-start.1 = (f32[4,6912]{1,0:T(4,128)S(1)}, f32[4,6912]{1,0:T(4,128)S(1)}, u32[]{:S(2)}, u32[]{:S(2)}) collective-permute-start(f32[4,6912]{1,0:T(4,128)S(1)} %get-tuple-element.32), channel_id=1, source_target_pairs={{0,32},{1,33},{2,34},{3,35},{4,36},{5,37},{6,38},{7,39},{8,40},{9,... | collective-permute-start | bytes 331784 | tf_op jit(solution)/shard_map/ppermute | solution.py:451
  4.6 8.2 %collective-permute-start.2 = (f32[4,6912]{1,0:T(4,128)S(1)}, f32[4,6912]{1,0:T(4,128)S(1)}, u32[]{:S(2)}, u32[]{:S(2)}) collective-permute-start(f32[4,6912]{1,0:T(4,128)S(1)} %get-tuple-element.33), channel_id=1, source_target_pairs={{0,64},{1,65},{2,66},{3,67},{4,68},{5,69},{6,70},{7,71},{8,72},{9,... | collective-permute-start | bytes 331784 | tf_op jit(solution)/shard_map/ppermute | solution.py:451
  7.9 7.4 %collective-permute-start.3 = (f32[4,6912]{1,0:T(4,128)S(1)}, f32[4,6912]{1,0:T(4,128)S(1)}, u32[]{:S(2)}, u32[]{:S(2)}) collective-permute-start(f32[4,6912]{1,0:T(4,128)S(1)} %get-tuple-element.34), channel_id=1, source_target_pairs={{0,96},{1,97},{2,98},{3,99},{4,100},{5,101},{6,102},{7,103},{8,104... | collective-permute-start | bytes 331784 | tf_op jit(solution)/shard_map/ppermute | solution.py:451
  7.9 10.7 %collective-permute-start = (f32[4,27648]{1,0:T(4,128)}, f32[4,27648]{1,0:T(4,128)S(1)}, u32[]{:S(2)}, u32[]{:S(2)}) collective-permute-start(f32[4,27648]{1,0:T(4,128)} %own.1), channel_id=1, source_target_pairs={{0,2},{1,3},{2,0},{3,1},{4,6},{5,7},{6,4},{7,5},{8,10},{9,11},{10,... | collective-permute-start | bytes 1327112 | tf_op jit(solution)/shard_map/ppermute | solution.py:451
  9.1 21.0 %collective-permute-start.5 = (f32[2,27648]{1,0:T(2,128)S(1)}, f32[2,27648]{1,0:T(2,128)S(1)}, u32[]{:S(2)}, u32[]{:S(2)}) collective-permute-start(f32[2,27648]{1,0:T(2,128)S(1)} %get-tuple-element.36), channel_id=1, source_target_pairs={{0,4},{1,5},{2,6},{3,7},{4,8},{5,9},{6,10},{7,11},{8,12},{9,13},{1... | collective-permute-start | bytes 663560 | tf_op jit(solution)/shard_map/ppermute | solution.py:451
  11.6 18.5 %collective-permute-start.6 = (f32[2,27648]{1,0:T(2,128)S(1)}, f32[2,27648]{1,0:T(2,128)S(1)}, u32[]{:S(2)}, u32[]{:S(2)}) collective-permute-start(f32[2,27648]{1,0:T(2,128)S(1)} %get-tuple-element.37), channel_id=1, source_target_pairs={{0,6},{1,7},{2,4},{3,5},{4,10},{5,11},{6,8},{7,9},{8,14},{9,15},{1... | collective-permute-start | bytes 663560 | tf_op jit(solution)/shard_map/ppermute | solution.py:451
  30.9 5.1 %collective-permute-start.7 = (f32[8,27648]{1,0:T(8,128)S(1)}, f32[8,27648]{1,0:T(8,128)S(1)}, u32[]{:S(2)}, u32[]{:S(2)}) collective-permute-start(f32[8,27648]{1,0:T(8,128)S(1)} %shard_map.78), channel_id=1, source_target_pairs={{0,1},{1,0},{2,3},{3,2},{4,5},{5,4},{6,7},{7,6},{8,9},{9,8},{10,11... | collective-permute-start | bytes 2654216 | tf_op jit(solution)/shard_map/ppermute | solution.py:451
  33.3 2.7 %collective-permute-start.4 = (f32[4,27648]{1,0:T(4,128)}, f32[4,27648]{1,0:T(4,128)S(1)}, u32[]{:S(2)}, u32[]{:S(2)}) collective-permute-start(f32[4,27648]{1,0:T(4,128)} %own.1), channel_id=1, source_target_pairs={{0,1},{1,0},{2,3},{3,2},{4,5},{5,4},{6,7},{7,6},{8,9},{9,8},{10,11... | collective-permute-start | bytes 1327112 | tf_op jit(solution)/shard_map/ppermute | solution.py:451
  53.9 13.6 %collective-permute-start.8 = (f32[10,27648]{1,0:T(8,128)S(1)}, f32[10,27648]{1,0:T(8,128)S(1)}, u32[]{:S(2)}, u32[]{:S(2)}) collective-permute-start(f32[10,27648]{1,0:T(8,128)S(1)} %get-tuple-element.49), channel_id=1, source_target_pairs={{0,1},{1,0},{2,3},{3,2},{4,5},{5,4},{6,7},{7,6},{8,9},{9,8},{10,11... | collective-permute-start | bytes 3317768 | tf_op jit(solution)/shard_map/ppermute | solution.py:451
  54.4 13.1 %collective-permute-start.12 = (f32[16,6912]{1,0:T(8,128)S(1)}, f32[16,6912]{1,0:T(8,128)S(1)}, u32[]{:S(2)}, u32[]{:S(2)}) collective-permute-start(f32[16,6912]{1,0:T(8,128)S(1)} %pad_maximum_fusion.own0), channel_id=1, source_target_pairs={{0,4},{1,5},{2,6},{3,7},{4,0},{5,1},{6,2},{7,3},{8,12},{9,13},{10,... | collective-permute-start | bytes 1327112 | tf_op jit(solution)/shard_map/ppermute | solution.py:451
  54.4 17.5 %collective-permute-start.13 = (f32[16,6912]{1,0:T(8,128)S(1)}, f32[16,6912]{1,0:T(8,128)S(1)}, u32[]{:S(2)}, u32[]{:S(2)}) collective-permute-start(f32[16,6912]{1,0:T(8,128)S(1)} %pad_maximum_fusion.own0), channel_id=1, source_target_pairs={{0,8},{1,9},{2,10},{3,11},{4,12},{5,13},{6,14},{7,15},{8,16},{9,17... | collective-permute-start | bytes 1327112 | tf_op jit(solution)/shard_map/ppermute | solution.py:451
  67.5 12.0 %collective-permute-start.14 = (f32[16,6912]{1,0:T(8,128)S(1)}, f32[16,6912]{1,0:T(8,128)S(1)}, u32[]{:S(2)}, u32[]{:S(2)}) collective-permute-start(f32[16,6912]{1,0:T(8,128)S(1)} %collective-permute-done.12.oth0), channel_id=1, source_target_pairs={{0,8},{1,9},{2,10},{3,11},{4,12},{5,13},{6,14},{7,15},{8,16},{9,17... | collective-permute-start | bytes 1327112 | tf_op jit(solution)/shard_map/ppermute | solution.py:451
  68.2 11.3 %collective-permute-start.10 = (f32[2,27648]{1,0:T(2,128)S(1)}, f32[2,27648]{1,0:T(2,128)S(1)}, u32[]{:S(2)}, u32[]{:S(2)}) collective-permute-start(f32[2,27648]{1,0:T(2,128)S(1)} %get-tuple-element.52), channel_id=1, source_target_pairs={{0,124},{1,125},{2,126},{3,127},{4,0},{5,1},{6,2},{7,3},{8,4},{9,5... | collective-permute-start | bytes 663560 | tf_op jit(solution)/shard_map/ppermute | solution.py:451
  69.6 12.6 %collective-permute-start.11 = (f32[2,27648]{1,0:T(2,128)S(1)}, f32[2,27648]{1,0:T(2,128)S(1)}, u32[]{:S(2)}, u32[]{:S(2)}) collective-permute-start(f32[2,27648]{1,0:T(2,128)S(1)} %get-tuple-element.53), channel_id=1, source_target_pairs={{0,126},{1,127},{2,124},{3,125},{4,2},{5,3},{6,0},{7,1},{8,6},{9,7... | collective-permute-start | bytes 663560 | tf_op jit(solution)/shard_map/ppermute | solution.py:451
  71.7 12.2 %collective-permute-start.9 = (f32[4,27648]{1,0:T(4,128)S(1)}, f32[4,27648]{1,0:T(4,128)S(1)}, u32[]{:S(2)}, u32[]{:S(2)}) collective-permute-start(f32[4,27648]{1,0:T(4,128)S(1)} %get-tuple-element.51), channel_id=1, source_target_pairs={{0,2},{1,3},{2,0},{3,1},{4,6},{5,7},{6,4},{7,5},{8,10},{9,11},{10,... | collective-permute-start | bytes 1327112 | tf_op jit(solution)/shard_map/ppermute | solution.py:451
  71.9 16.0 %collective-permute-start.17 = (f32[16,6912]{1,0:T(8,128)S(1)}, f32[16,6912]{1,0:T(8,128)S(1)}, u32[]{:S(2)}, u32[]{:S(2)}) collective-permute-start(f32[16,6912]{1,0:T(8,128)S(1)} %pad_maximum_fusion.own0), channel_id=1, source_target_pairs={{0,24},{1,25},{2,26},{3,27},{4,28},{5,29},{6,30},{7,31},{8,0},{9,1... | collective-permute-start | bytes 1327112 | tf_op jit(solution)/shard_map/ppermute | solution.py:451
  79.5 11.1 %collective-permute-start.15 = (f32[16,6912]{1,0:T(8,128)S(1)}, f32[16,6912]{1,0:T(8,128)S(1)}, u32[]{:S(2)}, u32[]{:S(2)}) collective-permute-start(f32[16,6912]{1,0:T(8,128)S(1)} %collective-permute-done.13.own1), channel_id=1, source_target_pairs={{0,8},{1,9},{2,10},{3,11},{4,12},{5,13},{6,14},{7,15},{8,16},{9,17... | collective-permute-start | bytes 1327112 | tf_op jit(solution)/shard_map/ppermute | solution.py:451
  79.5 12.2 %collective-permute-start.18 = (f32[16,6912]{1,0:T(8,128)S(1)}, f32[16,6912]{1,0:T(8,128)S(1)}, u32[]{:S(2)}, u32[]{:S(2)}) collective-permute-start(f32[16,6912]{1,0:T(8,128)S(1)} %collective-permute-done.12.oth0), channel_id=1, source_target_pairs={{0,24},{1,25},{2,26},{3,27},{4,28},{5,29},{6,30},{7,31},{8,0},{9,1... | collective-permute-start | bytes 1327112 | tf_op jit(solution)/shard_map/ppermute | solution.py:451
  82.2 17.9 %collective-permute-start.16 = (f32[16,6912]{1,0:T(8,128)S(1)}, f32[16,6912]{1,0:T(8,128)S(1)}, u32[]{:S(2)}, u32[]{:S(2)}) collective-permute-start(f32[16,6912]{1,0:T(8,128)S(1)} %collective-permute-done.14.oth1), channel_id=1, source_target_pairs={{0,8},{1,9},{2,10},{3,11},{4,12},{5,13},{6,14},{7,15},{8,16},{9,17... | collective-permute-start | bytes 1327112 | tf_op jit(solution)/shard_map/ppermute | solution.py:451
  85.3 14.7 %collective-permute-start.19 = (f32[4,6912]{1,0:T(4,128)S(1)}, f32[4,6912]{1,0:T(4,128)S(1)}, u32[]{:S(2)}, u32[]{:S(2)}) collective-permute-start(f32[4,6912]{1,0:T(4,128)S(1)} %get-tuple-element.57), channel_id=1, source_target_pairs={{0,32},{1,33},{2,34},{3,35},{4,36},{5,37},{6,38},{7,39},{8,40},{9,... | collective-permute-start | bytes 331784 | tf_op jit(solution)/shard_map/ppermute | solution.py:451
  87.9 12.2 %collective-permute-start.20 = (f32[4,6912]{1,0:T(4,128)S(1)}, f32[4,6912]{1,0:T(4,128)S(1)}, u32[]{:S(2)}, u32[]{:S(2)}) collective-permute-start(f32[4,6912]{1,0:T(4,128)S(1)} %get-tuple-element.58), channel_id=1, source_target_pairs={{0,64},{1,65},{2,66},{3,67},{4,68},{5,69},{6,70},{7,71},{8,72},{9,... | collective-permute-start | bytes 331784 | tf_op jit(solution)/shard_map/ppermute | solution.py:451
  90.6 9.5 %collective-permute-start.21 = (f32[4,6912]{1,0:T(4,128)S(1)}, f32[4,6912]{1,0:T(4,128)S(1)}, u32[]{:S(2)}, u32[]{:S(2)}) collective-permute-start(f32[4,6912]{1,0:T(4,128)S(1)} %get-tuple-element.59), channel_id=1, source_target_pairs={{0,96},{1,97},{2,98},{3,99},{4,100},{5,101},{6,102},{7,103},{8,104... | collective-permute-start | bytes 331784 | tf_op jit(solution)/shard_map/ppermute | solution.py:451
  (2 other events, 65.6 us)

commit v6 on v4

--- a/solution.py
+++ b/solution.py
@@ -366,7 +366,7 @@
 
 
 def chunk_of(where, k):
-    return pl.ds(pl.multiple_of((where[1] ^ k) * CHUNK, 128), CHUNK)
+    return pl.ds(pl.multiple_of((where[2] ^ k) * CHUNK, 128), CHUNK)
 
 
 def prepare_kernel(where, orbitals, sel_a, sel_b, *chunks):
@@ -428,10 +428,10 @@
         + lax.dot_general(fl, vt, dims, preferred_element_type=F32)
         + lax.dot_general(ft, vl, dims, preferred_element_type=F32)
     )
-    for dy in range(4):
-        for dz in range(4):
-            row = 32 * dy + 8 * dz
-            block[(z ^ dz) * 4 + (y + 4 - dy) % 4, :, :] = got[row : row + 8, :]
+    for dz in range(4):
+        for dy in range(4):
+            row = 32 * dz + 8 * dy
+            block[(z + 4 - dz) % 4 * 4 + (y ^ dy), :, :] = got[row : row + 8, :]
     out = block[...].reshape(128, 16).T * (1.0 / NCELL)
     turned = [out] + [pltpu.roll(out, 32 * r, 1) for r in (1, 2, 3)]
     third_of = lax.broadcasted_iota(jnp.int32, (16, 128), 1) // 32
@@ -441,9 +441,9 @@
         for j in range(3):
             picked = jnp.where(third_of == j, turned[(j - q_to) % 4], picked)
         picked = jnp.where(keep, picked, 0.0)
-        for dz in range(4):
-            row = jnp.sum(picked[4 * dz : 4 * dz + 4, :], axis=0, keepdims=True)
-            pieces[pl.ds((z ^ dz) * 4 + q_to, 1), :] = row
+        for dy in range(4):
+            row = jnp.sum(picked[4 * dy : 4 * dy + 4, :], axis=0, keepdims=True)
+            pieces[pl.ds((y ^ dy) * 4 + q_to, 1), :] = row
 
 
 def move(value, target):
@@ -456,12 +456,12 @@
     return lax.ppermute(value, BOTH, pairs)
 
 
-def along_z(value, flip):
-    return move(value, lambda z, y, h, q: (z ^ flip, y, h, q))
-
-
-def along_y(value, k):
-    return move(value, lambda z, y, h, q: (z, y + k, h, q))
+def along_y(value, flip):
+    return move(value, lambda z, y, h, q: (z, y ^ flip, h, q))
+
+
+def along_z(value, k):
+    return move(value, lambda z, y, h, q: (z + k, y, h, q))
 
 
 def within(value, flip):
@@ -482,11 +482,11 @@
     where = jnp.stack([q, b // 8, b // 2 % 4, b % 2])
     two = within(orbitals, 2)
     prepare = small_call(prepare_kernel, [(2, QCELL)] * 2 + [(4, CHUNK)] * 4)
-    sel_a, sel_b, *zc = prepare(where, orbitals)
+    sel_a, sel_b, *pc = prepare(where, orbitals)
     low_a = around(sel_a, 1, 0)
     low_b = around(sel_b, 1, 2)
     one = within(orbitals, 1)
-    pieces = [zc[0]] + [along_z(zc[k], k) for k in (1, 2, 3)]
+    pieces = [pc[0]] + [along_y(pc[k], k) for k in (1, 2, 3)]
     tables = plane_tables()
     together = jnp.concatenate(pieces, axis=0)
     two, together = lax.optimization_barrier((two, together))
@@ -495,8 +495,8 @@
     other = move(together, lambda z, y, h, q: (z, y, 1 - h, q))
     right, left, field = spectrum(q, (orbitals, two, one, low_a, low_b, core), tables[:2])
     (p0,) = small_call(pair_kernel, [(32, CHUNK)])(where, *pieces, other)
-    p1 = along_y(p0, 1)
-    p3 = along_y(p0, 3)
+    p1 = along_z(p0, 1)
+    p3 = along_z(p0, 3)
     near0, near2, cross, low0, low2 = terms(q, right, left, field, tables[2:])
     across = within(cross, 1)
     merge = small_call(merge_kernel, [(4, QCELL)] * 2 + [(2, QCELL)] * 2)
@@ -504,14 +504,14 @@
     far = within(both, 2)
     owed_a = around(owe_a, -1, 0)
     owed_b = around(owe_b, -1, 2)
-    p2a = along_y(p1[:16], 1)
-    p2b = along_y(p3[16:], 3)
+    p2a = along_z(p1[:16], 1)
+    p2b = along_z(p3[16:], 3)
     finalize = small_call(finalize_kernel, [(4, QCELL)] + [(4, CHUNK)] * 4)
     vectors, *vc = finalize(where, near, far, owed_a, owed_b)
-    given = [vc[0]] + [along_z(vc[k], k) for k in (1, 2, 3)]
+    given = [vc[0]] + [along_y(vc[k], k) for k in (1, 2, 3)]
     margin_part = small_call(margin_kernel, [(16, 128)], [pltpu.VMEM((16, 8, 16), F32)], 20)
     (sums,) = margin_part(where, p0, p1, p3, p2a, p2b, *given)
-    groups = [[(z * 8 + r) * 4 + p for z in range(4) for p in range(4)] for r in range(8)]
+    groups = [[(z * 8 + y * 2 + h) * 4 + p for y in range(4) for p in range(4)] for z in range(4) for h in range(2)]
     sums = lax.all_to_all(sums, BOTH, 0, 0, tiled=True, axis_index_groups=groups)
     margin = jnp.sum(sums, axis=0).reshape(4, 32).T
     return vectors, margin

time: 118 us -> 118 us (level)
  starting transfers between devices: 24.6 us -> 21.8 us
  waiting for transfers between devices: 54 us -> 56.7 us
    ppermute x20, starting transfers between devices: 24.6 us -> 21.8 us  [move(): return lax.ppermute(value, BOTH, pairs)]
    ppermute x20, waiting for transfers between devices: 54 us -> 56.7 us  [move(): return lax.ppermute(value, BOTH, pairs)]
where the time goes in v6:
time: 118 us; the launch traced here: 117 us
  waiting for transfers between devices  56.7 us (48%)
  Pallas kernels  27.1 us (23%)
  starting transfers between devices  21.8 us (18%)
  blocking collectives  9.65 us (8%)
    ppermute x20, waiting for transfers between devices, move(): return lax.ppermute(value, BOTH, pairs)  56.7 us
    ppermute x20, starting transfers between devices, move(): return lax.ppermute(value, BOTH, pairs)  21.8 us
    pallas_call x1, Pallas kernels, spectrum(): pl.pallas_call(spectrum_kernel, out_shape=[jax.ShapeDtypeStruct((NG, 8, P...  10.2 us
    all_to_all x1, blocking collectives, step(): lax.all_to_all(sums, BOTH, 0, 0, tiled=True, axis_index_groups=groups)  9.65 us
    pallas_call x1, Pallas kernels, terms(): pl.pallas_call(terms_kernel, out_shape=[jax.ShapeDtypeStruct(shape, F32)...  7.72 us
    pallas_call x6, Pallas kernels, call(): pl.pallas_call(body, out_shape=[jax.ShapeDtypeStruct(shape, F32) for shap...  7.23 us
  transfers between devices with their start and end apart: 20, of which 10 were waited for; matrix products, arithmetic and copies ran while one was open for 0% of the time, Pallas kernels for 19%

profile of v6, /device:TPU:1, one launch (start us, length us, event | category | flops | bytes accessed | tf_op | source)
XLA Modules:
  0.0 117.1 jit_solution(7397649890074311220)
XLA Ops:
  0.8 1.3 %shard_map.77 = (f32[2,27648]{1,0:T(2,128)S(1)}, f32[2,27648]{1,0:T(2,128)S(1)}, f32[4,6912]{1,0:T(4,128)S(1)}, f32[4,6912]{1,0:T(4,128)S(1)}, f32[4,6912]{1,0:T(4,128)S(1)}, /*index=5*/f32[4,6912]{1,0:T(4,128)S(1)}) custom-call(s32[4]{0:T(128)S(1)} %pad_add_fusion.where, f32[4,27648]{1,0:T(4,128)} %own.1), custom_call_target="tpu_custom_call" | custom-call | tf_op jit(solution)/shard_map/pallas_call | solution.py:356
  2.1 2.2 %collective-permute-start.1 = (f32[4,6912]{1,0:T(4,128)S(1)}, f32[4,6912]{1,0:T(4,128)S(1)}, u32[]{:S(2)}, u32[]{:S(2)}) collective-permute-start(f32[4,6912]{1,0:T(4,128)S(1)} %get-tuple-element.32), channel_id=1, source_target_pairs={{0,8},{1,9},{2,10},{3,11},{4,12},{5,13},{6,14},{7,15},{8,0},{9,1},... | collective-permute-start | bytes 331784 | tf_op jit(solution)/shard_map/ppermute | solution.py:456
  4.3 2.6 %collective-permute-start.2 = (f32[4,6912]{1,0:T(4,128)S(1)}, f32[4,6912]{1,0:T(4,128)S(1)}, u32[]{:S(2)}, u32[]{:S(2)}) collective-permute-start(f32[4,6912]{1,0:T(4,128)S(1)} %get-tuple-element.33), channel_id=1, source_target_pairs={{0,16},{1,17},{2,18},{3,19},{4,20},{5,21},{6,22},{7,23},{8,24},{9,... | collective-permute-start | bytes 331784 | tf_op jit(solution)/shard_map/ppermute | solution.py:456
  6.9 1.2 %collective-permute-start = (f32[4,27648]{1,0:T(4,128)}, f32[4,27648]{1,0:T(4,128)S(1)}, u32[]{:S(2)}, u32[]{:S(2)}) collective-permute-start(f32[4,27648]{1,0:T(4,128)} %own.1), channel_id=1, source_target_pairs={{0,2},{1,3},{2,0},{3,1},{4,6},{5,7},{6,4},{7,5},{8,10},{9,11},{10,... | collective-permute-start | bytes 1327112 | tf_op jit(solution)/shard_map/ppermute | solution.py:456
  8.1 2.5 %collective-permute-start.5 = (f32[2,27648]{1,0:T(2,128)S(1)}, f32[2,27648]{1,0:T(2,128)S(1)}, u32[]{:S(2)}, u32[]{:S(2)}) collective-permute-start(f32[2,27648]{1,0:T(2,128)S(1)} %get-tuple-element.36), channel_id=1, source_target_pairs={{0,4},{1,5},{2,6},{3,7},{4,8},{5,9},{6,10},{7,11},{8,12},{9,13},{1... | collective-permute-start | bytes 663560 | tf_op jit(solution)/shard_map/ppermute | solution.py:456
  10.6 1.2 %collective-permute-done.2.f2 = f32[4,6912]{1,0:T(4,128)S(1)} collective-permute-done((f32[4,6912]{1,0:T(4,128)S(1)}, f32[4,6912]{1,0:T(4,128)S(1)}, u32[]{:S(2)}, u32[]{:S(2)}) %collective-permute-start.2) | collective-permute-done | bytes 110624 | tf_op jit(solution)/shard_map/ppermute | solution.py:456
  11.7 2.6 %collective-permute-done.3.f3 = f32[4,6912]{1,0:T(4,128)S(1)} collective-permute-done((f32[4,6912]{1,0:T(4,128)S(1)}, f32[4,6912]{1,0:T(4,128)S(1)}, u32[]{:S(2)}, u32[]{:S(2)}) %collective-permute-start.3) | collective-permute-done | bytes 110624 | tf_op jit(solution)/shard_map/ppermute | solution.py:456
  14.4 3.1 %collective-permute-done.two = f32[4,27648]{1,0:T(4,128)S(1)} collective-permute-done((f32[4,27648]{1,0:T(4,128)}, f32[4,27648]{1,0:T(4,128)S(1)}, u32[]{:S(2)}, u32[]{:S(2)}) %collective-permute-start) | collective-permute-done | bytes 442400 | tf_op jit(solution)/shard_map/ppermute | solution.py:456
  17.5 12.6 %collective-permute-done.5.low_a = f32[2,27648]{1,0:T(2,128)S(1)} collective-permute-done((f32[2,27648]{1,0:T(2,128)S(1)}, f32[2,27648]{1,0:T(2,128)S(1)}, u32[]{:S(2)}, u32[]{:S(2)}) %collective-permute-start.5) | collective-permute-done | bytes 221216 | tf_op jit(solution)/shard_map/ppermute | solution.py:456
  30.9 2.5 %collective-permute-start.7 = (f32[8,27648]{1,0:T(8,128)S(1)}, f32[8,27648]{1,0:T(8,128)S(1)}, u32[]{:S(2)}, u32[]{:S(2)}) collective-permute-start(f32[8,27648]{1,0:T(8,128)S(1)} %shard_map.78), channel_id=1, source_target_pairs={{0,1},{1,0},{2,3},{3,2},{4,5},{5,4},{6,7},{7,6},{8,9},{9,8},{10,11... | collective-permute-start | bytes 2654216 | tf_op jit(solution)/shard_map/ppermute | solution.py:456
  33.4 1.9 %plane_tables.1 = (bf16[2,768,768]{2,1,0:T(8,128)(2,1)S(1)}, bf16[2,768,768]{2,1,0:T(8,128)(2,1)S(1)}, bf16[2,768,768]{2,1,0:T(8,128)(2,1)S(1)}, bf16[2,768,768]{2,1,0:T(8,128)(2,1)S(1)}) custom-call(f32[4,16,768]{2,1,0:T(8,128)S(1)} %copy-done.2, f32[2,48,768]{2,1,0:T(8,128)S(1)} %copy-done.1), custom_call_target="tpu_custom_call" | custom-call | tf_op jit(solution)/shard_map/plane_tables/pallas_call | solution.py:118
  36.0 10.2 %spectrum.1 = (f32[48,8,2304]{2,1,0:T(8,128)S(1)}, f32[48,8,2304]{2,1,0:T(8,128)S(1)}, f32[384,2304]{1,0:T(8,128)S(1)}) custom-call(s32[1]{0:T(128)} %bitcast.q_ref, f32[4,27648]{1,0:T(4,128)} %own.1, f32[4,27648]{1,0:T(4,128)S(1)} %collective-permute-done.two, f32[4,27648]{1,0:T(4,128)S(1)} %collective-permute-done.4.one, ...), custom_call_target="tpu_custom_call" | custom-call | tf_op jit(solution)/shard_map/spectrum/pallas_call | solution.py:325
  46.2 7.7 %terms.1 = (f32[4,27648]{1,0:T(4,128)S(1)}, f32[4,27648]{1,0:T(4,128)S(1)}, f32[10,27648]{1,0:T(8,128)S(1)}, f32[1,27648]{1,0:T(1,128)S(1)}, f32[1,27648]{1,0:T(1,128)S(1)}) custom-call(s32[1]{0:T(128)} %bitcast.q_ref, f32[48,8,2304]{2,1,0:T(8,128)S(1)} %get-tuple-element.40.right, f32[48,8,2304]{2,1,0:T(8,128)S(1)} %get-tuple-element.41.left, ...), custom_call_target="tpu_custom_call" | custom-call | tf_op jit(solution)/shard_map/terms/pallas_call | solution.py:337
  55.2 2.7 %collective-permute-start.14 = (f32[32,6912]{1,0:T(8,128)S(1)}, f32[32,6912]{1,0:T(8,128)S(1)}, u32[]{:S(2)}, u32[]{:S(2)}) collective-permute-start(f32[32,6912]{1,0:T(8,128)S(1)} %shard_map.81.p0), channel_id=1, source_target_pairs={{0,96},{1,97},{2,98},{3,99},{4,100},{5,101},{6,102},{7,103},{8,104... | collective-permute-start | bytes 2654216 | tf_op jit(solution)/shard_map/ppermute | solution.py:456
  58.7 18.8 %collective-permute-done.13.p1 = f32[32,6912]{1,0:T(8,128)S(1)} collective-permute-done((f32[32,6912]{1,0:T(8,128)S(1)}, f32[32,6912]{1,0:T(8,128)S(1)}, u32[]{:S(2)}, u32[]{:S(2)}) %collective-permute-start.13) | collective-permute-done | bytes 884768 | tf_op jit(solution)/shard_map/ppermute | solution.py:456
  77.8 2.7 %collective-permute-start.16 = (f32[16,6912]{1,0:T(8,128)S(1)}, f32[16,6912]{1,0:T(8,128)S(1)}, u32[]{:S(2)}, u32[]{:S(2)}) collective-permute-start(f32[16,6912]{1,0:T(8,128)S(1)} %slice.9), channel_id=1, source_target_pairs={{0,96},{1,97},{2,98},{3,99},{4,100},{5,101},{6,102},{7,103},{8,104... | collective-permute-start | bytes 1327112 | tf_op jit(solution)/shard_map/ppermute | solution.py:456
  81.2 6.4 %collective-permute-done.10.owed_a = f32[2,27648]{1,0:T(2,128)S(1)} collective-permute-done((f32[2,27648]{1,0:T(2,128)S(1)}, f32[2,27648]{1,0:T(2,128)S(1)}, u32[]{:S(2)}, u32[]{:S(2)}) %collective-permute-start.10) | collective-permute-done | bytes 221216 | tf_op jit(solution)/shard_map/ppermute | solution.py:456
  87.6 6.0 %collective-permute-done.11.owed_b = f32[2,27648]{1,0:T(2,128)S(1)} collective-permute-done((f32[2,27648]{1,0:T(2,128)S(1)}, f32[2,27648]{1,0:T(2,128)S(1)}, u32[]{:S(2)}, u32[]{:S(2)}) %collective-permute-start.11) | collective-permute-done | bytes 221216 | tf_op jit(solution)/shard_map/ppermute | solution.py:456
  93.6 1.5 %shard_map.80 = (f32[4,27648]{1,0:T(4,128)}, f32[4,6912]{1,0:T(4,128)S(1)}, f32[4,6912]{1,0:T(4,128)S(1)}, f32[4,6912]{1,0:T(4,128)S(1)}, f32[4,6912]{1,0:T(4,128)S(1)}) custom-call(s32[4]{0:T(128)S(1)} %pad_add_fusion.where, f32[4,27648]{1,0:T(4,128)S(1)} %get-tuple-element.50.near, f32[4,27648]{1,0:T(4,128)S(1)} %collective-permute-done.9.far, ...), custom_call_target="tpu_custom_call" | custom-call | tf_op jit(solution)/shard_map/pallas_call | solution.py:356
  95.6 3.3 %collective-permute-start.19 = (f32[4,6912]{1,0:T(4,128)S(1)}, f32[4,6912]{1,0:T(4,128)S(1)}, u32[]{:S(2)}, u32[]{:S(2)}) collective-permute-start(f32[4,6912]{1,0:T(4,128)S(1)} %get-tuple-element.59), channel_id=1, source_target_pairs={{0,24},{1,25},{2,26},{3,27},{4,28},{5,29},{6,30},{7,31},{8,16},{9,... | collective-permute-start | bytes 331784 | tf_op jit(solution)/shard_map/ppermute | solution.py:456
  99.0 1.8 %collective-permute-done.18.v2 = f32[4,6912]{1,0:T(4,128)S(1)} collective-permute-done((f32[4,6912]{1,0:T(4,128)S(1)}, f32[4,6912]{1,0:T(4,128)S(1)}, u32[]{:S(2)}, u32[]{:S(2)}) %collective-permute-start.18) | collective-permute-done | bytes 110624 | tf_op jit(solution)/shard_map/ppermute | solution.py:456
  100.8 3.7 %collective-permute-done.19.v3 = f32[4,6912]{1,0:T(4,128)S(1)} collective-permute-done((f32[4,6912]{1,0:T(4,128)S(1)}, f32[4,6912]{1,0:T(4,128)S(1)}, u32[]{:S(2)}, u32[]{:S(2)}) %collective-permute-start.19) | collective-permute-done | bytes 110624 | tf_op jit(solution)/shard_map/ppermute | solution.py:456
  104.4 2.2 %shard_map.82 = f32[16,128]{1,0:T(8,128)S(1)} custom-call(s32[4]{0:T(128)S(1)} %pad_add_fusion.where, f32[32,6912]{1,0:T(8,128)S(1)} %shard_map.81.p0, f32[32,6912]{1,0:T(8,128)S(1)} %collective-permute-done.13.p1, f32[32,6912]{1,0:T(8,128)S(1)} %collective-permute-done.14.p3, f32[16,6912]{1,0:T(8,128)S(1)} %collective-permute-done.15.p2a, ...), custom_call_target="tpu_custom_call" | custom-call | tf_op jit(solution)/shard_map/pallas_call | solution.py:356
  106.7 9.7 %all_to_all.9 = f32[16,1,128]{2,1,0:T(1,128)S(1)} all-to-all(f32[16,1,128]{2,1,0:T(1,128)S(1)} %bitcast.8), channel_id=1, replica_groups={{0,1,2,3,8,9,10,11,16,17,18,19,24,25,26,27},{4,5,6,7,12,13,14,15,20,21,..., dimensions={0} | all-to-all | bytes 16384 | tf_op jit(solution)/shard_map/all_to_all | solution.py:515
  (40 shorter events, 6.0 us)
Async XLA Ops:
  0.6 32.8 %copy-start.2 = (f32[4,16,768]{2,1,0:T(8,128)S(1)}, f32[4,16,768]{2,1,0:T(8,128)}, u32[]{:S(2)}) copy-start(f32[4,16,768]{2,1,0:T(8,128)} %constant.63.clone.tens) | copy-start | bytes 589828
  0.6 32.8 %copy-start.1 = (f32[2,48,768]{2,1,0:T(8,128)S(1)}, f32[2,48,768]{2,1,0:T(8,128)}, u32[]{:S(2)}) copy-start(f32[2,48,768]{2,1,0:T(8,128)} %constant.64.clone.zs) | copy-start | bytes 884740
  0.7 35.4 %copy-start = (f32[48,2304]{1,0:T(8,128)S(1)}, f32[48,2304]{1,0:T(8,128)}, u32[]{:S(2)}) copy-start(f32[48,2304]{1,0:T(8,128)} %constant.65.clone.kern) | copy-start | bytes 1327108
  0.7 35.3 %copy-start.3 = (f32[8,768]{1,0:T(8,128)S(1)}, f32[8,768]{1,0:T(8,128)}, u32[]{:S(2)}) copy-start(f32[8,768]{1,0:T(8,128)} %constant.66.clone.third) | copy-start | bytes 73732
  2.1 8.5 %collective-permute-start.1 = (f32[4,6912]{1,0:T(4,128)S(1)}, f32[4,6912]{1,0:T(4,128)S(1)}, u32[]{:S(2)}, u32[]{:S(2)}) collective-permute-start(f32[4,6912]{1,0:T(4,128)S(1)} %get-tuple-element.32), channel_id=1, source_target_pairs={{0,8},{1,9},{2,10},{3,11},{4,12},{5,13},{6,14},{7,15},{8,0},{9,1},... | collective-permute-start | bytes 331784 | tf_op jit(solution)/shard_map/ppermute | solution.py:456
  4.3 7.5 %collective-permute-start.2 = (f32[4,6912]{1,0:T(4,128)S(1)}, f32[4,6912]{1,0:T(4,128)S(1)}, u32[]{:S(2)}, u32[]{:S(2)}) collective-permute-start(f32[4,6912]{1,0:T(4,128)S(1)} %get-tuple-element.33), channel_id=1, source_target_pairs={{0,16},{1,17},{2,18},{3,19},{4,20},{5,21},{6,22},{7,23},{8,24},{9,... | collective-permute-start | bytes 331784 | tf_op jit(solution)/shard_map/ppermute | solution.py:456
  6.9 7.4 %collective-permute-start.3 = (f32[4,6912]{1,0:T(4,128)S(1)}, f32[4,6912]{1,0:T(4,128)S(1)}, u32[]{:S(2)}, u32[]{:S(2)}) collective-permute-start(f32[4,6912]{1,0:T(4,128)S(1)} %get-tuple-element.34), channel_id=1, source_target_pairs={{0,24},{1,25},{2,26},{3,27},{4,28},{5,29},{6,30},{7,31},{8,16},{9,... | collective-permute-start | bytes 331784 | tf_op jit(solution)/shard_map/ppermute | solution.py:456
  6.9 10.6 %collective-permute-start = (f32[4,27648]{1,0:T(4,128)}, f32[4,27648]{1,0:T(4,128)S(1)}, u32[]{:S(2)}, u32[]{:S(2)}) collective-permute-start(f32[4,27648]{1,0:T(4,128)} %own.1), channel_id=1, source_target_pairs={{0,2},{1,3},{2,0},{3,1},{4,6},{5,7},{6,4},{7,5},{8,10},{9,11},{10,... | collective-permute-start | bytes 1327112 | tf_op jit(solution)/shard_map/ppermute | solution.py:456
  8.1 22.0 %collective-permute-start.5 = (f32[2,27648]{1,0:T(2,128)S(1)}, f32[2,27648]{1,0:T(2,128)S(1)}, u32[]{:S(2)}, u32[]{:S(2)}) collective-permute-start(f32[2,27648]{1,0:T(2,128)S(1)} %get-tuple-element.36), channel_id=1, source_target_pairs={{0,4},{1,5},{2,6},{3,7},{4,8},{5,9},{6,10},{7,11},{8,12},{9,13},{1... | collective-permute-start | bytes 663560 | tf_op jit(solution)/shard_map/ppermute | solution.py:456
  10.6 19.6 %collective-permute-start.6 = (f32[2,27648]{1,0:T(2,128)S(1)}, f32[2,27648]{1,0:T(2,128)S(1)}, u32[]{:S(2)}, u32[]{:S(2)}) collective-permute-start(f32[2,27648]{1,0:T(2,128)S(1)} %get-tuple-element.37), channel_id=1, source_target_pairs={{0,6},{1,7},{2,4},{3,5},{4,10},{5,11},{6,8},{7,9},{8,14},{9,15},{1... | collective-permute-start | bytes 663560 | tf_op jit(solution)/shard_map/ppermute | solution.py:456
  30.9 5.1 %collective-permute-start.7 = (f32[8,27648]{1,0:T(8,128)S(1)}, f32[8,27648]{1,0:T(8,128)S(1)}, u32[]{:S(2)}, u32[]{:S(2)}) collective-permute-start(f32[8,27648]{1,0:T(8,128)S(1)} %shard_map.78), channel_id=1, source_target_pairs={{0,1},{1,0},{2,3},{3,2},{4,5},{5,4},{6,7},{7,6},{8,9},{9,8},{10,11... | collective-permute-start | bytes 2654216 | tf_op jit(solution)/shard_map/ppermute | solution.py:456
  33.3 2.7 %collective-permute-start.4 = (f32[4,27648]{1,0:T(4,128)}, f32[4,27648]{1,0:T(4,128)S(1)}, u32[]{:S(2)}, u32[]{:S(2)}) collective-permute-start(f32[4,27648]{1,0:T(4,128)} %own.1), channel_id=1, source_target_pairs={{0,1},{1,0},{2,3},{3,2},{4,5},{5,4},{6,7},{7,6},{8,9},{9,8},{10,11... | collective-permute-start | bytes 1327112 | tf_op jit(solution)/shard_map/ppermute | solution.py:456
  33.4 21.0 %collective-permute-start.12 = (f32[16,6912]{1,0:T(8,128)S(1)}, f32[16,6912]{1,0:T(8,128)S(1)}, u32[]{:S(2)}, u32[]{:S(2)}) collective-permute-start(f32[16,6912]{1,0:T(8,128)S(1)} %pad_maximum_fusion), channel_id=1, source_target_pairs={{0,4},{1,5},{2,6},{3,7},{4,0},{5,1},{6,2},{7,3},{8,12},{9,13},{10,... | collective-permute-start | bytes 1327112 | tf_op jit(solution)/shard_map/ppermute | solution.py:456
  53.9 3.9 %collective-permute-start.8 = (f32[10,27648]{1,0:T(8,128)S(1)}, f32[10,27648]{1,0:T(8,128)S(1)}, u32[]{:S(2)}, u32[]{:S(2)}) collective-permute-start(f32[10,27648]{1,0:T(8,128)S(1)} %get-tuple-element.49), channel_id=1, source_target_pairs={{0,1},{1,0},{2,3},{3,2},{4,5},{5,4},{6,7},{7,6},{8,9},{9,8},{10,11... | collective-permute-start | bytes 3317768 | tf_op jit(solution)/shard_map/ppermute | solution.py:456
  55.1 22.4 %collective-permute-start.13 = (f32[32,6912]{1,0:T(8,128)S(1)}, f32[32,6912]{1,0:T(8,128)S(1)}, u32[]{:S(2)}, u32[]{:S(2)}) collective-permute-start(f32[32,6912]{1,0:T(8,128)S(1)} %shard_map.81.p0), channel_id=1, source_target_pairs={{0,32},{1,33},{2,34},{3,35},{4,36},{5,37},{6,38},{7,39},{8,40},{9,... | collective-permute-start | bytes 2654216 | tf_op jit(solution)/shard_map/ppermute | solution.py:456
  55.2 22.6 %collective-permute-start.14 = (f32[32,6912]{1,0:T(8,128)S(1)}, f32[32,6912]{1,0:T(8,128)S(1)}, u32[]{:S(2)}, u32[]{:S(2)}) collective-permute-start(f32[32,6912]{1,0:T(8,128)S(1)} %shard_map.81.p0), channel_id=1, source_target_pairs={{0,96},{1,97},{2,98},{3,99},{4,100},{5,101},{6,102},{7,103},{8,104... | collective-permute-start | bytes 2654216 | tf_op jit(solution)/shard_map/ppermute | solution.py:456
  58.6 34.9 %collective-permute-start.9 = (f32[4,27648]{1,0:T(4,128)S(1)}, f32[4,27648]{1,0:T(4,128)S(1)}, u32[]{:S(2)}, u32[]{:S(2)}) collective-permute-start(f32[4,27648]{1,0:T(4,128)S(1)} %get-tuple-element.51), channel_id=1, source_target_pairs={{0,2},{1,3},{2,0},{3,1},{4,6},{5,7},{6,4},{7,5},{8,10},{9,11},{10,... | collective-permute-start | bytes 1327112 | tf_op jit(solution)/shard_map/ppermute | solution.py:456
  77.5 21.4 %collective-permute-start.15 = (f32[16,6912]{1,0:T(8,128)S(1)}, f32[16,6912]{1,0:T(8,128)S(1)}, u32[]{:S(2)}, u32[]{:S(2)}) collective-permute-start(f32[16,6912]{1,0:T(8,128)S(1)} %slice.8), channel_id=1, source_target_pairs={{0,32},{1,33},{2,34},{3,35},{4,36},{5,37},{6,38},{7,39},{8,40},{9,... | collective-permute-start | bytes 1327112 | tf_op jit(solution)/shard_map/ppermute | solution.py:456
  77.8 21.1 %collective-permute-start.16 = (f32[16,6912]{1,0:T(8,128)S(1)}, f32[16,6912]{1,0:T(8,128)S(1)}, u32[]{:S(2)}, u32[]{:S(2)}) collective-permute-start(f32[16,6912]{1,0:T(8,128)S(1)} %slice.9), channel_id=1, source_target_pairs={{0,96},{1,97},{2,98},{3,99},{4,100},{5,101},{6,102},{7,103},{8,104... | collective-permute-start | bytes 1327112 | tf_op jit(solution)/shard_map/ppermute | solution.py:456
  80.6 7.0 %collective-permute-start.10 = (f32[2,27648]{1,0:T(2,128)S(1)}, f32[2,27648]{1,0:T(2,128)S(1)}, u32[]{:S(2)}, u32[]{:S(2)}) collective-permute-start(f32[2,27648]{1,0:T(2,128)S(1)} %get-tuple-element.52), channel_id=1, source_target_pairs={{0,124},{1,125},{2,126},{3,127},{4,0},{5,1},{6,2},{7,3},{8,4},{9,5... | collective-permute-start | bytes 663560 | tf_op jit(solution)/shard_map/ppermute | solution.py:456
  80.6 13.0 %collective-permute-start.11 = (f32[2,27648]{1,0:T(2,128)S(1)}, f32[2,27648]{1,0:T(2,128)S(1)}, u32[]{:S(2)}, u32[]{:S(2)}) collective-permute-start(f32[2,27648]{1,0:T(2,128)S(1)} %get-tuple-element.53), channel_id=1, source_target_pairs={{0,126},{1,127},{2,124},{3,125},{4,2},{5,3},{6,0},{7,1},{8,6},{9,7... | collective-permute-start | bytes 663560 | tf_op jit(solution)/shard_map/ppermute | solution.py:456
  95.1 3.9 %collective-permute-start.17 = (f32[4,6912]{1,0:T(4,128)S(1)}, f32[4,6912]{1,0:T(4,128)S(1)}, u32[]{:S(2)}, u32[]{:S(2)}) collective-permute-start(f32[4,6912]{1,0:T(4,128)S(1)} %get-tuple-element.57), channel_id=1, source_target_pairs={{0,8},{1,9},{2,10},{3,11},{4,12},{5,13},{6,14},{7,15},{8,0},{9,1},... | collective-permute-start | bytes 331784 | tf_op jit(solution)/shard_map/ppermute | solution.py:456
  95.6 5.2 %collective-permute-start.18 = (f32[4,6912]{1,0:T(4,128)S(1)}, f32[4,6912]{1,0:T(4,128)S(1)}, u32[]{:S(2)}, u32[]{:S(2)}) collective-permute-start(f32[4,6912]{1,0:T(4,128)S(1)} %get-tuple-element.58), channel_id=1, source_target_pairs={{0,16},{1,17},{2,18},{3,19},{4,20},{5,21},{6,22},{7,23},{8,24},{9,... | collective-permute-start | bytes 331784 | tf_op jit(solution)/shard_map/ppermute | solution.py:456
  95.6 8.9 %collective-permute-start.19 = (f32[4,6912]{1,0:T(4,128)S(1)}, f32[4,6912]{1,0:T(4,128)S(1)}, u32[]{:S(2)}, u32[]{:S(2)}) collective-permute-start(f32[4,6912]{1,0:T(4,128)S(1)} %get-tuple-element.59), channel_id=1, source_target_pairs={{0,24},{1,25},{2,26},{3,27},{4,28},{5,29},{6,30},{7,31},{8,16},{9,... | collective-permute-start | bytes 331784 | tf_op jit(solution)/shard_map/ppermute | solution.py:456

commit v7 on v6

--- a/solution.py
+++ b/solution.py
@@ -369,11 +369,14 @@
     return pl.ds(pl.multiple_of((where[2] ^ k) * CHUNK, 128), CHUNK)
 
 
-def prepare_kernel(where, orbitals, sel_a, sel_b, *chunks):
+def rows_kernel(where, orbitals, sel_a, sel_b):
     lower = where[0] < 2
     a, b = orbitals[0:2, :], orbitals[2:4, :]
     sel_a[...] = jnp.where(lower, a, b)
     sel_b[...] = jnp.where(lower, b, a)
+
+
+def chunks_kernel(where, orbitals, *chunks):
     for k in range(4):
         chunks[k][...] = orbitals[:, chunk_of(where, k)]
 
@@ -394,14 +397,22 @@
         out[1:2, :] = jnp.where(first, b, a)
 
 
-def finalize_kernel(where, near, far, owed_a, owed_b, vectors, *chunks):
+def total_of(where, near, far, owed_a, owed_b, span):
     lower = where[0] < 2
-    a, b = owed_a[...], owed_b[...]
-    total = near[...] + far[...]
-    vectors[0:2, :] = total[0:2, :] + jnp.where(lower, a, b)
-    vectors[2:4, :] = total[2:4, :] + jnp.where(lower, b, a)
-    for k in range(4):
-        chunks[k][...] = vectors[:, chunk_of(where, k)]
+    a, b = owed_a[:, span], owed_b[:, span]
+    owed = jnp.concatenate([jnp.where(lower, a, b), jnp.where(lower, b, a)], axis=0)
+    return near[:, span] + far[:, span] + owed
+
+
+def finalize_kernel(where, near, far, owed_a, owed_b, *chunks):
+    for k in (1, 2, 3, 0):
+        chunks[k][...] = total_of(where, near, far, owed_a, owed_b, chunk_of(where, k))
+
+
+def vectors_kernel(where, near, far, owed_a, owed_b, vectors):
+    for c in range(4):
+        span = pl.ds(c * CHUNK, CHUNK)
+        vectors[:, span] = total_of(where, near, far, owed_a, owed_b, span)
 
 
 def pair_kernel(where, f0, f1, f2, f3, other, out):
@@ -480,16 +491,16 @@
     b = lax.axis_index("band").astype(jnp.int32)
     q = lax.axis_index("grid").astype(jnp.int32)
     where = jnp.stack([q, b // 8, b // 2 % 4, b % 2])
-    two = within(orbitals, 2)
-    prepare = small_call(prepare_kernel, [(2, QCELL)] * 2 + [(4, CHUNK)] * 4)
-    sel_a, sel_b, *pc = prepare(where, orbitals)
+    rows = small_call(rows_kernel, [(2, QCELL)] * 2)
+    sel_a, sel_b = rows(where, orbitals)
     low_a = around(sel_a, 1, 0)
     low_b = around(sel_b, 1, 2)
+    two = within(orbitals, 2)
     one = within(orbitals, 1)
+    pc = small_call(chunks_kernel, [(4, CHUNK)] * 4)(where, orbitals)
     pieces = [pc[0]] + [along_y(pc[k], k) for k in (1, 2, 3)]
     tables = plane_tables()
     together = jnp.concatenate(pieces, axis=0)
-    two, together = lax.optimization_barrier((two, together))
     (stacked,) = small_call(stack_kernel, [(8, QCELL)])(where, two, low_a, low_b)
     core = within(stacked, 1)
     other = move(together, lambda z, y, h, q: (z, y, 1 - h, q))
@@ -506,8 +517,9 @@
     owed_b = around(owe_b, -1, 2)
     p2a = along_z(p1[:16], 1)
     p2b = along_z(p3[16:], 3)
-    finalize = small_call(finalize_kernel, [(4, QCELL)] + [(4, CHUNK)] * 4)
-    vectors, *vc = finalize(where, near, far, owed_a, owed_b)
+    finalize = small_call(finalize_kernel, [(4, CHUNK)] * 4)
+    vc = finalize(where, near, far, owed_a, owed_b)
+    (vectors,) = small_call(vectors_kernel, [(4, QCELL)])(where, near, far, owed_a, owed_b)
     given = [vc[0]] + [along_y(vc[k], k) for k in (1, 2, 3)]
     margin_part = small_call(margin_kernel, [(16, 128)], [pltpu.VMEM((16, 8, 16), F32)], 20)
     (sums,) = margin_part(where, p0, p1, p3, p2a, p2b, *given)

time: 118 us -> 117 us (level)
  blocking collectives: 9.65 us -> 0 us
  starting transfers between devices: 21.8 us -> 29.8 us
  Pallas kernels: 27.1 us -> 29.3 us
  waiting for transfers between devices: 56.7 us -> 55.2 us
    all_to_all x1 -> x0, blocking collectives: 9.65 us -> none  [step(): lax.all_to_all(sums, BOTH, 0, 0, tiled=True, axis_index_groups=groups)]
    ppermute x20, waiting for transfers between devices: 56.7 us -> 51.1 us  [move(): return lax.ppermute(value, BOTH, pairs)]
    all_to_all x0 -> x1, starting transfers between devices: none -> 4.69 us  [step(): lax.all_to_all(sums, BOTH, 0, 0, tiled=True, axis_index_groups=groups)]
    all_to_all x0 -> x1, waiting for transfers between devices: none -> 4.03 us  [step(): lax.all_to_all(sums, BOTH, 0, 0, tiled=True, axis_index_groups=groups)]
    ppermute x20, starting transfers between devices: 21.8 us -> 25.1 us  [move(): return lax.ppermute(value, BOTH, pairs)]
    pallas_call x6 -> x8, Pallas kernels: 7.23 us -> 9.45 us  [call(): pl.pallas_call(body, out_shape=[jax.ShapeDtypeStruct(shape, F32) for shap...]
  transfers between devices with their start and end apart: 20 -> 21, of which waited for: 10 -> 9; matrix products, arithmetic and copies ran while one was open for 0% -> 0% of each run, Pallas kernels for 19% -> 23%
where the time goes in v7:
time: 117 us; the launch traced here: 116 us
  waiting for transfers between devices  55.2 us (47%)
  starting transfers between devices  29.8 us (25%)
  Pallas kernels  29.3 us (25%)
    ppermute x20, waiting for transfers between devices, move(): return lax.ppermute(value, BOTH, pairs)  51.1 us
    ppermute x20, starting transfers between devices, move(): return lax.ppermute(value, BOTH, pairs)  25.1 us
    pallas_call x1, Pallas kernels, spectrum(): pl.pallas_call(spectrum_kernel, out_shape=[jax.ShapeDtypeStruct((NG, 8, P...  10.2 us
    pallas_call x8, Pallas kernels, call(): pl.pallas_call(body, out_shape=[jax.ShapeDtypeStruct(shape, F32) for shap...  9.45 us
    pallas_call x1, Pallas kernels, terms(): pl.pallas_call(terms_kernel, out_shape=[jax.ShapeDtypeStruct(shape, F32)...  7.72 us
    all_to_all x1, starting transfers between devices, step(): lax.all_to_all(sums, BOTH, 0, 0, tiled=True, axis_index_groups=groups)  4.69 us
    all_to_all x1, waiting for transfers between devices, step(): lax.all_to_all(sums, BOTH, 0, 0, tiled=True, axis_index_groups=groups)  4.03 us
  transfers between devices with their start and end apart: 21, of which 9 were waited for; matrix products, arithmetic and copies ran while one was open for 0% of the time, Pallas kernels for 23%

profile of v7, /device:TPU:1, one launch (start us, length us, event | category | flops | bytes accessed | tf_op | source)
XLA Modules:
  0.0 116.1 jit_solution(16554243037334295623)
XLA Ops:
  0.7 2.1 %collective-permute-start = (f32[4,27648]{1,0:T(4,128)}, f32[4,27648]{1,0:T(4,128)S(1)}, u32[]{:S(2)}, u32[]{:S(2)}) collective-permute-start(f32[4,27648]{1,0:T(4,128)} %orbitals.3), channel_id=1, source_target_pairs={{0,2},{1,3},{2,0},{3,1},{4,6},{5,7},{6,4},{7,5},{8,10},{9,11},{10,... | collective-permute-start | bytes 1327112 | tf_op jit(solution)/shard_map/ppermute | solution.py:467
  2.9 1.1 shard_map.77
  4.0 2.5 %collective-permute-start.2 = (f32[2,27648]{1,0:T(2,128)S(1)}, f32[2,27648]{1,0:T(2,128)S(1)}, u32[]{:S(2)}, u32[]{:S(2)}) collective-permute-start(f32[2,27648]{1,0:T(2,128)S(1)} %get-tuple-element.28), channel_id=1, source_target_pairs={{0,4},{1,5},{2,6},{3,7},{4,8},{5,9},{6,10},{7,11},{8,12},{9,13},{1... | collective-permute-start | bytes 663560 | tf_op jit(solution)/shard_map/ppermute | solution.py:467
  6.5 1.2 %collective-permute-start.3 = (f32[2,27648]{1,0:T(2,128)S(1)}, f32[2,27648]{1,0:T(2,128)S(1)}, u32[]{:S(2)}, u32[]{:S(2)}) collective-permute-start(f32[2,27648]{1,0:T(2,128)S(1)} %get-tuple-element.29), channel_id=1, source_target_pairs={{0,6},{1,7},{2,4},{3,5},{4,10},{5,11},{6,8},{7,9},{8,14},{9,15},{1... | collective-permute-start | bytes 663560 | tf_op jit(solution)/shard_map/ppermute | solution.py:467
  8.8 2.7 %collective-permute-start.10 = (f32[4,6912]{1,0:T(4,128)S(1)}, f32[4,6912]{1,0:T(4,128)S(1)}, u32[]{:S(2)}, u32[]{:S(2)}) collective-permute-start(f32[4,6912]{1,0:T(4,128)S(1)} %get-tuple-element.48), channel_id=1, source_target_pairs={{0,16},{1,17},{2,18},{3,19},{4,20},{5,21},{6,22},{7,23},{8,24},{9,... | collective-permute-start | bytes 331784 | tf_op jit(solution)/shard_map/ppermute | solution.py:467
  12.6 13.1 %collective-permute-done.2.low_a = f32[2,27648]{1,0:T(2,128)S(1)} collective-permute-done((f32[2,27648]{1,0:T(2,128)S(1)}, f32[2,27648]{1,0:T(2,128)S(1)}, u32[]{:S(2)}, u32[]{:S(2)}) %collective-permute-start.2) | collective-permute-done | bytes 221216 | tf_op jit(solution)/shard_map/ppermute | solution.py:467
  25.7 1.6 %collective-permute-start.1 = (f32[4,27648]{1,0:T(4,128)}, f32[4,27648]{1,0:T(4,128)S(1)}, u32[]{:S(2)}, u32[]{:S(2)}) collective-permute-start(f32[4,27648]{1,0:T(4,128)} %orbitals.3), channel_id=1, source_target_pairs={{0,1},{1,0},{2,3},{3,2},{4,5},{5,4},{6,7},{7,6},{8,9},{9,8},{10,11... | collective-permute-start | bytes 1327112 | tf_op jit(solution)/shard_map/ppermute | solution.py:467
  28.2 1.1 collective-permute-done.9.f1
  29.5 1.9 %plane_tables.1 = (bf16[2,768,768]{2,1,0:T(8,128)(2,1)S(1)}, bf16[2,768,768]{2,1,0:T(8,128)(2,1)S(1)}, bf16[2,768,768]{2,1,0:T(8,128)(2,1)S(1)}, bf16[2,768,768]{2,1,0:T(8,128)(2,1)S(1)}) custom-call(f32[4,16,768]{2,1,0:T(8,128)S(1)} %copy-done.2, f32[2,48,768]{2,1,0:T(8,128)S(1)} %copy-done.1), custom_call_target="tpu_custom_call" | custom-call | tf_op jit(solution)/shard_map/plane_tables/pallas_call | solution.py:118
  31.5 10.2 %spectrum.1 = (f32[48,8,2304]{2,1,0:T(8,128)S(1)}, f32[48,8,2304]{2,1,0:T(8,128)S(1)}, f32[384,2304]{1,0:T(8,128)S(1)}) custom-call(s32[1]{0:T(128)} %bitcast.q_ref, f32[4,27648]{1,0:T(4,128)} %orbitals.3, f32[4,27648]{1,0:T(4,128)S(1)} %collective-permute-done.two, f32[4,27648]{1,0:T(4,128)S(1)} %collective-permute-done.1.one, ...), custom_call_target="tpu_custom_call" | custom-call | tf_op jit(solution)/shard_map/spectrum/pallas_call | solution.py:325
  41.7 7.7 %terms.1 = (f32[4,27648]{1,0:T(4,128)S(1)}, f32[4,27648]{1,0:T(4,128)S(1)}, f32[10,27648]{1,0:T(8,128)S(1)}, f32[1,27648]{1,0:T(1,128)S(1)}, f32[1,27648]{1,0:T(1,128)S(1)}) custom-call(s32[1]{0:T(128)} %bitcast.q_ref, f32[48,8,2304]{2,1,0:T(8,128)S(1)} %get-tuple-element.32.right, f32[48,8,2304]{2,1,0:T(8,128)S(1)} %get-tuple-element.33.left, ...), custom_call_target="tpu_custom_call" | custom-call | tf_op jit(solution)/shard_map/terms/pallas_call | solution.py:337
  49.4 2.9 %collective-permute-start.5 = (f32[10,27648]{1,0:T(8,128)S(1)}, f32[10,27648]{1,0:T(8,128)S(1)}, u32[]{:S(2)}, u32[]{:S(2)}) collective-permute-start(f32[10,27648]{1,0:T(8,128)S(1)} %get-tuple-element.41), channel_id=1, source_target_pairs={{0,1},{1,0},{2,3},{3,2},{4,5},{5,4},{6,7},{7,6},{8,9},{9,8},{10,11... | collective-permute-start | bytes 3317768 | tf_op jit(solution)/shard_map/ppermute | solution.py:467
  53.1 2.7 %collective-permute-start.14 = (f32[32,6912]{1,0:T(8,128)S(1)}, f32[32,6912]{1,0:T(8,128)S(1)}, u32[]{:S(2)}, u32[]{:S(2)}) collective-permute-start(f32[32,6912]{1,0:T(8,128)S(1)} %shard_map.82.p0), channel_id=1, source_target_pairs={{0,96},{1,97},{2,98},{3,99},{4,100},{5,101},{6,102},{7,103},{8,104... | collective-permute-start | bytes 2654216 | tf_op jit(solution)/shard_map/ppermute | solution.py:467
  56.8 18.7 %collective-permute-done.13.p1 = f32[32,6912]{1,0:T(8,128)S(1)} collective-permute-done((f32[32,6912]{1,0:T(8,128)S(1)}, f32[32,6912]{1,0:T(8,128)S(1)}, u32[]{:S(2)}, u32[]{:S(2)}) %collective-permute-start.13) | collective-permute-done | bytes 884768 | tf_op jit(solution)/shard_map/ppermute | solution.py:467
  75.8 2.7 %collective-permute-start.16 = (f32[16,6912]{1,0:T(8,128)S(1)}, f32[16,6912]{1,0:T(8,128)S(1)}, u32[]{:S(2)}, u32[]{:S(2)}) collective-permute-start(f32[16,6912]{1,0:T(8,128)S(1)} %slice.9), channel_id=1, source_target_pairs={{0,96},{1,97},{2,98},{3,99},{4,100},{5,101},{6,102},{7,103},{8,104... | collective-permute-start | bytes 1327112 | tf_op jit(solution)/shard_map/ppermute | solution.py:467
  79.6 6.6 %collective-permute-done.7.owed_a = f32[2,27648]{1,0:T(2,128)S(1)} collective-permute-done((f32[2,27648]{1,0:T(2,128)S(1)}, f32[2,27648]{1,0:T(2,128)S(1)}, u32[]{:S(2)}, u32[]{:S(2)}) %collective-permute-start.7) | collective-permute-done | bytes 221216 | tf_op jit(solution)/shard_map/ppermute | solution.py:467
  86.1 6.3 %collective-permute-done.8.owed_b = f32[2,27648]{1,0:T(2,128)S(1)} collective-permute-done((f32[2,27648]{1,0:T(2,128)S(1)}, f32[2,27648]{1,0:T(2,128)S(1)}, u32[]{:S(2)}, u32[]{:S(2)}) %collective-permute-start.8) | collective-permute-done | bytes 221216 | tf_op jit(solution)/shard_map/ppermute | solution.py:467
  93.7 3.4 %collective-permute-start.19 = (f32[4,6912]{1,0:T(4,128)S(1)}, f32[4,6912]{1,0:T(4,128)S(1)}, u32[]{:S(2)}, u32[]{:S(2)}) collective-permute-start(f32[4,6912]{1,0:T(4,128)S(1)} %get-tuple-element.53), channel_id=1, source_target_pairs={{0,24},{1,25},{2,26},{3,27},{4,28},{5,29},{6,30},{7,31},{8,16},{9,... | collective-permute-start | bytes 331784 | tf_op jit(solution)/shard_map/ppermute | solution.py:467
  97.3 1.3 %collective-permute-done.18.v2 = f32[4,6912]{1,0:T(4,128)S(1)} collective-permute-done((f32[4,6912]{1,0:T(4,128)S(1)}, f32[4,6912]{1,0:T(4,128)S(1)}, u32[]{:S(2)}, u32[]{:S(2)}) %collective-permute-start.18) | collective-permute-done | bytes 110624 | tf_op jit(solution)/shard_map/ppermute | solution.py:467
  98.7 3.7 %collective-permute-done.19.v3 = f32[4,6912]{1,0:T(4,128)S(1)} collective-permute-done((f32[4,6912]{1,0:T(4,128)S(1)}, f32[4,6912]{1,0:T(4,128)S(1)}, u32[]{:S(2)}, u32[]{:S(2)}) %collective-permute-start.19) | collective-permute-done | bytes 110624 | tf_op jit(solution)/shard_map/ppermute | solution.py:467
  102.4 2.9 %shard_map.84 = f32[16,128]{1,0:T(8,128)} custom-call(s32[4]{0:T(128)S(1)} %pad_add_fusion.where, f32[32,6912]{1,0:T(8,128)S(1)} %shard_map.82.p0, f32[32,6912]{1,0:T(8,128)S(1)} %collective-permute-done.13.p1, f32[32,6912]{1,0:T(8,128)S(1)} %collective-permute-done.14.p3, f32[16,6912]{1,0:T(8,128)S(1)} %collective-permute-done.15.p2a, ...), custom_call_target="tpu_custom_call" | custom-call | tf_op jit(solution)/shard_map/pallas_call | solution.py:356
  105.2 4.7 %all-to-all-start = ((f32[16,1,128]{2,1,0:T(1,128)}), f32[16,1,128]{2,1,0:T(1,128)S(1)}, u32[]{:S(2)}, u32[]{:S(2)}) async-start(f32[16,1,128]{2,1,0:T(1,128)} %bitcast.5), calls=%async_computation | async-start | bytes 16384 | tf_op jit(solution)/shard_map/all_to_all | solution.py:527
  109.9 1.5 %shard_map.80 = f32[4,27648]{1,0:T(4,128)} custom-call(s32[4]{0:T(128)S(1)} %pad_add_fusion.where, f32[4,27648]{1,0:T(4,128)S(1)} %get-tuple-element.42.near, f32[4,27648]{1,0:T(4,128)S(1)} %collective-permute-done.6.far, f32[2,27648]{1,0:T(2,128)S(1)} %collective-permute-done.7.owed_a, f32[2,27648]{1,0:T(2,128)S(1)} %collective-permute-done.8.owed_b), custom_call_target="tpu_custom_call" | custom-call | tf_op jit(solution)/shard_map/pallas_call | solution.py:356
  111.4 4.0 %all-to-all-done = f32[16,1,128]{2,1,0:T(1,128)S(1)} async-done(((f32[16,1,128]{2,1,0:T(1,128)}), f32[16,1,128]{2,1,0:T(1,128)S(1)}, u32[]{:S(2)}, u32[]{:S(2)}) %all-to-all-start) | async-done | bytes 8224 | tf_op jit(solution)/shard_map/all_to_all | solution.py:527
  (43 shorter events, 8.6 us)
Async XLA Ops:
  0.6 28.9 %copy-start.2 = (f32[4,16,768]{2,1,0:T(8,128)S(1)}, f32[4,16,768]{2,1,0:T(8,128)}, u32[]{:S(2)}) copy-start(f32[4,16,768]{2,1,0:T(8,128)} %constant.63.clone.tens) | copy-start | bytes 589828
  0.7 30.8 %copy-start = (f32[48,2304]{1,0:T(8,128)S(1)}, f32[48,2304]{1,0:T(8,128)}, u32[]{:S(2)}) copy-start(f32[48,2304]{1,0:T(8,128)} %constant.65.clone.kern) | copy-start | bytes 1327108
  0.7 30.8 %copy-start.3 = (f32[8,768]{1,0:T(8,128)S(1)}, f32[8,768]{1,0:T(8,128)}, u32[]{:S(2)}) copy-start(f32[8,768]{1,0:T(8,128)} %constant.66.clone.third) | copy-start | bytes 73732
  0.7 26.7 %collective-permute-start = (f32[4,27648]{1,0:T(4,128)}, f32[4,27648]{1,0:T(4,128)S(1)}, u32[]{:S(2)}, u32[]{:S(2)}) collective-permute-start(f32[4,27648]{1,0:T(4,128)} %orbitals.3), channel_id=1, source_target_pairs={{0,2},{1,3},{2,0},{3,1},{4,6},{5,7},{6,4},{7,5},{8,10},{9,11},{10,... | collective-permute-start | bytes 1327112 | tf_op jit(solution)/shard_map/ppermute | solution.py:467
  4.0 21.7 %collective-permute-start.2 = (f32[2,27648]{1,0:T(2,128)S(1)}, f32[2,27648]{1,0:T(2,128)S(1)}, u32[]{:S(2)}, u32[]{:S(2)}) collective-permute-start(f32[2,27648]{1,0:T(2,128)S(1)} %get-tuple-element.28), channel_id=1, source_target_pairs={{0,4},{1,5},{2,6},{3,7},{4,8},{5,9},{6,10},{7,11},{8,12},{9,13},{1... | collective-permute-start | bytes 663560 | tf_op jit(solution)/shard_map/ppermute | solution.py:467
  6.5 19.2 %collective-permute-start.3 = (f32[2,27648]{1,0:T(2,128)S(1)}, f32[2,27648]{1,0:T(2,128)S(1)}, u32[]{:S(2)}, u32[]{:S(2)}) collective-permute-start(f32[2,27648]{1,0:T(2,128)S(1)} %get-tuple-element.29), channel_id=1, source_target_pairs={{0,6},{1,7},{2,4},{3,5},{4,10},{5,11},{6,8},{7,9},{8,14},{9,15},{1... | collective-permute-start | bytes 663560 | tf_op jit(solution)/shard_map/ppermute | solution.py:467
  8.8 19.4 %collective-permute-start.10 = (f32[4,6912]{1,0:T(4,128)S(1)}, f32[4,6912]{1,0:T(4,128)S(1)}, u32[]{:S(2)}, u32[]{:S(2)}) collective-permute-start(f32[4,6912]{1,0:T(4,128)S(1)} %get-tuple-element.48), channel_id=1, source_target_pairs={{0,16},{1,17},{2,18},{3,19},{4,20},{5,21},{6,22},{7,23},{8,24},{9,... | collective-permute-start | bytes 331784 | tf_op jit(solution)/shard_map/ppermute | solution.py:467
  11.5 16.7 %collective-permute-start.11 = (f32[4,6912]{1,0:T(4,128)S(1)}, f32[4,6912]{1,0:T(4,128)S(1)}, u32[]{:S(2)}, u32[]{:S(2)}) collective-permute-start(f32[4,6912]{1,0:T(4,128)S(1)} %get-tuple-element.49), channel_id=1, source_target_pairs={{0,24},{1,25},{2,26},{3,27},{4,28},{5,29},{6,30},{7,31},{8,16},{9,... | collective-permute-start | bytes 331784 | tf_op jit(solution)/shard_map/ppermute | solution.py:467
  25.7 3.6 %collective-permute-start.9 = (f32[4,6912]{1,0:T(4,128)S(1)}, f32[4,6912]{1,0:T(4,128)S(1)}, u32[]{:S(2)}, u32[]{:S(2)}) collective-permute-start(f32[4,6912]{1,0:T(4,128)S(1)} %get-tuple-element.47), channel_id=1, source_target_pairs={{0,8},{1,9},{2,10},{3,11},{4,12},{5,13},{6,14},{7,15},{8,0},{9,1},... | collective-permute-start | bytes 331784 | tf_op jit(solution)/shard_map/ppermute | solution.py:467
  25.7 5.8 %collective-permute-start.1 = (f32[4,27648]{1,0:T(4,128)}, f32[4,27648]{1,0:T(4,128)S(1)}, u32[]{:S(2)}, u32[]{:S(2)}) collective-permute-start(f32[4,27648]{1,0:T(4,128)} %orbitals.3), channel_id=1, source_target_pairs={{0,1},{1,0},{2,3},{3,2},{4,5},{5,4},{6,7},{7,6},{8,9},{9,8},{10,11... | collective-permute-start | bytes 1327112 | tf_op jit(solution)/shard_map/ppermute | solution.py:467
  28.1 3.4 %collective-permute-start.4 = (f32[8,27648]{1,0:T(8,128)S(1)}, f32[8,27648]{1,0:T(8,128)S(1)}, u32[]{:S(2)}, u32[]{:S(2)}) collective-permute-start(f32[8,27648]{1,0:T(8,128)S(1)} %shard_map.78), channel_id=1, source_target_pairs={{0,1},{1,0},{2,3},{3,2},{4,5},{5,4},{6,7},{7,6},{8,9},{9,8},{10,11... | collective-permute-start | bytes 2654216 | tf_op jit(solution)/shard_map/ppermute | solution.py:467
  29.4 22.9 %collective-permute-start.12 = (f32[16,6912]{1,0:T(8,128)S(1)}, f32[16,6912]{1,0:T(8,128)S(1)}, u32[]{:S(2)}, u32[]{:S(2)}) collective-permute-start(f32[16,6912]{1,0:T(8,128)S(1)} %pad_maximum_fusion), channel_id=1, source_target_pairs={{0,4},{1,5},{2,6},{3,7},{4,0},{5,1},{6,2},{7,3},{8,12},{9,13},{10,... | collective-permute-start | bytes 1327112 | tf_op jit(solution)/shard_map/ppermute | solution.py:467
  49.4 6.3 %collective-permute-start.5 = (f32[10,27648]{1,0:T(8,128)S(1)}, f32[10,27648]{1,0:T(8,128)S(1)}, u32[]{:S(2)}, u32[]{:S(2)}) collective-permute-start(f32[10,27648]{1,0:T(8,128)S(1)} %get-tuple-element.41), channel_id=1, source_target_pairs={{0,1},{1,0},{2,3},{3,2},{4,5},{5,4},{6,7},{7,6},{8,9},{9,8},{10,11... | collective-permute-start | bytes 3317768 | tf_op jit(solution)/shard_map/ppermute | solution.py:467
  53.0 22.5 %collective-permute-start.13 = (f32[32,6912]{1,0:T(8,128)S(1)}, f32[32,6912]{1,0:T(8,128)S(1)}, u32[]{:S(2)}, u32[]{:S(2)}) collective-permute-start(f32[32,6912]{1,0:T(8,128)S(1)} %shard_map.82.p0), channel_id=1, source_target_pairs={{0,32},{1,33},{2,34},{3,35},{4,36},{5,37},{6,38},{7,39},{8,40},{9,... | collective-permute-start | bytes 2654216 | tf_op jit(solution)/shard_map/ppermute | solution.py:467
  53.1 22.7 %collective-permute-start.14 = (f32[32,6912]{1,0:T(8,128)S(1)}, f32[32,6912]{1,0:T(8,128)S(1)}, u32[]{:S(2)}, u32[]{:S(2)}) collective-permute-start(f32[32,6912]{1,0:T(8,128)S(1)} %shard_map.82.p0), channel_id=1, source_target_pairs={{0,96},{1,97},{2,98},{3,99},{4,100},{5,101},{6,102},{7,103},{8,104... | collective-permute-start | bytes 2654216 | tf_op jit(solution)/shard_map/ppermute | solution.py:467
  56.5 35.9 %collective-permute-start.6 = (f32[4,27648]{1,0:T(4,128)S(1)}, f32[4,27648]{1,0:T(4,128)S(1)}, u32[]{:S(2)}, u32[]{:S(2)}) collective-permute-start(f32[4,27648]{1,0:T(4,128)S(1)} %get-tuple-element.43), channel_id=1, source_target_pairs={{0,2},{1,3},{2,0},{3,1},{4,6},{5,7},{6,4},{7,5},{8,10},{9,11},{10,... | collective-permute-start | bytes 1327112 | tf_op jit(solution)/shard_map/ppermute | solution.py:467
  75.5 21.5 %collective-permute-start.15 = (f32[16,6912]{1,0:T(8,128)S(1)}, f32[16,6912]{1,0:T(8,128)S(1)}, u32[]{:S(2)}, u32[]{:S(2)}) collective-permute-start(f32[16,6912]{1,0:T(8,128)S(1)} %slice.8), channel_id=1, source_target_pairs={{0,32},{1,33},{2,34},{3,35},{4,36},{5,37},{6,38},{7,39},{8,40},{9,... | collective-permute-start | bytes 1327112 | tf_op jit(solution)/shard_map/ppermute | solution.py:467
  75.8 21.2 %collective-permute-start.16 = (f32[16,6912]{1,0:T(8,128)S(1)}, f32[16,6912]{1,0:T(8,128)S(1)}, u32[]{:S(2)}, u32[]{:S(2)}) collective-permute-start(f32[16,6912]{1,0:T(8,128)S(1)} %slice.9), channel_id=1, source_target_pairs={{0,96},{1,97},{2,98},{3,99},{4,100},{5,101},{6,102},{7,103},{8,104... | collective-permute-start | bytes 1327112 | tf_op jit(solution)/shard_map/ppermute | solution.py:467
  78.6 7.6 %collective-permute-start.7 = (f32[2,27648]{1,0:T(2,128)S(1)}, f32[2,27648]{1,0:T(2,128)S(1)}, u32[]{:S(2)}, u32[]{:S(2)}) collective-permute-start(f32[2,27648]{1,0:T(2,128)S(1)} %get-tuple-element.44), channel_id=1, source_target_pairs={{0,124},{1,125},{2,126},{3,127},{4,0},{5,1},{6,2},{7,3},{8,4},{9,5... | collective-permute-start | bytes 663560 | tf_op jit(solution)/shard_map/ppermute | solution.py:467
  79.6 12.8 %collective-permute-start.8 = (f32[2,27648]{1,0:T(2,128)S(1)}, f32[2,27648]{1,0:T(2,128)S(1)}, u32[]{:S(2)}, u32[]{:S(2)}) collective-permute-start(f32[2,27648]{1,0:T(2,128)S(1)} %get-tuple-element.45), channel_id=1, source_target_pairs={{0,126},{1,127},{2,124},{3,125},{4,2},{5,3},{6,0},{7,1},{8,6},{9,7... | collective-permute-start | bytes 663560 | tf_op jit(solution)/shard_map/ppermute | solution.py:467
  93.1 4.2 %collective-permute-start.17 = (f32[4,6912]{1,0:T(4,128)S(1)}, f32[4,6912]{1,0:T(4,128)S(1)}, u32[]{:S(2)}, u32[]{:S(2)}) collective-permute-start(f32[4,6912]{1,0:T(4,128)S(1)} %get-tuple-element.51), channel_id=1, source_target_pairs={{0,8},{1,9},{2,10},{3,11},{4,12},{5,13},{6,14},{7,15},{8,0},{9,1},... | collective-permute-start | bytes 331784 | tf_op jit(solution)/shard_map/ppermute | solution.py:467
  93.5 5.2 %collective-permute-start.18 = (f32[4,6912]{1,0:T(4,128)S(1)}, f32[4,6912]{1,0:T(4,128)S(1)}, u32[]{:S(2)}, u32[]{:S(2)}) collective-permute-start(f32[4,6912]{1,0:T(4,128)S(1)} %get-tuple-element.52), channel_id=1, source_target_pairs={{0,16},{1,17},{2,18},{3,19},{4,20},{5,21},{6,22},{7,23},{8,24},{9,... | collective-permute-start | bytes 331784 | tf_op jit(solution)/shard_map/ppermute | solution.py:467
  93.7 8.7 %collective-permute-start.19 = (f32[4,6912]{1,0:T(4,128)S(1)}, f32[4,6912]{1,0:T(4,128)S(1)}, u32[]{:S(2)}, u32[]{:S(2)}) collective-permute-start(f32[4,6912]{1,0:T(4,128)S(1)} %get-tuple-element.53), channel_id=1, source_target_pairs={{0,24},{1,25},{2,26},{3,27},{4,28},{5,29},{6,30},{7,31},{8,16},{9,... | collective-permute-start | bytes 331784 | tf_op jit(solution)/shard_map/ppermute | solution.py:467
  105.2 10.2 %all-to-all-start = ((f32[16,1,128]{2,1,0:T(1,128)}), f32[16,1,128]{2,1,0:T(1,128)S(1)}, u32[]{:S(2)}, u32[]{:S(2)}) async-start(f32[16,1,128]{2,1,0:T(1,128)} %bitcast.5), calls=%async_computation | async-start | bytes 16384 | tf_op jit(solution)/shard_map/all_to_all | solution.py:527
  (1 other events, 28.9 us)

commit v8 on v7

--- a/solution.py
+++ b/solution.py
@@ -32,17 +32,6 @@
         col = np.cos(2 * np.pi * b * u / 16) if kind == "C" else np.sin(2 * np.pi * b * u / 16)
         cols.append(col / np.linalg.norm(col))
     return np.stack(cols, 1)
-
-
-def forty_eight():
-    z = np.arange(NG)
-    cols, freqs = [], []
-    for g in range(25):
-        for kind in ("C", "S") if 0 < g < 24 else ("C",):
-            col = np.cos(2 * np.pi * g * z / NG) if kind == "C" else np.sin(2 * np.pi * g * z / NG)
-            cols.append(col / np.linalg.norm(col))
-            freqs.append(g)
-    return np.stack(cols, 1), np.array(freqs)
 
 
 def folded(g):
@@ -65,59 +54,63 @@
     return keys, np.array(freqs), np.array(norms)
 
 
+def lane_freqs(group):
+    out = []
+    for kind, b in ORDER:
+        if group == "A":
+            out.append(3 * b)
+        elif b in (0, 8):
+            out.append(16 + 3 * b)
+        else:
+            out.append(16 + 3 * b if (group == "u") == (kind == "C") else 16 - 3 * b)
+    return np.array(out)
+
+
 def kernel_values():
     _, gx, nx = x_basis()
-    _, gz = forty_eight()
-    gy = []
-    for slab in "Auv":
-        for kind, b in ORDER:
-            if slab == "A":
-                gy.append(3 * b)
-            elif b in (0, 8):
-                gy.append(16 + 3 * b)
-            else:
-                plus = (slab == "u") == (kind == "C")
-                gy.append(16 + 3 * b if plus else 16 - 3 * b)
-    gy = np.array(gy)
-    q = (folded(gx)[:, None, None] ** 2 + folded(gy)[None, :, None] ** 2 + folded(gz)[None, None, :] ** 2).astype(np.float64)
+    g = np.stack([lane_freqs(group) for group in "Auv"])
+    gy, gz = g[:, None, :, None], g[None, :, None, :]
+    q = folded(gx)[:, None, None, None, None] ** 2 + (folded(gy) ** 2 + folded(gz) ** 2)[None]
+    q = q.astype(np.float64)
     kern = np.where(q > 0, 40.0 * (1.0 - np.exp(-q / 16.0)) / np.where(q > 0, q, 1.0), 0.0)
-    return (kern / (3.0 * nx[:, None, None])).reshape(NG, PLANE).astype(np.float32)
+    return (kern / (9.0 * nx[:, None, None, None, None])).reshape(NG, PLANE).astype(np.float32)
+
+
+PLACES = np.array([0, 3, 6, 1, 4, 7, 2, 5])
+LANE_Y = np.repeat(np.concatenate([PLACES, 8 + PLACES]), 16)
+LANE_Z = np.tile(np.arange(16), 16)
 
 
 def thirds():
-    u = np.arange(SLAB) // NG
-    rows = [np.cos(2 * np.pi * (m + u) / 3) for m in range(3)] + [np.sin(2 * np.pi * (m + u) / 3) for m in range(3)]
-    return np.concatenate([np.stack(rows), np.zeros((2, SLAB))]).astype(np.float32)
+    rows = []
+    for lane in (LANE_Y, LANE_Z):
+        rows += [np.cos(2 * np.pi * (m + lane) / 3) for m in range(3)]
+        rows += [np.sin(2 * np.pi * (m + lane) / 3) for m in range(3)]
+    return np.concatenate([np.stack(rows), np.zeros((4, 256))]).astype(np.float32)
 
 
 def factor_tables():
-    za, _ = forty_eight()
-    ta, ts = sixteen(ORDER), sixteen(SWAPPED)
-    tens = np.stack([np.repeat(t, NG, 1) for t in (ta, ts, ta.T, ts.T)])
-    zs = np.stack([np.tile(z, (1, 16)) for z in (za, za.T)])
-    return [a.astype(np.float32) for a in (tens, zs)]
-
-
-def tables_kernel(tens, zs, hi_there, lo_there, hi_back, lo_back):
+    bases = sixteen(ORDER), sixteen(SWAPPED)
+    slow = [np.repeat(t[LANE_Y[::16]], 16, 1) for t in bases] + [t.T[:, LANE_Y] for t in bases]
+    fast = [np.tile(t, (1, 16)) for t in bases] + [np.tile(t.T, (1, 16)) for t in bases]
+    return np.stack(slow).astype(np.float32), np.stack(fast).astype(np.float32)
+
+
+def tables_kernel(slow, fast, hi_there, lo_there, hi_back, lo_back):
     for way, (hi, lo) in enumerate(((hi_there, lo_there), (hi_back, lo_back))):
-        for which in range(2):
-
-            def block(u, carry):
-                w = zs[way] * tens[2 * way + which, pl.ds(u, 1), :]
+        for k in range(4):
+            for u in range(16):
+                w = fast[2 * way + k % 2] * slow[2 * way + k // 2, u : u + 1, :]
                 top = w.astype(BF16)
-                rows = pl.ds(pl.multiple_of(u * NG, 16), NG)
-                hi[which, rows, :] = top
-                lo[which, rows, :] = (w - top.astype(F32)).astype(BF16)
-                return carry
-
-            lax.fori_loop(0, 16, block, 0)
+                hi[k, 16 * u : 16 * u + 16, :] = top
+                lo[k, 16 * u : 16 * u + 16, :] = (w - top.astype(F32)).astype(BF16)
 
 
 def plane_tables():
-    out = [jax.ShapeDtypeStruct((2, SLAB, SLAB), BF16)] * 4
+    out = [jax.ShapeDtypeStruct((4, 256, 256), BF16)] * 4
     return pl.pallas_call(
         tables_kernel, out_shape=out, name="plane_tables",
-        compiler_params=pltpu.CompilerParams(vmem_limit_bytes=16 << 20),
+        compiler_params=pltpu.CompilerParams(vmem_limit_bytes=8 << 20),
     )(*[jnp.asarray(a) for a in factor_tables()])
 
 
@@ -197,19 +190,45 @@
     return out
 
 
-def split(hi, lo, rows, m, value):
+def group(k, j):
+    return slice(k * SLAB + j * 256, k * SLAB + j * 256 + 256)
+
+
+def split(hi, lo, rows, span, value):
     top = value.astype(BF16)
-    span = slice(m * SLAB, (m + 1) * SLAB)
     hi[rows, span] = top
     lo[rows, span] = (value - top.astype(F32)).astype(BF16)
 
 
-def product(hi, lo, whi, wlo, m, k, cols):
-    span = slice(m * SLAB, (m + 1) * SLAB)
+def product(hi, lo, whi, wlo, k, j):
+    span = group(k, j)
     a, b = hi[:, span], lo[:, span]
+    w = (k // 2) * 2 + j // 2
     lhs = jnp.concatenate([a, b, a], axis=1)
-    w = jnp.concatenate([whi[k, :, cols], whi[k, :, cols], wlo[k, :, cols]], axis=0)
-    return jnp.dot(lhs, w, preferred_element_type=F32)
+    rhs = jnp.concatenate([whi[w], whi[w], wlo[w]], axis=0)
+    return jnp.dot(lhs, rhs, preferred_element_type=F32)
+
+
+def turn(value, lanes):
+    return pltpu.roll(value, lanes % 128, 1) if lanes % 128 else value
+
+
+def to_thirds(f, third, first):
+    c, s = third[first : first + 3], third[first + 3 : first + 6]
+    return (
+        f[0] + f[1] + f[2],
+        f[0] * c[0] + f[1] * c[1] + f[2] * c[2],
+        f[0] * s[0] + f[1] * s[1] + f[2] * s[2],
+    )
+
+
+def third_rows(third, h, rows):
+    lanes = slice(128 * h, 128 * h + 128)
+    return [jnp.broadcast_to(third[k : k + 1, lanes], (rows, 128)) for k in range(12)]
+
+
+def from_thirds(a, c, s, third, first):
+    return [a + c * third[first + m] + s * third[first + 3 + m] for m in range(3)]
 
 
 def spectrum_kernel(q_ref, own, two, one, low_a, low_b, core, kern, third, whi, wlo, right, left, field, hi, lo):
@@ -220,41 +239,60 @@
         (two, 0, low_b, 0),
         (core, 0, core, 6),
     )
+    sub = lax.broadcasted_iota(jnp.int32, (8, 128), 0)
+    to_right = sub % 4
+    to_left = jnp.where(sub < 4, q, 4 + q % 2)
+    place = lax.broadcasted_iota(jnp.int32, (8, 128), 1) // 16 % 3
     for delta, (bands_ref, first, low_ref, low_first) in enumerate(sources):
         base = (q ^ delta) * QX
 
-        def place(x, carry):
-            span = pl.ds(pl.multiple_of(x * PLANE, 128), PLANE)
-            bands = bands_ref[first : first + 4, span]
-            right[base + x, 0:4, :] = bands
-            right[base + x, 4:8, :] = bands
-            left[base + x, 0:4, :] = jnp.broadcast_to(bands_ref[pl.ds(first + q, 1), span], (4, PLANE))
-            left[base + x, 4:8, :] = jnp.broadcast_to(low_ref[pl.ds(low_first + q % 2, 1), span], (4, PLANE))
+        def densities(i, carry):
+            rows = pl.ds(pl.multiple_of(8 * base + 16 * i, 16), 16)
+            for h in range(2):
+                pairs = []
+                for half in range(2):
+                    x = base + 2 * i + half
+                    f = [[None] * 3 for _ in range(3)]
+                    for m in range(3):
+                        v = []
+                        for n in range(3):
+                            at = pl.ds(pl.multiple_of((2 * i + half) * PLANE + (m * SLAB + h * 384 + n * 128), 128), 128)
+                            low = low_ref[low_first : low_first + 2, at]
+                            v.append(jnp.concatenate([bands_ref[first : first + 4, at], low, low], axis=0))
+                        for j in range(3):
+                            got = jnp.where(place == j, v[0], jnp.where(place == (j + 1) % 3, v[1], v[2]))
+                            got = turn(got, -16 * j)
+                            r = jnp.take_along_axis(got, to_right, axis=0)
+                            l = jnp.take_along_axis(got, to_left, axis=0)
+                            span = slice(m * SLAB + j * 256 + h * 128, m * SLAB + j * 256 + h * 128 + 128)
+                            right[x, :, span] = r
+                            left[x, :, span] = l
+                            f[m][j] = r * l
+                    pairs.append(f)
+                thirds_h = third_rows(third, h, 8)
+                spec = []
+                for f in pairs:
+                    f = [to_thirds([f[m][j] for m in range(3)], thirds_h, 0) for j in range(3)]
+                    spec.append([to_thirds([f[n][k] for n in range(3)], thirds_h, 6) for k in range(3)])
+                for k in range(3):
+                    for j in range(3):
+                        span = slice(k * SLAB + j * 256 + h * 128, k * SLAB + j * 256 + h * 128 + 128)
+                        split(hi, lo, rows, span, jnp.concatenate([spec[0][k][j], spec[1][k][j]], axis=0))
             return carry
 
-        lax.fori_loop(0, QX, place, 0)
-
-    def densities(i, carry):
-        x = pl.ds(2 * i, 2)
-        rows = pl.ds(pl.multiple_of(16 * i, 16), 16)
-        f = []
-        for m in range(3):
-            span = slice(m * SLAB, (m + 1) * SLAB)
-            f.append((right[x, :, span] * left[x, :, span]).reshape(16, SLAB))
-        split(hi, lo, rows, 0, f[0] + f[1] + f[2])
-        split(hi, lo, rows, 1, f[0] * third[0:1, :] + f[1] * third[1:2, :] + f[2] * third[2:3, :])
-        split(hi, lo, rows, 2, f[0] * third[3:4, :] + f[1] * third[4:5, :] + f[2] * third[5:6, :])
-        return carry
-
-    lax.fori_loop(0, NG // 2, densities, 0)
-
-    for j in range(3):
-        cols = slice(j * 256, (j + 1) * 256)
-        field[:, cols] = product(hi, lo, whi, wlo, 0, 0, cols)
-        c = product(hi, lo, whi, wlo, 1, 0, cols)
-        s = product(hi, lo, whi, wlo, 2, 1, cols)
-        field[:, SLAB + j * 256 : SLAB + (j + 1) * 256] = c - s
-        field[:, 2 * SLAB + j * 256 : 2 * SLAB + (j + 1) * 256] = c + s
+        lax.fori_loop(0, QX // 2, densities, 0)
+
+    for k in (0, 1):
+        if k == 0:
+            rows_of = [[product(hi, lo, whi, wlo, 0, j)] for j in range(3)]
+        else:
+            both = [(product(hi, lo, whi, wlo, 1, j), product(hi, lo, whi, wlo, 2, j)) for j in range(3)]
+            rows_of = [[c - s, c + s] for c, s in both]
+        for n in range(len(rows_of[0])):
+            a, c, s = (rows_of[j][n] for j in range(3))
+            field[:, group(k + n, 0)] = a
+            field[:, group(k + n, 1)] = c - s
+            field[:, group(k + n, 2)] = c + s
 
     def along_x(i, carry):
         span = pl.ds(pl.multiple_of(128 * i, 128), 128)
@@ -272,50 +310,66 @@
 
     def unmix(i, carry):
         rows = pl.ds(pl.multiple_of(16 * i, 16), 16)
-        u = field[rows, SLAB : 2 * SLAB]
-        v = field[rows, 2 * SLAB : 3 * SLAB]
-        split(hi, lo, rows, 0, field[rows, 0:SLAB])
-        split(hi, lo, rows, 1, u + v)
-        split(hi, lo, rows, 2, v - u)
+        mixed = [[field[rows, group(k, j)] for j in range(3)] for k in range(3)]
+        mixed = [[a, u + v, v - u] for a, u, v in mixed]
+        for j in range(3):
+            a, u, v = (mixed[k][j] for k in range(3))
+            for k, value in enumerate((a, u + v, v - u)):
+                split(hi, lo, rows, group(k, j), value)
         return carry
 
     lax.fori_loop(0, NG // 2, unmix, 0)
-    for j in range(3):
-        cols = slice(j * 256, (j + 1) * 256)
-        for m, k in ((0, 0), (1, 0), (2, 1)):
-            back[:, m * SLAB + j * 256 : m * SLAB + (j + 1) * 256] = product(hi, lo, whi, wlo, m, k, cols)
-
-    mine = (lax.broadcasted_iota(jnp.int32, (8, SLAB), 0) == q).astype(F32)
+    for k in range(3):
+        for j in range(3):
+            back[:, group(k, j)] = product(hi, lo, whi, wlo, k, j)
+
+    sub = lax.broadcasted_iota(jnp.int32, (8, 128), 0)
+    mine = (sub == q).astype(F32)
+    place = lax.broadcasted_iota(jnp.int32, (8, 128), 1) // 16 % 3
 
     for delta in range(4):
         base = (q ^ delta) * QX
 
         def finish(i, carry):
-            x = base + i
-            rows = pl.ds(pl.multiple_of(x * 8, 8), 8)
-            a = back[rows, 0:SLAB]
-            c = back[rows, SLAB : 2 * SLAB]
-            s = back[rows, 2 * SLAB : 3 * SLAB]
-            for m in range(3):
-                span = slice(m * SLAB, (m + 1) * SLAB)
-                v = a + c * third[m : m + 1, :] + s * third[3 + m : 4 + m, :]
-                pr = v * right[x, :, span]
-                pr = pr + pltpu.roll(pr, 6, 0)
-                pr = pr + pltpu.roll(pr, 7, 0)
-                po = pltpu.roll(v * left[x, :, span], 4, 0) + mine * pr[0:1, :]
-                at = pl.ds(pl.multiple_of(i * PLANE + m * SLAB, SLAB), SLAB)
-                bands, low = -po[0:4, :], -pr[4:5, :]
-                if delta % 2:
-                    cross[delta // 2 * 4 : delta // 2 * 4 + 4, at] = bands
-                    cross[8 + delta // 2 : 9 + delta // 2, at] = low
-                else:
-                    (near0, near2)[delta // 2][:, at] = bands
-                    (low0, low2)[delta // 2][:, at] = low
+            for half in range(X_STEP):
+                x = base + X_STEP * i + half
+                rows = pl.ds(pl.multiple_of(x * 8, 8), 8)
+                for h in range(2):
+                    thirds_h = third_rows(third, h, 8)
+
+                    def spot(k, j):
+                        return slice(k * SLAB + j * 256 + h * 128, k * SLAB + j * 256 + h * 128 + 128)
+
+                    v = [from_thirds(*(back[rows, spot(k, j)] for j in range(3)), thirds_h, 6) for k in range(3)]
+                    v = [from_thirds(*(v[k][j] for k in range(3)), thirds_h, 0) for j in range(3)]
+                    for m in range(3):
+                        parts = []
+                        for j in range(3):
+                            pr = v[j][m] * right[x, :, spot(m, j)]
+                            pr = pr + swapped(pr, sub, 1)
+                            pr = pr + swapped(pr, sub, 2)
+                            po = swapped(v[j][m] * left[x, :, spot(m, j)], sub, 4) + mine * pr
+                            parts.append(turn(jnp.where(sub < 4, po, pr), 16 * j))
+                        for n in range(3):
+                            out = jnp.where(place == n, parts[0], jnp.where(place == (n + 1) % 3, parts[1], parts[2]))
+                            start = (X_STEP * i + half) * PLANE + (m * SLAB + h * 384 + n * 128)
+                            at = pl.ds(pl.multiple_of(start, 128), 128)
+                            if delta % 2:
+                                cross[delta // 2 * 4 : delta // 2 * 4 + 4, at] = out[0:4, :]
+                                cross[8 + delta // 2 : 9 + delta // 2, at] = out[4:5, :]
+                            else:
+                                (near0, near2)[delta // 2][:, at] = out[0:4, :]
+                                (low0, low2)[delta // 2][:, at] = out[4:5, :]
             return carry
 
-        lax.fori_loop(0, QX, finish, 0)
-
-
+        lax.fori_loop(0, QX // X_STEP, finish, 0)
+
+
+def swapped(value, sub, flip):
+    return jnp.take_along_axis(value, sub ^ flip, axis=0)
+
+
+X_STEP = 2
 VMEM_SPEC = pl.BlockSpec(memory_space=pltpu.VMEM)
 SMEM_SPEC = pl.BlockSpec(memory_space=pltpu.SMEM)
 SPLIT = [pltpu.VMEM((NG * 8, PLANE), BF16)] * 2
@@ -401,7 +455,7 @@
     lower = where[0] < 2
     a, b = owed_a[:, span], owed_b[:, span]
     owed = jnp.concatenate([jnp.where(lower, a, b), jnp.where(lower, b, a)], axis=0)
-    return near[:, span] + far[:, span] + owed
+    return -(near[:, span] + far[:, span] + owed)
 
 
 def finalize_kernel(where, near, far, owed_a, owed_b, *chunks):
@@ -423,7 +477,7 @@
         out[8 * k + 4 : 8 * k + 8, :] = jnp.where(first, b, a)
 
 
-def margin_kernel(where, p0, p1, p3, p2a, p2b, v0, v1, v2, v3, pieces, block):
+def margin_kernel(where, p0, p1, p2, p3, v0, v1, v2, v3, pieces, block):
     z, y = where[1], where[2]
 
     def halves(a):
@@ -432,7 +486,7 @@
 
     vt, vl = halves(jnp.concatenate([v0[...], v1[...], v2[...], v3[...]], axis=0))
     dims = (((1,), (1,)), ((), ()))
-    parts = jnp.concatenate([p0[...], p1[...], p2a[...], p2b[...], p3[...]], axis=0)
+    parts = jnp.concatenate([p0[...], p1[...], p2[...], p3[...]], axis=0)
     ft, fl = halves(parts)
     got = (
         lax.dot_general(ft, vt, dims, preferred_element_type=F32)
@@ -515,14 +569,13 @@
     far = within(both, 2)
     owed_a = around(owe_a, -1, 0)
     owed_b = around(owe_b, -1, 2)
-    p2a = along_z(p1[:16], 1)
-    p2b = along_z(p3[16:], 3)
+    p2 = along_z(p1, 1)
     finalize = small_call(finalize_kernel, [(4, CHUNK)] * 4)
     vc = finalize(where, near, far, owed_a, owed_b)
     (vectors,) = small_call(vectors_kernel, [(4, QCELL)])(where, near, far, owed_a, owed_b)
     given = [vc[0]] + [along_y(vc[k], k) for k in (1, 2, 3)]
     margin_part = small_call(margin_kernel, [(16, 128)], [pltpu.VMEM((16, 8, 16), F32)], 20)
-    (sums,) = margin_part(where, p0, p1, p3, p2a, p2b, *given)
+    (sums,) = margin_part(where, p0, p1, p2, p3, *given)
     groups = [[(z * 8 + y * 2 + h) * 4 + p for y in range(4) for p in range(4)] for z in range(4) for h in range(2)]
     sums = lax.all_to_all(sums, BOTH, 0, 0, tiled=True, axis_index_groups=groups)
     margin = jnp.sum(sums, axis=0).reshape(4, 32).T

time: 117 us -> 103 us (0.88)
  waiting for transfers between devices: 55.2 us -> 38.3 us
  starting transfers between devices: 29.8 us -> 38.5 us
  Pallas kernels: 29.3 us -> 22.3 us
    ppermute x20 -> x19, waiting for transfers between devices: 51.1 us -> 34.3 us  [move(): return lax.ppermute(value, BOTH, pairs)]
    all_to_all x1, starting transfers between devices: 4.69 us -> 9.26 us  [step(): lax.all_to_all(sums, BOTH, 0, 0, tiled=True, axis_index_groups=groups)]
    ppermute x20 -> x19, starting transfers between devices: 25.1 us -> 29.2 us  [move(): return lax.ppermute(value, BOTH, pairs)]
    pallas_call x1, Pallas kernels: 10.2 us -> 7.65 us  [spectrum(): pl.pallas_call(spectrum_kernel, out_shape=[jax.ShapeDtypeStruct((NG, 8, P...]
    pallas_call x1, Pallas kernels: 7.72 us -> 5.82 us  [terms(): pl.pallas_call(terms_kernel, out_shape=[jax.ShapeDtypeStruct(shape, F32)...]
    pallas_call x1, Pallas kernels: 1.94 us -> 0.33 us  [plane_tables(): pl.pallas_call(tables_kernel, out_shape=out, name='plane_tables', compile...]
  transfers between devices with their start and end apart: 21 -> 20, of which waited for: 9 -> 8; matrix products, arithmetic and copies ran while one was open for 0% -> 0% of each run, Pallas kernels for 23% -> 19%
where the time goes in v8:
time: 103 us; the launch traced here: 102 us
  starting transfers between devices  38.5 us (37%)
  waiting for transfers between devices  38.3 us (37%)
  Pallas kernels  22.3 us (22%)
  local copies, waits for them, and re-layouts  1.7 us (2%)
    ppermute x19, waiting for transfers between devices, move(): return lax.ppermute(value, BOTH, pairs)  34.3 us
    ppermute x19, starting transfers between devices, move(): return lax.ppermute(value, BOTH, pairs)  29.2 us
    all_to_all x1, starting transfers between devices, step(): lax.all_to_all(sums, BOTH, 0, 0, tiled=True, axis_index_groups=groups)  9.26 us
    pallas_call x8, Pallas kernels, call(): pl.pallas_call(body, out_shape=[jax.ShapeDtypeStruct(shape, F32) for shap...  8.48 us
    pallas_call x1, Pallas kernels, spectrum(): pl.pallas_call(spectrum_kernel, out_shape=[jax.ShapeDtypeStruct((NG, 8, P...  7.65 us
    pallas_call x1, Pallas kernels, terms(): pl.pallas_call(terms_kernel, out_shape=[jax.ShapeDtypeStruct(shape, F32)...  5.82 us
    all_to_all x1, waiting for transfers between devices, step(): lax.all_to_all(sums, BOTH, 0, 0, tiled=True, axis_index_groups=groups)  4.02 us
  transfers between devices with their start and end apart: 20, of which 8 were waited for; matrix products, arithmetic and copies ran while one was open for 0% of the time, Pallas kernels for 19%

profile of v8, /device:TPU:1, one launch (start us, length us, event | category | flops | bytes accessed | tf_op | source)
XLA Modules:
  0.0 101.8 jit_solution(10583060730573621568)
XLA Ops:
  0.7 2.1 %collective-permute-start = (f32[4,27648]{1,0:T(4,128)}, f32[4,27648]{1,0:T(4,128)S(1)}, u32[]{:S(2)}, u32[]{:S(2)}) collective-permute-start(f32[4,27648]{1,0:T(4,128)} %orbitals.3), channel_id=1, source_target_pairs={{0,2},{1,3},{2,0},{3,1},{4,6},{5,7},{6,4},{7,5},{8,10},{9,11},{10,... | collective-permute-start | bytes 1327112 | tf_op jit(solution)/shard_map/ppermute | solution.py:521
  4.5 2.5 %collective-permute-start.2 = (f32[2,27648]{1,0:T(2,128)S(1)}, f32[2,27648]{1,0:T(2,128)S(1)}, u32[]{:S(2)}, u32[]{:S(2)}) collective-permute-start(f32[2,27648]{1,0:T(2,128)S(1)} %get-tuple-element.28), channel_id=1, source_target_pairs={{0,4},{1,5},{2,6},{3,7},{4,8},{5,9},{6,10},{7,11},{8,12},{9,13},{1... | collective-permute-start | bytes 663560 | tf_op jit(solution)/shard_map/ppermute | solution.py:521
  7.0 1.2 %collective-permute-start.3 = (f32[2,27648]{1,0:T(2,128)S(1)}, f32[2,27648]{1,0:T(2,128)S(1)}, u32[]{:S(2)}, u32[]{:S(2)}) collective-permute-start(f32[2,27648]{1,0:T(2,128)S(1)} %get-tuple-element.29), channel_id=1, source_target_pairs={{0,6},{1,7},{2,4},{3,5},{4,10},{5,11},{6,8},{7,9},{8,14},{9,15},{1... | collective-permute-start | bytes 663560 | tf_op jit(solution)/shard_map/ppermute | solution.py:521
  8.8 2.7 %collective-permute-start.10 = (f32[4,6912]{1,0:T(4,128)S(1)}, f32[4,6912]{1,0:T(4,128)S(1)}, u32[]{:S(2)}, u32[]{:S(2)}) collective-permute-start(f32[4,6912]{1,0:T(4,128)S(1)} %get-tuple-element.48), channel_id=1, source_target_pairs={{0,16},{1,17},{2,18},{3,19},{4,20},{5,21},{6,22},{7,23},{8,24},{9,... | collective-permute-start | bytes 331784 | tf_op jit(solution)/shard_map/ppermute | solution.py:521
  11.5 1.1 %collective-permute-start.11 = (f32[4,6912]{1,0:T(4,128)S(1)}, f32[4,6912]{1,0:T(4,128)S(1)}, u32[]{:S(2)}, u32[]{:S(2)}) collective-permute-start(f32[4,6912]{1,0:T(4,128)S(1)} %get-tuple-element.49), channel_id=1, source_target_pairs={{0,24},{1,25},{2,26},{3,27},{4,28},{5,29},{6,30},{7,31},{8,16},{9,... | collective-permute-start | bytes 331784 | tf_op jit(solution)/shard_map/ppermute | solution.py:521
  12.6 13.1 %collective-permute-done.2.low_a = f32[2,27648]{1,0:T(2,128)S(1)} collective-permute-done((f32[2,27648]{1,0:T(2,128)S(1)}, f32[2,27648]{1,0:T(2,128)S(1)}, u32[]{:S(2)}, u32[]{:S(2)}) %collective-permute-start.2) | collective-permute-done | bytes 221216 | tf_op jit(solution)/shard_map/ppermute | solution.py:521
  26.4 1.6 %collective-permute-start.4 = (f32[8,27648]{1,0:T(8,128)S(1)}, f32[8,27648]{1,0:T(8,128)S(1)}, u32[]{:S(2)}, u32[]{:S(2)}) collective-permute-start(f32[8,27648]{1,0:T(8,128)S(1)} %shard_map.78), channel_id=1, source_target_pairs={{0,1},{1,0},{2,3},{3,2},{4,5},{5,4},{6,7},{7,6},{8,9},{9,8},{10,11... | collective-permute-start | bytes 2654216 | tf_op jit(solution)/shard_map/ppermute | solution.py:521
  28.1 1.2 %collective-permute-done.9.f1 = f32[4,6912]{1,0:T(4,128)S(1)} collective-permute-done((f32[4,6912]{1,0:T(4,128)S(1)}, f32[4,6912]{1,0:T(4,128)S(1)}, u32[]{:S(2)}, u32[]{:S(2)}) %collective-permute-start.9) | collective-permute-done | bytes 110624 | tf_op jit(solution)/shard_map/ppermute | solution.py:521
  29.5 2.8 %collective-permute-start.1 = (f32[4,27648]{1,0:T(4,128)S(1)}, f32[4,27648]{1,0:T(4,128)S(1)}, u32[]{:S(2)}, u32[]{:S(2)}) collective-permute-start(f32[4,27648]{1,0:T(4,128)S(1)} %copy-done.1), channel_id=1, source_target_pairs={{0,1},{1,0},{2,3},{3,2},{4,5},{5,4},{6,7},{7,6},{8,9},{9,8},{10,11... | collective-permute-start | bytes 1327112 | tf_op jit(solution)/shard_map/ppermute | solution.py:521
  32.2 7.8 %collective-permute-done.12.other = f32[16,6912]{1,0:T(8,128)S(1)} collective-permute-done((f32[16,6912]{1,0:T(8,128)S(1)}, f32[16,6912]{1,0:T(8,128)S(1)}, u32[]{:S(2)}, u32[]{:S(2)}) %collective-permute-start.12) | collective-permute-done | bytes 442400 | tf_op jit(solution)/shard_map/ppermute | solution.py:521
  40.7 1.8 %collective-permute-start.13 = (f32[32,6912]{1,0:T(8,128)S(1)}, f32[32,6912]{1,0:T(8,128)S(1)}, u32[]{:S(2)}, u32[]{:S(2)}) collective-permute-start(f32[32,6912]{1,0:T(8,128)S(1)} %shard_map.82.p0), channel_id=1, source_target_pairs={{0,32},{1,33},{2,34},{3,35},{4,36},{5,37},{6,38},{7,39},{8,40},{9,... | collective-permute-start | bytes 2654216 | tf_op jit(solution)/shard_map/ppermute | solution.py:521
  42.9 7.7 %spectrum.1 = (f32[48,8,2304]{2,1,0:T(8,128)S(1)}, f32[48,8,2304]{2,1,0:T(8,128)S(1)}, f32[384,2304]{1,0:T(8,128)S(1)}) custom-call(s32[1]{0:T(128)} %bitcast.q_ref, f32[4,27648]{1,0:T(4,128)S(1)} %copy-done.1, f32[4,27648]{1,0:T(4,128)S(1)} %collective-permute-done.two, f32[4,27648]{1,0:T(4,128)S(1)} %collective-permute-done.1.one, ...), custom_call_target="tpu_custom_call" | custom-call | tf_op jit(solution)/shard_map/spectrum/pallas_call | solution.py:379
  50.5 5.8 %terms.1 = (f32[4,27648]{1,0:T(4,128)S(1)}, f32[4,27648]{1,0:T(4,128)S(1)}, f32[10,27648]{1,0:T(8,128)S(1)}, f32[1,27648]{1,0:T(1,128)S(1)}, f32[1,27648]{1,0:T(1,128)S(1)}) custom-call(s32[1]{0:T(128)} %bitcast.q_ref, f32[48,8,2304]{2,1,0:T(8,128)S(1)} %get-tuple-element.32.right, f32[48,8,2304]{2,1,0:T(8,128)S(1)} %get-tuple-element.33.left, ...), custom_call_target="tpu_custom_call" | custom-call | tf_op jit(solution)/shard_map/terms/pallas_call | solution.py:391
  56.4 1.9 %collective-permute-start.5 = (f32[10,27648]{1,0:T(8,128)S(1)}, f32[10,27648]{1,0:T(8,128)S(1)}, u32[]{:S(2)}, u32[]{:S(2)}) collective-permute-start(f32[10,27648]{1,0:T(8,128)S(1)} %get-tuple-element.41), channel_id=1, source_target_pairs={{0,1},{1,0},{2,3},{3,2},{4,5},{5,4},{6,7},{7,6},{8,9},{9,8},{10,11... | collective-permute-start | bytes 3317768 | tf_op jit(solution)/shard_map/ppermute | solution.py:521
  58.3 2.9 %collective-permute-start.15 = (f32[32,6912]{1,0:T(8,128)S(1)}, f32[32,6912]{1,0:T(8,128)S(1)}, u32[]{:S(2)}, u32[]{:S(2)}) collective-permute-start(f32[32,6912]{1,0:T(8,128)S(1)} %shard_map.82.p0), channel_id=1, source_target_pairs={{0,96},{1,97},{2,98},{3,99},{4,100},{5,101},{6,102},{7,103},{8,104... | collective-permute-start | bytes 2654216 | tf_op jit(solution)/shard_map/ppermute | solution.py:521
  63.8 2.7 %collective-permute-start.8 = (f32[2,27648]{1,0:T(2,128)S(1)}, f32[2,27648]{1,0:T(2,128)S(1)}, u32[]{:S(2)}, u32[]{:S(2)}) collective-permute-start(f32[2,27648]{1,0:T(2,128)S(1)} %get-tuple-element.45), channel_id=1, source_target_pairs={{0,126},{1,127},{2,124},{3,125},{4,2},{5,3},{6,0},{7,1},{8,6},{9,7... | collective-permute-start | bytes 663560 | tf_op jit(solution)/shard_map/ppermute | solution.py:521
  66.6 9.2 %collective-permute-done.7.owed_a = f32[2,27648]{1,0:T(2,128)S(1)} collective-permute-done((f32[2,27648]{1,0:T(2,128)S(1)}, f32[2,27648]{1,0:T(2,128)S(1)}, u32[]{:S(2)}, u32[]{:S(2)}) %collective-permute-start.7) | collective-permute-done | bytes 221216 | tf_op jit(solution)/shard_map/ppermute | solution.py:521
  76.6 1.8 %collective-permute-start.17 = (f32[4,6912]{1,0:T(4,128)S(1)}, f32[4,6912]{1,0:T(4,128)S(1)}, u32[]{:S(2)}, u32[]{:S(2)}) collective-permute-start(f32[4,6912]{1,0:T(4,128)S(1)} %get-tuple-element.52), channel_id=1, source_target_pairs={{0,16},{1,17},{2,18},{3,19},{4,20},{5,21},{6,22},{7,23},{8,24},{9,... | collective-permute-start | bytes 331784 | tf_op jit(solution)/shard_map/ppermute | solution.py:521
  78.4 2.1 %collective-permute-start.18 = (f32[4,6912]{1,0:T(4,128)S(1)}, f32[4,6912]{1,0:T(4,128)S(1)}, u32[]{:S(2)}, u32[]{:S(2)}) collective-permute-start(f32[4,6912]{1,0:T(4,128)S(1)} %get-tuple-element.53), channel_id=1, source_target_pairs={{0,24},{1,25},{2,26},{3,27},{4,28},{5,29},{6,30},{7,31},{8,16},{9,... | collective-permute-start | bytes 331784 | tf_op jit(solution)/shard_map/ppermute | solution.py:521
  81.8 1.7 %collective-permute-done.18.v3 = f32[4,6912]{1,0:T(4,128)S(1)} collective-permute-done((f32[4,6912]{1,0:T(4,128)S(1)}, f32[4,6912]{1,0:T(4,128)S(1)}, u32[]{:S(2)}, u32[]{:S(2)}) %collective-permute-start.18) | collective-permute-done | bytes 110624 | tf_op jit(solution)/shard_map/ppermute | solution.py:521
  83.5 2.8 %shard_map.84 = f32[16,128]{1,0:T(8,128)} custom-call(s32[4]{0:T(128)S(1)} %pad_add_fusion.where, f32[32,6912]{1,0:T(8,128)S(1)} %shard_map.82.p0, f32[32,6912]{1,0:T(8,128)S(1)} %collective-permute-done.13.p1, f32[32,6912]{1,0:T(8,128)S(1)} %collective-permute-done.14.p2, f32[32,6912]{1,0:T(8,128)S(1)} %collective-permute-done.15.p3, ...), custom_call_target="tpu_custom_call" | custom-call | tf_op jit(solution)/shard_map/pallas_call | solution.py:410
  86.3 9.3 %all-to-all-start = ((f32[16,1,128]{2,1,0:T(1,128)}), f32[16,1,128]{2,1,0:T(1,128)S(1)}, u32[]{:S(2)}, u32[]{:S(2)}) async-start(f32[16,1,128]{2,1,0:T(1,128)} %bitcast.5), calls=%async_computation | async-start | bytes 16384 | tf_op jit(solution)/shard_map/all_to_all | solution.py:580
  95.6 1.5 %shard_map.80 = f32[4,27648]{1,0:T(4,128)} custom-call(s32[4]{0:T(128)S(1)} %pad_add_fusion.where, f32[4,27648]{1,0:T(4,128)S(1)} %get-tuple-element.42.near, f32[4,27648]{1,0:T(4,128)S(1)} %collective-permute-done.6.far, f32[2,27648]{1,0:T(2,128)S(1)} %collective-permute-done.7.owed_a, f32[2,27648]{1,0:T(2,128)S(1)} %collective-permute-done.8.owed_b), custom_call_target="tpu_custom_call" | custom-call | tf_op jit(solution)/shard_map/pallas_call | solution.py:410
  97.1 4.0 %all-to-all-done = f32[16,1,128]{2,1,0:T(1,128)S(1)} async-done(((f32[16,1,128]{2,1,0:T(1,128)}), f32[16,1,128]{2,1,0:T(1,128)S(1)}, u32[]{:S(2)}, u32[]{:S(2)}) %all-to-all-start) | async-done | bytes 8224 | tf_op jit(solution)/shard_map/all_to_all | solution.py:580
  (43 shorter events, 9.8 us)
Async XLA Ops:
  0.6 41.9 %copy-start.4 = (f32[4,16,256]{2,1,0:T(8,128)S(1)}, f32[4,16,256]{2,1,0:T(8,128)}, u32[]{:S(2)}) copy-start(f32[4,16,256]{2,1,0:T(8,128)} %constant.63.clone.slow) | copy-start | bytes 196612
  0.6 42.2 %copy-start.3 = (f32[16,256]{1,0:T(8,128)S(1)}, f32[16,256]{1,0:T(8,128)}, u32[]{:S(2)}) copy-start(f32[16,256]{1,0:T(8,128)} %constant.66.clone.third) | copy-start | bytes 49156
  0.7 25.0 %collective-permute-start = (f32[4,27648]{1,0:T(4,128)}, f32[4,27648]{1,0:T(4,128)S(1)}, u32[]{:S(2)}, u32[]{:S(2)}) collective-permute-start(f32[4,27648]{1,0:T(4,128)} %orbitals.3), channel_id=1, source_target_pairs={{0,2},{1,3},{2,0},{3,1},{4,6},{5,7},{6,4},{7,5},{8,10},{9,11},{10,... | collective-permute-start | bytes 1327112 | tf_op jit(solution)/shard_map/ppermute | solution.py:521
  3.9 38.6 %copy-start.5 = (f32[4,16,256]{2,1,0:T(8,128)S(1)}, f32[4,16,256]{2,1,0:T(8,128)}, u32[]{:S(2)}) copy-start(f32[4,16,256]{2,1,0:T(8,128)} %constant.64.clone.fast) | copy-start | bytes 196612
  3.9 39.0 %copy-start.2 = (f32[48,2304]{1,0:T(8,128)S(1)}, f32[48,2304]{1,0:T(8,128)}, u32[]{:S(2)}) copy-start(f32[48,2304]{1,0:T(8,128)} %constant.65.clone.kern) | copy-start | bytes 1327108
  4.5 21.1 %collective-permute-start.2 = (f32[2,27648]{1,0:T(2,128)S(1)}, f32[2,27648]{1,0:T(2,128)S(1)}, u32[]{:S(2)}, u32[]{:S(2)}) collective-permute-start(f32[2,27648]{1,0:T(2,128)S(1)} %get-tuple-element.28), channel_id=1, source_target_pairs={{0,4},{1,5},{2,6},{3,7},{4,8},{5,9},{6,10},{7,11},{8,12},{9,13},{1... | collective-permute-start | bytes 663560 | tf_op jit(solution)/shard_map/ppermute | solution.py:521
  7.0 18.6 %collective-permute-start.3 = (f32[2,27648]{1,0:T(2,128)S(1)}, f32[2,27648]{1,0:T(2,128)S(1)}, u32[]{:S(2)}, u32[]{:S(2)}) collective-permute-start(f32[2,27648]{1,0:T(2,128)S(1)} %get-tuple-element.29), channel_id=1, source_target_pairs={{0,6},{1,7},{2,4},{3,5},{4,10},{5,11},{6,8},{7,9},{8,14},{9,15},{1... | collective-permute-start | bytes 663560 | tf_op jit(solution)/shard_map/ppermute | solution.py:521
  8.8 19.2 %collective-permute-start.10 = (f32[4,6912]{1,0:T(4,128)S(1)}, f32[4,6912]{1,0:T(4,128)S(1)}, u32[]{:S(2)}, u32[]{:S(2)}) collective-permute-start(f32[4,6912]{1,0:T(4,128)S(1)} %get-tuple-element.48), channel_id=1, source_target_pairs={{0,16},{1,17},{2,18},{3,19},{4,20},{5,21},{6,22},{7,23},{8,24},{9,... | collective-permute-start | bytes 331784 | tf_op jit(solution)/shard_map/ppermute | solution.py:521
  11.5 16.5 %collective-permute-start.11 = (f32[4,6912]{1,0:T(4,128)S(1)}, f32[4,6912]{1,0:T(4,128)S(1)}, u32[]{:S(2)}, u32[]{:S(2)}) collective-permute-start(f32[4,6912]{1,0:T(4,128)S(1)} %get-tuple-element.49), channel_id=1, source_target_pairs={{0,24},{1,25},{2,26},{3,27},{4,28},{5,29},{6,30},{7,31},{8,16},{9,... | collective-permute-start | bytes 331784 | tf_op jit(solution)/shard_map/ppermute | solution.py:521
  25.7 3.6 %collective-permute-start.9 = (f32[4,6912]{1,0:T(4,128)S(1)}, f32[4,6912]{1,0:T(4,128)S(1)}, u32[]{:S(2)}, u32[]{:S(2)}) collective-permute-start(f32[4,6912]{1,0:T(4,128)S(1)} %get-tuple-element.47), channel_id=1, source_target_pairs={{0,8},{1,9},{2,10},{3,11},{4,12},{5,13},{6,14},{7,15},{8,0},{9,1},... | collective-permute-start | bytes 331784 | tf_op jit(solution)/shard_map/ppermute | solution.py:521
  26.4 16.4 %collective-permute-start.4 = (f32[8,27648]{1,0:T(8,128)S(1)}, f32[8,27648]{1,0:T(8,128)S(1)}, u32[]{:S(2)}, u32[]{:S(2)}) collective-permute-start(f32[8,27648]{1,0:T(8,128)S(1)} %shard_map.78), channel_id=1, source_target_pairs={{0,1},{1,0},{2,3},{3,2},{4,5},{5,4},{6,7},{7,6},{8,9},{9,8},{10,11... | collective-permute-start | bytes 2654216 | tf_op jit(solution)/shard_map/ppermute | solution.py:521
  29.4 10.6 %collective-permute-start.12 = (f32[16,6912]{1,0:T(8,128)S(1)}, f32[16,6912]{1,0:T(8,128)S(1)}, u32[]{:S(2)}, u32[]{:S(2)}) collective-permute-start(f32[16,6912]{1,0:T(8,128)S(1)} %pad_maximum_fusion), channel_id=1, source_target_pairs={{0,4},{1,5},{2,6},{3,7},{4,0},{5,1},{6,2},{7,3},{8,12},{9,13},{10,... | collective-permute-start | bytes 1327112 | tf_op jit(solution)/shard_map/ppermute | solution.py:521
  29.5 13.3 %collective-permute-start.1 = (f32[4,27648]{1,0:T(4,128)S(1)}, f32[4,27648]{1,0:T(4,128)S(1)}, u32[]{:S(2)}, u32[]{:S(2)}) collective-permute-start(f32[4,27648]{1,0:T(4,128)S(1)} %copy-done.1), channel_id=1, source_target_pairs={{0,1},{1,0},{2,3},{3,2},{4,5},{5,4},{6,7},{7,6},{8,9},{9,8},{10,11... | collective-permute-start | bytes 1327112 | tf_op jit(solution)/shard_map/ppermute | solution.py:521
  40.7 20.5 %collective-permute-start.13 = (f32[32,6912]{1,0:T(8,128)S(1)}, f32[32,6912]{1,0:T(8,128)S(1)}, u32[]{:S(2)}, u32[]{:S(2)}) collective-permute-start(f32[32,6912]{1,0:T(8,128)S(1)} %shard_map.82.p0), channel_id=1, source_target_pairs={{0,32},{1,33},{2,34},{3,35},{4,36},{5,37},{6,38},{7,39},{8,40},{9,... | collective-permute-start | bytes 2654216 | tf_op jit(solution)/shard_map/ppermute | solution.py:521
  56.4 5.8 %collective-permute-start.5 = (f32[10,27648]{1,0:T(8,128)S(1)}, f32[10,27648]{1,0:T(8,128)S(1)}, u32[]{:S(2)}, u32[]{:S(2)}) collective-permute-start(f32[10,27648]{1,0:T(8,128)S(1)} %get-tuple-element.41), channel_id=1, source_target_pairs={{0,1},{1,0},{2,3},{3,2},{4,5},{5,4},{6,7},{7,6},{8,9},{9,8},{10,11... | collective-permute-start | bytes 3317768 | tf_op jit(solution)/shard_map/ppermute | solution.py:521
  58.3 22.2 %collective-permute-start.15 = (f32[32,6912]{1,0:T(8,128)S(1)}, f32[32,6912]{1,0:T(8,128)S(1)}, u32[]{:S(2)}, u32[]{:S(2)}) collective-permute-start(f32[32,6912]{1,0:T(8,128)S(1)} %shard_map.82.p0), channel_id=1, source_target_pairs={{0,96},{1,97},{2,98},{3,99},{4,100},{5,101},{6,102},{7,103},{8,104... | collective-permute-start | bytes 2654216 | tf_op jit(solution)/shard_map/ppermute | solution.py:521
  61.2 19.6 %collective-permute-start.14 = (f32[32,6912]{1,0:T(8,128)S(1)}, f32[32,6912]{1,0:T(8,128)S(1)}, u32[]{:S(2)}, u32[]{:S(2)}) collective-permute-start(f32[32,6912]{1,0:T(8,128)S(1)} %collective-permute-done.13.p1), channel_id=1, source_target_pairs={{0,32},{1,33},{2,34},{3,35},{4,36},{5,37},{6,38},{7,39},{8,40},{9,... | collective-permute-start | bytes 2654216 | tf_op jit(solution)/shard_map/ppermute | solution.py:521
  62.9 12.9 %collective-permute-start.6 = (f32[4,27648]{1,0:T(4,128)S(1)}, f32[4,27648]{1,0:T(4,128)S(1)}, u32[]{:S(2)}, u32[]{:S(2)}) collective-permute-start(f32[4,27648]{1,0:T(4,128)S(1)} %get-tuple-element.43), channel_id=1, source_target_pairs={{0,2},{1,3},{2,0},{3,1},{4,6},{5,7},{6,4},{7,5},{8,10},{9,11},{10,... | collective-permute-start | bytes 1327112 | tf_op jit(solution)/shard_map/ppermute | solution.py:521
  63.0 12.8 %collective-permute-start.7 = (f32[2,27648]{1,0:T(2,128)S(1)}, f32[2,27648]{1,0:T(2,128)S(1)}, u32[]{:S(2)}, u32[]{:S(2)}) collective-permute-start(f32[2,27648]{1,0:T(2,128)S(1)} %get-tuple-element.44), channel_id=1, source_target_pairs={{0,124},{1,125},{2,126},{3,127},{4,0},{5,1},{6,2},{7,3},{8,4},{9,5... | collective-permute-start | bytes 663560 | tf_op jit(solution)/shard_map/ppermute | solution.py:521
  63.8 11.9 %collective-permute-start.8 = (f32[2,27648]{1,0:T(2,128)S(1)}, f32[2,27648]{1,0:T(2,128)S(1)}, u32[]{:S(2)}, u32[]{:S(2)}) collective-permute-start(f32[2,27648]{1,0:T(2,128)S(1)} %get-tuple-element.45), channel_id=1, source_target_pairs={{0,126},{1,127},{2,124},{3,125},{4,2},{5,3},{6,0},{7,1},{8,6},{9,7... | collective-permute-start | bytes 663560 | tf_op jit(solution)/shard_map/ppermute | solution.py:521
  76.5 4.3 %collective-permute-start.16 = (f32[4,6912]{1,0:T(4,128)S(1)}, f32[4,6912]{1,0:T(4,128)S(1)}, u32[]{:S(2)}, u32[]{:S(2)}) collective-permute-start(f32[4,6912]{1,0:T(4,128)S(1)} %get-tuple-element.51), channel_id=1, source_target_pairs={{0,8},{1,9},{2,10},{3,11},{4,12},{5,13},{6,14},{7,15},{8,0},{9,1},... | collective-permute-start | bytes 331784 | tf_op jit(solution)/shard_map/ppermute | solution.py:521
  76.6 5.2 %collective-permute-start.17 = (f32[4,6912]{1,0:T(4,128)S(1)}, f32[4,6912]{1,0:T(4,128)S(1)}, u32[]{:S(2)}, u32[]{:S(2)}) collective-permute-start(f32[4,6912]{1,0:T(4,128)S(1)} %get-tuple-element.52), channel_id=1, source_target_pairs={{0,16},{1,17},{2,18},{3,19},{4,20},{5,21},{6,22},{7,23},{8,24},{9,... | collective-permute-start | bytes 331784 | tf_op jit(solution)/shard_map/ppermute | solution.py:521
  78.4 5.1 %collective-permute-start.18 = (f32[4,6912]{1,0:T(4,128)S(1)}, f32[4,6912]{1,0:T(4,128)S(1)}, u32[]{:S(2)}, u32[]{:S(2)}) collective-permute-start(f32[4,6912]{1,0:T(4,128)S(1)} %get-tuple-element.53), channel_id=1, source_target_pairs={{0,24},{1,25},{2,26},{3,27},{4,28},{5,29},{6,30},{7,31},{8,16},{9,... | collective-permute-start | bytes 331784 | tf_op jit(solution)/shard_map/ppermute | solution.py:521
  86.3 14.8 %all-to-all-start = ((f32[16,1,128]{2,1,0:T(1,128)}), f32[16,1,128]{2,1,0:T(1,128)S(1)}, u32[]{:S(2)}, u32[]{:S(2)}) async-start(f32[16,1,128]{2,1,0:T(1,128)} %bitcast.5), calls=%async_computation | async-start | bytes 16384 | tf_op jit(solution)/shard_map/all_to_all | solution.py:580
  (2 other events, 26.6 us)

commit v9 on v8

--- a/solution.py
+++ b/solution.py
@@ -469,16 +469,8 @@
         vectors[:, span] = total_of(where, near, far, owed_a, owed_b, span)
 
 
-def pair_kernel(where, f0, f1, f2, f3, other, out):
-    first = where[3] == 0
-    for k, f in enumerate((f0, f1, f2, f3)):
-        a, b = f[...], other[4 * k : 4 * k + 4, :]
-        out[8 * k : 8 * k + 4, :] = jnp.where(first, a, b)
-        out[8 * k + 4 : 8 * k + 8, :] = jnp.where(first, b, a)
-
-
-def margin_kernel(where, p0, p1, p2, p3, v0, v1, v2, v3, pieces, block):
-    z, y = where[1], where[2]
+def margin_kernel(where, own0, oth0, own1, oth1, own2, oth2, own3, oth3, v0, v1, v2, v3, pieces, block):
+    z, y, h = where[1], where[2], where[3]
 
     def halves(a):
         top = a.astype(BF16)
@@ -486,7 +478,7 @@
 
     vt, vl = halves(jnp.concatenate([v0[...], v1[...], v2[...], v3[...]], axis=0))
     dims = (((1,), (1,)), ((), ()))
-    parts = jnp.concatenate([p0[...], p1[...], p2[...], p3[...]], axis=0)
+    parts = jnp.concatenate([r[...] for r in (own0, oth0, own1, oth1, own2, oth2, own3, oth3)], axis=0)
     ft, fl = halves(parts)
     got = (
         lax.dot_general(ft, vt, dims, preferred_element_type=F32)
@@ -495,8 +487,11 @@
     )
     for dz in range(4):
         for dy in range(4):
-            row = 32 * dz + 8 * dy
-            block[(z + 4 - dz) % 4 * 4 + (y ^ dy), :, :] = got[row : row + 8, :]
+            row = 32 * dz + 4 * dy
+            pair = got[row : row + 4, :], got[row + 16 : row + 20, :]
+            at = (z + 4 - dz) % 4 * 4 + (y ^ dy)
+            block[at, 0:4, :] = jnp.where(h == 0, pair[0], pair[1])
+            block[at, 4:8, :] = jnp.where(h == 0, pair[1], pair[0])
     out = block[...].reshape(128, 16).T * (1.0 / NCELL)
     turned = [out] + [pltpu.roll(out, 32 * r, 1) for r in (1, 2, 3)]
     third_of = lax.broadcasted_iota(jnp.int32, (16, 128), 1) // 32
@@ -558,24 +553,27 @@
     (stacked,) = small_call(stack_kernel, [(8, QCELL)])(where, two, low_a, low_b)
     core = within(stacked, 1)
     other = move(together, lambda z, y, h, q: (z, y, 1 - h, q))
+    own1 = along_z(together, 1)
+    own3 = along_z(together, 3)
     right, left, field = spectrum(q, (orbitals, two, one, low_a, low_b, core), tables[:2])
-    (p0,) = small_call(pair_kernel, [(32, CHUNK)])(where, *pieces, other)
-    p1 = along_z(p0, 1)
-    p3 = along_z(p0, 3)
     near0, near2, cross, low0, low2 = terms(q, right, left, field, tables[2:])
     across = within(cross, 1)
+    other, _ = lax.optimization_barrier((other, near0))
+    oth1 = along_z(other, 1)
+    oth3 = along_z(other, 3)
+    own2 = along_z(own1, 1)
     merge = small_call(merge_kernel, [(4, QCELL)] * 2 + [(2, QCELL)] * 2)
     near, both, owe_a, owe_b = merge(where, near0, near2, low0, low2, across)
     far = within(both, 2)
     owed_a = around(owe_a, -1, 0)
     owed_b = around(owe_b, -1, 2)
-    p2 = along_z(p1, 1)
+    oth2 = along_z(oth1, 1)
     finalize = small_call(finalize_kernel, [(4, CHUNK)] * 4)
     vc = finalize(where, near, far, owed_a, owed_b)
     (vectors,) = small_call(vectors_kernel, [(4, QCELL)])(where, near, far, owed_a, owed_b)
     given = [vc[0]] + [along_y(vc[k], k) for k in (1, 2, 3)]
     margin_part = small_call(margin_kernel, [(16, 128)], [pltpu.VMEM((16, 8, 16), F32)], 20)
-    (sums,) = margin_part(where, p0, p1, p2, p3, *given)
+    (sums,) = margin_part(where, together, other, own1, oth1, own2, oth2, own3, oth3, *given)
     groups = [[(z * 8 + y * 2 + h) * 4 + p for y in range(4) for p in range(4)] for z in range(4) for h in range(2)]
     sums = lax.all_to_all(sums, BOTH, 0, 0, tiled=True, axis_index_groups=groups)
     margin = jnp.sum(sums, axis=0).reshape(4, 32).T

time: 103 us -> 114 us (1.11)
  waiting for transfers between devices: 38.3 us -> 57.5 us
  starting transfers between devices: 38.5 us -> 25.9 us
  local copies, waits for them, and re-layouts: 1.7 us -> 7.11 us
    ppermute x19 -> x22, waiting for transfers between devices: 34.3 us -> 53.4 us  [move(): return lax.ppermute(value, BOTH, pairs)]
    ppermute x19 -> x22, starting transfers between devices: 29.2 us -> 20.1 us  [move(): return lax.ppermute(value, BOTH, pairs)]
    unnamed x12 -> x14, local copies, waits for them, and re-layouts: 1.04 us -> 6.45 us
    all_to_all x1, starting transfers between devices: 9.26 us -> 5.8 us  [step(): lax.all_to_all(sums, BOTH, 0, 0, tiled=True, axis_index_groups=groups)]
    pallas_call x8 -> x7, Pallas kernels: 8.48 us -> 7.79 us  [call(): pl.pallas_call(body, out_shape=[jax.ShapeDtypeStruct(shape, F32) for shap...]
  transfers between devices with their start and end apart: 20 -> 23, of which waited for: 8 -> 8; matrix products, arithmetic and copies ran while one was open for 0% -> 0% of each run, Pallas kernels for 19% -> 16%
where the time goes in v9:
time: 114 us; the launch traced here: 113 us
  waiting for transfers between devices  57.5 us (50%)
  starting transfers between devices  25.9 us (23%)
  Pallas kernels  21.6 us (19%)
  local copies, waits for them, and re-layouts  7.11 us (6%)
    ppermute x22, waiting for transfers between devices, move(): return lax.ppermute(value, BOTH, pairs)  53.4 us
    ppermute x22, starting transfers between devices, move(): return lax.ppermute(value, BOTH, pairs)  20.1 us
    pallas_call x7, Pallas kernels, call(): pl.pallas_call(body, out_shape=[jax.ShapeDtypeStruct(shape, F32) for shap...  7.79 us
    pallas_call x1, Pallas kernels, spectrum(): pl.pallas_call(spectrum_kernel, out_shape=[jax.ShapeDtypeStruct((NG, 8, P...  7.64 us
    unnamed x14, local copies, waits for them, and re-layouts  6.45 us
    pallas_call x1, Pallas kernels, terms(): pl.pallas_call(terms_kernel, out_shape=[jax.ShapeDtypeStruct(shape, F32)...  5.82 us
    all_to_all x1, starting transfers between devices, step(): lax.all_to_all(sums, BOTH, 0, 0, tiled=True, axis_index_groups=groups)  5.8 us
    all_to_all x1, waiting for transfers between devices, step(): lax.all_to_all(sums, BOTH, 0, 0, tiled=True, axis_index_groups=groups)  4.08 us
  transfers between devices with their start and end apart: 23, of which 8 were waited for; matrix products, arithmetic and copies ran while one was open for 0% of the time, Pallas kernels for 16%

profile of v9, /device:TPU:1, one launch (start us, length us, event | category | flops | bytes accessed | tf_op | source)
XLA Modules:
  0.0 113.1 jit_solution(3951966012579736514)
XLA Ops:
  0.6 2.1 %collective-permute-start = (f32[4,27648]{1,0:T(4,128)}, f32[4,27648]{1,0:T(4,128)S(1)}, u32[]{:S(2)}, u32[]{:S(2)}) collective-permute-start(f32[4,27648]{1,0:T(4,128)} %orbitals.3), channel_id=1, source_target_pairs={{0,2},{1,3},{2,0},{3,1},{4,6},{5,7},{6,4},{7,5},{8,10},{9,11},{10,... | collective-permute-start | bytes 1327112 | tf_op jit(solution)/shard_map/ppermute | solution.py:516
  2.8 1.0 copy-done
  4.5 2.5 %collective-permute-start.2 = (f32[2,27648]{1,0:T(2,128)S(1)}, f32[2,27648]{1,0:T(2,128)S(1)}, u32[]{:S(2)}, u32[]{:S(2)}) collective-permute-start(f32[2,27648]{1,0:T(2,128)S(1)} %get-tuple-element.29), channel_id=1, source_target_pairs={{0,4},{1,5},{2,6},{3,7},{4,8},{5,9},{6,10},{7,11},{8,12},{9,13},{1... | collective-permute-start | bytes 663560 | tf_op jit(solution)/shard_map/ppermute | solution.py:516
  7.0 1.2 %collective-permute-start.3 = (f32[2,27648]{1,0:T(2,128)S(1)}, f32[2,27648]{1,0:T(2,128)S(1)}, u32[]{:S(2)}, u32[]{:S(2)}) collective-permute-start(f32[2,27648]{1,0:T(2,128)S(1)} %get-tuple-element.30), channel_id=1, source_target_pairs={{0,6},{1,7},{2,4},{3,5},{4,10},{5,11},{6,8},{7,9},{8,14},{9,15},{1... | collective-permute-start | bytes 663560 | tf_op jit(solution)/shard_map/ppermute | solution.py:516
  8.2 17.4 %collective-permute-done.2.low_a = f32[2,27648]{1,0:T(2,128)S(1)} collective-permute-done((f32[2,27648]{1,0:T(2,128)S(1)}, f32[2,27648]{1,0:T(2,128)S(1)}, u32[]{:S(2)}, u32[]{:S(2)}) %collective-permute-start.2) | collective-permute-done | bytes 221216 | tf_op jit(solution)/shard_map/ppermute | solution.py:516
  26.4 1.6 %collective-permute-start.4 = (f32[8,27648]{1,0:T(8,128)S(1)}, f32[8,27648]{1,0:T(8,128)S(1)}, u32[]{:S(2)}, u32[]{:S(2)}) collective-permute-start(f32[8,27648]{1,0:T(8,128)S(1)} %shard_map.78), channel_id=1, source_target_pairs={{0,1},{1,0},{2,3},{3,2},{4,5},{5,4},{6,7},{7,6},{8,9},{9,8},{10,11... | collective-permute-start | bytes 2654216 | tf_op jit(solution)/shard_map/ppermute | solution.py:516
  28.1 1.0 copy-done.1
  29.9 2.5 %collective-permute-start.9 = (f32[4,6912]{1,0:T(4,128)S(1)}, f32[4,6912]{1,0:T(4,128)S(1)}, u32[]{:S(2)}, u32[]{:S(2)}) collective-permute-start(f32[4,6912]{1,0:T(4,128)S(1)} %get-tuple-element.48), channel_id=1, source_target_pairs={{0,8},{1,9},{2,10},{3,11},{4,12},{5,13},{6,14},{7,15},{8,0},{9,1},... | collective-permute-start | bytes 331784 | tf_op jit(solution)/shard_map/ppermute | solution.py:516
  37.2 7.6 %spectrum.1 = (f32[48,8,2304]{2,1,0:T(8,128)S(1)}, f32[48,8,2304]{2,1,0:T(8,128)S(1)}, f32[384,2304]{1,0:T(8,128)S(1)}) custom-call(s32[1]{0:T(128)} %bitcast.q_ref, f32[4,27648]{1,0:T(4,128)S(1)} %copy-done.2, f32[4,27648]{1,0:T(4,128)S(1)} %collective-permute-done.two, f32[4,27648]{1,0:T(4,128)S(1)} %collective-permute-done.1.one, ...), custom_call_target="tpu_custom_call" | custom-call | tf_op jit(solution)/shard_map/spectrum/pallas_call | solution.py:379
  44.9 5.8 %terms.1 = (f32[4,27648]{1,0:T(4,128)S(1)}, f32[4,27648]{1,0:T(4,128)S(1)}, f32[10,27648]{1,0:T(8,128)S(1)}, f32[1,27648]{1,0:T(1,128)S(1)}, f32[1,27648]{1,0:T(1,128)S(1)}) custom-call(s32[1]{0:T(128)} %bitcast.q_ref, f32[48,8,2304]{2,1,0:T(8,128)S(1)} %get-tuple-element.33.right, f32[48,8,2304]{2,1,0:T(8,128)S(1)} %get-tuple-element.34.left, ...), custom_call_target="tpu_custom_call" | custom-call | tf_op jit(solution)/shard_map/terms/pallas_call | solution.py:391
  50.7 1.3 %collective-permute-start.5 = (f32[10,27648]{1,0:T(8,128)S(1)}, f32[10,27648]{1,0:T(8,128)S(1)}, u32[]{:S(2)}, u32[]{:S(2)}) collective-permute-start(f32[10,27648]{1,0:T(8,128)S(1)} %get-tuple-element.42), channel_id=1, source_target_pairs={{0,1},{1,0},{2,3},{3,2},{4,5},{5,4},{6,7},{7,6},{8,9},{9,8},{10,11... | collective-permute-start | bytes 3317768 | tf_op jit(solution)/shard_map/ppermute | solution.py:516
  52.3 13.1 %collective-permute-done.12.oth0 = f32[16,6912]{1,0:T(8,128)S(1)} collective-permute-done((f32[16,6912]{1,0:T(8,128)S(1)}, f32[16,6912]{1,0:T(8,128)S(1)}, u32[]{:S(2)}, u32[]{:S(2)}) %collective-permute-start.12) | collective-permute-done | bytes 442400 | tf_op jit(solution)/shard_map/ppermute | solution.py:516
  66.2 2.8 %collective-permute-start.7 = (f32[2,27648]{1,0:T(2,128)S(1)}, f32[2,27648]{1,0:T(2,128)S(1)}, u32[]{:S(2)}, u32[]{:S(2)}) collective-permute-start(f32[2,27648]{1,0:T(2,128)S(1)} %get-tuple-element.45), channel_id=1, source_target_pairs={{0,124},{1,125},{2,126},{3,127},{4,0},{5,1},{6,2},{7,3},{8,4},{9,5... | collective-permute-start | bytes 663560 | tf_op jit(solution)/shard_map/ppermute | solution.py:516
  69.0 2.1 %collective-permute-start.8 = (f32[2,27648]{1,0:T(2,128)S(1)}, f32[2,27648]{1,0:T(2,128)S(1)}, u32[]{:S(2)}, u32[]{:S(2)}) collective-permute-start(f32[2,27648]{1,0:T(2,128)S(1)} %get-tuple-element.46), channel_id=1, source_target_pairs={{0,126},{1,127},{2,124},{3,125},{4,2},{5,3},{6,0},{7,1},{8,6},{9,7... | collective-permute-start | bytes 663560 | tf_op jit(solution)/shard_map/ppermute | solution.py:516
  71.3 6.1 %collective-permute-done.14.oth1 = f32[16,6912]{1,0:T(8,128)S(1)} collective-permute-done((f32[16,6912]{1,0:T(8,128)S(1)}, f32[16,6912]{1,0:T(8,128)S(1)}, u32[]{:S(2)}, u32[]{:S(2)}) %collective-permute-start.14) | collective-permute-done | bytes 442400 | tf_op jit(solution)/shard_map/ppermute | solution.py:516
  77.5 2.7 %collective-permute-start.18 = (f32[16,6912]{1,0:T(8,128)S(1)}, f32[16,6912]{1,0:T(8,128)S(1)}, u32[]{:S(2)}, u32[]{:S(2)}) collective-permute-start(f32[16,6912]{1,0:T(8,128)S(1)} %collective-permute-done.12.oth0), channel_id=1, source_target_pairs={{0,96},{1,97},{2,98},{3,99},{4,100},{5,101},{6,102},{7,103},{8,104... | collective-permute-start | bytes 1327112 | tf_op jit(solution)/shard_map/ppermute | solution.py:516
  80.2 3.1 %collective-permute-done.6.far = f32[4,27648]{1,0:T(4,128)S(1)} collective-permute-done((f32[4,27648]{1,0:T(4,128)S(1)}, f32[4,27648]{1,0:T(4,128)S(1)}, u32[]{:S(2)}, u32[]{:S(2)}) %collective-permute-start.6) | collective-permute-done | bytes 442400 | tf_op jit(solution)/shard_map/ppermute | solution.py:516
  84.2 4.5 %collective-permute-done.15.own2 = f32[16,6912]{1,0:T(8,128)S(1)} collective-permute-done((f32[16,6912]{1,0:T(8,128)S(1)}, f32[16,6912]{1,0:T(8,128)S(1)}, u32[]{:S(2)}, u32[]{:S(2)}) %collective-permute-start.15) | collective-permute-done | bytes 442400 | tf_op jit(solution)/shard_map/ppermute | solution.py:516
  89.0 1.5 %collective-permute-done.18.oth3 = f32[16,6912]{1,0:T(8,128)S(1)} collective-permute-done((f32[16,6912]{1,0:T(8,128)S(1)}, f32[16,6912]{1,0:T(8,128)S(1)}, u32[]{:S(2)}, u32[]{:S(2)}) %collective-permute-start.18) | collective-permute-done | bytes 442400 | tf_op jit(solution)/shard_map/ppermute | solution.py:516
  90.5 7.6 %collective-permute-done.16.oth2 = f32[16,6912]{1,0:T(8,128)S(1)} collective-permute-done((f32[16,6912]{1,0:T(8,128)S(1)}, f32[16,6912]{1,0:T(8,128)S(1)}, u32[]{:S(2)}, u32[]{:S(2)}) %collective-permute-start.16) | collective-permute-done | bytes 442400 | tf_op jit(solution)/shard_map/ppermute | solution.py:516
  98.2 2.8 %shard_map.83 = f32[16,128]{1,0:T(8,128)} custom-call(s32[4]{0:T(128)S(1)} %pad_add_fusion.where, f32[16,6912]{1,0:T(8,128)S(1)} %pad_maximum_fusion.own0, f32[16,6912]{1,0:T(8,128)S(1)} %collective-permute-done.12.oth0, f32[16,6912]{1,0:T(8,128)S(1)} %collective-permute-done.13.own1, f32[16,6912]{1,0:T(8,128)S(1)} %collective-permute-done.14.oth1, ...), custom_call_target="tpu_custom_call" | custom-call | tf_op jit(solution)/shard_map/pallas_call | solution.py:410
  101.0 5.8 %all-to-all-start = ((f32[16,1,128]{2,1,0:T(1,128)}), f32[16,1,128]{2,1,0:T(1,128)S(1)}, u32[]{:S(2)}, u32[]{:S(2)}) async-start(f32[16,1,128]{2,1,0:T(1,128)} %bitcast.5), calls=%async_computation | async-start | bytes 16384 | tf_op jit(solution)/shard_map/all_to_all | solution.py:578
  106.8 1.5 %shard_map.80 = f32[4,27648]{1,0:T(4,128)} custom-call(s32[4]{0:T(128)S(1)} %pad_add_fusion.where, f32[4,27648]{1,0:T(4,128)S(1)} %get-tuple-element.43.near, f32[4,27648]{1,0:T(4,128)S(1)} %collective-permute-done.6.far, f32[2,27648]{1,0:T(2,128)S(1)} %collective-permute-done.7.owed_a, f32[2,27648]{1,0:T(2,128)S(1)} %collective-permute-done.8.owed_b), custom_call_target="tpu_custom_call" | custom-call | tf_op jit(solution)/shard_map/pallas_call | solution.py:410
  108.3 4.1 %all-to-all-done = f32[16,1,128]{2,1,0:T(1,128)S(1)} async-done(((f32[16,1,128]{2,1,0:T(1,128)}), f32[16,1,128]{2,1,0:T(1,128)S(1)}, u32[]{:S(2)}, u32[]{:S(2)}) %all-to-all-start) | async-done | bytes 8224 | tf_op jit(solution)/shard_map/all_to_all | solution.py:578
  (50 shorter events, 10.4 us)
Async XLA Ops:
  0.6 25.0 %collective-permute-start = (f32[4,27648]{1,0:T(4,128)}, f32[4,27648]{1,0:T(4,128)S(1)}, u32[]{:S(2)}, u32[]{:S(2)}) collective-permute-start(f32[4,27648]{1,0:T(4,128)} %orbitals.3), channel_id=1, source_target_pairs={{0,2},{1,3},{2,0},{3,1},{4,6},{5,7},{6,4},{7,5},{8,10},{9,11},{10,... | collective-permute-start | bytes 1327112 | tf_op jit(solution)/shard_map/ppermute | solution.py:516
  4.5 21.2 %collective-permute-start.2 = (f32[2,27648]{1,0:T(2,128)S(1)}, f32[2,27648]{1,0:T(2,128)S(1)}, u32[]{:S(2)}, u32[]{:S(2)}) collective-permute-start(f32[2,27648]{1,0:T(2,128)S(1)} %get-tuple-element.29), channel_id=1, source_target_pairs={{0,4},{1,5},{2,6},{3,7},{4,8},{5,9},{6,10},{7,11},{8,12},{9,13},{1... | collective-permute-start | bytes 663560 | tf_op jit(solution)/shard_map/ppermute | solution.py:516
  7.0 18.6 %collective-permute-start.3 = (f32[2,27648]{1,0:T(2,128)S(1)}, f32[2,27648]{1,0:T(2,128)S(1)}, u32[]{:S(2)}, u32[]{:S(2)}) collective-permute-start(f32[2,27648]{1,0:T(2,128)S(1)} %get-tuple-element.30), channel_id=1, source_target_pairs={{0,6},{1,7},{2,4},{3,5},{4,10},{5,11},{6,8},{7,9},{8,14},{9,15},{1... | collective-permute-start | bytes 663560 | tf_op jit(solution)/shard_map/ppermute | solution.py:516
  26.4 8.0 %collective-permute-start.4 = (f32[8,27648]{1,0:T(8,128)S(1)}, f32[8,27648]{1,0:T(8,128)S(1)}, u32[]{:S(2)}, u32[]{:S(2)}) collective-permute-start(f32[8,27648]{1,0:T(8,128)S(1)} %shard_map.78), channel_id=1, source_target_pairs={{0,1},{1,0},{2,3},{3,2},{4,5},{5,4},{6,7},{7,6},{8,9},{9,8},{10,11... | collective-permute-start | bytes 2654216 | tf_op jit(solution)/shard_map/ppermute | solution.py:516
  28.0 6.4 %collective-permute-start.1 = (f32[4,27648]{1,0:T(4,128)}, f32[4,27648]{1,0:T(4,128)S(1)}, u32[]{:S(2)}, u32[]{:S(2)}) collective-permute-start(f32[4,27648]{1,0:T(4,128)} %orbitals.3), channel_id=1, source_target_pairs={{0,1},{1,0},{2,3},{3,2},{4,5},{5,4},{6,7},{7,6},{8,9},{9,8},{10,11... | collective-permute-start | bytes 1327112 | tf_op jit(solution)/shard_map/ppermute | solution.py:516
  29.7 22.3 %collective-permute-start.10 = (f32[4,6912]{1,0:T(4,128)S(1)}, f32[4,6912]{1,0:T(4,128)S(1)}, u32[]{:S(2)}, u32[]{:S(2)}) collective-permute-start(f32[4,6912]{1,0:T(4,128)S(1)} %get-tuple-element.49), channel_id=1, source_target_pairs={{0,16},{1,17},{2,18},{3,19},{4,20},{5,21},{6,22},{7,23},{8,24},{9,... | collective-permute-start | bytes 331784 | tf_op jit(solution)/shard_map/ppermute | solution.py:516
  29.8 22.2 %collective-permute-start.11 = (f32[4,6912]{1,0:T(4,128)S(1)}, f32[4,6912]{1,0:T(4,128)S(1)}, u32[]{:S(2)}, u32[]{:S(2)}) collective-permute-start(f32[4,6912]{1,0:T(4,128)S(1)} %get-tuple-element.50), channel_id=1, source_target_pairs={{0,24},{1,25},{2,26},{3,27},{4,28},{5,29},{6,30},{7,31},{8,16},{9,... | collective-permute-start | bytes 331784 | tf_op jit(solution)/shard_map/ppermute | solution.py:516
  29.9 22.1 %collective-permute-start.9 = (f32[4,6912]{1,0:T(4,128)S(1)}, f32[4,6912]{1,0:T(4,128)S(1)}, u32[]{:S(2)}, u32[]{:S(2)}) collective-permute-start(f32[4,6912]{1,0:T(4,128)S(1)} %get-tuple-element.48), channel_id=1, source_target_pairs={{0,8},{1,9},{2,10},{3,11},{4,12},{5,13},{6,14},{7,15},{8,0},{9,1},... | collective-permute-start | bytes 331784 | tf_op jit(solution)/shard_map/ppermute | solution.py:516
  34.5 1.0 copy-start.2
  50.7 14.8 %collective-permute-start.5 = (f32[10,27648]{1,0:T(8,128)S(1)}, f32[10,27648]{1,0:T(8,128)S(1)}, u32[]{:S(2)}, u32[]{:S(2)}) collective-permute-start(f32[10,27648]{1,0:T(8,128)S(1)} %get-tuple-element.42), channel_id=1, source_target_pairs={{0,1},{1,0},{2,3},{3,2},{4,5},{5,4},{6,7},{7,6},{8,9},{9,8},{10,11... | collective-permute-start | bytes 3317768 | tf_op jit(solution)/shard_map/ppermute | solution.py:516
  52.1 13.3 %collective-permute-start.12 = (f32[16,6912]{1,0:T(8,128)S(1)}, f32[16,6912]{1,0:T(8,128)S(1)}, u32[]{:S(2)}, u32[]{:S(2)}) collective-permute-start(f32[16,6912]{1,0:T(8,128)S(1)} %pad_maximum_fusion.own0), channel_id=1, source_target_pairs={{0,4},{1,5},{2,6},{3,7},{4,0},{5,1},{6,2},{7,3},{8,12},{9,13},{10,... | collective-permute-start | bytes 1327112 | tf_op jit(solution)/shard_map/ppermute | solution.py:516
  52.2 19.1 %collective-permute-start.13 = (f32[16,6912]{1,0:T(8,128)S(1)}, f32[16,6912]{1,0:T(8,128)S(1)}, u32[]{:S(2)}, u32[]{:S(2)}) collective-permute-start(f32[16,6912]{1,0:T(8,128)S(1)} %pad_maximum_fusion.own0), channel_id=1, source_target_pairs={{0,32},{1,33},{2,34},{3,35},{4,36},{5,37},{6,38},{7,39},{8,40},{9,... | collective-permute-start | bytes 1327112 | tf_op jit(solution)/shard_map/ppermute | solution.py:516
  65.4 12.0 %collective-permute-start.14 = (f32[16,6912]{1,0:T(8,128)S(1)}, f32[16,6912]{1,0:T(8,128)S(1)}, u32[]{:S(2)}, u32[]{:S(2)}) collective-permute-start(f32[16,6912]{1,0:T(8,128)S(1)} %collective-permute-done.12.oth0), channel_id=1, source_target_pairs={{0,32},{1,33},{2,34},{3,35},{4,36},{5,37},{6,38},{7,39},{8,40},{9,... | collective-permute-start | bytes 1327112 | tf_op jit(solution)/shard_map/ppermute | solution.py:516
  66.2 11.3 %collective-permute-start.7 = (f32[2,27648]{1,0:T(2,128)S(1)}, f32[2,27648]{1,0:T(2,128)S(1)}, u32[]{:S(2)}, u32[]{:S(2)}) collective-permute-start(f32[2,27648]{1,0:T(2,128)S(1)} %get-tuple-element.45), channel_id=1, source_target_pairs={{0,124},{1,125},{2,126},{3,127},{4,0},{5,1},{6,2},{7,3},{8,4},{9,5... | collective-permute-start | bytes 663560 | tf_op jit(solution)/shard_map/ppermute | solution.py:516
  69.0 11.2 %collective-permute-start.8 = (f32[2,27648]{1,0:T(2,128)S(1)}, f32[2,27648]{1,0:T(2,128)S(1)}, u32[]{:S(2)}, u32[]{:S(2)}) collective-permute-start(f32[2,27648]{1,0:T(2,128)S(1)} %get-tuple-element.46), channel_id=1, source_target_pairs={{0,126},{1,127},{2,124},{3,125},{4,2},{5,3},{6,0},{7,1},{8,6},{9,7... | collective-permute-start | bytes 663560 | tf_op jit(solution)/shard_map/ppermute | solution.py:516
  71.0 12.2 %collective-permute-start.6 = (f32[4,27648]{1,0:T(4,128)S(1)}, f32[4,27648]{1,0:T(4,128)S(1)}, u32[]{:S(2)}, u32[]{:S(2)}) collective-permute-start(f32[4,27648]{1,0:T(4,128)S(1)} %get-tuple-element.44), channel_id=1, source_target_pairs={{0,2},{1,3},{2,0},{3,1},{4,6},{5,7},{6,4},{7,5},{8,10},{9,11},{10,... | collective-permute-start | bytes 1327112 | tf_op jit(solution)/shard_map/ppermute | solution.py:516
  71.3 12.7 %collective-permute-start.17 = (f32[16,6912]{1,0:T(8,128)S(1)}, f32[16,6912]{1,0:T(8,128)S(1)}, u32[]{:S(2)}, u32[]{:S(2)}) collective-permute-start(f32[16,6912]{1,0:T(8,128)S(1)} %pad_maximum_fusion.own0), channel_id=1, source_target_pairs={{0,96},{1,97},{2,98},{3,99},{4,100},{5,101},{6,102},{7,103},{8,104... | collective-permute-start | bytes 1327112 | tf_op jit(solution)/shard_map/ppermute | solution.py:516
  77.5 11.2 %collective-permute-start.15 = (f32[16,6912]{1,0:T(8,128)S(1)}, f32[16,6912]{1,0:T(8,128)S(1)}, u32[]{:S(2)}, u32[]{:S(2)}) collective-permute-start(f32[16,6912]{1,0:T(8,128)S(1)} %collective-permute-done.13.own1), channel_id=1, source_target_pairs={{0,32},{1,33},{2,34},{3,35},{4,36},{5,37},{6,38},{7,39},{8,40},{9,... | collective-permute-start | bytes 1327112 | tf_op jit(solution)/shard_map/ppermute | solution.py:516
  77.5 13.1 %collective-permute-start.18 = (f32[16,6912]{1,0:T(8,128)S(1)}, f32[16,6912]{1,0:T(8,128)S(1)}, u32[]{:S(2)}, u32[]{:S(2)}) collective-permute-start(f32[16,6912]{1,0:T(8,128)S(1)} %collective-permute-done.12.oth0), channel_id=1, source_target_pairs={{0,96},{1,97},{2,98},{3,99},{4,100},{5,101},{6,102},{7,103},{8,104... | collective-permute-start | bytes 1327112 | tf_op jit(solution)/shard_map/ppermute | solution.py:516
  80.2 18.0 %collective-permute-start.16 = (f32[16,6912]{1,0:T(8,128)S(1)}, f32[16,6912]{1,0:T(8,128)S(1)}, u32[]{:S(2)}, u32[]{:S(2)}) collective-permute-start(f32[16,6912]{1,0:T(8,128)S(1)} %collective-permute-done.14.oth1), channel_id=1, source_target_pairs={{0,32},{1,33},{2,34},{3,35},{4,36},{5,37},{6,38},{7,39},{8,40},{9,... | collective-permute-start | bytes 1327112 | tf_op jit(solution)/shard_map/ppermute | solution.py:516
  84.0 14.2 %collective-permute-start.19 = (f32[4,6912]{1,0:T(4,128)S(1)}, f32[4,6912]{1,0:T(4,128)S(1)}, u32[]{:S(2)}, u32[]{:S(2)}) collective-permute-start(f32[4,6912]{1,0:T(4,128)S(1)} %get-tuple-element.53), channel_id=1, source_target_pairs={{0,8},{1,9},{2,10},{3,11},{4,12},{5,13},{6,14},{7,15},{8,0},{9,1},... | collective-permute-start | bytes 331784 | tf_op jit(solution)/shard_map/ppermute | solution.py:516
  84.1 14.1 %collective-permute-start.20 = (f32[4,6912]{1,0:T(4,128)S(1)}, f32[4,6912]{1,0:T(4,128)S(1)}, u32[]{:S(2)}, u32[]{:S(2)}) collective-permute-start(f32[4,6912]{1,0:T(4,128)S(1)} %get-tuple-element.54), channel_id=1, source_target_pairs={{0,16},{1,17},{2,18},{3,19},{4,20},{5,21},{6,22},{7,23},{8,24},{9,... | collective-permute-start | bytes 331784 | tf_op jit(solution)/shard_map/ppermute | solution.py:516
  88.7 9.5 %collective-permute-start.21 = (f32[4,6912]{1,0:T(4,128)S(1)}, f32[4,6912]{1,0:T(4,128)S(1)}, u32[]{:S(2)}, u32[]{:S(2)}) collective-permute-start(f32[4,6912]{1,0:T(4,128)S(1)} %get-tuple-element.55), channel_id=1, source_target_pairs={{0,24},{1,25},{2,26},{3,27},{4,28},{5,29},{6,30},{7,31},{8,16},{9,... | collective-permute-start | bytes 331784 | tf_op jit(solution)/shard_map/ppermute | solution.py:516
  101.0 11.4 %all-to-all-start = ((f32[16,1,128]{2,1,0:T(1,128)}), f32[16,1,128]{2,1,0:T(1,128)S(1)}, u32[]{:S(2)}, u32[]{:S(2)}) async-start(f32[16,1,128]{2,1,0:T(1,128)} %bitcast.5), calls=%async_computation | async-start | bytes 16384 | tf_op jit(solution)/shard_map/all_to_all | solution.py:578
  (6 other events, 5.4 us)

commit v10 on v9

--- a/solution.py
+++ b/solution.py
@@ -96,7 +96,9 @@
     return np.stack(slow).astype(np.float32), np.stack(fast).astype(np.float32)
 
 
-def tables_kernel(slow, fast, hi_there, lo_there, hi_back, lo_back):
+def tables_kernel(slow, fast, kern_in, third_in, hi_there, lo_there, hi_back, lo_back, kern, third):
+    kern[...] = kern_in[...]
+    third[...] = third_in[...]
     for way, (hi, lo) in enumerate(((hi_there, lo_there), (hi_back, lo_back))):
         for k in range(4):
             for u in range(16):
@@ -108,10 +110,11 @@
 
 def plane_tables():
     out = [jax.ShapeDtypeStruct((4, 256, 256), BF16)] * 4
+    out += [jax.ShapeDtypeStruct((NG, PLANE), F32), jax.ShapeDtypeStruct((16, 256), F32)]
     return pl.pallas_call(
         tables_kernel, out_shape=out, name="plane_tables",
         compiler_params=pltpu.CompilerParams(vmem_limit_bytes=8 << 20),
-    )(*[jnp.asarray(a) for a in factor_tables()])
+    )(*[jnp.asarray(a) for a in (*factor_tables(), kernel_values(), thirds())])
 
 
 def t16(f):
@@ -231,19 +234,19 @@
     return [a + c * third[first + m] + s * third[first + 3 + m] for m in range(3)]
 
 
-def spectrum_kernel(q_ref, own, two, one, low_a, low_b, core, kern, third, whi, wlo, right, left, field, hi, lo):
+def spectrum_kernel(q_ref, own, one, two, three, low_a, core_a, low_b, core_b, kern, third, whi, wlo, right, left, field, hi, lo):
     q = q_ref[0]
     sources = (
-        (own, 0, low_a, 0),
-        (one, 0, core, 4),
-        (two, 0, low_b, 0),
-        (core, 0, core, 6),
+        (own, low_a),
+        (one, core_a),
+        (two, low_b),
+        (three, core_b),
     )
     sub = lax.broadcasted_iota(jnp.int32, (8, 128), 0)
     to_right = sub % 4
     to_left = jnp.where(sub < 4, q, 4 + q % 2)
     place = lax.broadcasted_iota(jnp.int32, (8, 128), 1) // 16 % 3
-    for delta, (bands_ref, first, low_ref, low_first) in enumerate(sources):
+    for delta, (bands_ref, low_ref) in enumerate(sources):
         base = (q ^ delta) * QX
 
         def densities(i, carry):
@@ -257,8 +260,8 @@
                         v = []
                         for n in range(3):
                             at = pl.ds(pl.multiple_of((2 * i + half) * PLANE + (m * SLAB + h * 384 + n * 128), 128), 128)
-                            low = low_ref[low_first : low_first + 2, at]
-                            v.append(jnp.concatenate([bands_ref[first : first + 4, at], low, low], axis=0))
+                            low = low_ref[:, at]
+                            v.append(jnp.concatenate([bands_ref[:, at], low, low], axis=0))
                         for j in range(3):
                             got = jnp.where(place == j, v[0], jnp.where(place == (j + 1) % 3, v[1], v[2]))
                             got = turn(got, -16 * j)
@@ -375,19 +378,19 @@
 SPLIT = [pltpu.VMEM((NG * 8, PLANE), BF16)] * 2
 
 
-def spectrum(q, bands, tables):
+def spectrum(q, bands, kern, third, tables):
     return pl.pallas_call(
         spectrum_kernel,
         out_shape=[jax.ShapeDtypeStruct((NG, 8, PLANE), F32)] * 2 + [jax.ShapeDtypeStruct((NG * 8, PLANE), F32)],
-        in_specs=[SMEM_SPEC] + [VMEM_SPEC] * 10,
+        in_specs=[SMEM_SPEC] + [VMEM_SPEC] * 12,
         out_specs=[VMEM_SPEC] * 3,
         scratch_shapes=SPLIT,
         name="spectrum",
         compiler_params=pltpu.CompilerParams(vmem_limit_bytes=24 << 20),
-    )(q.reshape(1), *bands, jnp.asarray(kernel_values()), jnp.asarray(thirds()), *tables)
-
-
-def terms(q, right, left, field, tables):
+    )(q.reshape(1), *bands, kern, third, *tables)
+
+
+def terms(q, right, left, field, third, tables):
     return pl.pallas_call(
         terms_kernel,
         out_shape=[jax.ShapeDtypeStruct(shape, F32) for shape in [(4, QCELL)] * 2 + [(10, QCELL)] + [(1, QCELL)] * 2],
@@ -396,7 +399,7 @@
         scratch_shapes=SPLIT + [pltpu.VMEM((NG * 8, PLANE), F32)],
         name="terms",
         compiler_params=pltpu.CompilerParams(vmem_limit_bytes=28 << 20),
-    )(q.reshape(1), right, left, field, jnp.asarray(thirds()), *tables)
+    )(q.reshape(1), right, left, field, third, *tables)
 
 
 BOTH = ("band", "grid")
@@ -435,12 +438,6 @@
         chunks[k][...] = orbitals[:, chunk_of(where, k)]
 
 
-def stack_kernel(where, two, low_a, low_b, out):
-    out[0:4, :] = two[...]
-    out[4:6, :] = low_a[...]
-    out[6:8, :] = low_b[...]
-
-
 def merge_kernel(where, near0, near2, low0, low2, across, near, far, owed_a, owed_b):
     first = where[0] % 2 == 0
     near[...] = near0[...] + across[0:4, :]
@@ -476,15 +473,12 @@
         top = a.astype(BF16)
         return top, (a - top.astype(F32)).astype(BF16)
 
-    vt, vl = halves(jnp.concatenate([v0[...], v1[...], v2[...], v3[...]], axis=0))
-    dims = (((1,), (1,)), ((), ()))
+    v = jnp.concatenate(halves(jnp.concatenate([v0[...], v1[...], v2[...], v3[...]], axis=0)), axis=0)
     parts = jnp.concatenate([r[...] for r in (own0, oth0, own1, oth1, own2, oth2, own3, oth3)], axis=0)
-    ft, fl = halves(parts)
-    got = (
-        lax.dot_general(ft, vt, dims, preferred_element_type=F32)
-        + lax.dot_general(fl, vt, dims, preferred_element_type=F32)
-        + lax.dot_general(ft, vl, dims, preferred_element_type=F32)
-    )
+    f = jnp.concatenate(halves(parts), axis=0)
+    both = lax.dot_general(f, v, (((1,), (1,)), ((), ())), preferred_element_type=F32)
+    both = both[0:128, :] + both[128:256, :]
+    got = both[:, 0:16] + both[:, 16:32]
     for dz in range(4):
         for dy in range(4):
             row = 32 * dz + 4 * dy
@@ -548,26 +542,27 @@
     one = within(orbitals, 1)
     pc = small_call(chunks_kernel, [(4, CHUNK)] * 4)(where, orbitals)
     pieces = [pc[0]] + [along_y(pc[k], k) for k in (1, 2, 3)]
-    tables = plane_tables()
+    *tables, kern, third = plane_tables()
     together = jnp.concatenate(pieces, axis=0)
-    (stacked,) = small_call(stack_kernel, [(8, QCELL)])(where, two, low_a, low_b)
-    core = within(stacked, 1)
+    core_a = within(low_a, 1)
+    core_b = within(low_b, 1)
+    three = within(two, 1)
     other = move(together, lambda z, y, h, q: (z, y, 1 - h, q))
+    right, left, field = spectrum(q, (orbitals, one, two, three, low_a, core_a, low_b, core_b), kern, third, tables[:2])
+    near0, near2, cross, low0, low2 = terms(q, right, left, field, third, tables[2:4])
+    across = within(cross, 1)
+    together, other, _ = lax.optimization_barrier((together, other, near0))
     own1 = along_z(together, 1)
     own3 = along_z(together, 3)
-    right, left, field = spectrum(q, (orbitals, two, one, low_a, low_b, core), tables[:2])
-    near0, near2, cross, low0, low2 = terms(q, right, left, field, tables[2:])
-    across = within(cross, 1)
-    other, _ = lax.optimization_barrier((other, near0))
-    oth1 = along_z(other, 1)
-    oth3 = along_z(other, 3)
-    own2 = along_z(own1, 1)
     merge = small_call(merge_kernel, [(4, QCELL)] * 2 + [(2, QCELL)] * 2)
     near, both, owe_a, owe_b = merge(where, near0, near2, low0, low2, across)
     far = within(both, 2)
     owed_a = around(owe_a, -1, 0)
     owed_b = around(owe_b, -1, 2)
-    oth2 = along_z(oth1, 1)
+    oth1 = along_z(other, 1)
+    oth3 = along_z(other, 3)
+    own2 = along_z(own1, 1)
+    oth2 = along_z(oth3, 3)
     finalize = small_call(finalize_kernel, [(4, CHUNK)] * 4)
     vc = finalize(where, near, far, owed_a, owed_b)
     (vectors,) = small_call(vectors_kernel, [(4, QCELL)])(where, near, far, owed_a, owed_b)

time: 114 us -> 117 us (1.026)
  the two profiles are of different devices: /device:TPU:1 before, /device:TPU:5 now
where the time goes in v10:
time: 117 us; the launch traced here: 116 us
  starting transfers between devices  55.4 us (47%)
  waiting for transfers between devices  33.6 us (29%)
  Pallas kernels  22.5 us (19%)
  local copies, waits for them, and re-layouts  4.07 us (3%)
    ppermute x24, starting transfers between devices, move(): return lax.ppermute(value, BOTH, pairs)  43.9 us
    ppermute x24, waiting for transfers between devices, move(): return lax.ppermute(value, BOTH, pairs)  29.6 us
    all_to_all x1, starting transfers between devices, step(): lax.all_to_all(sums, BOTH, 0, 0, tiled=True, axis_index_groups=groups)  11.5 us
    pallas_call x1, Pallas kernels, spectrum(): pl.pallas_call(spectrum_kernel, out_shape=[jax.ShapeDtypeStruct((NG, 8, P...  8.72 us
    pallas_call x6, Pallas kernels, call(): pl.pallas_call(body, out_shape=[jax.ShapeDtypeStruct(shape, F32) for shap...  7.57 us
    pallas_call x1, Pallas kernels, terms(): pl.pallas_call(terms_kernel, out_shape=[jax.ShapeDtypeStruct(shape, F32)...  5.85 us
    all_to_all x1, waiting for transfers between devices, step(): lax.all_to_all(sums, BOTH, 0, 0, tiled=True, axis_index_groups=groups)  4.01 us
    unnamed x8, local copies, waits for them, and re-layouts  3.41 us
  transfers between devices with their start and end apart: 25, of which 9 were waited for; matrix products, arithmetic and copies ran while one was open for 0% of the time, Pallas kernels for 17%

profile of v10, /device:TPU:5, one launch (start us, length us, event | category | flops | bytes accessed | tf_op | source)
XLA Modules:
  0.0 116.4 jit_solution(14521051148920565119)
XLA Ops:
  2.9 1.6 %collective-permute-start.3 = (f32[2,27648]{1,0:T(2,128)S(1)}, f32[2,27648]{1,0:T(2,128)S(1)}, u32[]{:S(2)}, u32[]{:S(2)}) collective-permute-start(f32[2,27648]{1,0:T(2,128)S(1)} %get-tuple-element.32), channel_id=1, source_target_pairs={{0,4},{1,5},{2,6},{3,7},{4,8},{5,9},{6,10},{7,11},{8,12},{9,13},{1... | collective-permute-start | bytes 663560 | tf_op jit(solution)/shard_map/ppermute | solution.py:510
  5.7 1.5 %collective-permute-start = (f32[4,27648]{1,0:T(4,128)}, f32[4,27648]{1,0:T(4,128)S(1)}, u32[]{:S(2)}, u32[]{:S(2)}) collective-permute-start(f32[4,27648]{1,0:T(4,128)} %orbitals.3), channel_id=1, source_target_pairs={{0,1},{1,0},{2,3},{3,2},{4,5},{5,4},{6,7},{7,6},{8,9},{9,8},{10,11... | collective-permute-start | bytes 1327112 | tf_op jit(solution)/shard_map/ppermute | solution.py:510
  7.2 4.8 %collective-permute-done.1.two = f32[4,27648]{1,0:T(4,128)S(1)} collective-permute-done((f32[4,27648]{1,0:T(4,128)}, f32[4,27648]{1,0:T(4,128)S(1)}, u32[]{:S(2)}, u32[]{:S(2)}) %collective-permute-start.1) | collective-permute-done | bytes 442400 | tf_op jit(solution)/shard_map/ppermute | solution.py:510
  12.0 2.7 %collective-permute-start.2 = (f32[4,27648]{1,0:T(4,128)S(1)}, f32[4,27648]{1,0:T(4,128)S(1)}, u32[]{:S(2)}, u32[]{:S(2)}) collective-permute-start(f32[4,27648]{1,0:T(4,128)S(1)} %collective-permute-done.1.two), channel_id=1, source_target_pairs={{0,1},{1,0},{2,3},{3,2},{4,5},{5,4},{6,7},{7,6},{8,9},{9,8},{10,11... | collective-permute-start | bytes 1327112 | tf_op jit(solution)/shard_map/ppermute | solution.py:510
  14.6 2.0 %collective-permute-done.3.low_a = f32[2,27648]{1,0:T(2,128)S(1)} collective-permute-done((f32[2,27648]{1,0:T(2,128)S(1)}, f32[2,27648]{1,0:T(2,128)S(1)}, u32[]{:S(2)}, u32[]{:S(2)}) %collective-permute-start.3) | collective-permute-done | bytes 221216 | tf_op jit(solution)/shard_map/ppermute | solution.py:510
  16.7 1.5 %collective-permute-start.4 = (f32[2,27648]{1,0:T(2,128)S(1)}, f32[2,27648]{1,0:T(2,128)S(1)}, u32[]{:S(2)}, u32[]{:S(2)}) collective-permute-start(f32[2,27648]{1,0:T(2,128)S(1)} %collective-permute-done.3.low_a), channel_id=1, source_target_pairs={{0,1},{1,0},{2,3},{3,2},{4,5},{5,4},{6,7},{7,6},{8,9},{9,8},{10,11... | collective-permute-start | bytes 663560 | tf_op jit(solution)/shard_map/ppermute | solution.py:510
  20.7 2.6 %collective-permute-start.12 = (f32[4,6912]{1,0:T(4,128)S(1)}, f32[4,6912]{1,0:T(4,128)S(1)}, u32[]{:S(2)}, u32[]{:S(2)}) collective-permute-start(f32[4,6912]{1,0:T(4,128)S(1)} %get-tuple-element.54), channel_id=1, source_target_pairs={{0,16},{1,17},{2,18},{3,19},{4,20},{5,21},{6,22},{7,23},{8,24},{9,... | collective-permute-start | bytes 331784 | tf_op jit(solution)/shard_map/ppermute | solution.py:510
  27.1 8.7 %spectrum.1 = (f32[48,8,2304]{2,1,0:T(8,128)S(1)}, f32[48,8,2304]{2,1,0:T(8,128)S(1)}, f32[384,2304]{1,0:T(8,128)S(1)}) custom-call(s32[1]{0:T(128)} %bitcast.q_ref, f32[4,27648]{1,0:T(4,128)} %orbitals.3, f32[4,27648]{1,0:T(4,128)S(1)} %collective-permute-done.one, f32[4,27648]{1,0:T(4,128)S(1)} %collective-permute-done.1.two, ...), custom_call_target="tpu_custom_call" | custom-call | tf_op jit(solution)/shard_map/spectrum/pallas_call | solution.py:382
  35.8 5.9 %terms.1 = (f32[4,27648]{1,0:T(4,128)S(1)}, f32[4,27648]{1,0:T(4,128)S(1)}, f32[10,27648]{1,0:T(8,128)S(1)}, f32[1,27648]{1,0:T(1,128)S(1)}, f32[1,27648]{1,0:T(1,128)S(1)}) custom-call(s32[1]{0:T(128)} %bitcast.q_ref, f32[48,8,2304]{2,1,0:T(8,128)S(1)} %get-tuple-element.38.right, f32[48,8,2304]{2,1,0:T(8,128)S(1)} %get-tuple-element.39.left, ...), custom_call_target="tpu_custom_call" | custom-call | tf_op jit(solution)/shard_map/terms/pallas_call | solution.py:394
  43.2 8.5 %collective-permute-start.14 = (f32[16,6912]{1,0:T(8,128)S(1)}, f32[16,6912]{1,0:T(8,128)S(1)}, u32[]{:S(2)}, u32[]{:S(2)}) collective-permute-start(f32[16,6912]{1,0:T(8,128)S(1)} %pad_maximum_fusion.own0), channel_id=1, source_target_pairs={{0,4},{1,5},{2,6},{3,7},{4,0},{5,1},{6,2},{7,3},{8,12},{9,13},{10,... | collective-permute-start | bytes 1327112 | tf_op jit(solution)/shard_map/ppermute | solution.py:510
  51.6 10.5 %collective-permute-done.14.oth0 = f32[16,6912]{1,0:T(8,128)S(1)} collective-permute-done((f32[16,6912]{1,0:T(8,128)S(1)}, f32[16,6912]{1,0:T(8,128)S(1)}, u32[]{:S(2)}, u32[]{:S(2)}) %collective-permute-start.14) | collective-permute-done | bytes 442400 | tf_op jit(solution)/shard_map/ppermute | solution.py:510
  62.1 2.7 %collective-permute-start.18 = (f32[16,6912]{1,0:T(8,128)S(1)}, f32[16,6912]{1,0:T(8,128)S(1)}, u32[]{:S(2)}, u32[]{:S(2)}) collective-permute-start(f32[16,6912]{1,0:T(8,128)S(1)} %collective-permute-done.14.oth0), channel_id=1, source_target_pairs={{0,96},{1,97},{2,98},{3,99},{4,100},{5,101},{6,102},{7,103},{8,104... | collective-permute-start | bytes 1327112 | tf_op jit(solution)/shard_map/ppermute | solution.py:510
  65.5 1.5 %collective-permute-start.10 = (f32[2,27648]{1,0:T(2,128)S(1)}, f32[2,27648]{1,0:T(2,128)S(1)}, u32[]{:S(2)}, u32[]{:S(2)}) collective-permute-start(f32[2,27648]{1,0:T(2,128)S(1)} %get-tuple-element.51), channel_id=1, source_target_pairs={{0,126},{1,127},{2,124},{3,125},{4,2},{5,3},{6,0},{7,1},{8,6},{9,7... | collective-permute-start | bytes 663560 | tf_op jit(solution)/shard_map/ppermute | solution.py:510
  69.2 5.3 %collective-permute-done.15.own1 = f32[16,6912]{1,0:T(8,128)S(1)} collective-permute-done((f32[16,6912]{1,0:T(8,128)S(1)}, f32[16,6912]{1,0:T(8,128)S(1)}, u32[]{:S(2)}, u32[]{:S(2)}) %collective-permute-start.15) | collective-permute-done | bytes 442400 | tf_op jit(solution)/shard_map/ppermute | solution.py:510
  74.5 2.7 %collective-permute-start.20 = (f32[16,6912]{1,0:T(8,128)S(1)}, f32[16,6912]{1,0:T(8,128)S(1)}, u32[]{:S(2)}, u32[]{:S(2)}) collective-permute-start(f32[16,6912]{1,0:T(8,128)S(1)} %pad_maximum_fusion.own0), channel_id=1, source_target_pairs={{0,96},{1,97},{2,98},{3,99},{4,100},{5,101},{6,102},{7,103},{8,104... | collective-permute-start | bytes 1327112 | tf_op jit(solution)/shard_map/ppermute | solution.py:510
  77.2 2.7 %collective-permute-start.19 = (f32[16,6912]{1,0:T(8,128)S(1)}, f32[16,6912]{1,0:T(8,128)S(1)}, u32[]{:S(2)}, u32[]{:S(2)}) collective-permute-start(f32[16,6912]{1,0:T(8,128)S(1)} %collective-permute-done.18.oth3), channel_id=1, source_target_pairs={{0,96},{1,97},{2,98},{3,99},{4,100},{5,101},{6,102},{7,103},{8,104... | collective-permute-start | bytes 1327112 | tf_op jit(solution)/shard_map/ppermute | solution.py:510
  79.8 3.0 %collective-permute-done.8.far = f32[4,27648]{1,0:T(4,128)S(1)} collective-permute-done((f32[4,27648]{1,0:T(4,128)S(1)}, f32[4,27648]{1,0:T(4,128)S(1)}, u32[]{:S(2)}, u32[]{:S(2)}) %collective-permute-start.8) | collective-permute-done | bytes 442400 | tf_op jit(solution)/shard_map/ppermute | solution.py:510
  85.9 4.8 %collective-permute-start.22 = (f32[4,6912]{1,0:T(4,128)S(1)}, f32[4,6912]{1,0:T(4,128)S(1)}, u32[]{:S(2)}, u32[]{:S(2)}) collective-permute-start(f32[4,6912]{1,0:T(4,128)S(1)} %get-tuple-element.60), channel_id=1, source_target_pairs={{0,16},{1,17},{2,18},{3,19},{4,20},{5,21},{6,22},{7,23},{8,24},{9,... | collective-permute-start | bytes 331784 | tf_op jit(solution)/shard_map/ppermute | solution.py:510
  90.8 3.1 %collective-permute-start.23 = (f32[4,6912]{1,0:T(4,128)S(1)}, f32[4,6912]{1,0:T(4,128)S(1)}, u32[]{:S(2)}, u32[]{:S(2)}) collective-permute-start(f32[4,6912]{1,0:T(4,128)S(1)} %get-tuple-element.61), channel_id=1, source_target_pairs={{0,24},{1,25},{2,26},{3,27},{4,28},{5,29},{6,30},{7,31},{8,16},{9,... | collective-permute-start | bytes 331784 | tf_op jit(solution)/shard_map/ppermute | solution.py:510
  93.8 1.6 %collective-permute-done.17.own2 = f32[16,6912]{1,0:T(8,128)S(1)} collective-permute-done((f32[16,6912]{1,0:T(8,128)S(1)}, f32[16,6912]{1,0:T(8,128)S(1)}, u32[]{:S(2)}, u32[]{:S(2)}) %collective-permute-start.17) | collective-permute-done | bytes 442400 | tf_op jit(solution)/shard_map/ppermute | solution.py:510
  96.3 2.4 %shard_map.73 = f32[16,128]{1,0:T(8,128)} custom-call(s32[4]{0:T(128)S(1)} %pad_add_fusion.where, f32[16,6912]{1,0:T(8,128)S(1)} %pad_maximum_fusion.own0, f32[16,6912]{1,0:T(8,128)S(1)} %collective-permute-done.14.oth0, f32[16,6912]{1,0:T(8,128)S(1)} %collective-permute-done.15.own1, f32[16,6912]{1,0:T(8,128)S(1)} %collective-permute-done.16.oth1, ...), custom_call_target="tpu_custom_call" | custom-call | tf_op jit(solution)/shard_map/pallas_call | solution.py:413
  98.7 11.5 %all-to-all-start = ((f32[16,1,128]{2,1,0:T(1,128)}), f32[16,1,128]{2,1,0:T(1,128)S(1)}, u32[]{:S(2)}, u32[]{:S(2)}) async-start(f32[16,1,128]{2,1,0:T(1,128)} %bitcast.5), calls=%async_computation | async-start | bytes 16384 | tf_op jit(solution)/shard_map/all_to_all | solution.py:573
  110.2 1.5 %shard_map.70 = f32[4,27648]{1,0:T(4,128)} custom-call(s32[4]{0:T(128)S(1)} %pad_add_fusion.where, f32[4,27648]{1,0:T(4,128)S(1)} %get-tuple-element.48.near, f32[4,27648]{1,0:T(4,128)S(1)} %collective-permute-done.8.far, f32[2,27648]{1,0:T(2,128)S(1)} %collective-permute-done.9.owed_a, f32[2,27648]{1,0:T(2,128)S(1)} %collective-permute-done.10.owed_b), custom_call_target="tpu_custom_call" | custom-call | tf_op jit(solution)/shard_map/pallas_call | solution.py:413
  111.7 4.0 %all-to-all-done = f32[16,1,128]{2,1,0:T(1,128)S(1)} async-done(((f32[16,1,128]{2,1,0:T(1,128)}), f32[16,1,128]{2,1,0:T(1,128)S(1)}, u32[]{:S(2)}, u32[]{:S(2)}) %all-to-all-start) | async-done | bytes 8224 | tf_op jit(solution)/shard_map/all_to_all | solution.py:573
  (47 shorter events, 18.7 us)
Async XLA Ops:
  0.6 11.3 %collective-permute-start.1 = (f32[4,27648]{1,0:T(4,128)}, f32[4,27648]{1,0:T(4,128)S(1)}, u32[]{:S(2)}, u32[]{:S(2)}) collective-permute-start(f32[4,27648]{1,0:T(4,128)} %orbitals.3), channel_id=1, source_target_pairs={{0,2},{1,3},{2,0},{3,1},{4,6},{5,7},{6,4},{7,5},{8,10},{9,11},{10,... | collective-permute-start | bytes 1327112 | tf_op jit(solution)/shard_map/ppermute | solution.py:510
  2.9 13.8 %collective-permute-start.3 = (f32[2,27648]{1,0:T(2,128)S(1)}, f32[2,27648]{1,0:T(2,128)S(1)}, u32[]{:S(2)}, u32[]{:S(2)}) collective-permute-start(f32[2,27648]{1,0:T(2,128)S(1)} %get-tuple-element.32), channel_id=1, source_target_pairs={{0,4},{1,5},{2,6},{3,7},{4,8},{5,9},{6,10},{7,11},{8,12},{9,13},{1... | collective-permute-start | bytes 663560 | tf_op jit(solution)/shard_map/ppermute | solution.py:510
  4.5 13.8 %collective-permute-start.5 = (f32[2,27648]{1,0:T(2,128)S(1)}, f32[2,27648]{1,0:T(2,128)S(1)}, u32[]{:S(2)}, u32[]{:S(2)}) collective-permute-start(f32[2,27648]{1,0:T(2,128)S(1)} %get-tuple-element.33), channel_id=1, source_target_pairs={{0,6},{1,7},{2,4},{3,5},{4,10},{5,11},{6,8},{7,9},{8,14},{9,15},{1... | collective-permute-start | bytes 663560 | tf_op jit(solution)/shard_map/ppermute | solution.py:510
  5.7 21.4 %collective-permute-start = (f32[4,27648]{1,0:T(4,128)}, f32[4,27648]{1,0:T(4,128)S(1)}, u32[]{:S(2)}, u32[]{:S(2)}) collective-permute-start(f32[4,27648]{1,0:T(4,128)} %orbitals.3), channel_id=1, source_target_pairs={{0,1},{1,0},{2,3},{3,2},{4,5},{5,4},{6,7},{7,6},{8,9},{9,8},{10,11... | collective-permute-start | bytes 1327112 | tf_op jit(solution)/shard_map/ppermute | solution.py:510
  12.0 15.1 %collective-permute-start.2 = (f32[4,27648]{1,0:T(4,128)S(1)}, f32[4,27648]{1,0:T(4,128)S(1)}, u32[]{:S(2)}, u32[]{:S(2)}) collective-permute-start(f32[4,27648]{1,0:T(4,128)S(1)} %collective-permute-done.1.two), channel_id=1, source_target_pairs={{0,1},{1,0},{2,3},{3,2},{4,5},{5,4},{6,7},{7,6},{8,9},{9,8},{10,11... | collective-permute-start | bytes 1327112 | tf_op jit(solution)/shard_map/ppermute | solution.py:510
  18.2 5.1 %collective-permute-start.6 = (f32[2,27648]{1,0:T(2,128)S(1)}, f32[2,27648]{1,0:T(2,128)S(1)}, u32[]{:S(2)}, u32[]{:S(2)}) collective-permute-start(f32[2,27648]{1,0:T(2,128)S(1)} %collective-permute-done.5.low_b), channel_id=1, source_target_pairs={{0,1},{1,0},{2,3},{3,2},{4,5},{5,4},{6,7},{7,6},{8,9},{9,8},{10,11... | collective-permute-start | bytes 663560 | tf_op jit(solution)/shard_map/ppermute | solution.py:510
  19.3 23.8 %collective-permute-start.11 = (f32[4,6912]{1,0:T(4,128)S(1)}, f32[4,6912]{1,0:T(4,128)S(1)}, u32[]{:S(2)}, u32[]{:S(2)}) collective-permute-start(f32[4,6912]{1,0:T(4,128)S(1)} %get-tuple-element.53), channel_id=1, source_target_pairs={{0,8},{1,9},{2,10},{3,11},{4,12},{5,13},{6,14},{7,15},{8,0},{9,1},... | collective-permute-start | bytes 331784 | tf_op jit(solution)/shard_map/ppermute | solution.py:510
  20.7 22.4 %collective-permute-start.12 = (f32[4,6912]{1,0:T(4,128)S(1)}, f32[4,6912]{1,0:T(4,128)S(1)}, u32[]{:S(2)}, u32[]{:S(2)}) collective-permute-start(f32[4,6912]{1,0:T(4,128)S(1)} %get-tuple-element.54), channel_id=1, source_target_pairs={{0,16},{1,17},{2,18},{3,19},{4,20},{5,21},{6,22},{7,23},{8,24},{9,... | collective-permute-start | bytes 331784 | tf_op jit(solution)/shard_map/ppermute | solution.py:510
  23.3 19.8 %collective-permute-start.13 = (f32[4,6912]{1,0:T(4,128)S(1)}, f32[4,6912]{1,0:T(4,128)S(1)}, u32[]{:S(2)}, u32[]{:S(2)}) collective-permute-start(f32[4,6912]{1,0:T(4,128)S(1)} %get-tuple-element.55), channel_id=1, source_target_pairs={{0,24},{1,25},{2,26},{3,27},{4,28},{5,29},{6,30},{7,31},{8,16},{9,... | collective-permute-start | bytes 331784 | tf_op jit(solution)/shard_map/ppermute | solution.py:510
  41.7 23.1 %collective-permute-start.7 = (f32[10,27648]{1,0:T(8,128)S(1)}, f32[10,27648]{1,0:T(8,128)S(1)}, u32[]{:S(2)}, u32[]{:S(2)}) collective-permute-start(f32[10,27648]{1,0:T(8,128)S(1)} %get-tuple-element.47), channel_id=1, source_target_pairs={{0,1},{1,0},{2,3},{3,2},{4,5},{5,4},{6,7},{7,6},{8,9},{9,8},{10,11... | collective-permute-start | bytes 3317768 | tf_op jit(solution)/shard_map/ppermute | solution.py:510
  43.2 19.0 %collective-permute-start.14 = (f32[16,6912]{1,0:T(8,128)S(1)}, f32[16,6912]{1,0:T(8,128)S(1)}, u32[]{:S(2)}, u32[]{:S(2)}) collective-permute-start(f32[16,6912]{1,0:T(8,128)S(1)} %pad_maximum_fusion.own0), channel_id=1, source_target_pairs={{0,4},{1,5},{2,6},{3,7},{4,0},{5,1},{6,2},{7,3},{8,12},{9,13},{10,... | collective-permute-start | bytes 1327112 | tf_op jit(solution)/shard_map/ppermute | solution.py:510
  62.1 12.3 %collective-permute-start.15 = (f32[16,6912]{1,0:T(8,128)S(1)}, f32[16,6912]{1,0:T(8,128)S(1)}, u32[]{:S(2)}, u32[]{:S(2)}) collective-permute-start(f32[16,6912]{1,0:T(8,128)S(1)} %pad_maximum_fusion.own0), channel_id=1, source_target_pairs={{0,32},{1,33},{2,34},{3,35},{4,36},{5,37},{6,38},{7,39},{8,40},{9,... | collective-permute-start | bytes 1327112 | tf_op jit(solution)/shard_map/ppermute | solution.py:510
  62.1 12.3 %collective-permute-start.18 = (f32[16,6912]{1,0:T(8,128)S(1)}, f32[16,6912]{1,0:T(8,128)S(1)}, u32[]{:S(2)}, u32[]{:S(2)}) collective-permute-start(f32[16,6912]{1,0:T(8,128)S(1)} %collective-permute-done.14.oth0), channel_id=1, source_target_pairs={{0,96},{1,97},{2,98},{3,99},{4,100},{5,101},{6,102},{7,103},{8,104... | collective-permute-start | bytes 1327112 | tf_op jit(solution)/shard_map/ppermute | solution.py:510
  65.5 11.6 %collective-permute-start.10 = (f32[2,27648]{1,0:T(2,128)S(1)}, f32[2,27648]{1,0:T(2,128)S(1)}, u32[]{:S(2)}, u32[]{:S(2)}) collective-permute-start(f32[2,27648]{1,0:T(2,128)S(1)} %get-tuple-element.51), channel_id=1, source_target_pairs={{0,126},{1,127},{2,124},{3,125},{4,2},{5,3},{6,0},{7,1},{8,6},{9,7... | collective-permute-start | bytes 663560 | tf_op jit(solution)/shard_map/ppermute | solution.py:510
  67.0 10.1 %collective-permute-start.9 = (f32[2,27648]{1,0:T(2,128)S(1)}, f32[2,27648]{1,0:T(2,128)S(1)}, u32[]{:S(2)}, u32[]{:S(2)}) collective-permute-start(f32[2,27648]{1,0:T(2,128)S(1)} %get-tuple-element.50), channel_id=1, source_target_pairs={{0,124},{1,125},{2,126},{3,127},{4,0},{5,1},{6,2},{7,3},{8,4},{9,5... | collective-permute-start | bytes 663560 | tf_op jit(solution)/shard_map/ppermute | solution.py:510
  68.4 14.5 %collective-permute-start.8 = (f32[4,27648]{1,0:T(4,128)S(1)}, f32[4,27648]{1,0:T(4,128)S(1)}, u32[]{:S(2)}, u32[]{:S(2)}) collective-permute-start(f32[4,27648]{1,0:T(4,128)S(1)} %get-tuple-element.49), channel_id=1, source_target_pairs={{0,2},{1,3},{2,0},{3,1},{4,6},{5,7},{6,4},{7,5},{8,10},{9,11},{10,... | collective-permute-start | bytes 1327112 | tf_op jit(solution)/shard_map/ppermute | solution.py:510
  74.5 11.5 %collective-permute-start.16 = (f32[16,6912]{1,0:T(8,128)S(1)}, f32[16,6912]{1,0:T(8,128)S(1)}, u32[]{:S(2)}, u32[]{:S(2)}) collective-permute-start(f32[16,6912]{1,0:T(8,128)S(1)} %collective-permute-done.14.oth0), channel_id=1, source_target_pairs={{0,32},{1,33},{2,34},{3,35},{4,36},{5,37},{6,38},{7,39},{8,40},{9,... | collective-permute-start | bytes 1327112 | tf_op jit(solution)/shard_map/ppermute | solution.py:510
  74.5 16.3 %collective-permute-start.20 = (f32[16,6912]{1,0:T(8,128)S(1)}, f32[16,6912]{1,0:T(8,128)S(1)}, u32[]{:S(2)}, u32[]{:S(2)}) collective-permute-start(f32[16,6912]{1,0:T(8,128)S(1)} %pad_maximum_fusion.own0), channel_id=1, source_target_pairs={{0,96},{1,97},{2,98},{3,99},{4,100},{5,101},{6,102},{7,103},{8,104... | collective-permute-start | bytes 1327112 | tf_op jit(solution)/shard_map/ppermute | solution.py:510
  77.1 18.3 %collective-permute-start.17 = (f32[16,6912]{1,0:T(8,128)S(1)}, f32[16,6912]{1,0:T(8,128)S(1)}, u32[]{:S(2)}, u32[]{:S(2)}) collective-permute-start(f32[16,6912]{1,0:T(8,128)S(1)} %collective-permute-done.15.own1), channel_id=1, source_target_pairs={{0,32},{1,33},{2,34},{3,35},{4,36},{5,37},{6,38},{7,39},{8,40},{9,... | collective-permute-start | bytes 1327112 | tf_op jit(solution)/shard_map/ppermute | solution.py:510
  77.2 18.3 %collective-permute-start.19 = (f32[16,6912]{1,0:T(8,128)S(1)}, f32[16,6912]{1,0:T(8,128)S(1)}, u32[]{:S(2)}, u32[]{:S(2)}) collective-permute-start(f32[16,6912]{1,0:T(8,128)S(1)} %collective-permute-done.18.oth3), channel_id=1, source_target_pairs={{0,96},{1,97},{2,98},{3,99},{4,100},{5,101},{6,102},{7,103},{8,104... | collective-permute-start | bytes 1327112 | tf_op jit(solution)/shard_map/ppermute | solution.py:510
  83.5 11.9 %collective-permute-start.21 = (f32[4,6912]{1,0:T(4,128)S(1)}, f32[4,6912]{1,0:T(4,128)S(1)}, u32[]{:S(2)}, u32[]{:S(2)}) collective-permute-start(f32[4,6912]{1,0:T(4,128)S(1)} %get-tuple-element.59), channel_id=1, source_target_pairs={{0,8},{1,9},{2,10},{3,11},{4,12},{5,13},{6,14},{7,15},{8,0},{9,1},... | collective-permute-start | bytes 331784 | tf_op jit(solution)/shard_map/ppermute | solution.py:510
  85.9 9.5 %collective-permute-start.22 = (f32[4,6912]{1,0:T(4,128)S(1)}, f32[4,6912]{1,0:T(4,128)S(1)}, u32[]{:S(2)}, u32[]{:S(2)}) collective-permute-start(f32[4,6912]{1,0:T(4,128)S(1)} %get-tuple-element.60), channel_id=1, source_target_pairs={{0,16},{1,17},{2,18},{3,19},{4,20},{5,21},{6,22},{7,23},{8,24},{9,... | collective-permute-start | bytes 331784 | tf_op jit(solution)/shard_map/ppermute | solution.py:510
  90.8 5.5 %collective-permute-start.23 = (f32[4,6912]{1,0:T(4,128)S(1)}, f32[4,6912]{1,0:T(4,128)S(1)}, u32[]{:S(2)}, u32[]{:S(2)}) collective-permute-start(f32[4,6912]{1,0:T(4,128)S(1)} %get-tuple-element.61), channel_id=1, source_target_pairs={{0,24},{1,25},{2,26},{3,27},{4,28},{5,29},{6,30},{7,31},{8,16},{9,... | collective-permute-start | bytes 331784 | tf_op jit(solution)/shard_map/ppermute | solution.py:510
  98.7 17.0 %all-to-all-start = ((f32[16,1,128]{2,1,0:T(1,128)}), f32[16,1,128]{2,1,0:T(1,128)S(1)}, u32[]{:S(2)}, u32[]{:S(2)}) async-start(f32[16,1,128]{2,1,0:T(1,128)} %bitcast.5), calls=%async_computation | async-start | bytes 16384 | tf_op jit(solution)/shard_map/all_to_all | solution.py:573
  (5 other events, 7.4 us)

commit v11 on v10

--- a/solution.py
+++ b/solution.py
@@ -234,19 +234,12 @@
     return [a + c * third[first + m] + s * third[first + 3 + m] for m in range(3)]
 
 
-def spectrum_kernel(q_ref, own, one, two, three, low_a, core_a, low_b, core_b, kern, third, whi, wlo, right, left, field, hi, lo):
-    q = q_ref[0]
-    sources = (
-        (own, low_a),
-        (one, core_a),
-        (two, low_b),
-        (three, core_b),
-    )
+def densities_of(q, sources, third, right, left, hi, lo):
     sub = lax.broadcasted_iota(jnp.int32, (8, 128), 0)
     to_right = sub % 4
     to_left = jnp.where(sub < 4, q, 4 + q % 2)
     place = lax.broadcasted_iota(jnp.int32, (8, 128), 1) // 16 % 3
-    for delta, (bands_ref, low_ref) in enumerate(sources):
+    for delta, bands_ref, low_ref in sources:
         base = (q ^ delta) * QX
 
         def densities(i, carry):
@@ -285,6 +278,14 @@
 
         lax.fori_loop(0, QX // 2, densities, 0)
 
+
+def first_kernel(q_ref, own, one, low_a, core_a, third, right, left, hi, lo):
+    densities_of(q_ref[0], ((0, own, low_a), (1, one, core_a)), third, right, left, hi, lo)
+
+
+def spectrum_kernel(q_ref, two, three, low_b, core_b, kern, third, whi, wlo, right_in, left_in, hi_in, lo_in,
+                    right, left, hi, lo, field):
+    densities_of(q_ref[0], ((2, two, low_b), (3, three, core_b)), third, right, left, hi, lo)
     for k in (0, 1):
         if k == 0:
             rows_of = [[product(hi, lo, whi, wlo, 0, j)] for j in range(3)]
@@ -378,16 +379,30 @@
 SPLIT = [pltpu.VMEM((NG * 8, PLANE), BF16)] * 2
 
 
-def spectrum(q, bands, kern, third, tables):
+STATE = [jax.ShapeDtypeStruct((NG, 8, PLANE), F32)] * 2 + [jax.ShapeDtypeStruct((NG * 8, PLANE), BF16)] * 2
+
+
+def first_densities(q, bands, third):
+    return pl.pallas_call(
+        first_kernel,
+        out_shape=STATE,
+        in_specs=[SMEM_SPEC] + [VMEM_SPEC] * 5,
+        out_specs=[VMEM_SPEC] * 4,
+        name="first_densities",
+        compiler_params=pltpu.CompilerParams(vmem_limit_bytes=16 << 20),
+    )(q.reshape(1), *bands, third)
+
+
+def spectrum(q, bands, kern, third, tables, state):
     return pl.pallas_call(
         spectrum_kernel,
-        out_shape=[jax.ShapeDtypeStruct((NG, 8, PLANE), F32)] * 2 + [jax.ShapeDtypeStruct((NG * 8, PLANE), F32)],
+        out_shape=STATE + [jax.ShapeDtypeStruct((NG * 8, PLANE), F32)],
         in_specs=[SMEM_SPEC] + [VMEM_SPEC] * 12,
-        out_specs=[VMEM_SPEC] * 3,
-        scratch_shapes=SPLIT,
+        out_specs=[VMEM_SPEC] * 5,
+        input_output_aliases={9: 0, 10: 1, 11: 2, 12: 3},
         name="spectrum",
-        compiler_params=pltpu.CompilerParams(vmem_limit_bytes=24 << 20),
-    )(q.reshape(1), *bands, kern, third, *tables)
+        compiler_params=pltpu.CompilerParams(vmem_limit_bytes=28 << 20),
+    )(q.reshape(1), *bands, kern, third, *tables, *state)
 
 
 def terms(q, right, left, field, third, tables):
@@ -548,21 +563,22 @@
     core_b = within(low_b, 1)
     three = within(two, 1)
     other = move(together, lambda z, y, h, q: (z, y, 1 - h, q))
-    right, left, field = spectrum(q, (orbitals, one, two, three, low_a, core_a, low_b, core_b), kern, third, tables[:2])
+    own1 = along_z(together, 1)
+    own3 = along_z(together, 3)
+    state = first_densities(q, (orbitals, one, low_a, core_a), third)
+    right, left, _, _, field = spectrum(q, (two, three, low_b, core_b), kern, third, tables[:2], state)
     near0, near2, cross, low0, low2 = terms(q, right, left, field, third, tables[2:4])
     across = within(cross, 1)
-    together, other, _ = lax.optimization_barrier((together, other, near0))
-    own1 = along_z(together, 1)
-    own3 = along_z(together, 3)
+    other, _ = lax.optimization_barrier((other, near0))
+    oth1 = along_z(other, 1)
+    oth3 = along_z(other, 3)
+    own2 = along_z(own1, 1)
     merge = small_call(merge_kernel, [(4, QCELL)] * 2 + [(2, QCELL)] * 2)
     near, both, owe_a, owe_b = merge(where, near0, near2, low0, low2, across)
     far = within(both, 2)
     owed_a = around(owe_a, -1, 0)
     owed_b = around(owe_b, -1, 2)
-    oth1 = along_z(other, 1)
-    oth3 = along_z(other, 3)
-    own2 = along_z(own1, 1)
-    oth2 = along_z(oth3, 3)
+    oth2 = along_z(oth1, 1)
     finalize = small_call(finalize_kernel, [(4, CHUNK)] * 4)
     vc = finalize(where, near, far, owed_a, owed_b)
     (vectors,) = small_call(vectors_kernel, [(4, QCELL)])(where, near, far, owed_a, owed_b)

time: 117 us -> 112 us (0.957)
  the two profiles are of different devices: /device:TPU:5 before, /device:TPU:1 now
where the time goes in v11:
time: 112 us; the launch traced here: 111 us
  waiting for transfers between devices  51.4 us (46%)
  starting transfers between devices  33.2 us (30%)
  Pallas kernels  20.6 us (18%)
  local copies, waits for them, and re-layouts  5.09 us (5%)
    ppermute x24, waiting for transfers between devices, move(): return lax.ppermute(value, BOTH, pairs)  47.3 us
    ppermute x24, starting transfers between devices, move(): return lax.ppermute(value, BOTH, pairs)  27.3 us
    pallas_call x6, Pallas kernels, call(): pl.pallas_call(body, out_shape=[jax.ShapeDtypeStruct(shape, F32) for shap...  6.65 us
    all_to_all x1, starting transfers between devices, step(): lax.all_to_all(sums, BOTH, 0, 0, tiled=True, axis_index_groups=groups)  5.87 us
    pallas_call x1, Pallas kernels, terms(): pl.pallas_call(terms_kernel, out_shape=[jax.ShapeDtypeStruct(shape, F32)...  5.82 us
    pallas_call x1, Pallas kernels, spectrum(): pl.pallas_call(spectrum_kernel, out_shape=STATE + [jax.ShapeDtypeStruct((...  5.63 us
    unnamed x12, local copies, waits for them, and re-layouts  4.43 us
    all_to_all x1, waiting for transfers between devices, step(): lax.all_to_all(sums, BOTH, 0, 0, tiled=True, axis_index_groups=groups)  4.07 us
  transfers between devices with their start and end apart: 25, of which 11 were waited for; matrix products, arithmetic and copies ran while one was open for 0% of the time, Pallas kernels for 16%

profile of v11, /device:TPU:1, one launch (start us, length us, event | category | flops | bytes accessed | tf_op | source)
XLA Modules:
  0.0 111.3 jit_solution(1393143579651142683)
XLA Ops:
  0.6 2.1 %collective-permute-start = (f32[4,27648]{1,0:T(4,128)}, f32[4,27648]{1,0:T(4,128)S(1)}, u32[]{:S(2)}, u32[]{:S(2)}) collective-permute-start(f32[4,27648]{1,0:T(4,128)} %orbitals.3), channel_id=1, source_target_pairs={{0,2},{1,3},{2,0},{3,1},{4,6},{5,7},{6,4},{7,5},{8,10},{9,11},{10,... | collective-permute-start | bytes 1327112 | tf_op jit(solution)/shard_map/ppermute | solution.py:525
  4.5 2.5 %collective-permute-start.5 = (f32[2,27648]{1,0:T(2,128)S(1)}, f32[2,27648]{1,0:T(2,128)S(1)}, u32[]{:S(2)}, u32[]{:S(2)}) collective-permute-start(f32[2,27648]{1,0:T(2,128)S(1)} %get-tuple-element.40), channel_id=1, source_target_pairs={{0,4},{1,5},{2,6},{3,7},{4,8},{5,9},{6,10},{7,11},{8,12},{9,13},{1... | collective-permute-start | bytes 663560 | tf_op jit(solution)/shard_map/ppermute | solution.py:525
  9.5 2.9 %collective-permute-done.two = f32[4,27648]{1,0:T(4,128)S(1)} collective-permute-done((f32[4,27648]{1,0:T(4,128)}, f32[4,27648]{1,0:T(4,128)S(1)}, u32[]{:S(2)}, u32[]{:S(2)}) %collective-permute-start) | collective-permute-done | bytes 442400 | tf_op jit(solution)/shard_map/ppermute | solution.py:525
  12.4 2.9 %collective-permute-start.1 = (f32[4,27648]{1,0:T(4,128)S(1)}, f32[4,27648]{1,0:T(4,128)S(1)}, u32[]{:S(2)}, u32[]{:S(2)}) collective-permute-start(f32[4,27648]{1,0:T(4,128)S(1)} %collective-permute-done.two), channel_id=1, source_target_pairs={{0,1},{1,0},{2,3},{3,2},{4,5},{5,4},{6,7},{7,6},{8,9},{9,8},{10,11... | collective-permute-start | bytes 1327112 | tf_op jit(solution)/shard_map/ppermute | solution.py:525
  15.3 10.3 %collective-permute-done.5.low_a = f32[2,27648]{1,0:T(2,128)S(1)} collective-permute-done((f32[2,27648]{1,0:T(2,128)S(1)}, f32[2,27648]{1,0:T(2,128)S(1)}, u32[]{:S(2)}, u32[]{:S(2)}) %collective-permute-start.5) | collective-permute-done | bytes 221216 | tf_op jit(solution)/shard_map/ppermute | solution.py:525
  25.6 1.5 %collective-permute-start.6 = (f32[2,27648]{1,0:T(2,128)S(1)}, f32[2,27648]{1,0:T(2,128)S(1)}, u32[]{:S(2)}, u32[]{:S(2)}) collective-permute-start(f32[2,27648]{1,0:T(2,128)S(1)} %collective-permute-done.5.low_a), channel_id=1, source_target_pairs={{0,1},{1,0},{2,3},{3,2},{4,5},{5,4},{6,7},{7,6},{8,9},{9,8},{10,11... | collective-permute-start | bytes 663560 | tf_op jit(solution)/shard_map/ppermute | solution.py:525
  28.3 3.4 %collective-permute-start.13 = (f32[4,6912]{1,0:T(4,128)S(1)}, f32[4,6912]{1,0:T(4,128)S(1)}, u32[]{:S(2)}, u32[]{:S(2)}) collective-permute-start(f32[4,6912]{1,0:T(4,128)S(1)} %get-tuple-element.62), channel_id=1, source_target_pairs={{0,24},{1,25},{2,26},{3,27},{4,28},{5,29},{6,30},{7,31},{8,16},{9,... | collective-permute-start | bytes 331784 | tf_op jit(solution)/shard_map/ppermute | solution.py:525
  35.5 2.2 %first_densities.1 = (f32[48,8,2304]{2,1,0:T(8,128)S(1)}, f32[48,8,2304]{2,1,0:T(8,128)S(1)}, bf16[384,2304]{1,0:T(8,128)(2,1)S(1)}, bf16[384,2304]{1,0:T(8,128)(2,1)S(1)}) custom-call(s32[1]{0:T(128)} %bitcast.q_ref, f32[4,27648]{1,0:T(4,128)S(1)} %copy-done.1, f32[4,27648]{1,0:T(4,128)S(1)} %collective-permute-done.4.one, ...), custom_call_target="tpu_custom_call" | custom-call | tf_op jit(solution)/shard_map/first_densities/pallas_call | solution.py:386
  37.7 5.6 %spectrum.1 = (f32[48,8,2304]{2,1,0:T(8,128)S(1)}, f32[48,8,2304]{2,1,0:T(8,128)S(1)}, bf16[384,2304]{1,0:T(8,128)(2,1)S(1)}, bf16[384,2304]{1,0:T(8,128)(2,1)S(1)}, f32[384,2304]{1,0:T(8,128)S(1)}) custom-call(s32[1]{0:T(128)} %bitcast.q_ref, ...), custom_call_target="tpu_custom_call", output_to_operand_aliasing={{0}: (9, {}), {1}: (10, {}), {2}: (11, {}), {3}: (12, {})} | custom-call | tf_op jit(solution)/shard_map/spectrum/pallas_call | solution.py:397
  43.3 5.8 %terms.1 = (f32[4,27648]{1,0:T(4,128)S(1)}, f32[4,27648]{1,0:T(4,128)S(1)}, f32[10,27648]{1,0:T(8,128)S(1)}, f32[1,27648]{1,0:T(1,128)S(1)}, f32[1,27648]{1,0:T(1,128)S(1)}) custom-call(s32[1]{0:T(128)} %bitcast.q_ref, f32[48,8,2304]{2,1,0:T(8,128)S(1)} %get-tuple-element.45.right, f32[48,8,2304]{2,1,0:T(8,128)S(1)} %get-tuple-element.46.left, ...), custom_call_target="tpu_custom_call" | custom-call | tf_op jit(solution)/shard_map/terms/pallas_call | solution.py:409
  49.2 1.4 %collective-permute-start.7 = (f32[10,27648]{1,0:T(8,128)S(1)}, f32[10,27648]{1,0:T(8,128)S(1)}, u32[]{:S(2)}, u32[]{:S(2)}) collective-permute-start(f32[10,27648]{1,0:T(8,128)S(1)} %get-tuple-element.54), channel_id=1, source_target_pairs={{0,1},{1,0},{2,3},{3,2},{4,5},{5,4},{6,7},{7,6},{8,9},{9,8},{10,11... | collective-permute-start | bytes 3317768 | tf_op jit(solution)/shard_map/ppermute | solution.py:525
  50.9 13.1 %collective-permute-done.14.oth0 = f32[16,6912]{1,0:T(8,128)S(1)} collective-permute-done((f32[16,6912]{1,0:T(8,128)S(1)}, f32[16,6912]{1,0:T(8,128)S(1)}, u32[]{:S(2)}, u32[]{:S(2)}) %collective-permute-start.14) | collective-permute-done | bytes 442400 | tf_op jit(solution)/shard_map/ppermute | solution.py:525
  64.7 1.5 %collective-permute-start.10 = (f32[2,27648]{1,0:T(2,128)S(1)}, f32[2,27648]{1,0:T(2,128)S(1)}, u32[]{:S(2)}, u32[]{:S(2)}) collective-permute-start(f32[2,27648]{1,0:T(2,128)S(1)} %get-tuple-element.58), channel_id=1, source_target_pairs={{0,126},{1,127},{2,124},{3,125},{4,2},{5,3},{6,0},{7,1},{8,6},{9,7... | collective-permute-start | bytes 663560 | tf_op jit(solution)/shard_map/ppermute | solution.py:525
  66.3 2.1 %collective-permute-start.9 = (f32[2,27648]{1,0:T(2,128)S(1)}, f32[2,27648]{1,0:T(2,128)S(1)}, u32[]{:S(2)}, u32[]{:S(2)}) collective-permute-start(f32[2,27648]{1,0:T(2,128)S(1)} %get-tuple-element.57), channel_id=1, source_target_pairs={{0,124},{1,125},{2,126},{3,127},{4,0},{5,1},{6,2},{7,3},{8,4},{9,5... | collective-permute-start | bytes 663560 | tf_op jit(solution)/shard_map/ppermute | solution.py:525
  68.4 1.5 %collective-permute-start.8 = (f32[4,27648]{1,0:T(4,128)S(1)}, f32[4,27648]{1,0:T(4,128)S(1)}, u32[]{:S(2)}, u32[]{:S(2)}) collective-permute-start(f32[4,27648]{1,0:T(4,128)S(1)} %get-tuple-element.56), channel_id=1, source_target_pairs={{0,2},{1,3},{2,0},{3,1},{4,6},{5,7},{6,4},{7,5},{8,10},{9,11},{10,... | collective-permute-start | bytes 1327112 | tf_op jit(solution)/shard_map/ppermute | solution.py:525
  70.7 5.3 %collective-permute-done.16.oth1 = f32[16,6912]{1,0:T(8,128)S(1)} collective-permute-done((f32[16,6912]{1,0:T(8,128)S(1)}, f32[16,6912]{1,0:T(8,128)S(1)}, u32[]{:S(2)}, u32[]{:S(2)}) %collective-permute-start.16) | collective-permute-done | bytes 442400 | tf_op jit(solution)/shard_map/ppermute | solution.py:525
  76.8 3.6 %collective-permute-start.20 = (f32[16,6912]{1,0:T(8,128)S(1)}, f32[16,6912]{1,0:T(8,128)S(1)}, u32[]{:S(2)}, u32[]{:S(2)}) collective-permute-start(f32[16,6912]{1,0:T(8,128)S(1)} %collective-permute-done.14.oth0), channel_id=1, source_target_pairs={{0,96},{1,97},{2,98},{3,99},{4,100},{5,101},{6,102},{7,103},{8,104... | collective-permute-start | bytes 1327112 | tf_op jit(solution)/shard_map/ppermute | solution.py:525
  80.4 3.1 %collective-permute-done.8.far = f32[4,27648]{1,0:T(4,128)S(1)} collective-permute-done((f32[4,27648]{1,0:T(4,128)S(1)}, f32[4,27648]{1,0:T(4,128)S(1)}, u32[]{:S(2)}, u32[]{:S(2)}) %collective-permute-start.8) | collective-permute-done | bytes 442400 | tf_op jit(solution)/shard_map/ppermute | solution.py:525
  84.5 2.7 %collective-permute-done.17.own2 = f32[16,6912]{1,0:T(8,128)S(1)} collective-permute-done((f32[16,6912]{1,0:T(8,128)S(1)}, f32[16,6912]{1,0:T(8,128)S(1)}, u32[]{:S(2)}, u32[]{:S(2)}) %collective-permute-start.17) | collective-permute-done | bytes 442400 | tf_op jit(solution)/shard_map/ppermute | solution.py:525
  89.1 7.6 %collective-permute-done.18.oth2 = f32[16,6912]{1,0:T(8,128)S(1)} collective-permute-done((f32[16,6912]{1,0:T(8,128)S(1)}, f32[16,6912]{1,0:T(8,128)S(1)}, u32[]{:S(2)}, u32[]{:S(2)}) %collective-permute-start.18) | collective-permute-done | bytes 442400 | tf_op jit(solution)/shard_map/ppermute | solution.py:525
  96.7 2.4 %shard_map.73 = f32[16,128]{1,0:T(8,128)} custom-call(s32[4]{0:T(128)S(1)} %pad_add_fusion.where, f32[16,6912]{1,0:T(8,128)S(1)} %pad_maximum_fusion.own0, f32[16,6912]{1,0:T(8,128)S(1)} %collective-permute-done.14.oth0, f32[16,6912]{1,0:T(8,128)S(1)} %collective-permute-done.15.own1, f32[16,6912]{1,0:T(8,128)S(1)} %collective-permute-done.16.oth1, ...), custom_call_target="tpu_custom_call" | custom-call | tf_op jit(solution)/shard_map/pallas_call | solution.py:428
  99.2 5.9 %all-to-all-start = ((f32[16,1,128]{2,1,0:T(1,128)}), f32[16,1,128]{2,1,0:T(1,128)S(1)}, u32[]{:S(2)}, u32[]{:S(2)}) async-start(f32[16,1,128]{2,1,0:T(1,128)} %bitcast.5), calls=%async_computation | async-start | bytes 16384 | tf_op jit(solution)/shard_map/all_to_all | solution.py:589
  105.0 1.5 %shard_map.70 = f32[4,27648]{1,0:T(4,128)} custom-call(s32[4]{0:T(128)S(1)} %pad_add_fusion.where, f32[4,27648]{1,0:T(4,128)S(1)} %get-tuple-element.55.near, f32[4,27648]{1,0:T(4,128)S(1)} %collective-permute-done.8.far, f32[2,27648]{1,0:T(2,128)S(1)} %collective-permute-done.9.owed_a, f32[2,27648]{1,0:T(2,128)S(1)} %collective-permute-done.10.owed_b), custom_call_target="tpu_custom_call" | custom-call | tf_op jit(solution)/shard_map/pallas_call | solution.py:428
  106.5 4.1 %all-to-all-done = f32[16,1,128]{2,1,0:T(1,128)S(1)} async-done(((f32[16,1,128]{2,1,0:T(1,128)}), f32[16,1,128]{2,1,0:T(1,128)S(1)}, u32[]{:S(2)}, u32[]{:S(2)}) %all-to-all-start) | async-done | bytes 8224 | tf_op jit(solution)/shard_map/all_to_all | solution.py:589
  (52 shorter events, 15.2 us)
Async XLA Ops:
  0.6 11.8 %collective-permute-start = (f32[4,27648]{1,0:T(4,128)}, f32[4,27648]{1,0:T(4,128)S(1)}, u32[]{:S(2)}, u32[]{:S(2)}) collective-permute-start(f32[4,27648]{1,0:T(4,128)} %orbitals.3), channel_id=1, source_target_pairs={{0,2},{1,3},{2,0},{3,1},{4,6},{5,7},{6,4},{7,5},{8,10},{9,11},{10,... | collective-permute-start | bytes 1327112 | tf_op jit(solution)/shard_map/ppermute | solution.py:525
  4.5 21.2 %collective-permute-start.5 = (f32[2,27648]{1,0:T(2,128)S(1)}, f32[2,27648]{1,0:T(2,128)S(1)}, u32[]{:S(2)}, u32[]{:S(2)}) collective-permute-start(f32[2,27648]{1,0:T(2,128)S(1)} %get-tuple-element.40), channel_id=1, source_target_pairs={{0,4},{1,5},{2,6},{3,7},{4,8},{5,9},{6,10},{7,11},{8,12},{9,13},{1... | collective-permute-start | bytes 663560 | tf_op jit(solution)/shard_map/ppermute | solution.py:525
  7.0 21.3 %collective-permute-start.4 = (f32[4,27648]{1,0:T(4,128)S(1)}, f32[4,27648]{1,0:T(4,128)S(1)}, u32[]{:S(2)}, u32[]{:S(2)}) collective-permute-start(f32[4,27648]{1,0:T(4,128)S(1)} %copy-done), channel_id=1, source_target_pairs={{0,1},{1,0},{2,3},{3,2},{4,5},{5,4},{6,7},{7,6},{8,9},{9,8},{10,11... | collective-permute-start | bytes 1327112 | tf_op jit(solution)/shard_map/ppermute | solution.py:525
  8.3 18.9 %collective-permute-start.2 = (f32[2,27648]{1,0:T(2,128)S(1)}, f32[2,27648]{1,0:T(2,128)S(1)}, u32[]{:S(2)}, u32[]{:S(2)}) collective-permute-start(f32[2,27648]{1,0:T(2,128)S(1)} %get-tuple-element.35), channel_id=1, source_target_pairs={{0,6},{1,7},{2,4},{3,5},{4,10},{5,11},{6,8},{7,9},{8,14},{9,15},{1... | collective-permute-start | bytes 663560 | tf_op jit(solution)/shard_map/ppermute | solution.py:525
  12.4 25.3 %collective-permute-start.1 = (f32[4,27648]{1,0:T(4,128)S(1)}, f32[4,27648]{1,0:T(4,128)S(1)}, u32[]{:S(2)}, u32[]{:S(2)}) collective-permute-start(f32[4,27648]{1,0:T(4,128)S(1)} %collective-permute-done.two), channel_id=1, source_target_pairs={{0,1},{1,0},{2,3},{3,2},{4,5},{5,4},{6,7},{7,6},{8,9},{9,8},{10,11... | collective-permute-start | bytes 1327112 | tf_op jit(solution)/shard_map/ppermute | solution.py:525
  27.2 10.5 %collective-permute-start.3 = (f32[2,27648]{1,0:T(2,128)S(1)}, f32[2,27648]{1,0:T(2,128)S(1)}, u32[]{:S(2)}, u32[]{:S(2)}) collective-permute-start(f32[2,27648]{1,0:T(2,128)S(1)} %collective-permute-done.2.low_b), channel_id=1, source_target_pairs={{0,1},{1,0},{2,3},{3,2},{4,5},{5,4},{6,7},{7,6},{8,9},{9,8},{10,11... | collective-permute-start | bytes 663560 | tf_op jit(solution)/shard_map/ppermute | solution.py:525
  27.8 22.8 %collective-permute-start.11 = (f32[4,6912]{1,0:T(4,128)S(1)}, f32[4,6912]{1,0:T(4,128)S(1)}, u32[]{:S(2)}, u32[]{:S(2)}) collective-permute-start(f32[4,6912]{1,0:T(4,128)S(1)} %get-tuple-element.60), channel_id=1, source_target_pairs={{0,8},{1,9},{2,10},{3,11},{4,12},{5,13},{6,14},{7,15},{8,0},{9,1},... | collective-permute-start | bytes 331784 | tf_op jit(solution)/shard_map/ppermute | solution.py:525
  28.3 22.3 %collective-permute-start.12 = (f32[4,6912]{1,0:T(4,128)S(1)}, f32[4,6912]{1,0:T(4,128)S(1)}, u32[]{:S(2)}, u32[]{:S(2)}) collective-permute-start(f32[4,6912]{1,0:T(4,128)S(1)} %get-tuple-element.61), channel_id=1, source_target_pairs={{0,16},{1,17},{2,18},{3,19},{4,20},{5,21},{6,22},{7,23},{8,24},{9,... | collective-permute-start | bytes 331784 | tf_op jit(solution)/shard_map/ppermute | solution.py:525
  28.3 22.3 %collective-permute-start.13 = (f32[4,6912]{1,0:T(4,128)S(1)}, f32[4,6912]{1,0:T(4,128)S(1)}, u32[]{:S(2)}, u32[]{:S(2)}) collective-permute-start(f32[4,6912]{1,0:T(4,128)S(1)} %get-tuple-element.62), channel_id=1, source_target_pairs={{0,24},{1,25},{2,26},{3,27},{4,28},{5,29},{6,30},{7,31},{8,16},{9,... | collective-permute-start | bytes 331784 | tf_op jit(solution)/shard_map/ppermute | solution.py:525
  49.2 14.8 %collective-permute-start.7 = (f32[10,27648]{1,0:T(8,128)S(1)}, f32[10,27648]{1,0:T(8,128)S(1)}, u32[]{:S(2)}, u32[]{:S(2)}) collective-permute-start(f32[10,27648]{1,0:T(8,128)S(1)} %get-tuple-element.54), channel_id=1, source_target_pairs={{0,1},{1,0},{2,3},{3,2},{4,5},{5,4},{6,7},{7,6},{8,9},{9,8},{10,11... | collective-permute-start | bytes 3317768 | tf_op jit(solution)/shard_map/ppermute | solution.py:525
  50.7 13.3 %collective-permute-start.14 = (f32[16,6912]{1,0:T(8,128)S(1)}, f32[16,6912]{1,0:T(8,128)S(1)}, u32[]{:S(2)}, u32[]{:S(2)}) collective-permute-start(f32[16,6912]{1,0:T(8,128)S(1)} %pad_maximum_fusion.own0), channel_id=1, source_target_pairs={{0,4},{1,5},{2,6},{3,7},{4,0},{5,1},{6,2},{7,3},{8,12},{9,13},{10,... | collective-permute-start | bytes 1327112 | tf_op jit(solution)/shard_map/ppermute | solution.py:525
  50.8 19.1 %collective-permute-start.15 = (f32[16,6912]{1,0:T(8,128)S(1)}, f32[16,6912]{1,0:T(8,128)S(1)}, u32[]{:S(2)}, u32[]{:S(2)}) collective-permute-start(f32[16,6912]{1,0:T(8,128)S(1)} %pad_maximum_fusion.own0), channel_id=1, source_target_pairs={{0,32},{1,33},{2,34},{3,35},{4,36},{5,37},{6,38},{7,39},{8,40},{9,... | collective-permute-start | bytes 1327112 | tf_op jit(solution)/shard_map/ppermute | solution.py:525
  64.0 12.0 %collective-permute-start.16 = (f32[16,6912]{1,0:T(8,128)S(1)}, f32[16,6912]{1,0:T(8,128)S(1)}, u32[]{:S(2)}, u32[]{:S(2)}) collective-permute-start(f32[16,6912]{1,0:T(8,128)S(1)} %collective-permute-done.14.oth0), channel_id=1, source_target_pairs={{0,32},{1,33},{2,34},{3,35},{4,36},{5,37},{6,38},{7,39},{8,40},{9,... | collective-permute-start | bytes 1327112 | tf_op jit(solution)/shard_map/ppermute | solution.py:525
  64.7 12.1 %collective-permute-start.10 = (f32[2,27648]{1,0:T(2,128)S(1)}, f32[2,27648]{1,0:T(2,128)S(1)}, u32[]{:S(2)}, u32[]{:S(2)}) collective-permute-start(f32[2,27648]{1,0:T(2,128)S(1)} %get-tuple-element.58), channel_id=1, source_target_pairs={{0,126},{1,127},{2,124},{3,125},{4,2},{5,3},{6,0},{7,1},{8,6},{9,7... | collective-permute-start | bytes 663560 | tf_op jit(solution)/shard_map/ppermute | solution.py:525
  66.3 14.1 %collective-permute-start.9 = (f32[2,27648]{1,0:T(2,128)S(1)}, f32[2,27648]{1,0:T(2,128)S(1)}, u32[]{:S(2)}, u32[]{:S(2)}) collective-permute-start(f32[2,27648]{1,0:T(2,128)S(1)} %get-tuple-element.57), channel_id=1, source_target_pairs={{0,124},{1,125},{2,126},{3,127},{4,0},{5,1},{6,2},{7,3},{8,4},{9,5... | collective-permute-start | bytes 663560 | tf_op jit(solution)/shard_map/ppermute | solution.py:525
  68.4 15.2 %collective-permute-start.8 = (f32[4,27648]{1,0:T(4,128)S(1)}, f32[4,27648]{1,0:T(4,128)S(1)}, u32[]{:S(2)}, u32[]{:S(2)}) collective-permute-start(f32[4,27648]{1,0:T(4,128)S(1)} %get-tuple-element.56), channel_id=1, source_target_pairs={{0,2},{1,3},{2,0},{3,1},{4,6},{5,7},{6,4},{7,5},{8,10},{9,11},{10,... | collective-permute-start | bytes 1327112 | tf_op jit(solution)/shard_map/ppermute | solution.py:525
  69.9 14.5 %collective-permute-start.19 = (f32[16,6912]{1,0:T(8,128)S(1)}, f32[16,6912]{1,0:T(8,128)S(1)}, u32[]{:S(2)}, u32[]{:S(2)}) collective-permute-start(f32[16,6912]{1,0:T(8,128)S(1)} %pad_maximum_fusion.own0), channel_id=1, source_target_pairs={{0,96},{1,97},{2,98},{3,99},{4,100},{5,101},{6,102},{7,103},{8,104... | collective-permute-start | bytes 1327112 | tf_op jit(solution)/shard_map/ppermute | solution.py:525
  76.0 11.2 %collective-permute-start.17 = (f32[16,6912]{1,0:T(8,128)S(1)}, f32[16,6912]{1,0:T(8,128)S(1)}, u32[]{:S(2)}, u32[]{:S(2)}) collective-permute-start(f32[16,6912]{1,0:T(8,128)S(1)} %collective-permute-done.15.own1), channel_id=1, source_target_pairs={{0,32},{1,33},{2,34},{3,35},{4,36},{5,37},{6,38},{7,39},{8,40},{9,... | collective-permute-start | bytes 1327112 | tf_op jit(solution)/shard_map/ppermute | solution.py:525
  76.8 12.3 %collective-permute-start.20 = (f32[16,6912]{1,0:T(8,128)S(1)}, f32[16,6912]{1,0:T(8,128)S(1)}, u32[]{:S(2)}, u32[]{:S(2)}) collective-permute-start(f32[16,6912]{1,0:T(8,128)S(1)} %collective-permute-done.14.oth0), channel_id=1, source_target_pairs={{0,96},{1,97},{2,98},{3,99},{4,100},{5,101},{6,102},{7,103},{8,104... | collective-permute-start | bytes 1327112 | tf_op jit(solution)/shard_map/ppermute | solution.py:525
  80.4 16.3 %collective-permute-start.18 = (f32[16,6912]{1,0:T(8,128)S(1)}, f32[16,6912]{1,0:T(8,128)S(1)}, u32[]{:S(2)}, u32[]{:S(2)}) collective-permute-start(f32[16,6912]{1,0:T(8,128)S(1)} %collective-permute-done.16.oth1), channel_id=1, source_target_pairs={{0,32},{1,33},{2,34},{3,35},{4,36},{5,37},{6,38},{7,39},{8,40},{9,... | collective-permute-start | bytes 1327112 | tf_op jit(solution)/shard_map/ppermute | solution.py:525
  84.3 12.4 %collective-permute-start.21 = (f32[4,6912]{1,0:T(4,128)S(1)}, f32[4,6912]{1,0:T(4,128)S(1)}, u32[]{:S(2)}, u32[]{:S(2)}) collective-permute-start(f32[4,6912]{1,0:T(4,128)S(1)} %get-tuple-element.65), channel_id=1, source_target_pairs={{0,8},{1,9},{2,10},{3,11},{4,12},{5,13},{6,14},{7,15},{8,0},{9,1},... | collective-permute-start | bytes 331784 | tf_op jit(solution)/shard_map/ppermute | solution.py:525
  84.4 12.3 %collective-permute-start.22 = (f32[4,6912]{1,0:T(4,128)S(1)}, f32[4,6912]{1,0:T(4,128)S(1)}, u32[]{:S(2)}, u32[]{:S(2)}) collective-permute-start(f32[4,6912]{1,0:T(4,128)S(1)} %get-tuple-element.66), channel_id=1, source_target_pairs={{0,16},{1,17},{2,18},{3,19},{4,20},{5,21},{6,22},{7,23},{8,24},{9,... | collective-permute-start | bytes 331784 | tf_op jit(solution)/shard_map/ppermute | solution.py:525
  87.2 9.5 %collective-permute-start.23 = (f32[4,6912]{1,0:T(4,128)S(1)}, f32[4,6912]{1,0:T(4,128)S(1)}, u32[]{:S(2)}, u32[]{:S(2)}) collective-permute-start(f32[4,6912]{1,0:T(4,128)S(1)} %get-tuple-element.67), channel_id=1, source_target_pairs={{0,24},{1,25},{2,26},{3,27},{4,28},{5,29},{6,30},{7,31},{8,16},{9,... | collective-permute-start | bytes 331784 | tf_op jit(solution)/shard_map/ppermute | solution.py:525
  99.2 11.4 %all-to-all-start = ((f32[16,1,128]{2,1,0:T(1,128)}), f32[16,1,128]{2,1,0:T(1,128)S(1)}, u32[]{:S(2)}, u32[]{:S(2)}) async-start(f32[16,1,128]{2,1,0:T(1,128)} %bitcast.5), calls=%async_computation | async-start | bytes 16384 | tf_op jit(solution)/shard_map/all_to_all | solution.py:589
  (7 other events, 38.7 us)

commit v12 on v11

--- a/solution.py
+++ b/solution.py
@@ -373,7 +373,7 @@
     return jnp.take_along_axis(value, sub ^ flip, axis=0)
 
 
-X_STEP = 2
+X_STEP = 6
 VMEM_SPEC = pl.BlockSpec(memory_space=pltpu.VMEM)
 SMEM_SPEC = pl.BlockSpec(memory_space=pltpu.SMEM)
 SPLIT = [pltpu.VMEM((NG * 8, PLANE), BF16)] * 2
@@ -448,7 +448,8 @@
     sel_b[...] = jnp.where(lower, b, a)
 
 
-def chunks_kernel(where, orbitals, *chunks):
+def chunks_kernel(where, orbitals, copy, *chunks):
+    copy[...] = orbitals[...]
     for k in range(4):
         chunks[k][...] = orbitals[:, chunk_of(where, k)]
 
@@ -555,7 +556,8 @@
     low_b = around(sel_b, 1, 2)
     two = within(orbitals, 2)
     one = within(orbitals, 1)
-    pc = small_call(chunks_kernel, [(4, CHUNK)] * 4)(where, orbitals)
+    chunks = small_call(chunks_kernel, [(4, QCELL)] + [(4, CHUNK)] * 4)
+    own, *pc = chunks(where, orbitals)
     pieces = [pc[0]] + [along_y(pc[k], k) for k in (1, 2, 3)]
     *tables, kern, third = plane_tables()
     together = jnp.concatenate(pieces, axis=0)
@@ -565,7 +567,7 @@
     other = move(together, lambda z, y, h, q: (z, y, 1 - h, q))
     own1 = along_z(together, 1)
     own3 = along_z(together, 3)
-    state = first_densities(q, (orbitals, one, low_a, core_a), third)
+    state = first_densities(q, (own, one, low_a, core_a), third)
     right, left, _, _, field = spectrum(q, (two, three, low_b, core_b), kern, third, tables[:2], state)
     near0, near2, cross, low0, low2 = terms(q, right, left, field, third, tables[2:4])
     across = within(cross, 1)

time: 112 us -> 111 us (level)
    unnamed x12 -> x8, local copies, waits for them, and re-layouts: 4.43 us -> 3.41 us
  transfers between devices with their start and end apart: 25 -> 25, of which waited for: 11 -> 10; matrix products, arithmetic and copies ran while one was open for 0% -> 0% of each run, Pallas kernels for 16% -> 17%
where the time goes in v12:
time: 111 us
  waiting for transfers between devices  52 us (47%)
  starting transfers between devices  33 us (30%)
  Pallas kernels  20.8 us (19%)
  local copies, waits for them, and re-layouts  4.08 us (4%)
    ppermute x24, waiting for transfers between devices, move(): return lax.ppermute(value, BOTH, pairs)  48 us
    ppermute x24, starting transfers between devices, move(): return lax.ppermute(value, BOTH, pairs)  27.2 us
    pallas_call x6, Pallas kernels, call(): pl.pallas_call(body, out_shape=[jax.ShapeDtypeStruct(shape, F32) for shap...  7.65 us
    all_to_all x1, starting transfers between devices, step(): lax.all_to_all(sums, BOTH, 0, 0, tiled=True, axis_index_groups=groups)  5.8 us
    pallas_call x1, Pallas kernels, spectrum(): pl.pallas_call(spectrum_kernel, out_shape=STATE + [jax.ShapeDtypeStruct((...  5.62 us
    pallas_call x1, Pallas kernels, terms(): pl.pallas_call(terms_kernel, out_shape=[jax.ShapeDtypeStruct(shape, F32)...  5.02 us
    all_to_all x1, waiting for transfers between devices, step(): lax.all_to_all(sums, BOTH, 0, 0, tiled=True, axis_index_groups=groups)  4.08 us
    unnamed x8, local copies, waits for them, and re-layouts  3.41 us
  transfers between devices with their start and end apart: 25, of which 10 were waited for; matrix products, arithmetic and copies ran while one was open for 0% of the time, Pallas kernels for 17%

profile of v12, /device:TPU:1, one launch (start us, length us, event | category | flops | bytes accessed | tf_op | source)
XLA Modules:
  0.0 110.9 jit_solution(15644196478446233948)
XLA Ops:
  0.6 2.1 %collective-permute-start = (f32[4,27648]{1,0:T(4,128)}, f32[4,27648]{1,0:T(4,128)S(1)}, u32[]{:S(2)}, u32[]{:S(2)}) collective-permute-start(f32[4,27648]{1,0:T(4,128)} %orbitals.3), channel_id=1, source_target_pairs={{0,2},{1,3},{2,0},{3,1},{4,6},{5,7},{6,4},{7,5},{8,10},{9,11},{10,... | collective-permute-start | bytes 1327112 | tf_op jit(solution)/shard_map/ppermute | solution.py:526
  4.0 2.5 %collective-permute-start.5 = (f32[2,27648]{1,0:T(2,128)S(1)}, f32[2,27648]{1,0:T(2,128)S(1)}, u32[]{:S(2)}, u32[]{:S(2)}) collective-permute-start(f32[2,27648]{1,0:T(2,128)S(1)} %get-tuple-element.42), channel_id=1, source_target_pairs={{0,4},{1,5},{2,6},{3,7},{4,8},{5,9},{6,10},{7,11},{8,12},{9,13},{1... | collective-permute-start | bytes 663560 | tf_op jit(solution)/shard_map/ppermute | solution.py:526
  8.9 3.5 %collective-permute-done.two = f32[4,27648]{1,0:T(4,128)S(1)} collective-permute-done((f32[4,27648]{1,0:T(4,128)}, f32[4,27648]{1,0:T(4,128)S(1)}, u32[]{:S(2)}, u32[]{:S(2)}) %collective-permute-start) | collective-permute-done | bytes 442400 | tf_op jit(solution)/shard_map/ppermute | solution.py:526
  12.4 2.9 %collective-permute-start.1 = (f32[4,27648]{1,0:T(4,128)S(1)}, f32[4,27648]{1,0:T(4,128)S(1)}, u32[]{:S(2)}, u32[]{:S(2)}) collective-permute-start(f32[4,27648]{1,0:T(4,128)S(1)} %collective-permute-done.two), channel_id=1, source_target_pairs={{0,1},{1,0},{2,3},{3,2},{4,5},{5,4},{6,7},{7,6},{8,9},{9,8},{10,11... | collective-permute-start | bytes 1327112 | tf_op jit(solution)/shard_map/ppermute | solution.py:526
  15.3 10.3 %collective-permute-done.5.low_a = f32[2,27648]{1,0:T(2,128)S(1)} collective-permute-done((f32[2,27648]{1,0:T(2,128)S(1)}, f32[2,27648]{1,0:T(2,128)S(1)}, u32[]{:S(2)}, u32[]{:S(2)}) %collective-permute-start.5) | collective-permute-done | bytes 221216 | tf_op jit(solution)/shard_map/ppermute | solution.py:526
  25.6 1.5 %collective-permute-start.6 = (f32[2,27648]{1,0:T(2,128)S(1)}, f32[2,27648]{1,0:T(2,128)S(1)}, u32[]{:S(2)}, u32[]{:S(2)}) collective-permute-start(f32[2,27648]{1,0:T(2,128)S(1)} %collective-permute-done.5.low_a), channel_id=1, source_target_pairs={{0,1},{1,0},{2,3},{3,2},{4,5},{5,4},{6,7},{7,6},{8,9},{9,8},{10,11... | collective-permute-start | bytes 663560 | tf_op jit(solution)/shard_map/ppermute | solution.py:526
  28.5 3.7 %collective-permute-start.13 = (f32[4,6912]{1,0:T(4,128)S(1)}, f32[4,6912]{1,0:T(4,128)S(1)}, u32[]{:S(2)}, u32[]{:S(2)}) collective-permute-start(f32[4,6912]{1,0:T(4,128)S(1)} %get-tuple-element.64), channel_id=1, source_target_pairs={{0,24},{1,25},{2,26},{3,27},{4,28},{5,29},{6,30},{7,31},{8,16},{9,... | collective-permute-start | bytes 331784 | tf_op jit(solution)/shard_map/ppermute | solution.py:526
  36.0 2.2 %first_densities.1 = (f32[48,8,2304]{2,1,0:T(8,128)S(1)}, f32[48,8,2304]{2,1,0:T(8,128)S(1)}, bf16[384,2304]{1,0:T(8,128)(2,1)S(1)}, bf16[384,2304]{1,0:T(8,128)(2,1)S(1)}) custom-call(s32[1]{0:T(128)} %bitcast.q_ref, f32[4,27648]{1,0:T(4,128)S(1)} %get-tuple-element.41.own, f32[4,27648]{1,0:T(4,128)S(1)} %collective-permute-done.4.one, ...), custom_call_target="tpu_custom_call" | custom-call | tf_op jit(solution)/shard_map/first_densities/pallas_call | solution.py:386
  38.2 5.6 %spectrum.1 = (f32[48,8,2304]{2,1,0:T(8,128)S(1)}, f32[48,8,2304]{2,1,0:T(8,128)S(1)}, bf16[384,2304]{1,0:T(8,128)(2,1)S(1)}, bf16[384,2304]{1,0:T(8,128)(2,1)S(1)}, f32[384,2304]{1,0:T(8,128)S(1)}) custom-call(s32[1]{0:T(128)} %bitcast.q_ref, ...), custom_call_target="tpu_custom_call", output_to_operand_aliasing={{0}: (9, {}), {1}: (10, {}), {2}: (11, {}), {3}: (12, {})} | custom-call | tf_op jit(solution)/shard_map/spectrum/pallas_call | solution.py:397
  43.8 5.0 %terms.1 = (f32[4,27648]{1,0:T(4,128)S(1)}, f32[4,27648]{1,0:T(4,128)S(1)}, f32[10,27648]{1,0:T(8,128)S(1)}, f32[1,27648]{1,0:T(1,128)S(1)}, f32[1,27648]{1,0:T(1,128)S(1)}) custom-call(s32[1]{0:T(128)} %bitcast.q_ref, f32[48,8,2304]{2,1,0:T(8,128)S(1)} %get-tuple-element.47.right, f32[48,8,2304]{2,1,0:T(8,128)S(1)} %get-tuple-element.48.left, ...), custom_call_target="tpu_custom_call" | custom-call | tf_op jit(solution)/shard_map/terms/pallas_call | solution.py:409
  48.8 1.4 %collective-permute-start.7 = (f32[10,27648]{1,0:T(8,128)S(1)}, f32[10,27648]{1,0:T(8,128)S(1)}, u32[]{:S(2)}, u32[]{:S(2)}) collective-permute-start(f32[10,27648]{1,0:T(8,128)S(1)} %get-tuple-element.56), channel_id=1, source_target_pairs={{0,1},{1,0},{2,3},{3,2},{4,5},{5,4},{6,7},{7,6},{8,9},{9,8},{10,11... | collective-permute-start | bytes 3317768 | tf_op jit(solution)/shard_map/ppermute | solution.py:526
  50.6 13.1 %collective-permute-done.14.oth0 = f32[16,6912]{1,0:T(8,128)S(1)} collective-permute-done((f32[16,6912]{1,0:T(8,128)S(1)}, f32[16,6912]{1,0:T(8,128)S(1)}, u32[]{:S(2)}, u32[]{:S(2)}) %collective-permute-start.14) | collective-permute-done | bytes 442400 | tf_op jit(solution)/shard_map/ppermute | solution.py:526
  64.4 1.5 %collective-permute-start.10 = (f32[2,27648]{1,0:T(2,128)S(1)}, f32[2,27648]{1,0:T(2,128)S(1)}, u32[]{:S(2)}, u32[]{:S(2)}) collective-permute-start(f32[2,27648]{1,0:T(2,128)S(1)} %get-tuple-element.60), channel_id=1, source_target_pairs={{0,126},{1,127},{2,124},{3,125},{4,2},{5,3},{6,0},{7,1},{8,6},{9,7... | collective-permute-start | bytes 663560 | tf_op jit(solution)/shard_map/ppermute | solution.py:526
  66.0 2.1 %collective-permute-start.9 = (f32[2,27648]{1,0:T(2,128)S(1)}, f32[2,27648]{1,0:T(2,128)S(1)}, u32[]{:S(2)}, u32[]{:S(2)}) collective-permute-start(f32[2,27648]{1,0:T(2,128)S(1)} %get-tuple-element.59), channel_id=1, source_target_pairs={{0,124},{1,125},{2,126},{3,127},{4,0},{5,1},{6,2},{7,3},{8,4},{9,5... | collective-permute-start | bytes 663560 | tf_op jit(solution)/shard_map/ppermute | solution.py:526
  68.1 1.5 %collective-permute-start.8 = (f32[4,27648]{1,0:T(4,128)S(1)}, f32[4,27648]{1,0:T(4,128)S(1)}, u32[]{:S(2)}, u32[]{:S(2)}) collective-permute-start(f32[4,27648]{1,0:T(4,128)S(1)} %get-tuple-element.58), channel_id=1, source_target_pairs={{0,2},{1,3},{2,0},{3,1},{4,6},{5,7},{6,4},{7,5},{8,10},{9,11},{10,... | collective-permute-start | bytes 1327112 | tf_op jit(solution)/shard_map/ppermute | solution.py:526
  69.9 5.9 %collective-permute-done.16.oth1 = f32[16,6912]{1,0:T(8,128)S(1)} collective-permute-done((f32[16,6912]{1,0:T(8,128)S(1)}, f32[16,6912]{1,0:T(8,128)S(1)}, u32[]{:S(2)}, u32[]{:S(2)}) %collective-permute-start.16) | collective-permute-done | bytes 442400 | tf_op jit(solution)/shard_map/ppermute | solution.py:526
  76.5 3.6 %collective-permute-start.20 = (f32[16,6912]{1,0:T(8,128)S(1)}, f32[16,6912]{1,0:T(8,128)S(1)}, u32[]{:S(2)}, u32[]{:S(2)}) collective-permute-start(f32[16,6912]{1,0:T(8,128)S(1)} %collective-permute-done.14.oth0), channel_id=1, source_target_pairs={{0,96},{1,97},{2,98},{3,99},{4,100},{5,101},{6,102},{7,103},{8,104... | collective-permute-start | bytes 1327112 | tf_op jit(solution)/shard_map/ppermute | solution.py:526
  80.1 3.1 %collective-permute-done.8.far = f32[4,27648]{1,0:T(4,128)S(1)} collective-permute-done((f32[4,27648]{1,0:T(4,128)S(1)}, f32[4,27648]{1,0:T(4,128)S(1)}, u32[]{:S(2)}, u32[]{:S(2)}) %collective-permute-start.8) | collective-permute-done | bytes 442400 | tf_op jit(solution)/shard_map/ppermute | solution.py:526
  84.2 2.8 %collective-permute-done.17.own2 = f32[16,6912]{1,0:T(8,128)S(1)} collective-permute-done((f32[16,6912]{1,0:T(8,128)S(1)}, f32[16,6912]{1,0:T(8,128)S(1)}, u32[]{:S(2)}, u32[]{:S(2)}) %collective-permute-start.17) | collective-permute-done | bytes 442400 | tf_op jit(solution)/shard_map/ppermute | solution.py:526
  88.8 7.6 %collective-permute-done.18.oth2 = f32[16,6912]{1,0:T(8,128)S(1)} collective-permute-done((f32[16,6912]{1,0:T(8,128)S(1)}, f32[16,6912]{1,0:T(8,128)S(1)}, u32[]{:S(2)}, u32[]{:S(2)}) %collective-permute-start.18) | collective-permute-done | bytes 442400 | tf_op jit(solution)/shard_map/ppermute | solution.py:526
  96.4 2.4 %shard_map.73 = f32[16,128]{1,0:T(8,128)} custom-call(s32[4]{0:T(128)S(1)} %pad_add_fusion.where, f32[16,6912]{1,0:T(8,128)S(1)} %pad_maximum_fusion.own0, f32[16,6912]{1,0:T(8,128)S(1)} %collective-permute-done.14.oth0, f32[16,6912]{1,0:T(8,128)S(1)} %collective-permute-done.15.own1, f32[16,6912]{1,0:T(8,128)S(1)} %collective-permute-done.16.oth1, ...), custom_call_target="tpu_custom_call" | custom-call | tf_op jit(solution)/shard_map/pallas_call | solution.py:428
  98.8 5.8 %all-to-all-start = ((f32[16,1,128]{2,1,0:T(1,128)}), f32[16,1,128]{2,1,0:T(1,128)S(1)}, u32[]{:S(2)}, u32[]{:S(2)}) async-start(f32[16,1,128]{2,1,0:T(1,128)} %bitcast.5), calls=%async_computation | async-start | bytes 16384 | tf_op jit(solution)/shard_map/all_to_all | solution.py:591
  104.7 1.5 %shard_map.71 = f32[4,27648]{1,0:T(4,128)} custom-call(s32[4]{0:T(128)S(1)} %pad_add_fusion.where, f32[4,27648]{1,0:T(4,128)S(1)} %get-tuple-element.57.near, f32[4,27648]{1,0:T(4,128)S(1)} %collective-permute-done.8.far, f32[2,27648]{1,0:T(2,128)S(1)} %collective-permute-done.9.owed_a, f32[2,27648]{1,0:T(2,128)S(1)} %collective-permute-done.10.owed_b), custom_call_target="tpu_custom_call" | custom-call | tf_op jit(solution)/shard_map/pallas_call | solution.py:428
  106.1 4.1 %all-to-all-done = f32[16,1,128]{2,1,0:T(1,128)S(1)} async-done(((f32[16,1,128]{2,1,0:T(1,128)}), f32[16,1,128]{2,1,0:T(1,128)S(1)}, u32[]{:S(2)}, u32[]{:S(2)}) %all-to-all-start) | async-done | bytes 8224 | tf_op jit(solution)/shard_map/all_to_all | solution.py:591
  (48 shorter events, 14.3 us)
Async XLA Ops:
  0.6 11.8 %collective-permute-start = (f32[4,27648]{1,0:T(4,128)}, f32[4,27648]{1,0:T(4,128)S(1)}, u32[]{:S(2)}, u32[]{:S(2)}) collective-permute-start(f32[4,27648]{1,0:T(4,128)} %orbitals.3), channel_id=1, source_target_pairs={{0,2},{1,3},{2,0},{3,1},{4,6},{5,7},{6,4},{7,5},{8,10},{9,11},{10,... | collective-permute-start | bytes 1327112 | tf_op jit(solution)/shard_map/ppermute | solution.py:526
  4.0 21.7 %collective-permute-start.5 = (f32[2,27648]{1,0:T(2,128)S(1)}, f32[2,27648]{1,0:T(2,128)S(1)}, u32[]{:S(2)}, u32[]{:S(2)}) collective-permute-start(f32[2,27648]{1,0:T(2,128)S(1)} %get-tuple-element.42), channel_id=1, source_target_pairs={{0,4},{1,5},{2,6},{3,7},{4,8},{5,9},{6,10},{7,11},{8,12},{9,13},{1... | collective-permute-start | bytes 663560 | tf_op jit(solution)/shard_map/ppermute | solution.py:526
  6.5 22.0 %collective-permute-start.4 = (f32[4,27648]{1,0:T(4,128)}, f32[4,27648]{1,0:T(4,128)S(1)}, u32[]{:S(2)}, u32[]{:S(2)}) collective-permute-start(f32[4,27648]{1,0:T(4,128)} %orbitals.3), channel_id=1, source_target_pairs={{0,1},{1,0},{2,3},{3,2},{4,5},{5,4},{6,7},{7,6},{8,9},{9,8},{10,11... | collective-permute-start | bytes 1327112 | tf_op jit(solution)/shard_map/ppermute | solution.py:526
  7.7 19.5 %collective-permute-start.2 = (f32[2,27648]{1,0:T(2,128)S(1)}, f32[2,27648]{1,0:T(2,128)S(1)}, u32[]{:S(2)}, u32[]{:S(2)}) collective-permute-start(f32[2,27648]{1,0:T(2,128)S(1)} %get-tuple-element.36), channel_id=1, source_target_pairs={{0,6},{1,7},{2,4},{3,5},{4,10},{5,11},{6,8},{7,9},{8,14},{9,15},{1... | collective-permute-start | bytes 663560 | tf_op jit(solution)/shard_map/ppermute | solution.py:526
  12.4 25.8 %collective-permute-start.1 = (f32[4,27648]{1,0:T(4,128)S(1)}, f32[4,27648]{1,0:T(4,128)S(1)}, u32[]{:S(2)}, u32[]{:S(2)}) collective-permute-start(f32[4,27648]{1,0:T(4,128)S(1)} %collective-permute-done.two), channel_id=1, source_target_pairs={{0,1},{1,0},{2,3},{3,2},{4,5},{5,4},{6,7},{7,6},{8,9},{9,8},{10,11... | collective-permute-start | bytes 1327112 | tf_op jit(solution)/shard_map/ppermute | solution.py:526
  27.2 11.0 %collective-permute-start.3 = (f32[2,27648]{1,0:T(2,128)S(1)}, f32[2,27648]{1,0:T(2,128)S(1)}, u32[]{:S(2)}, u32[]{:S(2)}) collective-permute-start(f32[2,27648]{1,0:T(2,128)S(1)} %collective-permute-done.2.low_b), channel_id=1, source_target_pairs={{0,1},{1,0},{2,3},{3,2},{4,5},{5,4},{6,7},{7,6},{8,9},{9,8},{10,11... | collective-permute-start | bytes 663560 | tf_op jit(solution)/shard_map/ppermute | solution.py:526
  28.3 22.0 %collective-permute-start.11 = (f32[4,6912]{1,0:T(4,128)S(1)}, f32[4,6912]{1,0:T(4,128)S(1)}, u32[]{:S(2)}, u32[]{:S(2)}) collective-permute-start(f32[4,6912]{1,0:T(4,128)S(1)} %get-tuple-element.62), channel_id=1, source_target_pairs={{0,8},{1,9},{2,10},{3,11},{4,12},{5,13},{6,14},{7,15},{8,0},{9,1},... | collective-permute-start | bytes 331784 | tf_op jit(solution)/shard_map/ppermute | solution.py:526
  28.4 21.9 %collective-permute-start.12 = (f32[4,6912]{1,0:T(4,128)S(1)}, f32[4,6912]{1,0:T(4,128)S(1)}, u32[]{:S(2)}, u32[]{:S(2)}) collective-permute-start(f32[4,6912]{1,0:T(4,128)S(1)} %get-tuple-element.63), channel_id=1, source_target_pairs={{0,16},{1,17},{2,18},{3,19},{4,20},{5,21},{6,22},{7,23},{8,24},{9,... | collective-permute-start | bytes 331784 | tf_op jit(solution)/shard_map/ppermute | solution.py:526
  28.5 21.8 %collective-permute-start.13 = (f32[4,6912]{1,0:T(4,128)S(1)}, f32[4,6912]{1,0:T(4,128)S(1)}, u32[]{:S(2)}, u32[]{:S(2)}) collective-permute-start(f32[4,6912]{1,0:T(4,128)S(1)} %get-tuple-element.64), channel_id=1, source_target_pairs={{0,24},{1,25},{2,26},{3,27},{4,28},{5,29},{6,30},{7,31},{8,16},{9,... | collective-permute-start | bytes 331784 | tf_op jit(solution)/shard_map/ppermute | solution.py:526
  48.8 14.8 %collective-permute-start.7 = (f32[10,27648]{1,0:T(8,128)S(1)}, f32[10,27648]{1,0:T(8,128)S(1)}, u32[]{:S(2)}, u32[]{:S(2)}) collective-permute-start(f32[10,27648]{1,0:T(8,128)S(1)} %get-tuple-element.56), channel_id=1, source_target_pairs={{0,1},{1,0},{2,3},{3,2},{4,5},{5,4},{6,7},{7,6},{8,9},{9,8},{10,11... | collective-permute-start | bytes 3317768 | tf_op jit(solution)/shard_map/ppermute | solution.py:526
  50.4 13.3 %collective-permute-start.14 = (f32[16,6912]{1,0:T(8,128)S(1)}, f32[16,6912]{1,0:T(8,128)S(1)}, u32[]{:S(2)}, u32[]{:S(2)}) collective-permute-start(f32[16,6912]{1,0:T(8,128)S(1)} %pad_maximum_fusion.own0), channel_id=1, source_target_pairs={{0,4},{1,5},{2,6},{3,7},{4,0},{5,1},{6,2},{7,3},{8,12},{9,13},{10,... | collective-permute-start | bytes 1327112 | tf_op jit(solution)/shard_map/ppermute | solution.py:526
  50.5 19.1 %collective-permute-start.15 = (f32[16,6912]{1,0:T(8,128)S(1)}, f32[16,6912]{1,0:T(8,128)S(1)}, u32[]{:S(2)}, u32[]{:S(2)}) collective-permute-start(f32[16,6912]{1,0:T(8,128)S(1)} %pad_maximum_fusion.own0), channel_id=1, source_target_pairs={{0,32},{1,33},{2,34},{3,35},{4,36},{5,37},{6,38},{7,39},{8,40},{9,... | collective-permute-start | bytes 1327112 | tf_op jit(solution)/shard_map/ppermute | solution.py:526
  63.7 12.0 %collective-permute-start.16 = (f32[16,6912]{1,0:T(8,128)S(1)}, f32[16,6912]{1,0:T(8,128)S(1)}, u32[]{:S(2)}, u32[]{:S(2)}) collective-permute-start(f32[16,6912]{1,0:T(8,128)S(1)} %collective-permute-done.14.oth0), channel_id=1, source_target_pairs={{0,32},{1,33},{2,34},{3,35},{4,36},{5,37},{6,38},{7,39},{8,40},{9,... | collective-permute-start | bytes 1327112 | tf_op jit(solution)/shard_map/ppermute | solution.py:526
  64.4 12.1 %collective-permute-start.10 = (f32[2,27648]{1,0:T(2,128)S(1)}, f32[2,27648]{1,0:T(2,128)S(1)}, u32[]{:S(2)}, u32[]{:S(2)}) collective-permute-start(f32[2,27648]{1,0:T(2,128)S(1)} %get-tuple-element.60), channel_id=1, source_target_pairs={{0,126},{1,127},{2,124},{3,125},{4,2},{5,3},{6,0},{7,1},{8,6},{9,7... | collective-permute-start | bytes 663560 | tf_op jit(solution)/shard_map/ppermute | solution.py:526
  66.0 14.1 %collective-permute-start.9 = (f32[2,27648]{1,0:T(2,128)S(1)}, f32[2,27648]{1,0:T(2,128)S(1)}, u32[]{:S(2)}, u32[]{:S(2)}) collective-permute-start(f32[2,27648]{1,0:T(2,128)S(1)} %get-tuple-element.59), channel_id=1, source_target_pairs={{0,124},{1,125},{2,126},{3,127},{4,0},{5,1},{6,2},{7,3},{8,4},{9,5... | collective-permute-start | bytes 663560 | tf_op jit(solution)/shard_map/ppermute | solution.py:526
  68.1 15.2 %collective-permute-start.8 = (f32[4,27648]{1,0:T(4,128)S(1)}, f32[4,27648]{1,0:T(4,128)S(1)}, u32[]{:S(2)}, u32[]{:S(2)}) collective-permute-start(f32[4,27648]{1,0:T(4,128)S(1)} %get-tuple-element.58), channel_id=1, source_target_pairs={{0,2},{1,3},{2,0},{3,1},{4,6},{5,7},{6,4},{7,5},{8,10},{9,11},{10,... | collective-permute-start | bytes 1327112 | tf_op jit(solution)/shard_map/ppermute | solution.py:526
  69.6 14.5 %collective-permute-start.19 = (f32[16,6912]{1,0:T(8,128)S(1)}, f32[16,6912]{1,0:T(8,128)S(1)}, u32[]{:S(2)}, u32[]{:S(2)}) collective-permute-start(f32[16,6912]{1,0:T(8,128)S(1)} %pad_maximum_fusion.own0), channel_id=1, source_target_pairs={{0,96},{1,97},{2,98},{3,99},{4,100},{5,101},{6,102},{7,103},{8,104... | collective-permute-start | bytes 1327112 | tf_op jit(solution)/shard_map/ppermute | solution.py:526
  75.7 11.2 %collective-permute-start.17 = (f32[16,6912]{1,0:T(8,128)S(1)}, f32[16,6912]{1,0:T(8,128)S(1)}, u32[]{:S(2)}, u32[]{:S(2)}) collective-permute-start(f32[16,6912]{1,0:T(8,128)S(1)} %collective-permute-done.15.own1), channel_id=1, source_target_pairs={{0,32},{1,33},{2,34},{3,35},{4,36},{5,37},{6,38},{7,39},{8,40},{9,... | collective-permute-start | bytes 1327112 | tf_op jit(solution)/shard_map/ppermute | solution.py:526
  76.5 12.2 %collective-permute-start.20 = (f32[16,6912]{1,0:T(8,128)S(1)}, f32[16,6912]{1,0:T(8,128)S(1)}, u32[]{:S(2)}, u32[]{:S(2)}) collective-permute-start(f32[16,6912]{1,0:T(8,128)S(1)} %collective-permute-done.14.oth0), channel_id=1, source_target_pairs={{0,96},{1,97},{2,98},{3,99},{4,100},{5,101},{6,102},{7,103},{8,104... | collective-permute-start | bytes 1327112 | tf_op jit(solution)/shard_map/ppermute | solution.py:526
  80.1 16.3 %collective-permute-start.18 = (f32[16,6912]{1,0:T(8,128)S(1)}, f32[16,6912]{1,0:T(8,128)S(1)}, u32[]{:S(2)}, u32[]{:S(2)}) collective-permute-start(f32[16,6912]{1,0:T(8,128)S(1)} %collective-permute-done.16.oth1), channel_id=1, source_target_pairs={{0,32},{1,33},{2,34},{3,35},{4,36},{5,37},{6,38},{7,39},{8,40},{9,... | collective-permute-start | bytes 1327112 | tf_op jit(solution)/shard_map/ppermute | solution.py:526
  84.0 12.4 %collective-permute-start.21 = (f32[4,6912]{1,0:T(4,128)S(1)}, f32[4,6912]{1,0:T(4,128)S(1)}, u32[]{:S(2)}, u32[]{:S(2)}) collective-permute-start(f32[4,6912]{1,0:T(4,128)S(1)} %get-tuple-element.67), channel_id=1, source_target_pairs={{0,8},{1,9},{2,10},{3,11},{4,12},{5,13},{6,14},{7,15},{8,0},{9,1},... | collective-permute-start | bytes 331784 | tf_op jit(solution)/shard_map/ppermute | solution.py:526
  84.1 12.3 %collective-permute-start.22 = (f32[4,6912]{1,0:T(4,128)S(1)}, f32[4,6912]{1,0:T(4,128)S(1)}, u32[]{:S(2)}, u32[]{:S(2)}) collective-permute-start(f32[4,6912]{1,0:T(4,128)S(1)} %get-tuple-element.68), channel_id=1, source_target_pairs={{0,16},{1,17},{2,18},{3,19},{4,20},{5,21},{6,22},{7,23},{8,24},{9,... | collective-permute-start | bytes 331784 | tf_op jit(solution)/shard_map/ppermute | solution.py:526
  86.9 9.5 %collective-permute-start.23 = (f32[4,6912]{1,0:T(4,128)S(1)}, f32[4,6912]{1,0:T(4,128)S(1)}, u32[]{:S(2)}, u32[]{:S(2)}) collective-permute-start(f32[4,6912]{1,0:T(4,128)S(1)} %get-tuple-element.69), channel_id=1, source_target_pairs={{0,24},{1,25},{2,26},{3,27},{4,28},{5,29},{6,30},{7,31},{8,16},{9,... | collective-permute-start | bytes 331784 | tf_op jit(solution)/shard_map/ppermute | solution.py:526
  98.8 11.4 %all-to-all-start = ((f32[16,1,128]{2,1,0:T(1,128)}), f32[16,1,128]{2,1,0:T(1,128)S(1)}, u32[]{:S(2)}, u32[]{:S(2)}) async-start(f32[16,1,128]{2,1,0:T(1,128)} %bitcast.5), calls=%async_computation | async-start | bytes 16384 | tf_op jit(solution)/shard_map/all_to_all | solution.py:591
  (5 other events, 6.1 us)

commit v13 on v12

--- a/solution.py
+++ b/solution.py
@@ -482,7 +482,7 @@
         vectors[:, span] = total_of(where, near, far, owed_a, owed_b, span)
 
 
-def margin_kernel(where, own0, oth0, own1, oth1, own2, oth2, own3, oth3, v0, v1, v2, v3, pieces, block):
+def margin_kernel(where, own0, oth0, own1, oth1, own2, oth2a, oth2b, own3, oth3, v0, v1, v2, v3, pieces, block):
     z, y, h = where[1], where[2], where[3]
 
     def halves(a):
@@ -490,7 +490,7 @@
         return top, (a - top.astype(F32)).astype(BF16)
 
     v = jnp.concatenate(halves(jnp.concatenate([v0[...], v1[...], v2[...], v3[...]], axis=0)), axis=0)
-    parts = jnp.concatenate([r[...] for r in (own0, oth0, own1, oth1, own2, oth2, own3, oth3)], axis=0)
+    parts = jnp.concatenate([r[...] for r in (own0, oth0, own1, oth1, own2, oth2a, oth2b, own3, oth3)], axis=0)
     f = jnp.concatenate(halves(parts), axis=0)
     both = lax.dot_general(f, v, (((1,), (1,)), ((), ())), preferred_element_type=F32)
     both = both[0:128, :] + both[128:256, :]
@@ -574,19 +574,19 @@
     other, _ = lax.optimization_barrier((other, near0))
     oth1 = along_z(other, 1)
     oth3 = along_z(other, 3)
-    own2 = along_z(own1, 1)
     merge = small_call(merge_kernel, [(4, QCELL)] * 2 + [(2, QCELL)] * 2)
     near, both, owe_a, owe_b = merge(where, near0, near2, low0, low2, across)
     far = within(both, 2)
     owed_a = around(owe_a, -1, 0)
     owed_b = around(owe_b, -1, 2)
-    oth2 = along_z(oth1, 1)
+    own2 = along_z(own1, 1)
+    oth2 = [along_z(oth1[:8], 1), along_z(oth3[8:], 3)]
     finalize = small_call(finalize_kernel, [(4, CHUNK)] * 4)
     vc = finalize(where, near, far, owed_a, owed_b)
     (vectors,) = small_call(vectors_kernel, [(4, QCELL)])(where, near, far, owed_a, owed_b)
     given = [vc[0]] + [along_y(vc[k], k) for k in (1, 2, 3)]
     margin_part = small_call(margin_kernel, [(16, 128)], [pltpu.VMEM((16, 8, 16), F32)], 20)
-    (sums,) = margin_part(where, together, other, own1, oth1, own2, oth2, own3, oth3, *given)
+    (sums,) = margin_part(where, together, other, own1, oth1, own2, *oth2, own3, oth3, *given)
     groups = [[(z * 8 + y * 2 + h) * 4 + p for y in range(4) for p in range(4)] for z in range(4) for h in range(2)]
     sums = lax.all_to_all(sums, BOTH, 0, 0, tiled=True, axis_index_groups=groups)
     margin = jnp.sum(sums, axis=0).reshape(4, 32).T

time: 111 us -> 115 us (1.036)
  starting transfers between devices: 33 us -> 37.6 us
  waiting for transfers between devices: 52 us -> 50.7 us
    ppermute x24 -> x25, starting transfers between devices: 27.2 us -> 30 us  [move(): return lax.ppermute(value, BOTH, pairs)]
    all_to_all x1, starting transfers between devices: 5.8 us -> 7.52 us  [step(): lax.all_to_all(sums, BOTH, 0, 0, tiled=True, axis_index_groups=groups)]
    ppermute x24 -> x25, waiting for transfers between devices: 48 us -> 46.6 us  [move(): return lax.ppermute(value, BOTH, pairs)]
  transfers between devices with their start and end apart: 25 -> 26, of which waited for: 10 -> 8; matrix products, arithmetic and copies ran while one was open for 0% -> 0% of each run, Pallas kernels for 17% -> 16%
where the time goes in v13:
time: 115 us; the launch traced here: 114 us
  waiting for transfers between devices  50.7 us (44%)
  starting transfers between devices  37.6 us (33%)
  Pallas kernels  20.8 us (18%)
  local copies, waits for them, and re-layouts  4.1 us (4%)
    ppermute x25, waiting for transfers between devices, move(): return lax.ppermute(value, BOTH, pairs)  46.6 us
    ppermute x25, starting transfers between devices, move(): return lax.ppermute(value, BOTH, pairs)  30 us
    pallas_call x6, Pallas kernels, call(): pl.pallas_call(body, out_shape=[jax.ShapeDtypeStruct(shape, F32) for shap...  7.64 us
    all_to_all x1, starting transfers between devices, step(): lax.all_to_all(sums, BOTH, 0, 0, tiled=True, axis_index_groups=groups)  7.52 us
    pallas_call x1, Pallas kernels, spectrum(): pl.pallas_call(spectrum_kernel, out_shape=STATE + [jax.ShapeDtypeStruct((...  5.62 us
    pallas_call x1, Pallas kernels, terms(): pl.pallas_call(terms_kernel, out_shape=[jax.ShapeDtypeStruct(shape, F32)...  5.03 us
    all_to_all x1, waiting for transfers between devices, step(): lax.all_to_all(sums, BOTH, 0, 0, tiled=True, axis_index_groups=groups)  4.01 us
    unnamed x8, local copies, waits for them, and re-layouts  3.41 us
  transfers between devices with their start and end apart: 26, of which 8 were waited for; matrix products, arithmetic and copies ran while one was open for 0% of the time, Pallas kernels for 16%

profile of v13, /device:TPU:1, one launch (start us, length us, event | category | flops | bytes accessed | tf_op | source)
XLA Modules:
  0.0 114.2 jit_solution(4807092270769161437)
XLA Ops:
  0.6 2.1 %collective-permute-start = (f32[4,27648]{1,0:T(4,128)}, f32[4,27648]{1,0:T(4,128)S(1)}, u32[]{:S(2)}, u32[]{:S(2)}) collective-permute-start(f32[4,27648]{1,0:T(4,128)} %orbitals.3), channel_id=1, source_target_pairs={{0,2},{1,3},{2,0},{3,1},{4,6},{5,7},{6,4},{7,5},{8,10},{9,11},{10,... | collective-permute-start | bytes 1327112 | tf_op jit(solution)/shard_map/ppermute | solution.py:526
  4.0 2.5 %collective-permute-start.5 = (f32[2,27648]{1,0:T(2,128)S(1)}, f32[2,27648]{1,0:T(2,128)S(1)}, u32[]{:S(2)}, u32[]{:S(2)}) collective-permute-start(f32[2,27648]{1,0:T(2,128)S(1)} %get-tuple-element.42), channel_id=1, source_target_pairs={{0,4},{1,5},{2,6},{3,7},{4,8},{5,9},{6,10},{7,11},{8,12},{9,13},{1... | collective-permute-start | bytes 663560 | tf_op jit(solution)/shard_map/ppermute | solution.py:526
  8.9 3.5 %collective-permute-done.two = f32[4,27648]{1,0:T(4,128)S(1)} collective-permute-done((f32[4,27648]{1,0:T(4,128)}, f32[4,27648]{1,0:T(4,128)S(1)}, u32[]{:S(2)}, u32[]{:S(2)}) %collective-permute-start) | collective-permute-done | bytes 442400 | tf_op jit(solution)/shard_map/ppermute | solution.py:526
  12.4 2.9 %collective-permute-start.1 = (f32[4,27648]{1,0:T(4,128)S(1)}, f32[4,27648]{1,0:T(4,128)S(1)}, u32[]{:S(2)}, u32[]{:S(2)}) collective-permute-start(f32[4,27648]{1,0:T(4,128)S(1)} %collective-permute-done.two), channel_id=1, source_target_pairs={{0,1},{1,0},{2,3},{3,2},{4,5},{5,4},{6,7},{7,6},{8,9},{9,8},{10,11... | collective-permute-start | bytes 1327112 | tf_op jit(solution)/shard_map/ppermute | solution.py:526
  15.3 10.3 %collective-permute-done.5.low_a = f32[2,27648]{1,0:T(2,128)S(1)} collective-permute-done((f32[2,27648]{1,0:T(2,128)S(1)}, f32[2,27648]{1,0:T(2,128)S(1)}, u32[]{:S(2)}, u32[]{:S(2)}) %collective-permute-start.5) | collective-permute-done | bytes 221216 | tf_op jit(solution)/shard_map/ppermute | solution.py:526
  25.6 1.5 %collective-permute-start.6 = (f32[2,27648]{1,0:T(2,128)S(1)}, f32[2,27648]{1,0:T(2,128)S(1)}, u32[]{:S(2)}, u32[]{:S(2)}) collective-permute-start(f32[2,27648]{1,0:T(2,128)S(1)} %collective-permute-done.5.low_a), channel_id=1, source_target_pairs={{0,1},{1,0},{2,3},{3,2},{4,5},{5,4},{6,7},{7,6},{8,9},{9,8},{10,11... | collective-permute-start | bytes 663560 | tf_op jit(solution)/shard_map/ppermute | solution.py:526
  28.5 3.7 %collective-permute-start.13 = (f32[4,6912]{1,0:T(4,128)S(1)}, f32[4,6912]{1,0:T(4,128)S(1)}, u32[]{:S(2)}, u32[]{:S(2)}) collective-permute-start(f32[4,6912]{1,0:T(4,128)S(1)} %get-tuple-element.64), channel_id=1, source_target_pairs={{0,24},{1,25},{2,26},{3,27},{4,28},{5,29},{6,30},{7,31},{8,16},{9,... | collective-permute-start | bytes 331784 | tf_op jit(solution)/shard_map/ppermute | solution.py:526
  36.0 2.2 %first_densities.1 = (f32[48,8,2304]{2,1,0:T(8,128)S(1)}, f32[48,8,2304]{2,1,0:T(8,128)S(1)}, bf16[384,2304]{1,0:T(8,128)(2,1)S(1)}, bf16[384,2304]{1,0:T(8,128)(2,1)S(1)}) custom-call(s32[1]{0:T(128)} %bitcast.q_ref, f32[4,27648]{1,0:T(4,128)S(1)} %get-tuple-element.41.own, f32[4,27648]{1,0:T(4,128)S(1)} %collective-permute-done.4.one, ...), custom_call_target="tpu_custom_call" | custom-call | tf_op jit(solution)/shard_map/first_densities/pallas_call | solution.py:386
  38.2 5.6 %spectrum.1 = (f32[48,8,2304]{2,1,0:T(8,128)S(1)}, f32[48,8,2304]{2,1,0:T(8,128)S(1)}, bf16[384,2304]{1,0:T(8,128)(2,1)S(1)}, bf16[384,2304]{1,0:T(8,128)(2,1)S(1)}, f32[384,2304]{1,0:T(8,128)S(1)}) custom-call(s32[1]{0:T(128)} %bitcast.q_ref, ...), custom_call_target="tpu_custom_call", output_to_operand_aliasing={{0}: (9, {}), {1}: (10, {}), {2}: (11, {}), {3}: (12, {})} | custom-call | tf_op jit(solution)/shard_map/spectrum/pallas_call | solution.py:397
  43.8 5.0 %terms.1 = (f32[4,27648]{1,0:T(4,128)S(1)}, f32[4,27648]{1,0:T(4,128)S(1)}, f32[10,27648]{1,0:T(8,128)S(1)}, f32[1,27648]{1,0:T(1,128)S(1)}, f32[1,27648]{1,0:T(1,128)S(1)}) custom-call(s32[1]{0:T(128)} %bitcast.q_ref, f32[48,8,2304]{2,1,0:T(8,128)S(1)} %get-tuple-element.47.right, f32[48,8,2304]{2,1,0:T(8,128)S(1)} %get-tuple-element.48.left, ...), custom_call_target="tpu_custom_call" | custom-call | tf_op jit(solution)/shard_map/terms/pallas_call | solution.py:409
  48.8 1.4 %collective-permute-start.7 = (f32[10,27648]{1,0:T(8,128)S(1)}, f32[10,27648]{1,0:T(8,128)S(1)}, u32[]{:S(2)}, u32[]{:S(2)}) collective-permute-start(f32[10,27648]{1,0:T(8,128)S(1)} %get-tuple-element.56), channel_id=1, source_target_pairs={{0,1},{1,0},{2,3},{3,2},{4,5},{5,4},{6,7},{7,6},{8,9},{9,8},{10,11... | collective-permute-start | bytes 3317768 | tf_op jit(solution)/shard_map/ppermute | solution.py:526
  50.5 13.1 %collective-permute-done.14.oth0 = f32[16,6912]{1,0:T(8,128)S(1)} collective-permute-done((f32[16,6912]{1,0:T(8,128)S(1)}, f32[16,6912]{1,0:T(8,128)S(1)}, u32[]{:S(2)}, u32[]{:S(2)}) %collective-permute-start.14) | collective-permute-done | bytes 442400 | tf_op jit(solution)/shard_map/ppermute | solution.py:526
  63.7 2.7 %collective-permute-start.19 = (f32[16,6912]{1,0:T(8,128)S(1)}, f32[16,6912]{1,0:T(8,128)S(1)}, u32[]{:S(2)}, u32[]{:S(2)}) collective-permute-start(f32[16,6912]{1,0:T(8,128)S(1)} %collective-permute-done.14.oth0), channel_id=1, source_target_pairs={{0,96},{1,97},{2,98},{3,99},{4,100},{5,101},{6,102},{7,103},{8,104... | collective-permute-start | bytes 1327112 | tf_op jit(solution)/shard_map/ppermute | solution.py:526
  67.3 1.4 %collective-permute-start.17 = (f32[16,6912]{1,0:T(8,128)S(1)}, f32[16,6912]{1,0:T(8,128)S(1)}, u32[]{:S(2)}, u32[]{:S(2)}) collective-permute-start(f32[16,6912]{1,0:T(8,128)S(1)} %collective-permute-done.15.own1), channel_id=1, source_target_pairs={{0,32},{1,33},{2,34},{3,35},{4,36},{5,37},{6,38},{7,39},{8,40},{9,... | collective-permute-start | bytes 1327112 | tf_op jit(solution)/shard_map/ppermute | solution.py:526
  68.7 7.0 %collective-permute-done.16.oth1 = f32[16,6912]{1,0:T(8,128)S(1)} collective-permute-done((f32[16,6912]{1,0:T(8,128)S(1)}, f32[16,6912]{1,0:T(8,128)S(1)}, u32[]{:S(2)}, u32[]{:S(2)}) %collective-permute-start.16) | collective-permute-done | bytes 442400 | tf_op jit(solution)/shard_map/ppermute | solution.py:526
  75.7 2.1 %collective-permute-start.9 = (f32[2,27648]{1,0:T(2,128)S(1)}, f32[2,27648]{1,0:T(2,128)S(1)}, u32[]{:S(2)}, u32[]{:S(2)}) collective-permute-start(f32[2,27648]{1,0:T(2,128)S(1)} %get-tuple-element.59), channel_id=1, source_target_pairs={{0,124},{1,125},{2,126},{3,127},{4,0},{5,1},{6,2},{7,3},{8,4},{9,5... | collective-permute-start | bytes 663560 | tf_op jit(solution)/shard_map/ppermute | solution.py:526
  77.9 10.0 %collective-permute-done.10.owed_b = f32[2,27648]{1,0:T(2,128)S(1)} collective-permute-done((f32[2,27648]{1,0:T(2,128)S(1)}, f32[2,27648]{1,0:T(2,128)S(1)}, u32[]{:S(2)}, u32[]{:S(2)}) %collective-permute-start.10) | collective-permute-done | bytes 221216 | tf_op jit(solution)/shard_map/ppermute | solution.py:526
  87.9 2.7 %collective-permute-start.20 = (f32[8,6912]{1,0:T(8,128)S(1)}, f32[8,6912]{1,0:T(8,128)S(1)}, u32[]{:S(2)}, u32[]{:S(2)}) collective-permute-start(f32[8,6912]{1,0:T(8,128)S(1)} %slice.9), channel_id=1, source_target_pairs={{0,96},{1,97},{2,98},{3,99},{4,100},{5,101},{6,102},{7,103},{8,104... | collective-permute-start | bytes 663560 | tf_op jit(solution)/shard_map/ppermute | solution.py:526
  92.3 2.9 %collective-permute-start.24 = (f32[4,6912]{1,0:T(4,128)S(1)}, f32[4,6912]{1,0:T(4,128)S(1)}, u32[]{:S(2)}, u32[]{:S(2)}) collective-permute-start(f32[4,6912]{1,0:T(4,128)S(1)} %get-tuple-element.69), channel_id=1, source_target_pairs={{0,24},{1,25},{2,26},{3,27},{4,28},{5,29},{6,30},{7,31},{8,16},{9,... | collective-permute-start | bytes 331784 | tf_op jit(solution)/shard_map/ppermute | solution.py:526
  95.3 2.1 %collective-permute-done.23.v2 = f32[4,6912]{1,0:T(4,128)S(1)} collective-permute-done((f32[4,6912]{1,0:T(4,128)S(1)}, f32[4,6912]{1,0:T(4,128)S(1)}, u32[]{:S(2)}, u32[]{:S(2)}) %collective-permute-start.23) | collective-permute-done | bytes 110624 | tf_op jit(solution)/shard_map/ppermute | solution.py:526
  98.0 2.4 %shard_map.73 = f32[16,128]{1,0:T(8,128)} custom-call(s32[4]{0:T(128)S(1)} %pad_add_fusion.where, f32[16,6912]{1,0:T(8,128)S(1)} %pad_maximum_fusion.own0, f32[16,6912]{1,0:T(8,128)S(1)} %collective-permute-done.14.oth0, f32[16,6912]{1,0:T(8,128)S(1)} %collective-permute-done.15.own1, f32[16,6912]{1,0:T(8,128)S(1)} %collective-permute-done.16.oth1, ...), custom_call_target="tpu_custom_call" | custom-call | tf_op jit(solution)/shard_map/pallas_call | solution.py:428
  100.4 7.5 %all-to-all-start = ((f32[16,1,128]{2,1,0:T(1,128)}), f32[16,1,128]{2,1,0:T(1,128)S(1)}, u32[]{:S(2)}, u32[]{:S(2)}) async-start(f32[16,1,128]{2,1,0:T(1,128)} %bitcast.5), calls=%async_computation | async-start | bytes 16384 | tf_op jit(solution)/shard_map/all_to_all | solution.py:591
  108.0 1.5 %shard_map.71 = f32[4,27648]{1,0:T(4,128)} custom-call(s32[4]{0:T(128)S(1)} %pad_add_fusion.where, f32[4,27648]{1,0:T(4,128)S(1)} %get-tuple-element.57.near, f32[4,27648]{1,0:T(4,128)S(1)} %collective-permute-done.8.far, f32[2,27648]{1,0:T(2,128)S(1)} %collective-permute-done.9.owed_a, f32[2,27648]{1,0:T(2,128)S(1)} %collective-permute-done.10.owed_b), custom_call_target="tpu_custom_call" | custom-call | tf_op jit(solution)/shard_map/pallas_call | solution.py:428
  109.4 4.0 %all-to-all-done = f32[16,1,128]{2,1,0:T(1,128)S(1)} async-done(((f32[16,1,128]{2,1,0:T(1,128)}), f32[16,1,128]{2,1,0:T(1,128)S(1)}, u32[]{:S(2)}, u32[]{:S(2)}) %all-to-all-start) | async-done | bytes 8224 | tf_op jit(solution)/shard_map/all_to_all | solution.py:591
  (52 shorter events, 13.0 us)
Async XLA Ops:
  0.6 11.8 %collective-permute-start = (f32[4,27648]{1,0:T(4,128)}, f32[4,27648]{1,0:T(4,128)S(1)}, u32[]{:S(2)}, u32[]{:S(2)}) collective-permute-start(f32[4,27648]{1,0:T(4,128)} %orbitals.3), channel_id=1, source_target_pairs={{0,2},{1,3},{2,0},{3,1},{4,6},{5,7},{6,4},{7,5},{8,10},{9,11},{10,... | collective-permute-start | bytes 1327112 | tf_op jit(solution)/shard_map/ppermute | solution.py:526
  4.0 21.7 %collective-permute-start.5 = (f32[2,27648]{1,0:T(2,128)S(1)}, f32[2,27648]{1,0:T(2,128)S(1)}, u32[]{:S(2)}, u32[]{:S(2)}) collective-permute-start(f32[2,27648]{1,0:T(2,128)S(1)} %get-tuple-element.42), channel_id=1, source_target_pairs={{0,4},{1,5},{2,6},{3,7},{4,8},{5,9},{6,10},{7,11},{8,12},{9,13},{1... | collective-permute-start | bytes 663560 | tf_op jit(solution)/shard_map/ppermute | solution.py:526
  6.5 22.0 %collective-permute-start.4 = (f32[4,27648]{1,0:T(4,128)}, f32[4,27648]{1,0:T(4,128)S(1)}, u32[]{:S(2)}, u32[]{:S(2)}) collective-permute-start(f32[4,27648]{1,0:T(4,128)} %orbitals.3), channel_id=1, source_target_pairs={{0,1},{1,0},{2,3},{3,2},{4,5},{5,4},{6,7},{7,6},{8,9},{9,8},{10,11... | collective-permute-start | bytes 1327112 | tf_op jit(solution)/shard_map/ppermute | solution.py:526
  7.7 19.5 %collective-permute-start.2 = (f32[2,27648]{1,0:T(2,128)S(1)}, f32[2,27648]{1,0:T(2,128)S(1)}, u32[]{:S(2)}, u32[]{:S(2)}) collective-permute-start(f32[2,27648]{1,0:T(2,128)S(1)} %get-tuple-element.36), channel_id=1, source_target_pairs={{0,6},{1,7},{2,4},{3,5},{4,10},{5,11},{6,8},{7,9},{8,14},{9,15},{1... | collective-permute-start | bytes 663560 | tf_op jit(solution)/shard_map/ppermute | solution.py:526
  12.4 25.8 %collective-permute-start.1 = (f32[4,27648]{1,0:T(4,128)S(1)}, f32[4,27648]{1,0:T(4,128)S(1)}, u32[]{:S(2)}, u32[]{:S(2)}) collective-permute-start(f32[4,27648]{1,0:T(4,128)S(1)} %collective-permute-done.two), channel_id=1, source_target_pairs={{0,1},{1,0},{2,3},{3,2},{4,5},{5,4},{6,7},{7,6},{8,9},{9,8},{10,11... | collective-permute-start | bytes 1327112 | tf_op jit(solution)/shard_map/ppermute | solution.py:526
  27.2 11.0 %collective-permute-start.3 = (f32[2,27648]{1,0:T(2,128)S(1)}, f32[2,27648]{1,0:T(2,128)S(1)}, u32[]{:S(2)}, u32[]{:S(2)}) collective-permute-start(f32[2,27648]{1,0:T(2,128)S(1)} %collective-permute-done.2.low_b), channel_id=1, source_target_pairs={{0,1},{1,0},{2,3},{3,2},{4,5},{5,4},{6,7},{7,6},{8,9},{9,8},{10,11... | collective-permute-start | bytes 663560 | tf_op jit(solution)/shard_map/ppermute | solution.py:526
  28.3 22.0 %collective-permute-start.11 = (f32[4,6912]{1,0:T(4,128)S(1)}, f32[4,6912]{1,0:T(4,128)S(1)}, u32[]{:S(2)}, u32[]{:S(2)}) collective-permute-start(f32[4,6912]{1,0:T(4,128)S(1)} %get-tuple-element.62), channel_id=1, source_target_pairs={{0,8},{1,9},{2,10},{3,11},{4,12},{5,13},{6,14},{7,15},{8,0},{9,1},... | collective-permute-start | bytes 331784 | tf_op jit(solution)/shard_map/ppermute | solution.py:526
  28.4 21.9 %collective-permute-start.12 = (f32[4,6912]{1,0:T(4,128)S(1)}, f32[4,6912]{1,0:T(4,128)S(1)}, u32[]{:S(2)}, u32[]{:S(2)}) collective-permute-start(f32[4,6912]{1,0:T(4,128)S(1)} %get-tuple-element.63), channel_id=1, source_target_pairs={{0,16},{1,17},{2,18},{3,19},{4,20},{5,21},{6,22},{7,23},{8,24},{9,... | collective-permute-start | bytes 331784 | tf_op jit(solution)/shard_map/ppermute | solution.py:526
  28.5 21.8 %collective-permute-start.13 = (f32[4,6912]{1,0:T(4,128)S(1)}, f32[4,6912]{1,0:T(4,128)S(1)}, u32[]{:S(2)}, u32[]{:S(2)}) collective-permute-start(f32[4,6912]{1,0:T(4,128)S(1)} %get-tuple-element.64), channel_id=1, source_target_pairs={{0,24},{1,25},{2,26},{3,27},{4,28},{5,29},{6,30},{7,31},{8,16},{9,... | collective-permute-start | bytes 331784 | tf_op jit(solution)/shard_map/ppermute | solution.py:526
  48.8 17.5 %collective-permute-start.7 = (f32[10,27648]{1,0:T(8,128)S(1)}, f32[10,27648]{1,0:T(8,128)S(1)}, u32[]{:S(2)}, u32[]{:S(2)}) collective-permute-start(f32[10,27648]{1,0:T(8,128)S(1)} %get-tuple-element.56), channel_id=1, source_target_pairs={{0,1},{1,0},{2,3},{3,2},{4,5},{5,4},{6,7},{7,6},{8,9},{9,8},{10,11... | collective-permute-start | bytes 3317768 | tf_op jit(solution)/shard_map/ppermute | solution.py:526
  50.4 13.3 %collective-permute-start.14 = (f32[16,6912]{1,0:T(8,128)S(1)}, f32[16,6912]{1,0:T(8,128)S(1)}, u32[]{:S(2)}, u32[]{:S(2)}) collective-permute-start(f32[16,6912]{1,0:T(8,128)S(1)} %pad_maximum_fusion.own0), channel_id=1, source_target_pairs={{0,4},{1,5},{2,6},{3,7},{4,0},{5,1},{6,2},{7,3},{8,12},{9,13},{10,... | collective-permute-start | bytes 1327112 | tf_op jit(solution)/shard_map/ppermute | solution.py:526
  50.5 16.8 %collective-permute-start.15 = (f32[16,6912]{1,0:T(8,128)S(1)}, f32[16,6912]{1,0:T(8,128)S(1)}, u32[]{:S(2)}, u32[]{:S(2)}) collective-permute-start(f32[16,6912]{1,0:T(8,128)S(1)} %pad_maximum_fusion.own0), channel_id=1, source_target_pairs={{0,32},{1,33},{2,34},{3,35},{4,36},{5,37},{6,38},{7,39},{8,40},{9,... | collective-permute-start | bytes 1327112 | tf_op jit(solution)/shard_map/ppermute | solution.py:526
  63.7 12.0 %collective-permute-start.16 = (f32[16,6912]{1,0:T(8,128)S(1)}, f32[16,6912]{1,0:T(8,128)S(1)}, u32[]{:S(2)}, u32[]{:S(2)}) collective-permute-start(f32[16,6912]{1,0:T(8,128)S(1)} %collective-permute-done.14.oth0), channel_id=1, source_target_pairs={{0,32},{1,33},{2,34},{3,35},{4,36},{5,37},{6,38},{7,39},{8,40},{9,... | collective-permute-start | bytes 1327112 | tf_op jit(solution)/shard_map/ppermute | solution.py:526
  63.7 12.1 %collective-permute-start.19 = (f32[16,6912]{1,0:T(8,128)S(1)}, f32[16,6912]{1,0:T(8,128)S(1)}, u32[]{:S(2)}, u32[]{:S(2)}) collective-permute-start(f32[16,6912]{1,0:T(8,128)S(1)} %collective-permute-done.14.oth0), channel_id=1, source_target_pairs={{0,96},{1,97},{2,98},{3,99},{4,100},{5,101},{6,102},{7,103},{8,104... | collective-permute-start | bytes 1327112 | tf_op jit(solution)/shard_map/ppermute | solution.py:526
  67.1 23.5 %collective-permute-start.8 = (f32[4,27648]{1,0:T(4,128)S(1)}, f32[4,27648]{1,0:T(4,128)S(1)}, u32[]{:S(2)}, u32[]{:S(2)}) collective-permute-start(f32[4,27648]{1,0:T(4,128)S(1)} %get-tuple-element.58), channel_id=1, source_target_pairs={{0,2},{1,3},{2,0},{3,1},{4,6},{5,7},{6,4},{7,5},{8,10},{9,11},{10,... | collective-permute-start | bytes 1327112 | tf_op jit(solution)/shard_map/ppermute | solution.py:526
  67.2 24.3 %collective-permute-start.21 = (f32[16,6912]{1,0:T(8,128)S(1)}, f32[16,6912]{1,0:T(8,128)S(1)}, u32[]{:S(2)}, u32[]{:S(2)}) collective-permute-start(f32[16,6912]{1,0:T(8,128)S(1)} %pad_maximum_fusion.own0), channel_id=1, source_target_pairs={{0,96},{1,97},{2,98},{3,99},{4,100},{5,101},{6,102},{7,103},{8,104... | collective-permute-start | bytes 1327112 | tf_op jit(solution)/shard_map/ppermute | solution.py:526
  67.3 25.1 %collective-permute-start.17 = (f32[16,6912]{1,0:T(8,128)S(1)}, f32[16,6912]{1,0:T(8,128)S(1)}, u32[]{:S(2)}, u32[]{:S(2)}) collective-permute-start(f32[16,6912]{1,0:T(8,128)S(1)} %collective-permute-done.15.own1), channel_id=1, source_target_pairs={{0,32},{1,33},{2,34},{3,35},{4,36},{5,37},{6,38},{7,39},{8,40},{9,... | collective-permute-start | bytes 1327112 | tf_op jit(solution)/shard_map/ppermute | solution.py:526
  75.7 12.2 %collective-permute-start.10 = (f32[2,27648]{1,0:T(2,128)S(1)}, f32[2,27648]{1,0:T(2,128)S(1)}, u32[]{:S(2)}, u32[]{:S(2)}) collective-permute-start(f32[2,27648]{1,0:T(2,128)S(1)} %get-tuple-element.60), channel_id=1, source_target_pairs={{0,126},{1,127},{2,124},{3,125},{4,2},{5,3},{6,0},{7,1},{8,6},{9,7... | collective-permute-start | bytes 663560 | tf_op jit(solution)/shard_map/ppermute | solution.py:526
  75.7 12.2 %collective-permute-start.9 = (f32[2,27648]{1,0:T(2,128)S(1)}, f32[2,27648]{1,0:T(2,128)S(1)}, u32[]{:S(2)}, u32[]{:S(2)}) collective-permute-start(f32[2,27648]{1,0:T(2,128)S(1)} %get-tuple-element.59), channel_id=1, source_target_pairs={{0,124},{1,125},{2,126},{3,127},{4,0},{5,1},{6,2},{7,3},{8,4},{9,5... | collective-permute-start | bytes 663560 | tf_op jit(solution)/shard_map/ppermute | solution.py:526
  87.9 7.4 %collective-permute-start.18 = (f32[8,6912]{1,0:T(8,128)S(1)}, f32[8,6912]{1,0:T(8,128)S(1)}, u32[]{:S(2)}, u32[]{:S(2)}) collective-permute-start(f32[8,6912]{1,0:T(8,128)S(1)} %slice.8), channel_id=1, source_target_pairs={{0,32},{1,33},{2,34},{3,35},{4,36},{5,37},{6,38},{7,39},{8,40},{9,... | collective-permute-start | bytes 663560 | tf_op jit(solution)/shard_map/ppermute | solution.py:526
  87.9 7.4 %collective-permute-start.20 = (f32[8,6912]{1,0:T(8,128)S(1)}, f32[8,6912]{1,0:T(8,128)S(1)}, u32[]{:S(2)}, u32[]{:S(2)}) collective-permute-start(f32[8,6912]{1,0:T(8,128)S(1)} %slice.9), channel_id=1, source_target_pairs={{0,96},{1,97},{2,98},{3,99},{4,100},{5,101},{6,102},{7,103},{8,104... | collective-permute-start | bytes 663560 | tf_op jit(solution)/shard_map/ppermute | solution.py:526
  91.4 5.9 %collective-permute-start.23 = (f32[4,6912]{1,0:T(4,128)S(1)}, f32[4,6912]{1,0:T(4,128)S(1)}, u32[]{:S(2)}, u32[]{:S(2)}) collective-permute-start(f32[4,6912]{1,0:T(4,128)S(1)} %get-tuple-element.68), channel_id=1, source_target_pairs={{0,16},{1,17},{2,18},{3,19},{4,20},{5,21},{6,22},{7,23},{8,24},{9,... | collective-permute-start | bytes 331784 | tf_op jit(solution)/shard_map/ppermute | solution.py:526
  92.3 5.6 %collective-permute-start.24 = (f32[4,6912]{1,0:T(4,128)S(1)}, f32[4,6912]{1,0:T(4,128)S(1)}, u32[]{:S(2)}, u32[]{:S(2)}) collective-permute-start(f32[4,6912]{1,0:T(4,128)S(1)} %get-tuple-element.69), channel_id=1, source_target_pairs={{0,24},{1,25},{2,26},{3,27},{4,28},{5,29},{6,30},{7,31},{8,16},{9,... | collective-permute-start | bytes 331784 | tf_op jit(solution)/shard_map/ppermute | solution.py:526
  100.4 13.0 %all-to-all-start = ((f32[16,1,128]{2,1,0:T(1,128)}), f32[16,1,128]{2,1,0:T(1,128)S(1)}, u32[]{:S(2)}, u32[]{:S(2)}) async-start(f32[16,1,128]{2,1,0:T(1,128)} %bitcast.5), calls=%async_computation | async-start | bytes 16384 | tf_op jit(solution)/shard_map/all_to_all | solution.py:591
  (6 other events, 10.1 us)

commit v14 on v13

--- a/solution.py
+++ b/solution.py
@@ -96,13 +96,21 @@
     return np.stack(slow).astype(np.float32), np.stack(fast).astype(np.float32)
 
 
-def tables_kernel(slow, fast, kern_in, third_in, hi_there, lo_there, hi_back, lo_back, kern, third):
-    kern[...] = kern_in[...]
-    third[...] = third_in[...]
+def packed_tables():
+    slow, fast = factor_tables()
+    kern = kernel_values().reshape(3, 16, 9, 256).transpose(2, 0, 1, 3).reshape(27, 16, 256)
+    return np.concatenate([slow, fast, thirds()[None], kern])
+
+
+def tables_kernel(packed, hi_there, lo_there, hi_back, lo_back, kern, third):
+    third[...] = packed[8]
+    for g in range(9):
+        for r in range(3):
+            kern[16 * r : 16 * r + 16, 256 * g : 256 * g + 256] = packed[9 + 3 * g + r]
     for way, (hi, lo) in enumerate(((hi_there, lo_there), (hi_back, lo_back))):
         for k in range(4):
             for u in range(16):
-                w = fast[2 * way + k % 2] * slow[2 * way + k // 2, u : u + 1, :]
+                w = packed[4 + 2 * way + k % 2] * packed[2 * way + k // 2, u : u + 1, :]
                 top = w.astype(BF16)
                 hi[k, 16 * u : 16 * u + 16, :] = top
                 lo[k, 16 * u : 16 * u + 16, :] = (w - top.astype(F32)).astype(BF16)
@@ -114,7 +122,7 @@
     return pl.pallas_call(
         tables_kernel, out_shape=out, name="plane_tables",
         compiler_params=pltpu.CompilerParams(vmem_limit_bytes=8 << 20),
-    )(*[jnp.asarray(a) for a in (*factor_tables(), kernel_values(), thirds())])
+    )(jnp.asarray(packed_tables()))
 
 
 def t16(f):

time: 115 us -> 112 us (0.974)
  local copies, waits for them, and re-layouts: 4.1 us -> 1.76 us
    unnamed x8 -> x2, local copies, waits for them, and re-layouts: 3.41 us -> 1.06 us
where the time goes in v14:
time: 112 us
  waiting for transfers between devices  50.5 us (45%)
  starting transfers between devices  37.5 us (33%)
  Pallas kernels  20.8 us (19%)
  local copies, waits for them, and re-layouts  1.76 us (2%)
    ppermute x25, waiting for transfers between devices, move(): return lax.ppermute(value, BOTH, pairs)  46.7 us
    ppermute x25, starting transfers between devices, move(): return lax.ppermute(value, BOTH, pairs)  30 us
    pallas_call x6, Pallas kernels, call(): pl.pallas_call(body, out_shape=[jax.ShapeDtypeStruct(shape, F32) for shap...  7.64 us
    all_to_all x1, starting transfers between devices, step(): lax.all_to_all(sums, BOTH, 0, 0, tiled=True, axis_index_groups=groups)  7.51 us
    pallas_call x1, Pallas kernels, spectrum(): pl.pallas_call(spectrum_kernel, out_shape=STATE + [jax.ShapeDtypeStruct((...  5.62 us
    pallas_call x1, Pallas kernels, terms(): pl.pallas_call(terms_kernel, out_shape=[jax.ShapeDtypeStruct(shape, F32)...  5.03 us
    all_to_all x1, waiting for transfers between devices, step(): lax.all_to_all(sums, BOTH, 0, 0, tiled=True, axis_index_groups=groups)  3.87 us
  transfers between devices with their start and end apart: 26, of which 8 were waited for; matrix products, arithmetic and copies ran while one was open for 0% of the time, Pallas kernels for 16%

profile of v14, /device:TPU:1, one launch (start us, length us, event | category | flops | bytes accessed | tf_op | source)
XLA Modules:
  0.0 111.7 jit_solution(5089768639436391746)
XLA Ops:
  0.6 2.1 %collective-permute-start = (f32[4,27648]{1,0:T(4,128)}, f32[4,27648]{1,0:T(4,128)S(1)}, u32[]{:S(2)}, u32[]{:S(2)}) collective-permute-start(f32[4,27648]{1,0:T(4,128)} %orbitals.3), channel_id=1, source_target_pairs={{0,2},{1,3},{2,0},{3,1},{4,6},{5,7},{6,4},{7,5},{8,10},{9,11},{10,... | collective-permute-start | bytes 1327112 | tf_op jit(solution)/shard_map/ppermute | solution.py:534
  4.0 2.5 %collective-permute-start.5 = (f32[2,27648]{1,0:T(2,128)S(1)}, f32[2,27648]{1,0:T(2,128)S(1)}, u32[]{:S(2)}, u32[]{:S(2)}) collective-permute-start(f32[2,27648]{1,0:T(2,128)S(1)} %get-tuple-element.42), channel_id=1, source_target_pairs={{0,4},{1,5},{2,6},{3,7},{4,8},{5,9},{6,10},{7,11},{8,12},{9,13},{1... | collective-permute-start | bytes 663560 | tf_op jit(solution)/shard_map/ppermute | solution.py:534
  8.9 3.5 %collective-permute-done.two = f32[4,27648]{1,0:T(4,128)S(1)} collective-permute-done((f32[4,27648]{1,0:T(4,128)}, f32[4,27648]{1,0:T(4,128)S(1)}, u32[]{:S(2)}, u32[]{:S(2)}) %collective-permute-start) | collective-permute-done | bytes 442400 | tf_op jit(solution)/shard_map/ppermute | solution.py:534
  12.4 2.9 %collective-permute-start.1 = (f32[4,27648]{1,0:T(4,128)S(1)}, f32[4,27648]{1,0:T(4,128)S(1)}, u32[]{:S(2)}, u32[]{:S(2)}) collective-permute-start(f32[4,27648]{1,0:T(4,128)S(1)} %collective-permute-done.two), channel_id=1, source_target_pairs={{0,1},{1,0},{2,3},{3,2},{4,5},{5,4},{6,7},{7,6},{8,9},{9,8},{10,11... | collective-permute-start | bytes 1327112 | tf_op jit(solution)/shard_map/ppermute | solution.py:534
  15.3 10.3 %collective-permute-done.5.low_a = f32[2,27648]{1,0:T(2,128)S(1)} collective-permute-done((f32[2,27648]{1,0:T(2,128)S(1)}, f32[2,27648]{1,0:T(2,128)S(1)}, u32[]{:S(2)}, u32[]{:S(2)}) %collective-permute-start.5) | collective-permute-done | bytes 221216 | tf_op jit(solution)/shard_map/ppermute | solution.py:534
  25.6 1.5 %collective-permute-start.6 = (f32[2,27648]{1,0:T(2,128)S(1)}, f32[2,27648]{1,0:T(2,128)S(1)}, u32[]{:S(2)}, u32[]{:S(2)}) collective-permute-start(f32[2,27648]{1,0:T(2,128)S(1)} %collective-permute-done.5.low_a), channel_id=1, source_target_pairs={{0,1},{1,0},{2,3},{3,2},{4,5},{5,4},{6,7},{7,6},{8,9},{9,8},{10,11... | collective-permute-start | bytes 663560 | tf_op jit(solution)/shard_map/ppermute | solution.py:534
  28.5 3.7 %collective-permute-start.13 = (f32[4,6912]{1,0:T(4,128)S(1)}, f32[4,6912]{1,0:T(4,128)S(1)}, u32[]{:S(2)}, u32[]{:S(2)}) collective-permute-start(f32[4,6912]{1,0:T(4,128)S(1)} %get-tuple-element.64), channel_id=1, source_target_pairs={{0,24},{1,25},{2,26},{3,27},{4,28},{5,29},{6,30},{7,31},{8,16},{9,... | collective-permute-start | bytes 331784 | tf_op jit(solution)/shard_map/ppermute | solution.py:534
  33.6 2.2 %first_densities.1 = (f32[48,8,2304]{2,1,0:T(8,128)S(1)}, f32[48,8,2304]{2,1,0:T(8,128)S(1)}, bf16[384,2304]{1,0:T(8,128)(2,1)S(1)}, bf16[384,2304]{1,0:T(8,128)(2,1)S(1)}) custom-call(s32[1]{0:T(128)} %bitcast.q_ref, f32[4,27648]{1,0:T(4,128)S(1)} %get-tuple-element.41.own, f32[4,27648]{1,0:T(4,128)S(1)} %collective-permute-done.4.one, ...), custom_call_target="tpu_custom_call" | custom-call | tf_op jit(solution)/shard_map/first_densities/pallas_call | solution.py:394
  35.8 5.6 %spectrum.1 = (f32[48,8,2304]{2,1,0:T(8,128)S(1)}, f32[48,8,2304]{2,1,0:T(8,128)S(1)}, bf16[384,2304]{1,0:T(8,128)(2,1)S(1)}, bf16[384,2304]{1,0:T(8,128)(2,1)S(1)}, f32[384,2304]{1,0:T(8,128)S(1)}) custom-call(s32[1]{0:T(128)} %bitcast.q_ref, ...), custom_call_target="tpu_custom_call", output_to_operand_aliasing={{0}: (9, {}), {1}: (10, {}), {2}: (11, {}), {3}: (12, {})} | custom-call | tf_op jit(solution)/shard_map/spectrum/pallas_call | solution.py:405
  41.5 5.0 %terms.1 = (f32[4,27648]{1,0:T(4,128)S(1)}, f32[4,27648]{1,0:T(4,128)S(1)}, f32[10,27648]{1,0:T(8,128)S(1)}, f32[1,27648]{1,0:T(1,128)S(1)}, f32[1,27648]{1,0:T(1,128)S(1)}) custom-call(s32[1]{0:T(128)} %bitcast.q_ref, f32[48,8,2304]{2,1,0:T(8,128)S(1)} %get-tuple-element.47.right, f32[48,8,2304]{2,1,0:T(8,128)S(1)} %get-tuple-element.48.left, ...), custom_call_target="tpu_custom_call" | custom-call | tf_op jit(solution)/shard_map/terms/pallas_call | solution.py:417
  46.5 1.4 %collective-permute-start.7 = (f32[10,27648]{1,0:T(8,128)S(1)}, f32[10,27648]{1,0:T(8,128)S(1)}, u32[]{:S(2)}, u32[]{:S(2)}) collective-permute-start(f32[10,27648]{1,0:T(8,128)S(1)} %get-tuple-element.56), channel_id=1, source_target_pairs={{0,1},{1,0},{2,3},{3,2},{4,5},{5,4},{6,7},{7,6},{8,9},{9,8},{10,11... | collective-permute-start | bytes 3317768 | tf_op jit(solution)/shard_map/ppermute | solution.py:534
  48.2 13.1 %collective-permute-done.14.oth0 = f32[16,6912]{1,0:T(8,128)S(1)} collective-permute-done((f32[16,6912]{1,0:T(8,128)S(1)}, f32[16,6912]{1,0:T(8,128)S(1)}, u32[]{:S(2)}, u32[]{:S(2)}) %collective-permute-start.14) | collective-permute-done | bytes 442400 | tf_op jit(solution)/shard_map/ppermute | solution.py:534
  61.3 2.7 %collective-permute-start.19 = (f32[16,6912]{1,0:T(8,128)S(1)}, f32[16,6912]{1,0:T(8,128)S(1)}, u32[]{:S(2)}, u32[]{:S(2)}) collective-permute-start(f32[16,6912]{1,0:T(8,128)S(1)} %collective-permute-done.14.oth0), channel_id=1, source_target_pairs={{0,96},{1,97},{2,98},{3,99},{4,100},{5,101},{6,102},{7,103},{8,104... | collective-permute-start | bytes 1327112 | tf_op jit(solution)/shard_map/ppermute | solution.py:534
  64.9 1.4 %collective-permute-start.17 = (f32[16,6912]{1,0:T(8,128)S(1)}, f32[16,6912]{1,0:T(8,128)S(1)}, u32[]{:S(2)}, u32[]{:S(2)}) collective-permute-start(f32[16,6912]{1,0:T(8,128)S(1)} %collective-permute-done.15.own1), channel_id=1, source_target_pairs={{0,32},{1,33},{2,34},{3,35},{4,36},{5,37},{6,38},{7,39},{8,40},{9,... | collective-permute-start | bytes 1327112 | tf_op jit(solution)/shard_map/ppermute | solution.py:534
  66.4 7.0 %collective-permute-done.16.oth1 = f32[16,6912]{1,0:T(8,128)S(1)} collective-permute-done((f32[16,6912]{1,0:T(8,128)S(1)}, f32[16,6912]{1,0:T(8,128)S(1)}, u32[]{:S(2)}, u32[]{:S(2)}) %collective-permute-start.16) | collective-permute-done | bytes 442400 | tf_op jit(solution)/shard_map/ppermute | solution.py:534
  73.4 2.1 %collective-permute-start.9 = (f32[2,27648]{1,0:T(2,128)S(1)}, f32[2,27648]{1,0:T(2,128)S(1)}, u32[]{:S(2)}, u32[]{:S(2)}) collective-permute-start(f32[2,27648]{1,0:T(2,128)S(1)} %get-tuple-element.59), channel_id=1, source_target_pairs={{0,124},{1,125},{2,126},{3,127},{4,0},{5,1},{6,2},{7,3},{8,4},{9,5... | collective-permute-start | bytes 663560 | tf_op jit(solution)/shard_map/ppermute | solution.py:534
  75.5 10.1 %collective-permute-done.10.owed_b = f32[2,27648]{1,0:T(2,128)S(1)} collective-permute-done((f32[2,27648]{1,0:T(2,128)S(1)}, f32[2,27648]{1,0:T(2,128)S(1)}, u32[]{:S(2)}, u32[]{:S(2)}) %collective-permute-start.10) | collective-permute-done | bytes 221216 | tf_op jit(solution)/shard_map/ppermute | solution.py:534
  85.6 2.7 %collective-permute-start.20 = (f32[8,6912]{1,0:T(8,128)S(1)}, f32[8,6912]{1,0:T(8,128)S(1)}, u32[]{:S(2)}, u32[]{:S(2)}) collective-permute-start(f32[8,6912]{1,0:T(8,128)S(1)} %slice.9), channel_id=1, source_target_pairs={{0,96},{1,97},{2,98},{3,99},{4,100},{5,101},{6,102},{7,103},{8,104... | collective-permute-start | bytes 663560 | tf_op jit(solution)/shard_map/ppermute | solution.py:534
  90.0 3.0 %collective-permute-start.24 = (f32[4,6912]{1,0:T(4,128)S(1)}, f32[4,6912]{1,0:T(4,128)S(1)}, u32[]{:S(2)}, u32[]{:S(2)}) collective-permute-start(f32[4,6912]{1,0:T(4,128)S(1)} %get-tuple-element.69), channel_id=1, source_target_pairs={{0,24},{1,25},{2,26},{3,27},{4,28},{5,29},{6,30},{7,31},{8,16},{9,... | collective-permute-start | bytes 331784 | tf_op jit(solution)/shard_map/ppermute | solution.py:534
  93.0 2.1 %collective-permute-done.23.v2 = f32[4,6912]{1,0:T(4,128)S(1)} collective-permute-done((f32[4,6912]{1,0:T(4,128)S(1)}, f32[4,6912]{1,0:T(4,128)S(1)}, u32[]{:S(2)}, u32[]{:S(2)}) %collective-permute-start.23) | collective-permute-done | bytes 110624 | tf_op jit(solution)/shard_map/ppermute | solution.py:534
  95.7 2.4 %shard_map.46 = f32[16,128]{1,0:T(8,128)} custom-call(s32[4]{0:T(128)S(1)} %pad_add_fusion.where, f32[16,6912]{1,0:T(8,128)S(1)} %pad_maximum_fusion.own0, f32[16,6912]{1,0:T(8,128)S(1)} %collective-permute-done.14.oth0, f32[16,6912]{1,0:T(8,128)S(1)} %collective-permute-done.15.own1, f32[16,6912]{1,0:T(8,128)S(1)} %collective-permute-done.16.oth1, ...), custom_call_target="tpu_custom_call" | custom-call | tf_op jit(solution)/shard_map/pallas_call | solution.py:436
  98.1 7.5 %all-to-all-start = ((f32[16,1,128]{2,1,0:T(1,128)}), f32[16,1,128]{2,1,0:T(1,128)S(1)}, u32[]{:S(2)}, u32[]{:S(2)}) async-start(f32[16,1,128]{2,1,0:T(1,128)} %bitcast.5), calls=%async_computation | async-start | bytes 16384 | tf_op jit(solution)/shard_map/all_to_all | solution.py:599
  105.6 1.5 %shard_map.44 = f32[4,27648]{1,0:T(4,128)} custom-call(s32[4]{0:T(128)S(1)} %pad_add_fusion.where, f32[4,27648]{1,0:T(4,128)S(1)} %get-tuple-element.57.near, f32[4,27648]{1,0:T(4,128)S(1)} %collective-permute-done.8.far, f32[2,27648]{1,0:T(2,128)S(1)} %collective-permute-done.9.owed_a, f32[2,27648]{1,0:T(2,128)S(1)} %collective-permute-done.10.owed_b), custom_call_target="tpu_custom_call" | custom-call | tf_op jit(solution)/shard_map/pallas_call | solution.py:436
  107.1 3.9 %all-to-all-done = f32[16,1,128]{2,1,0:T(1,128)S(1)} async-done(((f32[16,1,128]{2,1,0:T(1,128)}), f32[16,1,128]{2,1,0:T(1,128)S(1)}, u32[]{:S(2)}, u32[]{:S(2)}) %all-to-all-start) | async-done | bytes 8224 | tf_op jit(solution)/shard_map/all_to_all | solution.py:599
  (46 shorter events, 10.6 us)
Async XLA Ops:
  0.6 11.8 %collective-permute-start = (f32[4,27648]{1,0:T(4,128)}, f32[4,27648]{1,0:T(4,128)S(1)}, u32[]{:S(2)}, u32[]{:S(2)}) collective-permute-start(f32[4,27648]{1,0:T(4,128)} %orbitals.3), channel_id=1, source_target_pairs={{0,2},{1,3},{2,0},{3,1},{4,6},{5,7},{6,4},{7,5},{8,10},{9,11},{10,... | collective-permute-start | bytes 1327112 | tf_op jit(solution)/shard_map/ppermute | solution.py:534
  4.0 21.7 %collective-permute-start.5 = (f32[2,27648]{1,0:T(2,128)S(1)}, f32[2,27648]{1,0:T(2,128)S(1)}, u32[]{:S(2)}, u32[]{:S(2)}) collective-permute-start(f32[2,27648]{1,0:T(2,128)S(1)} %get-tuple-element.42), channel_id=1, source_target_pairs={{0,4},{1,5},{2,6},{3,7},{4,8},{5,9},{6,10},{7,11},{8,12},{9,13},{1... | collective-permute-start | bytes 663560 | tf_op jit(solution)/shard_map/ppermute | solution.py:534
  6.5 22.0 %collective-permute-start.4 = (f32[4,27648]{1,0:T(4,128)}, f32[4,27648]{1,0:T(4,128)S(1)}, u32[]{:S(2)}, u32[]{:S(2)}) collective-permute-start(f32[4,27648]{1,0:T(4,128)} %orbitals.3), channel_id=1, source_target_pairs={{0,1},{1,0},{2,3},{3,2},{4,5},{5,4},{6,7},{7,6},{8,9},{9,8},{10,11... | collective-permute-start | bytes 1327112 | tf_op jit(solution)/shard_map/ppermute | solution.py:534
  7.7 19.5 %collective-permute-start.2 = (f32[2,27648]{1,0:T(2,128)S(1)}, f32[2,27648]{1,0:T(2,128)S(1)}, u32[]{:S(2)}, u32[]{:S(2)}) collective-permute-start(f32[2,27648]{1,0:T(2,128)S(1)} %get-tuple-element.36), channel_id=1, source_target_pairs={{0,6},{1,7},{2,4},{3,5},{4,10},{5,11},{6,8},{7,9},{8,14},{9,15},{1... | collective-permute-start | bytes 663560 | tf_op jit(solution)/shard_map/ppermute | solution.py:534
  12.4 23.4 %collective-permute-start.1 = (f32[4,27648]{1,0:T(4,128)S(1)}, f32[4,27648]{1,0:T(4,128)S(1)}, u32[]{:S(2)}, u32[]{:S(2)}) collective-permute-start(f32[4,27648]{1,0:T(4,128)S(1)} %collective-permute-done.two), channel_id=1, source_target_pairs={{0,1},{1,0},{2,3},{3,2},{4,5},{5,4},{6,7},{7,6},{8,9},{9,8},{10,11... | collective-permute-start | bytes 1327112 | tf_op jit(solution)/shard_map/ppermute | solution.py:534
  27.2 8.6 %collective-permute-start.3 = (f32[2,27648]{1,0:T(2,128)S(1)}, f32[2,27648]{1,0:T(2,128)S(1)}, u32[]{:S(2)}, u32[]{:S(2)}) collective-permute-start(f32[2,27648]{1,0:T(2,128)S(1)} %collective-permute-done.2.low_b), channel_id=1, source_target_pairs={{0,1},{1,0},{2,3},{3,2},{4,5},{5,4},{6,7},{7,6},{8,9},{9,8},{10,11... | collective-permute-start | bytes 663560 | tf_op jit(solution)/shard_map/ppermute | solution.py:534
  28.3 19.6 %collective-permute-start.11 = (f32[4,6912]{1,0:T(4,128)S(1)}, f32[4,6912]{1,0:T(4,128)S(1)}, u32[]{:S(2)}, u32[]{:S(2)}) collective-permute-start(f32[4,6912]{1,0:T(4,128)S(1)} %get-tuple-element.62), channel_id=1, source_target_pairs={{0,8},{1,9},{2,10},{3,11},{4,12},{5,13},{6,14},{7,15},{8,0},{9,1},... | collective-permute-start | bytes 331784 | tf_op jit(solution)/shard_map/ppermute | solution.py:534
  28.4 19.5 %collective-permute-start.12 = (f32[4,6912]{1,0:T(4,128)S(1)}, f32[4,6912]{1,0:T(4,128)S(1)}, u32[]{:S(2)}, u32[]{:S(2)}) collective-permute-start(f32[4,6912]{1,0:T(4,128)S(1)} %get-tuple-element.63), channel_id=1, source_target_pairs={{0,16},{1,17},{2,18},{3,19},{4,20},{5,21},{6,22},{7,23},{8,24},{9,... | collective-permute-start | bytes 331784 | tf_op jit(solution)/shard_map/ppermute | solution.py:534
  28.5 19.4 %collective-permute-start.13 = (f32[4,6912]{1,0:T(4,128)S(1)}, f32[4,6912]{1,0:T(4,128)S(1)}, u32[]{:S(2)}, u32[]{:S(2)}) collective-permute-start(f32[4,6912]{1,0:T(4,128)S(1)} %get-tuple-element.64), channel_id=1, source_target_pairs={{0,24},{1,25},{2,26},{3,27},{4,28},{5,29},{6,30},{7,31},{8,16},{9,... | collective-permute-start | bytes 331784 | tf_op jit(solution)/shard_map/ppermute | solution.py:534
  46.5 17.5 %collective-permute-start.7 = (f32[10,27648]{1,0:T(8,128)S(1)}, f32[10,27648]{1,0:T(8,128)S(1)}, u32[]{:S(2)}, u32[]{:S(2)}) collective-permute-start(f32[10,27648]{1,0:T(8,128)S(1)} %get-tuple-element.56), channel_id=1, source_target_pairs={{0,1},{1,0},{2,3},{3,2},{4,5},{5,4},{6,7},{7,6},{8,9},{9,8},{10,11... | collective-permute-start | bytes 3317768 | tf_op jit(solution)/shard_map/ppermute | solution.py:534
  48.0 13.3 %collective-permute-start.14 = (f32[16,6912]{1,0:T(8,128)S(1)}, f32[16,6912]{1,0:T(8,128)S(1)}, u32[]{:S(2)}, u32[]{:S(2)}) collective-permute-start(f32[16,6912]{1,0:T(8,128)S(1)} %pad_maximum_fusion.own0), channel_id=1, source_target_pairs={{0,4},{1,5},{2,6},{3,7},{4,0},{5,1},{6,2},{7,3},{8,12},{9,13},{10,... | collective-permute-start | bytes 1327112 | tf_op jit(solution)/shard_map/ppermute | solution.py:534
  48.1 16.8 %collective-permute-start.15 = (f32[16,6912]{1,0:T(8,128)S(1)}, f32[16,6912]{1,0:T(8,128)S(1)}, u32[]{:S(2)}, u32[]{:S(2)}) collective-permute-start(f32[16,6912]{1,0:T(8,128)S(1)} %pad_maximum_fusion.own0), channel_id=1, source_target_pairs={{0,32},{1,33},{2,34},{3,35},{4,36},{5,37},{6,38},{7,39},{8,40},{9,... | collective-permute-start | bytes 1327112 | tf_op jit(solution)/shard_map/ppermute | solution.py:534
  61.3 12.0 %collective-permute-start.16 = (f32[16,6912]{1,0:T(8,128)S(1)}, f32[16,6912]{1,0:T(8,128)S(1)}, u32[]{:S(2)}, u32[]{:S(2)}) collective-permute-start(f32[16,6912]{1,0:T(8,128)S(1)} %collective-permute-done.14.oth0), channel_id=1, source_target_pairs={{0,32},{1,33},{2,34},{3,35},{4,36},{5,37},{6,38},{7,39},{8,40},{9,... | collective-permute-start | bytes 1327112 | tf_op jit(solution)/shard_map/ppermute | solution.py:534
  61.3 12.1 %collective-permute-start.19 = (f32[16,6912]{1,0:T(8,128)S(1)}, f32[16,6912]{1,0:T(8,128)S(1)}, u32[]{:S(2)}, u32[]{:S(2)}) collective-permute-start(f32[16,6912]{1,0:T(8,128)S(1)} %collective-permute-done.14.oth0), channel_id=1, source_target_pairs={{0,96},{1,97},{2,98},{3,99},{4,100},{5,101},{6,102},{7,103},{8,104... | collective-permute-start | bytes 1327112 | tf_op jit(solution)/shard_map/ppermute | solution.py:534
  64.8 23.5 %collective-permute-start.8 = (f32[4,27648]{1,0:T(4,128)S(1)}, f32[4,27648]{1,0:T(4,128)S(1)}, u32[]{:S(2)}, u32[]{:S(2)}) collective-permute-start(f32[4,27648]{1,0:T(4,128)S(1)} %get-tuple-element.58), channel_id=1, source_target_pairs={{0,2},{1,3},{2,0},{3,1},{4,6},{5,7},{6,4},{7,5},{8,10},{9,11},{10,... | collective-permute-start | bytes 1327112 | tf_op jit(solution)/shard_map/ppermute | solution.py:534
  64.8 24.3 %collective-permute-start.21 = (f32[16,6912]{1,0:T(8,128)S(1)}, f32[16,6912]{1,0:T(8,128)S(1)}, u32[]{:S(2)}, u32[]{:S(2)}) collective-permute-start(f32[16,6912]{1,0:T(8,128)S(1)} %pad_maximum_fusion.own0), channel_id=1, source_target_pairs={{0,96},{1,97},{2,98},{3,99},{4,100},{5,101},{6,102},{7,103},{8,104... | collective-permute-start | bytes 1327112 | tf_op jit(solution)/shard_map/ppermute | solution.py:534
  64.9 25.1 %collective-permute-start.17 = (f32[16,6912]{1,0:T(8,128)S(1)}, f32[16,6912]{1,0:T(8,128)S(1)}, u32[]{:S(2)}, u32[]{:S(2)}) collective-permute-start(f32[16,6912]{1,0:T(8,128)S(1)} %collective-permute-done.15.own1), channel_id=1, source_target_pairs={{0,32},{1,33},{2,34},{3,35},{4,36},{5,37},{6,38},{7,39},{8,40},{9,... | collective-permute-start | bytes 1327112 | tf_op jit(solution)/shard_map/ppermute | solution.py:534
  73.4 12.2 %collective-permute-start.10 = (f32[2,27648]{1,0:T(2,128)S(1)}, f32[2,27648]{1,0:T(2,128)S(1)}, u32[]{:S(2)}, u32[]{:S(2)}) collective-permute-start(f32[2,27648]{1,0:T(2,128)S(1)} %get-tuple-element.60), channel_id=1, source_target_pairs={{0,126},{1,127},{2,124},{3,125},{4,2},{5,3},{6,0},{7,1},{8,6},{9,7... | collective-permute-start | bytes 663560 | tf_op jit(solution)/shard_map/ppermute | solution.py:534
  73.4 12.2 %collective-permute-start.9 = (f32[2,27648]{1,0:T(2,128)S(1)}, f32[2,27648]{1,0:T(2,128)S(1)}, u32[]{:S(2)}, u32[]{:S(2)}) collective-permute-start(f32[2,27648]{1,0:T(2,128)S(1)} %get-tuple-element.59), channel_id=1, source_target_pairs={{0,124},{1,125},{2,126},{3,127},{4,0},{5,1},{6,2},{7,3},{8,4},{9,5... | collective-permute-start | bytes 663560 | tf_op jit(solution)/shard_map/ppermute | solution.py:534
  85.6 7.4 %collective-permute-start.18 = (f32[8,6912]{1,0:T(8,128)S(1)}, f32[8,6912]{1,0:T(8,128)S(1)}, u32[]{:S(2)}, u32[]{:S(2)}) collective-permute-start(f32[8,6912]{1,0:T(8,128)S(1)} %slice.8), channel_id=1, source_target_pairs={{0,32},{1,33},{2,34},{3,35},{4,36},{5,37},{6,38},{7,39},{8,40},{9,... | collective-permute-start | bytes 663560 | tf_op jit(solution)/shard_map/ppermute | solution.py:534
  85.6 7.4 %collective-permute-start.20 = (f32[8,6912]{1,0:T(8,128)S(1)}, f32[8,6912]{1,0:T(8,128)S(1)}, u32[]{:S(2)}, u32[]{:S(2)}) collective-permute-start(f32[8,6912]{1,0:T(8,128)S(1)} %slice.9), channel_id=1, source_target_pairs={{0,96},{1,97},{2,98},{3,99},{4,100},{5,101},{6,102},{7,103},{8,104... | collective-permute-start | bytes 663560 | tf_op jit(solution)/shard_map/ppermute | solution.py:534
  89.1 5.9 %collective-permute-start.23 = (f32[4,6912]{1,0:T(4,128)S(1)}, f32[4,6912]{1,0:T(4,128)S(1)}, u32[]{:S(2)}, u32[]{:S(2)}) collective-permute-start(f32[4,6912]{1,0:T(4,128)S(1)} %get-tuple-element.68), channel_id=1, source_target_pairs={{0,16},{1,17},{2,18},{3,19},{4,20},{5,21},{6,22},{7,23},{8,24},{9,... | collective-permute-start | bytes 331784 | tf_op jit(solution)/shard_map/ppermute | solution.py:534
  90.0 5.7 %collective-permute-start.24 = (f32[4,6912]{1,0:T(4,128)S(1)}, f32[4,6912]{1,0:T(4,128)S(1)}, u32[]{:S(2)}, u32[]{:S(2)}) collective-permute-start(f32[4,6912]{1,0:T(4,128)S(1)} %get-tuple-element.69), channel_id=1, source_target_pairs={{0,24},{1,25},{2,26},{3,27},{4,28},{5,29},{6,30},{7,31},{8,16},{9,... | collective-permute-start | bytes 331784 | tf_op jit(solution)/shard_map/ppermute | solution.py:534
  98.1 12.9 %all-to-all-start = ((f32[16,1,128]{2,1,0:T(1,128)}), f32[16,1,128]{2,1,0:T(1,128)S(1)}, u32[]{:S(2)}, u32[]{:S(2)}) async-start(f32[16,1,128]{2,1,0:T(1,128)} %bitcast.5), calls=%async_computation | async-start | bytes 16384 | tf_op jit(solution)/shard_map/all_to_all | solution.py:599
  (3 other events, 7.8 us)
